TPU v7x, 128 devices: a whole 4x4x4 slice. The times are simulated.
128 devices in a mesh: gx: 32 (over z, x, core), gy: 4 (over y).
Axes of the slice: x: 4, y: 4, z: 4, core: 2. Of those that a mesh axis runs over, the one named last changes fastest.
Arguments:
- right_side: float32 [192, 64, 16, 128], P(None, 'gx', 'gy'), may hold values from -6 to 6
- coefficient: float32 [64, 16, 128], P('gx', 'gy'), may hold values from 0.5 to 2
- orientation: int32 [6, 64, 16, 128], P(None, 'gx', 'gy'), may hold values from 0 to 1
- aggregate_map: int32 [64, 16, 128], P('gx', 'gy'), may hold values from 0 to 511
- owner_map: int32 [65536, 1], P(('gx', 'gy')), may hold values from 0 to 31; in each aligned block of 512 rows (0 to 511, 512 to 1023, ...) at most 32 rows name the same one
- stiffness: float32 [192, 192], replicated, may hold values from -1 to 2
- face_blocks: float32 [6, 2, 192, 48], replicated, may hold values from -0.21875 to 0.21875
- prolong_basis: float32 [192, 24], replicated, may hold values from -0.4375 to 0.4375
- coarse_inverse: float32 [128, 32, 32, 24, 24], P(('gx', 'gy')), may hold values from -3 to 3
Outputs:
- solution_field: float32 [192, 64, 16, 128], P(None, 'gx', 'gy')
- residual: float32 [192, 64, 16, 128], P(None, 'gx', 'gy')
Inputs may be any that keep to these rules, and one draw needn't show every extreme that they name: `aggregate_map`: each value names an aggregate of the element's own device. `owner_map`: among the aggregates of one device (aligned blocks of 512 rows) no owner is named more than 32 times, a bound that some block reaches.
All inputs are finite; a program needn't handle non-finite values.
Results may differ from a plain program's by a relative error of at most 0.00011.
Values sent between devices are 32-bit elements; how exact they have to be, the bound alone decides.
No kernel may reach another device: no remote copies, remote signals or barrier semaphores. Data moves between devices by JAX's collectives and lax.ppermute only.
A program may use at most 128 MiB of HBM per device.

v0:
```python
import jax
import jax.numpy as jnp
from jax import lax
from jax.sharding import PartitionSpec as P

BLOCK = 192
TRACE = 48
CW = 24
DEGREE = 3


low_bound = 0.25
high_bound = 4.0


def padded(cells, sides, width):
    for axis, dim in sides:
        count = lax.axis_size(axis)
        ends = count - 1
        head = lax.slice_in_dim(cells, 0, width, axis=dim)
        tail = lax.slice_in_dim(cells, cells.shape[dim] - width, cells.shape[dim], axis=dim)
        cells = jnp.concatenate(
            [
                lax.ppermute(tail, axis, [(i, (i + 1) % count) for i in range(ends)]),
                cells,
                lax.ppermute(head, axis, [((i + 1) % count, i) for i in range(ends)]),
            ],
            axis=dim,
        )
    return cells


def face_traces(scaled):
    size_x, size_y, size_z = scaled.shape[1:]
    nodes = scaled.reshape(3, 4, 4, 4, size_x, size_y, size_z)

    def flat(t):
        return t.reshape(48, size_x, size_y, size_z)

    return (
        flat(nodes[:, 0]),
        flat(nodes[:, 3]),
        flat(nodes[:, :, 0]),
        flat(nodes[:, :, 3]),
        flat(nodes[:, :, :, 0]),
        flat(nodes[:, :, :, 3]),
    )


def neighbour_traces(scaled):
    first_x, last_x, first_y, last_y, first_z, last_z = face_traces(scaled)
    size_x, size_y, size_z = scaled.shape[1:]
    blank = jnp.zeros((48, size_x, size_y, 1), jnp.float32)
    lower_z = jnp.concatenate([blank, last_z[:, :, :, :-1]], axis=3)
    upper_z = jnp.concatenate([first_z[:, :, :, 1:], blank], axis=3)
    stacked = jnp.stack([first_x, last_x, first_y, last_y])
    wide = padded(stacked, (("gx", 2), ("gy", 3)), 1)
    lower_x = wide[1, :, 0:size_x, 1 : size_y + 1]
    upper_x = wide[0, :, 2 : size_x + 2, 1 : size_y + 1]
    lower_y = wide[3, :, 1 : size_x + 1, 0:size_y]
    upper_y = wide[2, :, 1 : size_x + 1, 2 : size_y + 2]
    return (lower_x, upper_x, lower_y, upper_y, lower_z, upper_z)


def operate(field, coefficient, orientation, stiffness, face_pairs):
    scaled = field * coefficient[None]
    neighbours = neighbour_traces(scaled)
    result = jnp.dot(stiffness, scaled.reshape(BLOCK, -1), precision=lax.Precision.HIGHEST)
    for direction in range(6):
        both = jnp.dot(
            face_pairs[direction],
            neighbours[direction].reshape(48, -1),
            precision=lax.Precision.HIGHEST,
        )
        pick = orientation[direction].reshape(1, -1) == 1
        result = result + jnp.where(pick, both[BLOCK:], both[:BLOCK])
    return result.reshape(field.shape)


def smooth(state, resid, apply_op):
    theta = 0.5 * (high_bound + low_bound)
    delta = 0.5 * (high_bound - low_bound)
    sigma = theta / delta
    rho = 1.0 / sigma
    step_dir = resid / theta
    state = state + step_dir
    resid = resid - apply_op(step_dir)
    for turn in range(DEGREE - 1):
        rho_new = 1.0 / (2.0 * sigma - rho)
        step_dir = rho_new * rho * step_dir + 2.0 * rho_new / delta * resid
        rho = rho_new
        state = state + step_dir
        resid = resid - apply_op(step_dir)
    return (state, resid)


def shards(
    right_side,
    coefficient,
    orientation,
    aggregate_map,
    owner_map,
    stiffness,
    face_blocks,
    prolong_basis,
    coarse_inverse,
):
    face_pairs = face_blocks.reshape(6, 2 * BLOCK, TRACE)

    def apply_op(v):
        return operate(v, coefficient, orientation, stiffness, face_pairs)

    state, resid = smooth(jnp.zeros_like(right_side), right_side, apply_op)
    agg_count = owner_map.shape[0]
    owner_count = coarse_inverse.shape[1]
    capacity = coarse_inverse.shape[2]
    element_hot = (
        aggregate_map.reshape(-1)[:, None] == jnp.arange(agg_count, dtype=jnp.int32)[None, :]
    ).astype(jnp.float32)
    owners = owner_map[:, 0]
    owner_hot = (owners[:, None] == jnp.arange(owner_count, dtype=jnp.int32)[None, :]).astype(
        jnp.int32
    )
    before = jnp.cumsum(owner_hot, axis=0) - owner_hot
    slot = jnp.sum(before * owner_hot, axis=1)
    target = owners * capacity + slot
    route_hot = (
        target[:, None] == jnp.arange(owner_count * capacity, dtype=jnp.int32)[None, :]
    ).astype(jnp.float32)
    projected = jnp.dot(prolong_basis.T, resid.reshape(BLOCK, -1), precision=lax.Precision.HIGHEST)
    coarse_rhs = jnp.dot(projected, element_hot, precision=lax.Precision.HIGHEST)
    outgoing = jnp.dot(coarse_rhs, route_hot, precision=lax.Precision.HIGHEST).reshape(
        CW, owner_count, capacity
    )
    arrived = lax.all_to_all(outgoing, "gx", split_axis=1, concat_axis=1, tiled=True)
    solved = jnp.einsum(
        "skab,bsk->ask", coarse_inverse[0], arrived, precision=lax.Precision.HIGHEST
    )
    returned = lax.all_to_all(solved, "gx", split_axis=1, concat_axis=1, tiled=True)
    coarse_sol = jnp.dot(returned.reshape(CW, -1), route_hot.T, precision=lax.Precision.HIGHEST)
    per_element = jnp.dot(coarse_sol, element_hot.T, precision=lax.Precision.HIGHEST)
    lifted = jnp.dot(prolong_basis, per_element, precision=lax.Precision.HIGHEST).reshape(
        right_side.shape
    )
    state = state + lifted
    resid = resid - apply_op(lifted)
    return smooth(state, resid, apply_op)


def solution(mesh):
    in_specs = (
        P(None, "gx", "gy", None),
        P("gx", "gy", None),
        P(None, "gx", "gy", None),
        P("gx", "gy", None),
        P(("gx", "gy"), None),
        P(),
        P(),
        P(),
        P(("gx", "gy"), None, None, None, None),
    )
    out_specs = (P(None, "gx", "gy", None), P(None, "gx", "gy", None))
    return jax.shard_map(shards, mesh=mesh, in_specs=in_specs, out_specs=out_specs, check_vma=False)
```

profile of v0, /device:TPU:32, one launch (start us, length us, event | category | flops | bytes accessed | tf_op | source)
XLA Modules:
  0.0 397.0 jit_solution(7097072410241259716)
XLA Ops:
  5.8 5.8 %collective-permute-start.1 = (f32[4,48,1,4,128]{4,3,2,1,0:T(4,128)}, f32[4,48,1,4,128]{4,3,2,1,0:T(4,128)S(1)}, u32[]{:S(2)}, u32[]{:S(2)}) collective-permute-start(f32[4,48,1,4,128]{4,3,2,1,0:T(4,128)} %get-tuple-element.98), channel_id=1, source_target_pairs={{4,0},{8,4},{12,8},{16,12},{20,16},{24,20},{28,24},{32,28},{36,32}... | collective-permute-start | bytes 1179656 | tf_op jit(solution)/shard_map/ppermute | solution.py:26
  23.2 4.4 %collective-permute-start.2 = (f32[4,48,4,1,128]{4,3,2,1,0:T(1,128)}, f32[4,48,4,1,128]{4,3,2,1,0:T(1,128)}, u32[]{:S(2)}, u32[]{:S(2)}) collective-permute-start(f32[4,48,4,1,128]{4,3,2,1,0:T(1,128)} %get-tuple-element.38), channel_id=1, source_target_pairs={{0,1},{1,2},{2,3},{4,5},{5,6},{6,7},{8,9},{9,10},{10,11},{12,13},{... | collective-permute-start | bytes 1179656 | tf_op jit(solution)/shard_map/ppermute | solution.py:24
  34.7 3.4 collective-permute-done.3
  51.4 5.8 %collective-permute-start.5 = (f32[4,48,1,4,128]{4,3,2,1,0:T(4,128)}, f32[4,48,1,4,128]{4,3,2,1,0:T(4,128)}, u32[]{:S(2)}, u32[]{:S(2)}) collective-permute-start(f32[4,48,1,4,128]{4,3,2,1,0:T(4,128)} %get-tuple-element.90), channel_id=1, source_target_pairs={{4,0},{8,4},{12,8},{16,12},{20,16},{24,20},{28,24},{32,28},{36,32}... | collective-permute-start | bytes 1179656 | tf_op jit(solution)/shard_map/ppermute | solution.py:26
  63.9 3.6 convolution_bitcast_fusion.30
  67.5 2.8 pad_maximum_fusion.42
  70.3 3.5 collective-permute-start.6
  105.2 5.8 %collective-permute-start.9 = (f32[4,48,1,4,128]{4,3,2,1,0:T(4,128)}, f32[4,48,1,4,128]{4,3,2,1,0:T(4,128)S(1)}, u32[]{:S(2)}, u32[]{:S(2)}) collective-permute-start(f32[4,48,1,4,128]{4,3,2,1,0:T(4,128)} %get-tuple-element.82), channel_id=1, source_target_pairs={{4,0},{8,4},{12,8},{16,12},{20,16},{24,20},{28,24},{32,28},{36,32}... | collective-permute-start | bytes 1179656 | tf_op jit(solution)/shard_map/ppermute | solution.py:26
  117.7 3.5 convolution_bitcast_fusion.24
  123.8 3.4 collective-permute-start.10
  149.8 14.3 %all_to_all.10 = f32[32,1,768]{2,1,0:T(1,128)S(1)} all-to-all(f32[32,1,768]{2,1,0:T(1,128)S(1)} %reshape.249), channel_id=1, replica_groups=mesh['gx'=32,'gy'=4] {'gx'}, dimensions={0} | all-to-all | bytes 196608 | tf_op jit(solution)/shard_map/all_to_all | solution.py:135
  165.6 5.8 %fusion = f32[32,32,24]{1,2,0:T(8,128)S(1)} fusion(f32[1,32,32,24,24]{2,4,3,1,0:T(8,128)} %param.17, f32[32,32,24]{1,2,0:T(8,128)S(1)} %bitcast_bitcast_fusion.1), kind=kLoop, calls=%fused_computation.1 | loop fusion | flops 1155072 | bytes 2555904 | tf_op jit(solution)/shard_map/skab,bsk->ask/dot_general | solution.py:136
  171.7 11.0 %all_to_all.11 = f32[32,1,768]{2,1,0:T(1,128)S(1)} all-to-all(f32[32,1,768]{2,1,0:T(1,128)S(1)} %reshape.251), channel_id=1, replica_groups=mesh['gx'=32,'gy'=4] {'gx'}, dimensions={0} | all-to-all | bytes 196608 | tf_op jit(solution)/shard_map/all_to_all | solution.py:139
  190.8 5.7 %collective-permute-start.13 = (f32[4,48,1,4,128]{4,3,2,1,0:T(4,128)}, f32[4,48,1,4,128]{4,3,2,1,0:T(4,128)}, u32[]{:S(2)}, u32[]{:S(2)}) collective-permute-start(f32[4,48,1,4,128]{4,3,2,1,0:T(4,128)} %get-tuple-element.74), channel_id=1, source_target_pairs={{4,0},{8,4},{12,8},{16,12},{20,16},{24,20},{28,24},{32,28},{36,32}... | collective-permute-start | bytes 1179656 | tf_op jit(solution)/shard_map/ppermute | solution.py:26
  203.2 3.6 convolution_bitcast_fusion.18
  206.8 2.8 pad_maximum_fusion.30
  220.7 3.6 convolution_bitcast_fusion.22
  240.7 5.8 %collective-permute-start.17 = (f32[4,48,1,4,128]{4,3,2,1,0:T(4,128)}, f32[4,48,1,4,128]{4,3,2,1,0:T(4,128)}, u32[]{:S(2)}, u32[]{:S(2)}) collective-permute-start(f32[4,48,1,4,128]{4,3,2,1,0:T(4,128)} %get-tuple-element.66), channel_id=1, source_target_pairs={{4,0},{8,4},{12,8},{16,12},{20,16},{24,20},{28,24},{32,28},{36,32}... | collective-permute-start | bytes 1179656 | tf_op jit(solution)/shard_map/ppermute | solution.py:26
  253.2 3.6 convolution_bitcast_fusion.12
  256.8 2.8 pad_maximum_fusion.24
  259.6 5.3 %collective-permute-start.18 = (f32[4,48,4,1,128]{4,3,2,1,0:T(1,128)}, f32[4,48,4,1,128]{4,3,2,1,0:T(1,128)}, u32[]{:S(2)}, u32[]{:S(2)}) collective-permute-start(f32[4,48,4,1,128]{4,3,2,1,0:T(1,128)} %get-tuple-element.22), channel_id=1, source_target_pairs={{0,1},{1,2},{2,3},{4,5},{5,6},{6,7},{8,9},{9,10},{10,11},{12,13},{... | collective-permute-start | bytes 1179656 | tf_op jit(solution)/shard_map/ppermute | solution.py:24
  289.0 6.2 %collective-permute-start.21 = (f32[4,48,1,4,128]{4,3,2,1,0:T(4,128)}, f32[4,48,1,4,128]{4,3,2,1,0:T(4,128)}, u32[]{:S(2)}, u32[]{:S(2)}) collective-permute-start(f32[4,48,1,4,128]{4,3,2,1,0:T(4,128)} %get-tuple-element.58), channel_id=1, source_target_pairs={{4,0},{8,4},{12,8},{16,12},{20,16},{24,20},{28,24},{32,28},{36,32}... | collective-permute-start | bytes 1179656 | tf_op jit(solution)/shard_map/ppermute | solution.py:26
  301.9 3.6 convolution_bitcast_fusion.6
  305.6 2.8 pad_maximum_fusion.18
  308.4 4.3 %collective-permute-start.22 = (f32[4,48,4,1,128]{4,3,2,1,0:T(1,128)}, f32[4,48,4,1,128]{4,3,2,1,0:T(1,128)}, u32[]{:S(2)}, u32[]{:S(2)}) collective-permute-start(f32[4,48,4,1,128]{4,3,2,1,0:T(1,128)} %get-tuple-element.18), channel_id=1, source_target_pairs={{0,1},{1,2},{2,3},{4,5},{5,6},{6,7},{8,9},{9,10},{10,11},{12,13},{... | collective-permute-start | bytes 1179656 | tf_op jit(solution)/shard_map/ppermute | solution.py:24
  321.2 3.5 convolution_bitcast_fusion.10
  343.9 5.9 %collective-permute-start.25 = (f32[4,48,1,4,128]{4,3,2,1,0:T(4,128)}, f32[4,48,1,4,128]{4,3,2,1,0:T(4,128)}, u32[]{:S(2)}, u32[]{:S(2)}) collective-permute-start(f32[4,48,1,4,128]{4,3,2,1,0:T(4,128)} %get-tuple-element.50), channel_id=1, source_target_pairs={{4,0},{8,4},{12,8},{16,12},{20,16},{24,20},{28,24},{32,28},{36,32}... | collective-permute-start | bytes 1179656 | tf_op jit(solution)/shard_map/ppermute | solution.py:26
  356.6 3.6 convolution_bitcast_fusion
  360.1 2.8 pad_maximum_fusion.12
  363.0 5.3 %collective-permute-start.26 = (f32[4,48,4,1,128]{4,3,2,1,0:T(1,128)}, f32[4,48,4,1,128]{4,3,2,1,0:T(1,128)}, u32[]{:S(2)}, u32[]{:S(2)}) collective-permute-start(f32[4,48,4,1,128]{4,3,2,1,0:T(1,128)} %get-tuple-element.14), channel_id=1, source_target_pairs={{0,1},{1,2},{2,3},{4,5},{5,6},{6,7},{8,9},{9,10},{10,11},{12,13},{... | collective-permute-start | bytes 1179656 | tf_op jit(solution)/shard_map/ppermute | solution.py:24
  386.5 3.4 fusion.16
  392.5 4.3 %fusion.59 = (f32[192,2,4,128]{3,2,1,0:T(4,128)}, f32[192,2,4,128]{3,2,1,0:T(4,128)}) fusion(f32[192,2,4,128]{3,2,1,0:T(4,128)} %get-tuple-element.3, f32[192,2,4,128]{3,2,1,0:T(4,128)} %reshape.245, f32[192,2,4,128]{3,2,1,0:T(4,128)} %copy-done.6, f32[192,2,4,128]{3,2,1,0:T(4,128)S(1)} %bitcast.419, f32[192,2,4,128]{3,2,1,0:T(4,128)} %reshape.226, ...), kind=kLoop, calls=%fused_computation.366 | loop fusion | flops 4128768 | bytes 7864320 | tf_op jit(solution)/shard_map/sub | solution.py:93
  (439 shorter events, 242.5 us)
Async XLA Ops:
  3.9 18.0 %collective-permute-start = (f32[4,48,1,4,128]{4,3,2,1,0:T(4,128)}, f32[4,48,1,4,128]{4,3,2,1,0:T(4,128)S(1)}, u32[]{:S(2)}, u32[]{:S(2)}) collective-permute-start(f32[4,48,1,4,128]{4,3,2,1,0:T(4,128)} %get-tuple-element.97), channel_id=1, source_target_pairs={{0,4},{4,8},{8,12},{12,16},{16,20},{20,24},{24,28},{28,32},{32,36}... | collective-permute-start | bytes 1179656 | tf_op jit(solution)/shard_map/ppermute | solution.py:24
  5.8 16.1 %collective-permute-start.1 = (f32[4,48,1,4,128]{4,3,2,1,0:T(4,128)}, f32[4,48,1,4,128]{4,3,2,1,0:T(4,128)S(1)}, u32[]{:S(2)}, u32[]{:S(2)}) collective-permute-start(f32[4,48,1,4,128]{4,3,2,1,0:T(4,128)} %get-tuple-element.98), channel_id=1, source_target_pairs={{4,0},{8,4},{12,8},{16,12},{20,16},{24,20},{28,24},{32,28},{36,32}... | collective-permute-start | bytes 1179656 | tf_op jit(solution)/shard_map/ppermute | solution.py:26
  11.6 269.8 %copy-start.79 = (pred[1,2,4,128]{3,2,1,0:T(4,128)(4,1)}, pred[1,2,4,128]{3,2,1,0:T(4,128)(4,1)S(1)}, u32[]{:S(2)}) copy-start(pred[1,2,4,128]{3,2,1,0:T(4,128)(4,1)S(1)} %get-tuple-element.114) | copy-start | bytes 3076
  11.6 269.8 %copy-start.81 = (pred[1,2,4,128]{3,2,1,0:T(4,128)(4,1)}, pred[1,2,4,128]{3,2,1,0:T(4,128)(4,1)S(1)}, u32[]{:S(2)}) copy-start(pred[1,2,4,128]{3,2,1,0:T(4,128)(4,1)S(1)} %get-tuple-element.115) | copy-start | bytes 3076
  11.7 269.8 %copy-start.83 = (pred[1,2,4,128]{3,2,1,0:T(4,128)(4,1)}, pred[1,2,4,128]{3,2,1,0:T(4,128)(4,1)S(1)}, u32[]{:S(2)}) copy-start(pred[1,2,4,128]{3,2,1,0:T(4,128)(4,1)S(1)} %get-tuple-element.116) | copy-start | bytes 3076
  18.9 247.5 %copy-start.16 = (f32[384,48]{0,1:T(8,128)}, f32[384,48]{0,1:T(8,128)S(1)}, u32[]{:S(2)}) copy-start(f32[384,48]{0,1:T(8,128)S(1)} %squeeze.18) | copy-start | bytes 221188
  23.2 11.5 %collective-permute-start.2 = (f32[4,48,4,1,128]{4,3,2,1,0:T(1,128)}, f32[4,48,4,1,128]{4,3,2,1,0:T(1,128)}, u32[]{:S(2)}, u32[]{:S(2)}) collective-permute-start(f32[4,48,4,1,128]{4,3,2,1,0:T(1,128)} %get-tuple-element.38), channel_id=1, source_target_pairs={{0,1},{1,2},{2,3},{4,5},{5,6},{6,7},{8,9},{9,10},{10,11},{12,13},{... | collective-permute-start | bytes 1179656 | tf_op jit(solution)/shard_map/ppermute | solution.py:24
  27.6 10.5 %collective-permute-start.3 = (f32[4,48,4,1,128]{4,3,2,1,0:T(1,128)S(1)}, f32[4,48,4,1,128]{4,3,2,1,0:T(1,128)}, u32[]{:S(2)}, u32[]{:S(2)}) collective-permute-start(f32[4,48,4,1,128]{4,3,2,1,0:T(1,128)S(1)} %get-tuple-element.39), channel_id=1, source_target_pairs={{1,0},{2,1},{3,2},{5,4},{6,5},{7,6},{9,8},{10,9},{11,10},{13,12},{... | collective-permute-start | bytes 1179656 | tf_op jit(solution)/shard_map/ppermute | solution.py:26
  49.5 18.0 %collective-permute-start.4 = (f32[4,48,1,4,128]{4,3,2,1,0:T(4,128)}, f32[4,48,1,4,128]{4,3,2,1,0:T(4,128)}, u32[]{:S(2)}, u32[]{:S(2)}) collective-permute-start(f32[4,48,1,4,128]{4,3,2,1,0:T(4,128)} %get-tuple-element.89), channel_id=1, source_target_pairs={{0,4},{4,8},{8,12},{12,16},{16,20},{20,24},{24,28},{28,32},{32,36}... | collective-permute-start | bytes 1179656 | tf_op jit(solution)/shard_map/ppermute | solution.py:24
  51.4 16.1 %collective-permute-start.5 = (f32[4,48,1,4,128]{4,3,2,1,0:T(4,128)}, f32[4,48,1,4,128]{4,3,2,1,0:T(4,128)}, u32[]{:S(2)}, u32[]{:S(2)}) collective-permute-start(f32[4,48,1,4,128]{4,3,2,1,0:T(4,128)} %get-tuple-element.90), channel_id=1, source_target_pairs={{4,0},{8,4},{12,8},{16,12},{20,16},{24,20},{28,24},{32,28},{36,32}... | collective-permute-start | bytes 1179656 | tf_op jit(solution)/shard_map/ppermute | solution.py:26
  70.3 12.4 %collective-permute-start.6 = (f32[4,48,4,1,128]{4,3,2,1,0:T(1,128)}, f32[4,48,4,1,128]{4,3,2,1,0:T(1,128)}, u32[]{:S(2)}, u32[]{:S(2)}) collective-permute-start(f32[4,48,4,1,128]{4,3,2,1,0:T(1,128)} %get-tuple-element.34), channel_id=1, source_target_pairs={{0,1},{1,2},{2,3},{4,5},{5,6},{6,7},{8,9},{9,10},{10,11},{12,13},{... | collective-permute-start | bytes 1179656 | tf_op jit(solution)/shard_map/ppermute | solution.py:24
  73.8 10.9 %collective-permute-start.7 = (f32[4,48,4,1,128]{4,3,2,1,0:T(1,128)}, f32[4,48,4,1,128]{4,3,2,1,0:T(1,128)}, u32[]{:S(2)}, u32[]{:S(2)}) collective-permute-start(f32[4,48,4,1,128]{4,3,2,1,0:T(1,128)} %get-tuple-element.35), channel_id=1, source_target_pairs={{1,0},{2,1},{3,2},{5,4},{6,5},{7,6},{9,8},{10,9},{11,10},{13,12},{... | collective-permute-start | bytes 1179656 | tf_op jit(solution)/shard_map/ppermute | solution.py:26
  103.2 18.1 %collective-permute-start.8 = (f32[4,48,1,4,128]{4,3,2,1,0:T(4,128)}, f32[4,48,1,4,128]{4,3,2,1,0:T(4,128)}, u32[]{:S(2)}, u32[]{:S(2)}) collective-permute-start(f32[4,48,1,4,128]{4,3,2,1,0:T(4,128)} %get-tuple-element.81), channel_id=1, source_target_pairs={{0,4},{4,8},{8,12},{12,16},{16,20},{20,24},{24,28},{28,32},{32,36}... | collective-permute-start | bytes 1179656 | tf_op jit(solution)/shard_map/ppermute | solution.py:24
  105.2 16.0 %collective-permute-start.9 = (f32[4,48,1,4,128]{4,3,2,1,0:T(4,128)}, f32[4,48,1,4,128]{4,3,2,1,0:T(4,128)S(1)}, u32[]{:S(2)}, u32[]{:S(2)}) collective-permute-start(f32[4,48,1,4,128]{4,3,2,1,0:T(4,128)} %get-tuple-element.82), channel_id=1, source_target_pairs={{4,0},{8,4},{12,8},{16,12},{20,16},{24,20},{28,24},{32,28},{36,32}... | collective-permute-start | bytes 1179656 | tf_op jit(solution)/shard_map/ppermute | solution.py:26
  123.8 11.4 %collective-permute-start.10 = (f32[4,48,4,1,128]{4,3,2,1,0:T(1,128)}, f32[4,48,4,1,128]{4,3,2,1,0:T(1,128)}, u32[]{:S(2)}, u32[]{:S(2)}) collective-permute-start(f32[4,48,4,1,128]{4,3,2,1,0:T(1,128)} %get-tuple-element.30), channel_id=1, source_target_pairs={{0,1},{1,2},{2,3},{4,5},{5,6},{6,7},{8,9},{9,10},{10,11},{12,13},{... | collective-permute-start | bytes 1179656 | tf_op jit(solution)/shard_map/ppermute | solution.py:24
  127.2 10.2 %collective-permute-start.11 = (f32[4,48,4,1,128]{4,3,2,1,0:T(1,128)}, f32[4,48,4,1,128]{4,3,2,1,0:T(1,128)}, u32[]{:S(2)}, u32[]{:S(2)}) collective-permute-start(f32[4,48,4,1,128]{4,3,2,1,0:T(1,128)} %get-tuple-element.31), channel_id=1, source_target_pairs={{1,0},{2,1},{3,2},{5,4},{6,5},{7,6},{9,8},{10,9},{11,10},{13,12},{... | collective-permute-start | bytes 1179656 | tf_op jit(solution)/shard_map/ppermute | solution.py:26
  188.7 18.0 %collective-permute-start.12 = (f32[4,48,1,4,128]{4,3,2,1,0:T(4,128)}, f32[4,48,1,4,128]{4,3,2,1,0:T(4,128)}, u32[]{:S(2)}, u32[]{:S(2)}) collective-permute-start(f32[4,48,1,4,128]{4,3,2,1,0:T(4,128)} %get-tuple-element.73), channel_id=1, source_target_pairs={{0,4},{4,8},{8,12},{12,16},{16,20},{20,24},{24,28},{28,32},{32,36}... | collective-permute-start | bytes 1179656 | tf_op jit(solution)/shard_map/ppermute | solution.py:24
  190.8 16.0 %collective-permute-start.13 = (f32[4,48,1,4,128]{4,3,2,1,0:T(4,128)}, f32[4,48,1,4,128]{4,3,2,1,0:T(4,128)}, u32[]{:S(2)}, u32[]{:S(2)}) collective-permute-start(f32[4,48,1,4,128]{4,3,2,1,0:T(4,128)} %get-tuple-element.74), channel_id=1, source_target_pairs={{4,0},{8,4},{12,8},{16,12},{20,16},{24,20},{28,24},{32,28},{36,32}... | collective-permute-start | bytes 1179656 | tf_op jit(solution)/shard_map/ppermute | solution.py:26
  209.6 14.7 %collective-permute-start.14 = (f32[4,48,4,1,128]{4,3,2,1,0:T(1,128)}, f32[4,48,4,1,128]{4,3,2,1,0:T(1,128)}, u32[]{:S(2)}, u32[]{:S(2)}) collective-permute-start(f32[4,48,4,1,128]{4,3,2,1,0:T(1,128)} %get-tuple-element.26), channel_id=1, source_target_pairs={{0,1},{1,2},{2,3},{4,5},{5,6},{6,7},{8,9},{9,10},{10,11},{12,13},{... | collective-permute-start | bytes 1179656 | tf_op jit(solution)/shard_map/ppermute | solution.py:24
  212.0 12.3 %collective-permute-start.15 = (f32[4,48,4,1,128]{4,3,2,1,0:T(1,128)}, f32[4,48,4,1,128]{4,3,2,1,0:T(1,128)}, u32[]{:S(2)}, u32[]{:S(2)}) collective-permute-start(f32[4,48,4,1,128]{4,3,2,1,0:T(1,128)} %get-tuple-element.27), channel_id=1, source_target_pairs={{1,0},{2,1},{3,2},{5,4},{6,5},{7,6},{9,8},{10,9},{11,10},{13,12},{... | collective-permute-start | bytes 1179656 | tf_op jit(solution)/shard_map/ppermute | solution.py:26
  238.8 18.0 %collective-permute-start.16 = (f32[4,48,1,4,128]{4,3,2,1,0:T(4,128)}, f32[4,48,1,4,128]{4,3,2,1,0:T(4,128)}, u32[]{:S(2)}, u32[]{:S(2)}) collective-permute-start(f32[4,48,1,4,128]{4,3,2,1,0:T(4,128)} %get-tuple-element.65), channel_id=1, source_target_pairs={{0,4},{4,8},{8,12},{12,16},{16,20},{20,24},{24,28},{28,32},{32,36}... | collective-permute-start | bytes 1179656 | tf_op jit(solution)/shard_map/ppermute | solution.py:24
  240.7 16.1 %collective-permute-start.17 = (f32[4,48,1,4,128]{4,3,2,1,0:T(4,128)}, f32[4,48,1,4,128]{4,3,2,1,0:T(4,128)}, u32[]{:S(2)}, u32[]{:S(2)}) collective-permute-start(f32[4,48,1,4,128]{4,3,2,1,0:T(4,128)} %get-tuple-element.66), channel_id=1, source_target_pairs={{4,0},{8,4},{12,8},{16,12},{20,16},{24,20},{28,24},{32,28},{36,32}... | collective-permute-start | bytes 1179656 | tf_op jit(solution)/shard_map/ppermute | solution.py:26
  259.6 14.2 %collective-permute-start.18 = (f32[4,48,4,1,128]{4,3,2,1,0:T(1,128)}, f32[4,48,4,1,128]{4,3,2,1,0:T(1,128)}, u32[]{:S(2)}, u32[]{:S(2)}) collective-permute-start(f32[4,48,4,1,128]{4,3,2,1,0:T(1,128)} %get-tuple-element.22), channel_id=1, source_target_pairs={{0,1},{1,2},{2,3},{4,5},{5,6},{6,7},{8,9},{9,10},{10,11},{12,13},{... | collective-permute-start | bytes 1179656 | tf_op jit(solution)/shard_map/ppermute | solution.py:24
  264.9 10.0 %collective-permute-start.19 = (f32[4,48,4,1,128]{4,3,2,1,0:T(1,128)}, f32[4,48,4,1,128]{4,3,2,1,0:T(1,128)}, u32[]{:S(2)}, u32[]{:S(2)}) collective-permute-start(f32[4,48,4,1,128]{4,3,2,1,0:T(1,128)} %get-tuple-element.23), channel_id=1, source_target_pairs={{1,0},{2,1},{3,2},{5,4},{6,5},{7,6},{9,8},{10,9},{11,10},{13,12},{... | collective-permute-start | bytes 1179656 | tf_op jit(solution)/shard_map/ppermute | solution.py:26
  287.0 18.5 %collective-permute-start.20 = (f32[4,48,1,4,128]{4,3,2,1,0:T(4,128)}, f32[4,48,1,4,128]{4,3,2,1,0:T(4,128)}, u32[]{:S(2)}, u32[]{:S(2)}) collective-permute-start(f32[4,48,1,4,128]{4,3,2,1,0:T(4,128)} %get-tuple-element.57), channel_id=1, source_target_pairs={{0,4},{4,8},{8,12},{12,16},{16,20},{20,24},{24,28},{28,32},{32,36}... | collective-permute-start | bytes 1179656 | tf_op jit(solution)/shard_map/ppermute | solution.py:24
  289.0 16.6 %collective-permute-start.21 = (f32[4,48,1,4,128]{4,3,2,1,0:T(4,128)}, f32[4,48,1,4,128]{4,3,2,1,0:T(4,128)}, u32[]{:S(2)}, u32[]{:S(2)}) collective-permute-start(f32[4,48,1,4,128]{4,3,2,1,0:T(4,128)} %get-tuple-element.58), channel_id=1, source_target_pairs={{4,0},{8,4},{12,8},{16,12},{20,16},{24,20},{28,24},{32,28},{36,32}... | collective-permute-start | bytes 1179656 | tf_op jit(solution)/shard_map/ppermute | solution.py:26
  308.4 16.3 %collective-permute-start.22 = (f32[4,48,4,1,128]{4,3,2,1,0:T(1,128)}, f32[4,48,4,1,128]{4,3,2,1,0:T(1,128)}, u32[]{:S(2)}, u32[]{:S(2)}) collective-permute-start(f32[4,48,4,1,128]{4,3,2,1,0:T(1,128)} %get-tuple-element.18), channel_id=1, source_target_pairs={{0,1},{1,2},{2,3},{4,5},{5,6},{6,7},{8,9},{9,10},{10,11},{12,13},{... | collective-permute-start | bytes 1179656 | tf_op jit(solution)/shard_map/ppermute | solution.py:24
  312.7 12.1 %collective-permute-start.23 = (f32[4,48,4,1,128]{4,3,2,1,0:T(1,128)}, f32[4,48,4,1,128]{4,3,2,1,0:T(1,128)}, u32[]{:S(2)}, u32[]{:S(2)}) collective-permute-start(f32[4,48,4,1,128]{4,3,2,1,0:T(1,128)} %get-tuple-element.19), channel_id=1, source_target_pairs={{1,0},{2,1},{3,2},{5,4},{6,5},{7,6},{9,8},{10,9},{11,10},{13,12},{... | collective-permute-start | bytes 1179656 | tf_op jit(solution)/shard_map/ppermute | solution.py:26
  342.0 18.2 %collective-permute-start.24 = (f32[4,48,1,4,128]{4,3,2,1,0:T(4,128)}, f32[4,48,1,4,128]{4,3,2,1,0:T(4,128)}, u32[]{:S(2)}, u32[]{:S(2)}) collective-permute-start(f32[4,48,1,4,128]{4,3,2,1,0:T(4,128)} %get-tuple-element.49), channel_id=1, source_target_pairs={{0,4},{4,8},{8,12},{12,16},{16,20},{20,24},{24,28},{28,32},{32,36}... | collective-permute-start | bytes 1179656 | tf_op jit(solution)/shard_map/ppermute | solution.py:24
  343.9 16.2 %collective-permute-start.25 = (f32[4,48,1,4,128]{4,3,2,1,0:T(4,128)}, f32[4,48,1,4,128]{4,3,2,1,0:T(4,128)}, u32[]{:S(2)}, u32[]{:S(2)}) collective-permute-start(f32[4,48,1,4,128]{4,3,2,1,0:T(4,128)} %get-tuple-element.50), channel_id=1, source_target_pairs={{4,0},{8,4},{12,8},{16,12},{20,16},{24,20},{28,24},{32,28},{36,32}... | collective-permute-start | bytes 1179656 | tf_op jit(solution)/shard_map/ppermute | solution.py:26
  363.0 14.1 %collective-permute-start.26 = (f32[4,48,4,1,128]{4,3,2,1,0:T(1,128)}, f32[4,48,4,1,128]{4,3,2,1,0:T(1,128)}, u32[]{:S(2)}, u32[]{:S(2)}) collective-permute-start(f32[4,48,4,1,128]{4,3,2,1,0:T(1,128)} %get-tuple-element.14), channel_id=1, source_target_pairs={{0,1},{1,2},{2,3},{4,5},{5,6},{6,7},{8,9},{9,10},{10,11},{12,13},{... | collective-permute-start | bytes 1179656 | tf_op jit(solution)/shard_map/ppermute | solution.py:24
  368.3 10.0 %collective-permute-start.27 = (f32[4,48,4,1,128]{4,3,2,1,0:T(1,128)}, f32[4,48,4,1,128]{4,3,2,1,0:T(1,128)}, u32[]{:S(2)}, u32[]{:S(2)}) collective-permute-start(f32[4,48,4,1,128]{4,3,2,1,0:T(1,128)} %get-tuple-element.15), channel_id=1, source_target_pairs={{1,0},{2,1},{3,2},{5,4},{6,5},{7,6},{9,8},{10,9},{11,10},{13,12},{... | collective-permute-start | bytes 1179656 | tf_op jit(solution)/shard_map/ppermute | solution.py:26
  (85 other events, 765.9 us)
where the time goes:
time: 404 us; the launch traced here: 397 us
  matrix products  114 us (28%)
  starting transfers between devices  93.2 us (23%)
  local copies, waits for them, and re-layouts  89.4 us (22%)
  other arithmetic  62 us (15%)
  blocking collectives  25.3 us (6%)
  waiting for transfers between devices  9.81 us (2%)
    dot_general x42, matrix products, operate(): jnp.dot(face_pairs[direction], neighbours[direction].reshape(48, -1), pre...  94.2 us
    ppermute x14, starting transfers between devices, padded(): lax.ppermute(head, axis, [((i + 1) % count, i) for i in range(ends)])  51 us
    ppermute x14, starting transfers between devices, padded(): lax.ppermute(tail, axis, [(i, (i + 1) % count) for i in range(ends)])  42.2 us
    reshape x14, local copies, waits for them, and re-layouts, operate(): neighbours[direction].reshape(48, -1)  20.4 us
    slice x7, other arithmetic, padded(): lax.slice_in_dim(cells, cells.shape[dim] - width, cells.shape[dim], axis=...  18 us
    concatenate x14, other arithmetic, padded(): jnp.concatenate([lax.ppermute(tail, axis, [(i, (i + 1) % count) for i in...  16.7 us
    another operation x28, local copies, waits for them, and re-layouts, operate(): neighbours[direction].reshape(48, -1)  15.4 us
    dot_general x7, matrix products, operate(): jnp.dot(stiffness, scaled.reshape(BLOCK, -1), precision=lax.Precision.HIG...  14.9 us
  transfers between devices with their start and end apart: 28, of which 5 were waited for; matrix products, arithmetic and copies ran while one was open for 32% of the time, Pallas kernels for 0%

commit v1 on v0

v1 whole, which is shorter than its diff:
```python
import functools

import jax
import jax.numpy as jnp
import ml_dtypes
import numpy as np
from jax import lax
from jax.experimental import pallas as pl
from jax.experimental.pallas import tpu as pltpu
from jax.sharding import PartitionSpec as P

BLOCK = 192
TRACE = 48
CW = 24
DEGREE = 3
COLS = 8
LANES = 128
ELEMS = COLS * LANES
OWNERS = 32
CAP = 32
AGG = 512

F32 = jnp.float32
BF16 = jnp.bfloat16

THETA = 0.5 * (4.0 + 0.25)
DELTA = 0.5 * (4.0 - 0.25)
SIGMA = THETA / DELTA


def chebyshev():
    rho = 1.0 / SIGMA
    steps = []
    for _ in range(DEGREE - 1):
        rho_new = 1.0 / (2.0 * SIGMA - rho)
        steps.append((rho_new * rho, 2.0 * rho_new / DELTA))
        rho = rho_new
    return steps


def selection():
    sel = np.zeros((192, 192), np.float32)
    t = np.arange(48)
    for group, rows in enumerate(
        (16 * (t // 4) + t % 4, 16 * (t // 4) + t % 4 + 12, 4 * t, 4 * t + 3)
    ):
        sel[48 * group + t, rows] = 1.0
    return sel.astype(ml_dtypes.bfloat16)


def dot(a, b):
    return jnp.dot(a, b, preferred_element_type=F32)


def dot_nt(a, b):
    return lax.dot_general(a, b, (((1,), (1,)), ((), ())), preferred_element_type=F32)


def split(v):
    high = v.astype(BF16)
    return high, (v - high.astype(F32)).astype(BF16)


def dot3(a_high, a_low, b_high, b_low):
    return dot(a_high, b_high) + dot(a_high, b_low) + dot(a_low, b_high)


def lanes(col):
    return slice(LANES * col, LANES * (col + 1))


def face_rows(v, node):
    at = 16 * node
    return jnp.concatenate([v[64 * c + at : 64 * c + at + 16] for c in range(3)], axis=0)


def tile_coef(coef_ref, col):
    return coef_ref[col : col + 1, :]


def emit_traces(w_of, sel_ref, par_ref, sends):
    sx_in, sx_out, sy_in, sy_out = sends
    even_x = par_ref[0] == 0
    even_y = par_ref[1] == 0
    for y in range(4):
        low = face_rows(w_of(y), 0)
        high = face_rows(w_of(4 + y), 3)
        sx_in[:, lanes(y)] = jnp.where(even_x, high, low)
        sx_out[:, lanes(y)] = jnp.where(even_x, low, high)
    pick = sel_ref[0:96, :]
    for x in range(2):
        ends = []
        for y, rows in ((0, slice(0, 48)), (3, slice(48, 96))):
            high, low = split(w_of(4 * x + y))
            ends.append(dot(pick[rows], high) + dot(pick[rows], low))
        sy_in[:, lanes(x)] = jnp.where(even_y, ends[1], ends[0])
        sy_out[:, lanes(x)] = jnp.where(even_y, ends[0], ends[1])


def first_kernel(rs_ref, coef_ref, sel_ref, par_ref, r_ref, d_ref, *sends):
    for col in range(COLS):
        v = rs_ref[pl.ds(col, BLOCK, stride=COLS), :]
        r_ref[:, lanes(col)] = v
        d_ref[:, lanes(col)] = v * (1.0 / THETA)
    emit_traces(
        lambda col: d_ref[:, lanes(col)] * tile_coef(coef_ref, col), sel_ref, par_ref, sends
    )


def weights_kernel(stiff_ref, faces_ref, pt_ref, wh_ref, wl_ref, pth_ref, ptl_ref, ph_ref, pl_ref):
    high, low = split(stiff_ref[...])
    wh_ref[:, 0:BLOCK] = high
    wl_ref[:, 0:BLOCK] = low
    for piece in range(3):
        high, low = split(faces_ref[192 * piece : 192 * (piece + 1), :].T)
        wh_ref[:, 192 * (piece + 1) : 192 * (piece + 2)] = high
        wl_ref[:, 192 * (piece + 1) : 192 * (piece + 2)] = low
    pt = pt_ref[...]
    high, low = split(pt)
    pth_ref[...] = high
    ptl_ref[...] = low
    row = lax.broadcasted_iota(jnp.int32, (CW, 32), 0)
    col = lax.broadcasted_iota(jnp.int32, (CW, 32), 1)
    spread = ((row & 3) * 8 + (row >> 2) == col).astype(F32)
    p = pt.T
    p_high, p_low = split(p)
    spread = spread.astype(BF16)
    ph_ref[...] = dot(p_high, spread).astype(BF16)
    pl_ref[...] = dot(p_low, spread).astype(BF16)


def interior_kernel(d_ref, coef_ref, ori_ref, wh_ref, wl_ref, sel_ref, out_ref, xh_ref, xl_ref, t_ref):
    for col in range(COLS):
        high, low = split(d_ref[:, lanes(col)] * tile_coef(coef_ref, col))
        xh_ref[0:BLOCK, lanes(col)] = high
        xl_ref[0:BLOCK, lanes(col)] = low
    lane = lax.broadcasted_iota(jnp.int32, (48, LANES), 1)
    for x_ref in (xh_ref, xl_ref):
        t_ref[...] = dot(sel_ref[...], x_ref[0:BLOCK, :])
        for col in range(COLS):
            x, y = col // 4, col % 4
            for direction in range(6):
                trace = None
                if direction == 0 and x == 1:
                    trace = face_rows(x_ref[0:BLOCK, lanes(col - 4)], 3).astype(F32)
                elif direction == 1 and x == 0:
                    trace = face_rows(x_ref[0:BLOCK, lanes(col + 4)], 0).astype(F32)
                elif direction == 2 and y > 0:
                    trace = t_ref[48:96, lanes(col - 1)]
                elif direction == 3 and y < 3:
                    trace = t_ref[0:48, lanes(col + 1)]
                elif direction == 4:
                    trace = jnp.where(lane == 0, 0.0, pltpu.roll(t_ref[144:192, lanes(col)], 1, 1))
                elif direction == 5:
                    trace = jnp.where(
                        lane == LANES - 1, 0.0, pltpu.roll(t_ref[96:144, lanes(col)], LANES - 1, 1)
                    )
                at = BLOCK + 96 * direction
                if trace is None:
                    x_ref[at : at + 96, lanes(col)] = jnp.zeros((96, LANES), BF16)
                    continue
                row = COLS * direction + col
                picked = ori_ref[row : row + 1, :] == 1
                x_ref[at : at + 48, lanes(col)] = jnp.where(picked, 0.0, trace).astype(BF16)
                x_ref[at + 48 : at + 96, lanes(col)] = jnp.where(picked, trace, 0.0).astype(BF16)
    for half in range(2):
        span = slice(512 * half, 512 * (half + 1))
        out_ref[:, span] = dot3(wh_ref[...], wl_ref[...], xh_ref[:, span], xl_ref[:, span])


def halo_product(halo, cols, direction, ori_ref, wh_ref, wl_ref):
    highs, lows = [], []
    for n, col in enumerate(cols):
        trace = halo(n)
        row = COLS * direction + col
        picked = ori_ref[row : row + 1, :] == 1
        both = jnp.concatenate([jnp.where(picked, 0.0, trace), jnp.where(picked, trace, 0.0)], axis=0)
        high, low = split(both)
        highs.append(high)
        lows.append(low)
    at = BLOCK + 96 * direction
    return dot3(
        wh_ref[:, at : at + 96],
        wl_ref[:, at : at + 96],
        jnp.concatenate(highs, axis=1),
        jnp.concatenate(lows, axis=1),
    )


def halo_sum(part_ref, ori_ref, wh_ref, wl_ref, par_ref, gets, ad_ref):
    gx_in, gx_out, gy_in, gy_out = gets
    even_x = par_ref[0] == 0
    even_y = par_ref[1] == 0

    def lower(inside, outside, even):
        return lambda n: jnp.where(even, outside[:, lanes(n)], inside[:, lanes(n)])

    def upper(inside, outside, even):
        return lambda n: jnp.where(even, inside[:, lanes(n)], outside[:, lanes(n)])

    weights = (ori_ref, wh_ref, wl_ref)
    ad_ref[:, 0:512] = part_ref[:, 0:512] + halo_product(
        lower(gx_in, gx_out, even_x), (0, 1, 2, 3), 0, *weights
    )
    ad_ref[:, 512:1024] = part_ref[:, 512:1024] + halo_product(
        upper(gx_in, gx_out, even_x), (4, 5, 6, 7), 1, *weights
    )
    for cols, direction, pick in (((0, 4), 2, lower), ((3, 7), 3, upper)):
        both = halo_product(pick(gy_in, gy_out, even_y), cols, direction, *weights)
        for n, col in enumerate(cols):
            ad_ref[:, lanes(col)] += both[:, lanes(n)]


def step_kernel(
    scales, part_ref, r_ref, d_ref, x_ref, coef_ref, ori_ref, wh_ref, wl_ref, sel_ref, par_ref,
    gx_in, gx_out, gy_in, gy_out, r_out, d_out, x_out, sx_in, sx_out, sy_in, sy_out, ad_ref,
):
    halo_sum(part_ref, ori_ref, wh_ref, wl_ref, par_ref, (gx_in, gx_out, gy_in, gy_out), ad_ref)
    keep, gain = scales
    for col in range(COLS):
        at = lanes(col)
        resid = r_ref[:, at] - ad_ref[:, at]
        step = gain * resid
        if keep:
            step = keep * d_ref[:, at] + step
        r_out[:, at] = resid
        d_out[:, at] = step
        x_out[:, at] = x_ref[:, at] + step
    emit_traces(
        lambda col: d_out[:, lanes(col)] * tile_coef(coef_ref, col),
        sel_ref,
        par_ref,
        (sx_in, sx_out, sy_in, sy_out),
    )


def last_kernel(
    part_ref, r_ref, x_ref, ori_ref, wh_ref, wl_ref, par_ref, gx_in, gx_out, gy_in, gy_out,
    x_out, r_out, ad_ref,
):
    halo_sum(part_ref, ori_ref, wh_ref, wl_ref, par_ref, (gx_in, gx_out, gy_in, gy_out), ad_ref)
    for col in range(COLS):
        at = lanes(col)
        rows = pl.ds(col, BLOCK, stride=COLS)
        x_out[rows, :] = x_ref[:, at]
        r_out[rows, :] = r_ref[:, at] - ad_ref[:, at]


def pack_kernel(in_ref, out_ref):
    for s in range(in_ref.shape[0]):
        for m in range(6):
            out_ref[s, m] = jnp.concatenate([in_ref[s, 4 * m + q] for q in range(4)], axis=-1)


def slots_kernel(agg_ref, owner_ref, hot_ref):
    owner = owner_ref[...]
    owner_hot = lax.broadcasted_iota(jnp.int32, (OWNERS, AGG), 0) == owner
    before = lax.broadcasted_iota(jnp.int32, (AGG, AGG), 0) < lax.broadcasted_iota(
        jnp.int32, (AGG, AGG), 1
    )
    counts = dot(owner_hot.astype(BF16), before.astype(BF16))
    slot = jnp.sum(jnp.where(owner_hot, counts, 0.0), axis=0, keepdims=True)
    first = lax.broadcasted_iota(jnp.int32, (8, AGG), 0) == 0
    table = jnp.where(first, owner.astype(F32), slot).astype(BF16)
    for col in range(COLS):
        at = lanes(col)
        member = lax.broadcasted_iota(jnp.int32, (AGG, LANES), 0) == agg_ref[col : col + 1, :]
        found = dot(table, member.astype(BF16))
        target = (found[0:1] * float(CAP) + found[1:2]).astype(jnp.int32)
        hot = lax.broadcasted_iota(jnp.int32, (OWNERS * CAP, LANES), 0) == target
        hot_ref[:, at] = hot.astype(BF16)


def coarse_kernel(
    r_ref, x_ref, coef_ref, hot_ref, inv_ref, pth_ref, ptl_ref, ph_ref, pl_ref, sel_ref, par_ref,
    d_out, x_out, sx_in, sx_out, sy_in, sy_out, y_ref, sol_ref,
):
    r_high, r_low = split(r_ref[...])
    proj = dot3(pth_ref[...], ptl_ref[...], r_high, r_low)
    p_high, p_low = split(proj)
    rhs = dot_nt(p_high, hot_ref[...]) + dot_nt(p_low, hot_ref[...])
    group = lax.broadcasted_iota(jnp.int32, (CW, LANES), 1) >> 5
    for o in range(OWNERS):
        part = jnp.where(group == o % 4, rhs[:, lanes(o // 4)], 0.0)
        part = part + pltpu.roll(part, 32, 1)
        part = part + pltpu.roll(part, 64, 1)
        y_ref[o, 0:6, :] = jnp.sum(inv_ref[o] * part[None], axis=1)
        y_ref[o, 6:8, :] = jnp.zeros((2, LANES), F32)
    group = lax.broadcasted_iota(jnp.int32, (8, LANES), 1) >> 5
    for q in range(4):
        for j in range(8):
            total = jnp.zeros((8, LANES), F32)
            for g in range(4):
                moved = y_ref[4 * j + g]
                if g != q:
                    moved = pltpu.roll(moved, 32 * ((g - q) % 4), 1)
                total = jnp.where(group == g, moved, total)
            sol_ref[8 * q : 8 * q + 8, lanes(j)] = total
    s_high, s_low = split(sol_ref[...])
    each = dot(s_high, hot_ref[...]) + dot(s_low, hot_ref[...])
    e_high, e_low = split(each)
    for half in range(2):
        span = slice(512 * half, 512 * (half + 1))
        lift = dot3(ph_ref[...], pl_ref[...], e_high[:, span], e_low[:, span])
        d_out[:, span] = lift
        x_out[:, span] = x_ref[:, span] + lift
    emit_traces(
        lambda col: d_out[:, lanes(col)] * tile_coef(coef_ref, col),
        sel_ref,
        par_ref,
        (sx_in, sx_out, sy_in, sy_out),
    )


def field(*shape, dtype=F32):
    return pltpu.VMEM(shape, dtype)


def call(kernel, outs, args, scratch=(), smem=(), limit=48):
    vmem = pl.BlockSpec(memory_space=pltpu.VMEM)
    scalar = pl.BlockSpec(memory_space=pltpu.SMEM)
    specs = [scalar if n in smem else vmem for n in range(len(args))]
    placed = [
        a if n in smem else pltpu.with_memory_space_constraint(a, pltpu.VMEM)
        for n, a in enumerate(args)
    ]
    return pl.pallas_call(
        kernel,
        out_shape=outs,
        in_specs=specs,
        out_specs=[vmem] * len(outs),
        scratch_shapes=list(scratch),
        compiler_params=pltpu.CompilerParams(vmem_limit_bytes=limit << 20),
    )(*placed)


def swap_even(v, axis):
    count = lax.axis_size(axis)
    return lax.ppermute(v, axis, [(i, i ^ 1) for i in range(count)])


def swap_odd(v, axis):
    count = lax.axis_size(axis)
    return lax.ppermute(v, axis, [(i, i + 1 if i % 2 else i - 1) for i in range(1, count - 1)])


def exchange(sends):
    return (
        swap_even(sends[0], "gx"),
        swap_odd(sends[1], "gx"),
        swap_even(sends[2], "gy"),
        swap_odd(sends[3], "gy"),
    )


SENDS = [field(48, 512), field(48, 512), field(48, 256), field(48, 256)]


def shards(
    right_side,
    coefficient,
    orientation,
    aggregate_map,
    owner_map,
    stiffness,
    face_blocks,
    prolong_basis,
    coarse_inverse,
):
    shape = right_side.shape
    par = jnp.stack([lax.axis_index("gx") & 1, lax.axis_index("gy") & 1]).astype(jnp.int32)
    sel = jnp.asarray(selection())
    coef = coefficient.reshape(COLS, LANES)
    ori = orientation.reshape(6 * COLS, LANES)

    packed = pl.pallas_call(
        pack_kernel,
        out_shape=jax.ShapeDtypeStruct((OWNERS, 6, CW, LANES), F32),
        grid=(8,),
        in_specs=[pl.BlockSpec((4, CW, CW, CAP), lambda s: (s, 0, 0, 0))],
        out_specs=pl.BlockSpec((4, 6, CW, LANES), lambda s: (s, 0, 0, 0)),
    )(jnp.transpose(coarse_inverse[0], (0, 2, 3, 1)))
    inverse = lax.all_to_all(packed, "gx", split_axis=0, concat_axis=0, tiled=True)

    full = field(BLOCK, ELEMS)
    r, d, *sends = call(
        first_kernel,
        [full, full, *SENDS],
        [right_side.reshape(BLOCK * COLS, LANES), coef, sel, par],
        smem=(3,),
    )
    wide = field(BLOCK, 768, dtype=BF16)
    wh, wl, pth, ptl, ph, plo = call(
        weights_kernel,
        [wide, wide, field(CW, BLOCK, dtype=BF16), field(CW, BLOCK, dtype=BF16),
         field(BLOCK, 32, dtype=BF16), field(BLOCK, 32, dtype=BF16)],
        [stiffness, jnp.transpose(face_blocks, (0, 1, 3, 2)).reshape(576, BLOCK), prolong_basis.T],
    )
    hot = call(
        slots_kernel,
        [field(ELEMS, ELEMS, dtype=BF16)],
        [aggregate_map.reshape(COLS, LANES), owner_map.reshape(1, AGG)],
    )[0]

    def interior(step):
        return call(
            interior_kernel,
            [full],
            [step, coef, ori, wh, wl, sel],
            scratch=[
                pltpu.VMEM((768, ELEMS), BF16),
                pltpu.VMEM((768, ELEMS), BF16),
                pltpu.VMEM((BLOCK, ELEMS), F32),
            ],
        )[0]

    accumulator = [pltpu.VMEM((BLOCK, ELEMS), F32)]

    def advance(scales, r, d, x, sends):
        gets = exchange(sends)
        part = interior(d)
        return call(
            functools.partial(step_kernel, scales),
            [full, full, full, *SENDS],
            [part, r, d, x, coef, ori, wh, wl, sel, par, *gets],
            scratch=accumulator,
            smem=(9,),
        )

    steps = chebyshev()
    x = d
    for scales in steps:
        r, d, x, *sends = advance(scales, r, d, x, sends)
    r, _, _, *_ = advance((0.0, 1.0 / THETA), r, d, x, sends)
    d, x, *sends = call(
        coarse_kernel,
        [full, full, *SENDS],
        [r, x, coef, hot, inverse, pth, ptl, ph, plo, sel, par],
        scratch=[pltpu.VMEM((OWNERS, 8, LANES), F32), pltpu.VMEM((32, ELEMS), F32)],
        smem=(10,),
    )
    r, d, x, *sends = advance((0.0, 1.0 / THETA), r, d, x, sends)
    for scales in steps:
        r, d, x, *sends = advance(scales, r, d, x, sends)
    gets = exchange(sends)
    part = interior(d)
    x, r = call(
        last_kernel,
        [jax.ShapeDtypeStruct((BLOCK * COLS, LANES), F32)] * 2,
        [part, r, x, ori, wh, wl, par, *gets],
        scratch=accumulator,
        smem=(6,),
    )
    return x.reshape(shape), r.reshape(shape)


def solution(mesh):
    in_specs = (
        P(None, "gx", "gy", None),
        P("gx", "gy", None),
        P(None, "gx", "gy", None),
        P("gx", "gy", None),
        P(("gx", "gy"), None),
        P(),
        P(),
        P(),
        P(("gx", "gy"), None, None, None, None),
    )
    out_specs = (P(None, "gx", "gy", None), P(None, "gx", "gy", None))
    return jax.shard_map(shards, mesh=mesh, in_specs=in_specs, out_specs=out_specs, check_vma=False)
```

time: 404 us -> 132 us (0.33)
  the two profiles are of different devices: /device:TPU:32 before, /device:TPU:47 now
where the time goes in v1:
time: 132 us; the launch traced here: 131 us
  starting transfers between devices  61.1 us (46%)
  Pallas kernels  41.3 us (31%)
  waiting for transfers between devices  19.5 us (15%)
  local copies, waits for them, and re-layouts  8.31 us (6%)
    ppermute x14, starting transfers between devices, swap_odd(): lax.ppermute(v, axis, [(i, i + 1 if i % 2 else i - 1) for i in range(1, c...  48.4 us
    pallas_call x18, Pallas kernels, call(): pl.pallas_call(kernel, out_shape=outs, in_specs=specs, out_specs=[vmem] *...  33.1 us
    ppermute x14, waiting for transfers between devices, swap_odd(): lax.ppermute(v, axis, [(i, i + 1 if i % 2 else i - 1) for i in range(1, c...  19.4 us
    all_to_all x1, starting transfers between devices, shards(): lax.all_to_all(packed, 'gx', split_axis=0, concat_axis=0, tiled=True)  8.41 us
    unnamed x36, local copies, waits for them, and re-layouts  8.31 us
    pallas_call x1, Pallas kernels, shards(): pl.pallas_call(pack_kernel, out_shape=jax.ShapeDtypeStruct((OWNERS, 6, CW...  8.25 us
    ppermute x14, starting transfers between devices, swap_even(): return lax.ppermute(v, axis, [(i, i ^ 1) for i in range(count)])  4.35 us
  transfers between devices with their start and end apart: 29, of which 6 were waited for; matrix products, arithmetic and copies ran while one was open for 0% of the time, Pallas kernels for 16%

profile of v1, /device:TPU:47, one launch (start us, length us, event | category | flops | bytes accessed | tf_op | source)
XLA Modules:
  0.0 131.5 jit_solution(5567175902576587048)
XLA Ops:
  0.6 8.2 %shard_map.122 = f32[32,6,24,128]{3,2,1,0:T(8,128)} custom-call(f32[32,24,24,32]{3,2,1,0:T(8,128)} %bitcast.50), custom_call_target="tpu_custom_call" | custom-call | tf_op jit(solution)/shard_map/pallas_call | solution.py:376
  8.9 8.4 %all-to-all-start = ((f32[32,6,24,128]{3,2,1,0:T(8,128)}), f32[32,6,24,128]{3,2,1,0:T(8,128)S(1)}, u32[]{:S(2)}, u32[]{:S(2)}) async-start(f32[32,6,24,128]{3,2,1,0:T(8,128)} %shard_map.122), calls=%async_computation | async-start | bytes 4718592 | tf_op jit(solution)/shard_map/all_to_all | solution.py:383
  20.0 3.1 %collective-permute-start.1 = (f32[48,512]{1,0:T(8,128)S(1)}, f32[48,512]{1,0:T(8,128)S(1)}, u32[]{:S(2)}, u32[]{:S(2)}) collective-permute-start(f32[48,512]{1,0:T(8,128)S(1)} %get-tuple-element.63), channel_id=1, source_target_pairs={{4,8},{8,4},{12,16},{16,12},{20,24},{24,20},{28,32},{32,28},{36,40... | collective-permute-start | bytes 294920 | tf_op jit(solution)/shard_map/ppermute | solution.py:344
  23.3 4.0 %collective-permute-start.3 = (f32[48,256]{1,0:T(8,128)S(1)}, f32[48,256]{1,0:T(8,128)S(1)}, u32[]{:S(2)}, u32[]{:S(2)}) collective-permute-start(f32[48,256]{1,0:T(8,128)S(1)} %get-tuple-element.65), channel_id=1, source_target_pairs={{1,2},{2,1},{5,6},{6,5},{9,10},{10,9},{13,14},{14,13},{17,18},{18,... | collective-permute-start | bytes 147464 | tf_op jit(solution)/shard_map/ppermute | solution.py:344
  28.9 1.8 %shard_map.115.part_ref = f32[192,1024]{1,0:T(8,128)S(1)} custom-call(f32[192,1024]{1,0:T(8,128)S(1)} %get-tuple-element.58.d_ref.x_ref, f32[8,128]{1,0:T(8,128)S(1)} %bitcast.31, s32[48,128]{1,0:T(8,128)S(1)} %bitcast.16, bf16[192,768]{1,0:T(8,128)(2,1)S(1)} %get-tuple-element.59.wh_ref, bf16[192,768]{1,0:T(8,128)(2,1)S(1)} %get-tuple-element.60.wl_ref, ...), custom_call_target="tpu_custom_call" | custom-call | tf_op jit(solution)/shard_map/pallas_call | solution.py:327
  30.7 15.8 %collective-permute-done.1.gx_out = f32[48,512]{1,0:T(8,128)S(1)} collective-permute-done((f32[48,512]{1,0:T(8,128)S(1)}, f32[48,512]{1,0:T(8,128)S(1)}, u32[]{:S(2)}, u32[]{:S(2)}) %collective-permute-start.1) | collective-permute-done | bytes 98336 | tf_op jit(solution)/shard_map/ppermute | solution.py:344
  49.4 1.9 %collective-permute-start.5 = (f32[48,512]{1,0:T(8,128)S(1)}, f32[48,512]{1,0:T(8,128)S(1)}, u32[]{:S(2)}, u32[]{:S(2)}) collective-permute-start(f32[48,512]{1,0:T(8,128)S(1)} %get-tuple-element.70), channel_id=1, source_target_pairs={{4,8},{8,4},{12,16},{16,12},{20,24},{24,20},{28,32},{32,28},{36,40... | collective-permute-start | bytes 294920 | tf_op jit(solution)/shard_map/ppermute | solution.py:344
  51.6 4.0 %collective-permute-start.7 = (f32[48,256]{1,0:T(8,128)S(1)}, f32[48,256]{1,0:T(8,128)S(1)}, u32[]{:S(2)}, u32[]{:S(2)}) collective-permute-start(f32[48,256]{1,0:T(8,128)S(1)} %get-tuple-element.72), channel_id=1, source_target_pairs={{1,2},{2,1},{5,6},{6,5},{9,10},{10,9},{13,14},{14,13},{17,18},{18,... | collective-permute-start | bytes 147464 | tf_op jit(solution)/shard_map/ppermute | solution.py:344
  55.6 1.8 %shard_map.117.part_ref = f32[192,1024]{1,0:T(8,128)S(1)} custom-call(f32[192,1024]{1,0:T(8,128)S(1)} %get-tuple-element.66.d_ref, f32[8,128]{1,0:T(8,128)S(1)} %bitcast.33, s32[48,128]{1,0:T(8,128)S(1)} %bitcast.18, bf16[192,768]{1,0:T(8,128)(2,1)S(1)} %get-tuple-element.59.wh_ref, bf16[192,768]{1,0:T(8,128)(2,1)S(1)} %get-tuple-element.60.wl_ref, ...), custom_call_target="tpu_custom_call" | custom-call | tf_op jit(solution)/shard_map/pallas_call | solution.py:327
  57.5 1.7 %shard_map.118 = (f32[192,1024]{1,0:T(8,128)S(1)}, f32[192,1024]{1,0:T(8,128)S(1)}, f32[192,1024]{1,0:T(8,128)S(1)}, f32[48,512]{1,0:T(8,128)S(1)}, f32[48,512]{...) custom-call(f32[192,1024]{1,0:T(8,128)S(1)} %shard_map.117.part_ref, ...), custom_call_target="tpu_custom_call" | custom-call | tf_op jit(solution)/shard_map/pallas_call | solution.py:327
  60.1 5.7 %collective-permute-start.9 = (f32[48,512]{1,0:T(8,128)S(1)}, f32[48,512]{1,0:T(8,128)S(1)}, u32[]{:S(2)}, u32[]{:S(2)}) collective-permute-start(f32[48,512]{1,0:T(8,128)S(1)} %get-tuple-element.77), channel_id=1, source_target_pairs={{4,8},{8,4},{12,16},{16,12},{20,24},{24,20},{28,32},{32,28},{36,40... | collective-permute-start | bytes 294920 | tf_op jit(solution)/shard_map/ppermute | solution.py:344
  65.9 3.8 %collective-permute-start.11 = (f32[48,256]{1,0:T(8,128)S(1)}, f32[48,256]{1,0:T(8,128)S(1)}, u32[]{:S(2)}, u32[]{:S(2)}) collective-permute-start(f32[48,256]{1,0:T(8,128)S(1)} %get-tuple-element.79), channel_id=1, source_target_pairs={{1,2},{2,1},{5,6},{6,5},{9,10},{10,9},{13,14},{14,13},{17,18},{18,... | collective-permute-start | bytes 147464 | tf_op jit(solution)/shard_map/ppermute | solution.py:344
  72.6 1.8 %shard_map.119.part_ref = f32[192,1024]{1,0:T(8,128)S(1)} custom-call(f32[192,1024]{1,0:T(8,128)S(1)} %get-tuple-element.73.d_ref, f32[8,128]{1,0:T(8,128)S(1)} %bitcast.35, s32[48,128]{1,0:T(8,128)S(1)} %bitcast.20, bf16[192,768]{1,0:T(8,128)(2,1)S(1)} %get-tuple-element.59.wh_ref, bf16[192,768]{1,0:T(8,128)(2,1)S(1)} %get-tuple-element.60.wl_ref, ...), custom_call_target="tpu_custom_call" | custom-call | tf_op jit(solution)/shard_map/pallas_call | solution.py:327
  74.5 2.6 %shard_map.120 = (f32[192,1024]{1,0:T(8,128)S(1)}, f32[192,1024]{1,0:T(8,128)}, f32[192,1024]{1,0:T(8,128)}, f32[48,512]{1,0:T(8,128)}, f32[48,512]{1,0:T(8,128)}, /*index=5*/f32[48,256]{1,0:T(8,128)}, f32[48,256]{1,0:T(8,128)}) custom-call(f32[192,1024]{1,0:T(8,128)S(1)} %shard_map.119.part_ref, f32[192,1024]{1,0:T(8,128)S(1)} %get-tuple-element.74.r_ref, ...), custom_call_target="tpu_custom_call" | custom-call | tf_op jit(solution)/shard_map/pallas_call | solution.py:327
  78.0 1.6 %copy-done.2 = bf16[1024,1024]{1,0:T(8,128)(2,1)S(1)} copy-done((bf16[1024,1024]{1,0:T(8,128)(2,1)S(1)}, bf16[1024,1024]{1,0:T(8,128)(2,1)}, u32[]{:S(2)}) %copy-start.2) | copy-done | bytes 2097176
  81.9 3.9 %shard_map.123 = (f32[192,1024]{1,0:T(8,128)S(1)}, f32[192,1024]{1,0:T(8,128)S(1)}, f32[48,512]{1,0:T(8,128)S(1)}, f32[48,512]{1,0:T(8,128)S(1)}, f32[48,256]{1,0:T(8,128)S(1)}, /*index=5*/f32[48,256]{1,0:T(8,128)S(1)}) custom-call(f32[192,1024]{1,0:T(8,128)S(1)} %copy-done.7, f32[192,1024]{1,0:T(8,128)S(1)} %copy-done.5, f32[8,128]{1,0:T(8,128)S(1)} %bitcast.37, ...), custom_call_target="tpu_custom_call" | custom-call | tf_op jit(solution)/shard_map/pallas_call | solution.py:327
  85.9 2.4 %collective-permute-start.13 = (f32[48,512]{1,0:T(8,128)S(1)}, f32[48,512]{1,0:T(8,128)S(1)}, u32[]{:S(2)}, u32[]{:S(2)}) collective-permute-start(f32[48,512]{1,0:T(8,128)S(1)} %get-tuple-element.88), channel_id=1, source_target_pairs={{4,8},{8,4},{12,16},{16,12},{20,24},{24,20},{28,32},{32,28},{36,40... | collective-permute-start | bytes 294920 | tf_op jit(solution)/shard_map/ppermute | solution.py:344
  88.4 2.1 %collective-permute-start.15 = (f32[48,256]{1,0:T(8,128)S(1)}, f32[48,256]{1,0:T(8,128)S(1)}, u32[]{:S(2)}, u32[]{:S(2)}) collective-permute-start(f32[48,256]{1,0:T(8,128)S(1)} %get-tuple-element.90), channel_id=1, source_target_pairs={{1,2},{2,1},{5,6},{6,5},{9,10},{10,9},{13,14},{14,13},{17,18},{18,... | collective-permute-start | bytes 147464 | tf_op jit(solution)/shard_map/ppermute | solution.py:344
  90.5 1.8 %shard_map.124.part_ref = f32[192,1024]{1,0:T(8,128)S(1)} custom-call(f32[192,1024]{1,0:T(8,128)S(1)} %get-tuple-element.85.d_ref, f32[8,128]{1,0:T(8,128)S(1)} %bitcast.38, s32[48,128]{1,0:T(8,128)S(1)} %bitcast.22, bf16[192,768]{1,0:T(8,128)(2,1)S(1)} %get-tuple-element.59.wh_ref, bf16[192,768]{1,0:T(8,128)(2,1)S(1)} %get-tuple-element.60.wl_ref, ...), custom_call_target="tpu_custom_call" | custom-call | tf_op jit(solution)/shard_map/pallas_call | solution.py:327
  94.1 1.7 %shard_map.125 = (f32[192,1024]{1,0:T(8,128)S(1)}, f32[192,1024]{1,0:T(8,128)S(1)}, f32[192,1024]{1,0:T(8,128)S(1)}, f32[48,512]{1,0:T(8,128)S(1)}, f32[48,512]{...) custom-call(f32[192,1024]{1,0:T(8,128)S(1)} %shard_map.124.part_ref, f32[192,1024]{1,0:T(8,128)S(1)} %copy-done.8, ...), custom_call_target="tpu_custom_call" | custom-call | tf_op jit(solution)/shard_map/pallas_call | solution.py:327
  96.3 5.4 %collective-permute-start.17 = (f32[48,512]{1,0:T(8,128)S(1)}, f32[48,512]{1,0:T(8,128)S(1)}, u32[]{:S(2)}, u32[]{:S(2)}) collective-permute-start(f32[48,512]{1,0:T(8,128)S(1)} %get-tuple-element.95), channel_id=1, source_target_pairs={{4,8},{8,4},{12,16},{16,12},{20,24},{24,20},{28,32},{32,28},{36,40... | collective-permute-start | bytes 294920 | tf_op jit(solution)/shard_map/ppermute | solution.py:344
  101.7 2.4 %collective-permute-start.19 = (f32[48,256]{1,0:T(8,128)S(1)}, f32[48,256]{1,0:T(8,128)S(1)}, u32[]{:S(2)}, u32[]{:S(2)}) collective-permute-start(f32[48,256]{1,0:T(8,128)S(1)} %get-tuple-element.97), channel_id=1, source_target_pairs={{1,2},{2,1},{5,6},{6,5},{9,10},{10,9},{13,14},{14,13},{17,18},{18,... | collective-permute-start | bytes 147464 | tf_op jit(solution)/shard_map/ppermute | solution.py:344
  104.1 1.8 %shard_map.126.part_ref = f32[192,1024]{1,0:T(8,128)S(1)} custom-call(f32[192,1024]{1,0:T(8,128)S(1)} %get-tuple-element.91.d_ref, f32[8,128]{1,0:T(8,128)S(1)} %bitcast.40, s32[48,128]{1,0:T(8,128)S(1)} %bitcast.24, bf16[192,768]{1,0:T(8,128)(2,1)S(1)} %get-tuple-element.59.wh_ref, bf16[192,768]{1,0:T(8,128)(2,1)S(1)} %get-tuple-element.60.wl_ref, ...), custom_call_target="tpu_custom_call" | custom-call | tf_op jit(solution)/shard_map/pallas_call | solution.py:327
  106.6 1.7 %shard_map.127 = (f32[192,1024]{1,0:T(8,128)S(1)}, f32[192,1024]{1,0:T(8,128)S(1)}, f32[192,1024]{1,0:T(8,128)S(1)}, f32[48,512]{1,0:T(8,128)S(1)}, f32[48,512]{...) custom-call(f32[192,1024]{1,0:T(8,128)S(1)} %shard_map.126.part_ref, ...), custom_call_target="tpu_custom_call" | custom-call | tf_op jit(solution)/shard_map/pallas_call | solution.py:327
  108.4 3.5 %collective-permute-start.21 = (f32[48,512]{1,0:T(8,128)S(1)}, f32[48,512]{1,0:T(8,128)S(1)}, u32[]{:S(2)}, u32[]{:S(2)}) collective-permute-start(f32[48,512]{1,0:T(8,128)S(1)} %get-tuple-element.102), channel_id=1, source_target_pairs={{4,8},{8,4},{12,16},{16,12},{20,24},{24,20},{28,32},{32,28},{36,40... | collective-permute-start | bytes 294920 | tf_op jit(solution)/shard_map/ppermute | solution.py:344
  111.9 2.5 %collective-permute-start.23 = (f32[48,256]{1,0:T(8,128)S(1)}, f32[48,256]{1,0:T(8,128)S(1)}, u32[]{:S(2)}, u32[]{:S(2)}) collective-permute-start(f32[48,256]{1,0:T(8,128)S(1)} %get-tuple-element.104), channel_id=1, source_target_pairs={{1,2},{2,1},{5,6},{6,5},{9,10},{10,9},{13,14},{14,13},{17,18},{18,... | collective-permute-start | bytes 147464 | tf_op jit(solution)/shard_map/ppermute | solution.py:344
  114.5 1.8 %shard_map.128.part_ref = f32[192,1024]{1,0:T(8,128)S(1)} custom-call(f32[192,1024]{1,0:T(8,128)S(1)} %get-tuple-element.98.d_ref, f32[8,128]{1,0:T(8,128)S(1)} %bitcast.42, s32[48,128]{1,0:T(8,128)S(1)} %bitcast.26, bf16[192,768]{1,0:T(8,128)(2,1)S(1)} %get-tuple-element.59.wh_ref, bf16[192,768]{1,0:T(8,128)(2,1)S(1)} %get-tuple-element.60.wl_ref, ...), custom_call_target="tpu_custom_call" | custom-call | tf_op jit(solution)/shard_map/pallas_call | solution.py:327
  116.8 1.8 %shard_map.129 = (f32[192,1024]{1,0:T(8,128)S(1)}, f32[192,1024]{1,0:T(8,128)S(1)}, f32[192,1024]{1,0:T(8,128)S(1)}, f32[48,512]{1,0:T(8,128)S(1)}, f32[48,512]{...) custom-call(f32[192,1024]{1,0:T(8,128)S(1)} %shard_map.128.part_ref, ...), custom_call_target="tpu_custom_call" | custom-call | tf_op jit(solution)/shard_map/pallas_call | solution.py:327
  118.8 5.3 %collective-permute-start.25 = (f32[48,512]{1,0:T(8,128)S(1)}, f32[48,512]{1,0:T(8,128)S(1)}, u32[]{:S(2)}, u32[]{:S(2)}) collective-permute-start(f32[48,512]{1,0:T(8,128)S(1)} %get-tuple-element.109), channel_id=1, source_target_pairs={{4,8},{8,4},{12,16},{16,12},{20,24},{24,20},{28,32},{32,28},{36,40... | collective-permute-start | bytes 294920 | tf_op jit(solution)/shard_map/ppermute | solution.py:344
  124.1 2.3 %collective-permute-start.27 = (f32[48,256]{1,0:T(8,128)S(1)}, f32[48,256]{1,0:T(8,128)S(1)}, u32[]{:S(2)}, u32[]{:S(2)}) collective-permute-start(f32[48,256]{1,0:T(8,128)S(1)} %get-tuple-element.111), channel_id=1, source_target_pairs={{1,2},{2,1},{5,6},{6,5},{9,10},{10,9},{13,14},{14,13},{17,18},{18,... | collective-permute-start | bytes 147464 | tf_op jit(solution)/shard_map/ppermute | solution.py:344
  126.5 1.8 %shard_map.130.part_ref = f32[192,1024]{1,0:T(8,128)S(1)} custom-call(f32[192,1024]{1,0:T(8,128)S(1)} %get-tuple-element.105.d_ref, f32[8,128]{1,0:T(8,128)S(1)} %bitcast.44, s32[48,128]{1,0:T(8,128)S(1)} %bitcast.28, bf16[192,768]{1,0:T(8,128)(2,1)S(1)} %get-tuple-element.59.wh_ref, bf16[192,768]{1,0:T(8,128)(2,1)S(1)} %get-tuple-element.60.wl_ref, ...), custom_call_target="tpu_custom_call" | custom-call | tf_op jit(solution)/shard_map/pallas_call | solution.py:327
  129.0 2.5 %shard_map.131 = (f32[1536,128]{1,0:T(8,128)}, f32[1536,128]{1,0:T(8,128)}) custom-call(f32[192,1024]{1,0:T(8,128)S(1)} %shard_map.130.part_ref, f32[192,1024]{1,0:T(8,128)S(1)} %get-tuple-element.106.r_ref, f32[192,1024]{1,0:T(8,128)S(1)} %get-tuple-element.107.x_ref, s32[48,128]{1,0:T(8,128)S(1)} %bitcast.29, ...), custom_call_target="tpu_custom_call" | custom-call | tf_op jit(solution)/shard_map/pallas_call | solution.py:327
  (82 shorter events, 19.3 us)
Async XLA Ops:
  8.9 18.5 %copy-start.15 = (f32[192,24]{0,1:T(8,128)S(1)}, f32[192,24]{0,1:T(8,128)}, u32[]{:S(2)}) copy-start(f32[192,24]{0,1:T(8,128)} %param.17) | copy-start | bytes 55300
  8.9 20.0 %copy-start.3 = (s32[6,2,4,128]{3,2,1,0:T(4,128)S(1)}, s32[6,2,4,128]{3,2,1,0:T(4,128)}, u32[]{:S(2)}) copy-start(s32[6,2,4,128]{3,2,1,0:T(4,128)} %param.12) | copy-start | bytes 73732
  8.9 69.1 %all-to-all-start = ((f32[32,6,24,128]{3,2,1,0:T(8,128)}), f32[32,6,24,128]{3,2,1,0:T(8,128)S(1)}, u32[]{:S(2)}, u32[]{:S(2)}) async-start(f32[32,6,24,128]{3,2,1,0:T(8,128)} %shard_map.122), calls=%async_computation | async-start | bytes 4718592 | tf_op jit(solution)/shard_map/all_to_all | solution.py:383
  17.4 30.7 %copy-start.13 = (s32[2]{0:T(128)}, s32[2]{0:T(128)S(1)}, u32[]{:S(2)}) copy-start(s32[2]{0:T(128)S(1)} %pad_add_fusion.par_ref) | copy-start | bytes 28
  19.5 11.2 %collective-permute-start = (f32[48,512]{1,0:T(8,128)S(1)}, f32[48,512]{1,0:T(8,128)S(1)}, u32[]{:S(2)}, u32[]{:S(2)}) collective-permute-start(f32[48,512]{1,0:T(8,128)S(1)} %get-tuple-element.62), channel_id=1, source_target_pairs={{0,4},{4,0},{8,12},{12,8},{16,20},{20,16},{24,28},{28,24},{32,36},... | collective-permute-start | bytes 294920 | tf_op jit(solution)/shard_map/ppermute | solution.py:339
  20.0 26.5 %collective-permute-start.1 = (f32[48,512]{1,0:T(8,128)S(1)}, f32[48,512]{1,0:T(8,128)S(1)}, u32[]{:S(2)}, u32[]{:S(2)}) collective-permute-start(f32[48,512]{1,0:T(8,128)S(1)} %get-tuple-element.63), channel_id=1, source_target_pairs={{4,8},{8,4},{12,16},{16,12},{20,24},{24,20},{28,32},{32,28},{36,40... | collective-permute-start | bytes 294920 | tf_op jit(solution)/shard_map/ppermute | solution.py:344
  23.1 7.6 %collective-permute-start.2 = (f32[48,256]{1,0:T(8,128)S(1)}, f32[48,256]{1,0:T(8,128)S(1)}, u32[]{:S(2)}, u32[]{:S(2)}) collective-permute-start(f32[48,256]{1,0:T(8,128)S(1)} %get-tuple-element.64), channel_id=1, source_target_pairs={{0,1},{1,0},{2,3},{3,2},{4,5},{5,4},{6,7},{7,6},{8,9},{9,8},{10,11... | collective-permute-start | bytes 147464 | tf_op jit(solution)/shard_map/ppermute | solution.py:339
  23.3 7.4 %collective-permute-start.3 = (f32[48,256]{1,0:T(8,128)S(1)}, f32[48,256]{1,0:T(8,128)S(1)}, u32[]{:S(2)}, u32[]{:S(2)}) collective-permute-start(f32[48,256]{1,0:T(8,128)S(1)} %get-tuple-element.65), channel_id=1, source_target_pairs={{1,2},{2,1},{5,6},{6,5},{9,10},{10,9},{13,14},{14,13},{17,18},{18,... | collective-permute-start | bytes 147464 | tf_op jit(solution)/shard_map/ppermute | solution.py:344
  48.1 9.4 %collective-permute-start.4 = (f32[48,512]{1,0:T(8,128)S(1)}, f32[48,512]{1,0:T(8,128)S(1)}, u32[]{:S(2)}, u32[]{:S(2)}) collective-permute-start(f32[48,512]{1,0:T(8,128)S(1)} %get-tuple-element.69), channel_id=1, source_target_pairs={{0,4},{4,0},{8,12},{12,8},{16,20},{20,16},{24,28},{28,24},{32,36},... | collective-permute-start | bytes 294920 | tf_op jit(solution)/shard_map/ppermute | solution.py:339
  49.4 8.1 %collective-permute-start.5 = (f32[48,512]{1,0:T(8,128)S(1)}, f32[48,512]{1,0:T(8,128)S(1)}, u32[]{:S(2)}, u32[]{:S(2)}) collective-permute-start(f32[48,512]{1,0:T(8,128)S(1)} %get-tuple-element.70), channel_id=1, source_target_pairs={{4,8},{8,4},{12,16},{16,12},{20,24},{24,20},{28,32},{32,28},{36,40... | collective-permute-start | bytes 294920 | tf_op jit(solution)/shard_map/ppermute | solution.py:344
  51.3 6.1 %collective-permute-start.6 = (f32[48,256]{1,0:T(8,128)S(1)}, f32[48,256]{1,0:T(8,128)S(1)}, u32[]{:S(2)}, u32[]{:S(2)}) collective-permute-start(f32[48,256]{1,0:T(8,128)S(1)} %get-tuple-element.71), channel_id=1, source_target_pairs={{0,1},{1,0},{2,3},{3,2},{4,5},{5,4},{6,7},{7,6},{8,9},{9,8},{10,11... | collective-permute-start | bytes 147464 | tf_op jit(solution)/shard_map/ppermute | solution.py:339
  51.6 5.9 %collective-permute-start.7 = (f32[48,256]{1,0:T(8,128)S(1)}, f32[48,256]{1,0:T(8,128)S(1)}, u32[]{:S(2)}, u32[]{:S(2)}) collective-permute-start(f32[48,256]{1,0:T(8,128)S(1)} %get-tuple-element.72), channel_id=1, source_target_pairs={{1,2},{2,1},{5,6},{6,5},{9,10},{10,9},{13,14},{14,13},{17,18},{18,... | collective-permute-start | bytes 147464 | tf_op jit(solution)/shard_map/ppermute | solution.py:344
  59.2 15.3 %collective-permute-start.8 = (f32[48,512]{1,0:T(8,128)S(1)}, f32[48,512]{1,0:T(8,128)S(1)}, u32[]{:S(2)}, u32[]{:S(2)}) collective-permute-start(f32[48,512]{1,0:T(8,128)S(1)} %get-tuple-element.76), channel_id=1, source_target_pairs={{0,4},{4,0},{8,12},{12,8},{16,20},{20,16},{24,28},{28,24},{32,36},... | collective-permute-start | bytes 294920 | tf_op jit(solution)/shard_map/ppermute | solution.py:339
  60.1 14.4 %collective-permute-start.9 = (f32[48,512]{1,0:T(8,128)S(1)}, f32[48,512]{1,0:T(8,128)S(1)}, u32[]{:S(2)}, u32[]{:S(2)}) collective-permute-start(f32[48,512]{1,0:T(8,128)S(1)} %get-tuple-element.77), channel_id=1, source_target_pairs={{4,8},{8,4},{12,16},{16,12},{20,24},{24,20},{28,32},{32,28},{36,40... | collective-permute-start | bytes 294920 | tf_op jit(solution)/shard_map/ppermute | solution.py:344
  65.8 8.7 %collective-permute-start.10 = (f32[48,256]{1,0:T(8,128)S(1)}, f32[48,256]{1,0:T(8,128)S(1)}, u32[]{:S(2)}, u32[]{:S(2)}) collective-permute-start(f32[48,256]{1,0:T(8,128)S(1)} %get-tuple-element.78), channel_id=1, source_target_pairs={{0,1},{1,0},{2,3},{3,2},{4,5},{5,4},{6,7},{7,6},{8,9},{9,8},{10,11... | collective-permute-start | bytes 147464 | tf_op jit(solution)/shard_map/ppermute | solution.py:339
  65.9 8.6 %collective-permute-start.11 = (f32[48,256]{1,0:T(8,128)S(1)}, f32[48,256]{1,0:T(8,128)S(1)}, u32[]{:S(2)}, u32[]{:S(2)}) collective-permute-start(f32[48,256]{1,0:T(8,128)S(1)} %get-tuple-element.79), channel_id=1, source_target_pairs={{1,2},{2,1},{5,6},{6,5},{9,10},{10,9},{13,14},{14,13},{17,18},{18,... | collective-permute-start | bytes 147464 | tf_op jit(solution)/shard_map/ppermute | solution.py:344
  85.8 7.8 %collective-permute-start.12 = (f32[48,512]{1,0:T(8,128)S(1)}, f32[48,512]{1,0:T(8,128)S(1)}, u32[]{:S(2)}, u32[]{:S(2)}) collective-permute-start(f32[48,512]{1,0:T(8,128)S(1)} %get-tuple-element.87), channel_id=1, source_target_pairs={{0,4},{4,0},{8,12},{12,8},{16,20},{20,16},{24,28},{28,24},{32,36},... | collective-permute-start | bytes 294920 | tf_op jit(solution)/shard_map/ppermute | solution.py:339
  85.9 8.2 %collective-permute-start.13 = (f32[48,512]{1,0:T(8,128)S(1)}, f32[48,512]{1,0:T(8,128)S(1)}, u32[]{:S(2)}, u32[]{:S(2)}) collective-permute-start(f32[48,512]{1,0:T(8,128)S(1)} %get-tuple-element.88), channel_id=1, source_target_pairs={{4,8},{8,4},{12,16},{16,12},{20,24},{24,20},{28,32},{32,28},{36,40... | collective-permute-start | bytes 294920 | tf_op jit(solution)/shard_map/ppermute | solution.py:344
  88.3 4.0 %collective-permute-start.14 = (f32[48,256]{1,0:T(8,128)S(1)}, f32[48,256]{1,0:T(8,128)S(1)}, u32[]{:S(2)}, u32[]{:S(2)}) collective-permute-start(f32[48,256]{1,0:T(8,128)S(1)} %get-tuple-element.89), channel_id=1, source_target_pairs={{0,1},{1,0},{2,3},{3,2},{4,5},{5,4},{6,7},{7,6},{8,9},{9,8},{10,11... | collective-permute-start | bytes 147464 | tf_op jit(solution)/shard_map/ppermute | solution.py:339
  88.4 5.2 %collective-permute-start.15 = (f32[48,256]{1,0:T(8,128)S(1)}, f32[48,256]{1,0:T(8,128)S(1)}, u32[]{:S(2)}, u32[]{:S(2)}) collective-permute-start(f32[48,256]{1,0:T(8,128)S(1)} %get-tuple-element.90), channel_id=1, source_target_pairs={{1,2},{2,1},{5,6},{6,5},{9,10},{10,9},{13,14},{14,13},{17,18},{18,... | collective-permute-start | bytes 147464 | tf_op jit(solution)/shard_map/ppermute | solution.py:344
  95.8 10.7 %collective-permute-start.16 = (f32[48,512]{1,0:T(8,128)S(1)}, f32[48,512]{1,0:T(8,128)S(1)}, u32[]{:S(2)}, u32[]{:S(2)}) collective-permute-start(f32[48,512]{1,0:T(8,128)S(1)} %get-tuple-element.94), channel_id=1, source_target_pairs={{0,4},{4,0},{8,12},{12,8},{16,20},{20,16},{24,28},{28,24},{32,36},... | collective-permute-start | bytes 294920 | tf_op jit(solution)/shard_map/ppermute | solution.py:339
  96.3 10.3 %collective-permute-start.17 = (f32[48,512]{1,0:T(8,128)S(1)}, f32[48,512]{1,0:T(8,128)S(1)}, u32[]{:S(2)}, u32[]{:S(2)}) collective-permute-start(f32[48,512]{1,0:T(8,128)S(1)} %get-tuple-element.95), channel_id=1, source_target_pairs={{4,8},{8,4},{12,16},{16,12},{20,24},{24,20},{28,32},{32,28},{36,40... | collective-permute-start | bytes 294920 | tf_op jit(solution)/shard_map/ppermute | solution.py:344
  101.6 4.3 %collective-permute-start.18 = (f32[48,256]{1,0:T(8,128)S(1)}, f32[48,256]{1,0:T(8,128)S(1)}, u32[]{:S(2)}, u32[]{:S(2)}) collective-permute-start(f32[48,256]{1,0:T(8,128)S(1)} %get-tuple-element.96), channel_id=1, source_target_pairs={{0,1},{1,0},{2,3},{3,2},{4,5},{5,4},{6,7},{7,6},{8,9},{9,8},{10,11... | collective-permute-start | bytes 147464 | tf_op jit(solution)/shard_map/ppermute | solution.py:339
  101.7 4.8 %collective-permute-start.19 = (f32[48,256]{1,0:T(8,128)S(1)}, f32[48,256]{1,0:T(8,128)S(1)}, u32[]{:S(2)}, u32[]{:S(2)}) collective-permute-start(f32[48,256]{1,0:T(8,128)S(1)} %get-tuple-element.97), channel_id=1, source_target_pairs={{1,2},{2,1},{5,6},{6,5},{9,10},{10,9},{13,14},{14,13},{17,18},{18,... | collective-permute-start | bytes 147464 | tf_op jit(solution)/shard_map/ppermute | solution.py:344
  108.3 8.5 %collective-permute-start.20 = (f32[48,512]{1,0:T(8,128)S(1)}, f32[48,512]{1,0:T(8,128)S(1)}, u32[]{:S(2)}, u32[]{:S(2)}) collective-permute-start(f32[48,512]{1,0:T(8,128)S(1)} %get-tuple-element.101), channel_id=1, source_target_pairs={{0,4},{4,0},{8,12},{12,8},{16,20},{20,16},{24,28},{28,24},{32,36},... | collective-permute-start | bytes 294920 | tf_op jit(solution)/shard_map/ppermute | solution.py:339
  108.4 8.4 %collective-permute-start.21 = (f32[48,512]{1,0:T(8,128)S(1)}, f32[48,512]{1,0:T(8,128)S(1)}, u32[]{:S(2)}, u32[]{:S(2)}) collective-permute-start(f32[48,512]{1,0:T(8,128)S(1)} %get-tuple-element.102), channel_id=1, source_target_pairs={{4,8},{8,4},{12,16},{16,12},{20,24},{24,20},{28,32},{32,28},{36,40... | collective-permute-start | bytes 294920 | tf_op jit(solution)/shard_map/ppermute | solution.py:344
  111.9 4.4 %collective-permute-start.22 = (f32[48,256]{1,0:T(8,128)S(1)}, f32[48,256]{1,0:T(8,128)S(1)}, u32[]{:S(2)}, u32[]{:S(2)}) collective-permute-start(f32[48,256]{1,0:T(8,128)S(1)} %get-tuple-element.103), channel_id=1, source_target_pairs={{0,1},{1,0},{2,3},{3,2},{4,5},{5,4},{6,7},{7,6},{8,9},{9,8},{10,11... | collective-permute-start | bytes 147464 | tf_op jit(solution)/shard_map/ppermute | solution.py:339
  111.9 4.8 %collective-permute-start.23 = (f32[48,256]{1,0:T(8,128)S(1)}, f32[48,256]{1,0:T(8,128)S(1)}, u32[]{:S(2)}, u32[]{:S(2)}) collective-permute-start(f32[48,256]{1,0:T(8,128)S(1)} %get-tuple-element.104), channel_id=1, source_target_pairs={{1,2},{2,1},{5,6},{6,5},{9,10},{10,9},{13,14},{14,13},{17,18},{18,... | collective-permute-start | bytes 147464 | tf_op jit(solution)/shard_map/ppermute | solution.py:344
  118.6 10.4 %collective-permute-start.24 = (f32[48,512]{1,0:T(8,128)S(1)}, f32[48,512]{1,0:T(8,128)S(1)}, u32[]{:S(2)}, u32[]{:S(2)}) collective-permute-start(f32[48,512]{1,0:T(8,128)S(1)} %get-tuple-element.108), channel_id=1, source_target_pairs={{0,4},{4,0},{8,12},{12,8},{16,20},{20,16},{24,28},{28,24},{32,36},... | collective-permute-start | bytes 294920 | tf_op jit(solution)/shard_map/ppermute | solution.py:339
  118.8 10.2 %collective-permute-start.25 = (f32[48,512]{1,0:T(8,128)S(1)}, f32[48,512]{1,0:T(8,128)S(1)}, u32[]{:S(2)}, u32[]{:S(2)}) collective-permute-start(f32[48,512]{1,0:T(8,128)S(1)} %get-tuple-element.109), channel_id=1, source_target_pairs={{4,8},{8,4},{12,16},{16,12},{20,24},{24,20},{28,32},{32,28},{36,40... | collective-permute-start | bytes 294920 | tf_op jit(solution)/shard_map/ppermute | solution.py:344
  124.0 4.3 %collective-permute-start.26 = (f32[48,256]{1,0:T(8,128)S(1)}, f32[48,256]{1,0:T(8,128)S(1)}, u32[]{:S(2)}, u32[]{:S(2)}) collective-permute-start(f32[48,256]{1,0:T(8,128)S(1)} %get-tuple-element.110), channel_id=1, source_target_pairs={{0,1},{1,0},{2,3},{3,2},{4,5},{5,4},{6,7},{7,6},{8,9},{9,8},{10,11... | collective-permute-start | bytes 147464 | tf_op jit(solution)/shard_map/ppermute | solution.py:339
  124.1 4.8 %collective-permute-start.27 = (f32[48,256]{1,0:T(8,128)S(1)}, f32[48,256]{1,0:T(8,128)S(1)}, u32[]{:S(2)}, u32[]{:S(2)}) collective-permute-start(f32[48,256]{1,0:T(8,128)S(1)} %get-tuple-element.111), channel_id=1, source_target_pairs={{1,2},{2,1},{5,6},{6,5},{9,10},{10,9},{13,14},{14,13},{17,18},{18,... | collective-permute-start | bytes 147464 | tf_op jit(solution)/shard_map/ppermute | solution.py:344
  (15 other events, 104.2 us)

commit v2 on v1

--- a/solution.py
+++ b/solution.py
@@ -119,14 +119,9 @@
     high, low = split(pt)
     pth_ref[...] = high
     ptl_ref[...] = low
-    row = lax.broadcasted_iota(jnp.int32, (CW, 32), 0)
-    col = lax.broadcasted_iota(jnp.int32, (CW, 32), 1)
-    spread = ((row & 3) * 8 + (row >> 2) == col).astype(F32)
-    p = pt.T
-    p_high, p_low = split(p)
-    spread = spread.astype(BF16)
-    ph_ref[...] = dot(p_high, spread).astype(BF16)
-    pl_ref[...] = dot(p_low, spread).astype(BF16)
+    high, low = split(pt.T)
+    ph_ref[...] = high
+    pl_ref[...] = low
 
 
 def interior_kernel(d_ref, coef_ref, ori_ref, wh_ref, wl_ref, sel_ref, out_ref, xh_ref, xl_ref, t_ref):
@@ -192,21 +187,26 @@
     even_x = par_ref[0] == 0
     even_y = par_ref[1] == 0
 
-    def lower(inside, outside, even):
-        return lambda n: jnp.where(even, outside[:, lanes(n)], inside[:, lanes(n)])
-
-    def upper(inside, outside, even):
-        return lambda n: jnp.where(even, inside[:, lanes(n)], outside[:, lanes(n)])
+    def lower(inside, outside, even, there):
+        return lambda n: jnp.where(
+            there, jnp.where(even, outside[:, lanes(n)], inside[:, lanes(n)]), 0.0
+        )
+
+    def upper(inside, outside, even, there):
+        return lambda n: jnp.where(
+            there, jnp.where(even, inside[:, lanes(n)], outside[:, lanes(n)]), 0.0
+        )
 
     weights = (ori_ref, wh_ref, wl_ref)
     ad_ref[:, 0:512] = part_ref[:, 0:512] + halo_product(
-        lower(gx_in, gx_out, even_x), (0, 1, 2, 3), 0, *weights
+        lower(gx_in, gx_out, even_x, par_ref[2] == 1), (0, 1, 2, 3), 0, *weights
     )
     ad_ref[:, 512:1024] = part_ref[:, 512:1024] + halo_product(
-        upper(gx_in, gx_out, even_x), (4, 5, 6, 7), 1, *weights
+        upper(gx_in, gx_out, even_x, par_ref[3] == 1), (4, 5, 6, 7), 1, *weights
     )
     for cols, direction, pick in (((0, 4), 2, lower), ((3, 7), 3, upper)):
-        both = halo_product(pick(gy_in, gy_out, even_y), cols, direction, *weights)
+        there = par_ref[direction + 2] == 1
+        both = halo_product(pick(gy_in, gy_out, even_y, there), cols, direction, *weights)
         for n, col in enumerate(cols):
             ad_ref[:, lanes(col)] += both[:, lanes(n)]
 
@@ -248,8 +248,10 @@
 
 def pack_kernel(in_ref, out_ref):
     for s in range(in_ref.shape[0]):
-        for m in range(6):
-            out_ref[s, m] = jnp.concatenate([in_ref[s, 4 * m + q] for q in range(4)], axis=-1)
+        for column in range(CW):
+            tiles = [in_ref[s, 8 * q : 8 * q + 8, column, :] for q in range(3)]
+            tiles.append(jnp.zeros((8, CAP), F32))
+            out_ref[s, column] = jnp.concatenate(tiles, axis=-1)
 
 
 def slots_kernel(agg_ref, owner_ref, hot_ref):
@@ -271,27 +273,47 @@
         hot_ref[:, at] = hot.astype(BF16)
 
 
-def coarse_kernel(
-    r_ref, x_ref, coef_ref, hot_ref, inv_ref, pth_ref, ptl_ref, ph_ref, pl_ref, sel_ref, par_ref,
-    d_out, x_out, sx_in, sx_out, sy_in, sy_out, y_ref, sol_ref,
-):
+def restrict_kernel(r_ref, hot_ref, pth_ref, ptl_ref, out_ref, rhs_ref):
     r_high, r_low = split(r_ref[...])
     proj = dot3(pth_ref[...], ptl_ref[...], r_high, r_low)
     p_high, p_low = split(proj)
-    rhs = dot_nt(p_high, hot_ref[...]) + dot_nt(p_low, hot_ref[...])
-    group = lax.broadcasted_iota(jnp.int32, (CW, LANES), 1) >> 5
+    rhs_ref[...] = dot_nt(p_high, hot_ref[...]) + dot_nt(p_low, hot_ref[...])
+    group = lax.broadcasted_iota(jnp.int32, (8, LANES), 1) >> 5
     for o in range(OWNERS):
-        part = jnp.where(group == o % 4, rhs[:, lanes(o // 4)], 0.0)
-        part = part + pltpu.roll(part, 32, 1)
-        part = part + pltpu.roll(part, 64, 1)
-        y_ref[o, 0:6, :] = jnp.sum(inv_ref[o] * part[None], axis=1)
-        y_ref[o, 6:8, :] = jnp.zeros((2, LANES), F32)
+        total = jnp.zeros((8, LANES), F32)
+        for q in range(3):
+            moved = rhs_ref[8 * q : 8 * q + 8, lanes(o // 4)]
+            if q != o % 4:
+                moved = pltpu.roll(moved, 32 * ((q - o) % 4), 1)
+            total = jnp.where(group == q, moved, total)
+        out_ref[o] = total
+
+
+def solve_kernel(rhs_ref, inv_ref, out_ref, wide_ref):
     group = lax.broadcasted_iota(jnp.int32, (8, LANES), 1) >> 5
-    for q in range(4):
+    for s in range(OWNERS):
+        tile = rhs_ref[s]
+        for q in range(3):
+            part = jnp.where(group == q, tile, 0.0)
+            part = part + pltpu.roll(part, 32, 1)
+            wide_ref[s, 8 * q : 8 * q + 8, :] = part + pltpu.roll(part, 64, 1)
+        total = None
+        for b in range(CW):
+            term = inv_ref[s, b] * wide_ref[s, b : b + 1, :]
+            total = term if total is None else total + term
+        out_ref[s] = total
+
+
+def lift_kernel(
+    sol_in, x_ref, coef_ref, hot_ref, ph_ref, pl_ref, sel_ref, par_ref,
+    d_out, x_out, sx_in, sx_out, sy_in, sy_out, sol_ref,
+):
+    group = lax.broadcasted_iota(jnp.int32, (8, LANES), 1) >> 5
+    for q in range(3):
         for j in range(8):
             total = jnp.zeros((8, LANES), F32)
             for g in range(4):
-                moved = y_ref[4 * j + g]
+                moved = sol_in[4 * j + g]
                 if g != q:
                     moved = pltpu.roll(moved, 32 * ((g - q) % 4), 1)
                 total = jnp.where(group == g, moved, total)
@@ -316,7 +338,7 @@
     return pltpu.VMEM(shape, dtype)
 
 
-def call(kernel, outs, args, scratch=(), smem=(), limit=48):
+def call(kernel, outs, args, scratch=(), smem=(), limit=20):
     vmem = pl.BlockSpec(memory_space=pltpu.VMEM)
     scalar = pl.BlockSpec(memory_space=pltpu.SMEM)
     specs = [scalar if n in smem else vmem for n in range(len(args))]
@@ -341,7 +363,9 @@
 
 def swap_odd(v, axis):
     count = lax.axis_size(axis)
-    return lax.ppermute(v, axis, [(i, i + 1 if i % 2 else i - 1) for i in range(1, count - 1)])
+    return lax.ppermute(
+        v, axis, [(i, (i + 1 if i % 2 else i - 1) % count) for i in range(count)]
+    )
 
 
 def exchange(sends):
@@ -368,19 +392,20 @@
     coarse_inverse,
 ):
     shape = right_side.shape
-    par = jnp.stack([lax.axis_index("gx") & 1, lax.axis_index("gy") & 1]).astype(jnp.int32)
+    at_x, at_y = lax.axis_index("gx"), lax.axis_index("gy")
+    par = jnp.stack(
+        [
+            at_x & 1,
+            at_y & 1,
+            at_x > 0,
+            at_x < lax.axis_size("gx") - 1,
+            at_y > 0,
+            at_y < lax.axis_size("gy") - 1,
+        ]
+    ).astype(jnp.int32)
     sel = jnp.asarray(selection())
     coef = coefficient.reshape(COLS, LANES)
     ori = orientation.reshape(6 * COLS, LANES)
-
-    packed = pl.pallas_call(
-        pack_kernel,
-        out_shape=jax.ShapeDtypeStruct((OWNERS, 6, CW, LANES), F32),
-        grid=(8,),
-        in_specs=[pl.BlockSpec((4, CW, CW, CAP), lambda s: (s, 0, 0, 0))],
-        out_specs=pl.BlockSpec((4, 6, CW, LANES), lambda s: (s, 0, 0, 0)),
-    )(jnp.transpose(coarse_inverse[0], (0, 2, 3, 1)))
-    inverse = lax.all_to_all(packed, "gx", split_axis=0, concat_axis=0, tiled=True)
 
     full = field(BLOCK, ELEMS)
     r, d, *sends = call(
@@ -393,7 +418,7 @@
     wh, wl, pth, ptl, ph, plo = call(
         weights_kernel,
         [wide, wide, field(CW, BLOCK, dtype=BF16), field(CW, BLOCK, dtype=BF16),
-         field(BLOCK, 32, dtype=BF16), field(BLOCK, 32, dtype=BF16)],
+         field(BLOCK, CW, dtype=BF16), field(BLOCK, CW, dtype=BF16)],
         [stiffness, jnp.transpose(face_blocks, (0, 1, 3, 2)).reshape(576, BLOCK), prolong_basis.T],
     )
     hot = call(
@@ -432,12 +457,29 @@
     for scales in steps:
         r, d, x, *sends = advance(scales, r, d, x, sends)
     r, _, _, *_ = advance((0.0, 1.0 / THETA), r, d, x, sends)
+    packets = field(OWNERS, 8, LANES)
+    rhs = call(
+        restrict_kernel, [packets], [r, hot, pth, ptl], scratch=[pltpu.VMEM((CW, ELEMS), F32)]
+    )[0]
+    rhs = lax.all_to_all(rhs, "gx", split_axis=0, concat_axis=0, tiled=True)
+    inverse = pl.pallas_call(
+        pack_kernel,
+        out_shape=field(OWNERS, CW, 8, LANES),
+        grid=(8,),
+        in_specs=[pl.BlockSpec((4, CW, CW, CAP), lambda s: (s, 0, 0, 0))],
+        out_specs=pl.BlockSpec((4, CW, 8, LANES), lambda s: (s, 0, 0, 0)),
+        compiler_params=pltpu.CompilerParams(vmem_limit_bytes=16 << 20),
+    )(jnp.transpose(coarse_inverse[0], (0, 2, 3, 1)))
+    sol = call(
+        solve_kernel, [packets], [rhs, inverse], scratch=[pltpu.VMEM((OWNERS, CW, LANES), F32)]
+    )[0]
+    sol = lax.all_to_all(sol, "gx", split_axis=0, concat_axis=0, tiled=True)
     d, x, *sends = call(
-        coarse_kernel,
+        lift_kernel,
         [full, full, *SENDS],
-        [r, x, coef, hot, inverse, pth, ptl, ph, plo, sel, par],
-        scratch=[pltpu.VMEM((OWNERS, 8, LANES), F32), pltpu.VMEM((32, ELEMS), F32)],
-        smem=(10,),
+        [sol, x, coef, hot, ph, plo, sel, par],
+        scratch=[pltpu.VMEM((CW, ELEMS), F32)],
+        smem=(7,),
     )
     r, d, x, *sends = advance((0.0, 1.0 / THETA), r, d, x, sends)
     for scales in steps:

time: 132 us -> 119 us (0.902)
  the two profiles are of different devices: /device:TPU:47 before, /device:TPU:0 now
where the time goes in v2:
time: 119 us; the launch traced here: 118 us
  Pallas kernels  37.9 us (32%)
  starting transfers between devices  37.9 us (32%)
  local copies, waits for them, and re-layouts  15.9 us (13%)
  blocking collectives  15.1 us (13%)
  waiting for transfers between devices  10.3 us (9%)
    pallas_call x20, Pallas kernels, call(): pl.pallas_call(kernel, out_shape=outs, in_specs=specs, out_specs=[vmem] *...  32.7 us
    ppermute x14, starting transfers between devices, swap_odd(): lax.ppermute(v, axis, [(i, (i + 1 if i % 2 else i - 1) % count) for i in...  29.3 us
    unnamed x42, local copies, waits for them, and re-layouts  15.9 us
    all_to_all x1, blocking collectives, shards(): sol = lax.all_to_all(sol, 'gx', split_axis=0, concat_axis=0, tiled=True)  15.1 us
    ppermute x14, waiting for transfers between devices, swap_odd(): lax.ppermute(v, axis, [(i, (i + 1 if i % 2 else i - 1) % count) for i in...  9.12 us
    pallas_call x1, Pallas kernels, shards(): pl.pallas_call(pack_kernel, out_shape=field(OWNERS, CW, 8, LANES), grid=(...  5.15 us
    ppermute x14, starting transfers between devices, swap_even(): return lax.ppermute(v, axis, [(i, i ^ 1) for i in range(count)])  4.82 us
    all_to_all x1, starting transfers between devices, shards(): rhs = lax.all_to_all(rhs, 'gx', split_axis=0, concat_axis=0, tiled=True)  3.86 us
  transfers between devices with their start and end apart: 29, of which 10 were waited for; matrix products, arithmetic and copies ran while one was open for 0% of the time, Pallas kernels for 17%

profile of v2, /device:TPU:0, one launch (start us, length us, event | category | flops | bytes accessed | tf_op | source)
XLA Modules:
  0.0 118.1 jit_solution(7454059949440796603)
XLA Ops:
  4.5 6.4 %collective-permute-start.1 = (f32[48,512]{1,0:T(8,128)S(1)}, f32[48,512]{1,0:T(8,128)S(1)}, u32[]{:S(2)}, u32[]{:S(2)}) collective-permute-start(f32[48,512]{1,0:T(8,128)S(1)} %get-tuple-element.63), channel_id=1, source_target_pairs={{0,124},{4,8},{8,4},{12,16},{16,12},{20,24},{24,20},{28,32},{32,28... | collective-permute-start | bytes 294920 | tf_op jit(solution)/shard_map/ppermute | solution.py:366
  10.9 1.6 %collective-permute-start.2 = (f32[48,256]{1,0:T(8,128)S(1)}, f32[48,256]{1,0:T(8,128)S(1)}, u32[]{:S(2)}, u32[]{:S(2)}) collective-permute-start(f32[48,256]{1,0:T(8,128)S(1)} %get-tuple-element.64), channel_id=1, source_target_pairs={{0,1},{1,0},{2,3},{3,2},{4,5},{5,4},{6,7},{7,6},{8,9},{9,8},{10,11... | collective-permute-start | bytes 147464 | tf_op jit(solution)/shard_map/ppermute | solution.py:361
  12.5 2.2 %collective-permute-start.3 = (f32[48,256]{1,0:T(8,128)S(1)}, f32[48,256]{1,0:T(8,128)S(1)}, u32[]{:S(2)}, u32[]{:S(2)}) collective-permute-start(f32[48,256]{1,0:T(8,128)S(1)} %get-tuple-element.65), channel_id=1, source_target_pairs={{0,3},{1,2},{2,1},{3,0},{4,7},{5,6},{6,5},{7,4},{8,11},{9,10},{10,... | collective-permute-start | bytes 147464 | tf_op jit(solution)/shard_map/ppermute | solution.py:366
  20.2 1.8 %shard_map.115.part_ref = f32[192,1024]{1,0:T(8,128)S(1)} custom-call(f32[192,1024]{1,0:T(8,128)S(1)} %get-tuple-element.58.d_ref.x_ref, f32[8,128]{1,0:T(8,128)S(1)} %bitcast.36, s32[48,128]{1,0:T(8,128)S(1)} %bitcast.21, bf16[192,768]{1,0:T(8,128)(2,1)S(1)} %get-tuple-element.59.wh_ref, bf16[192,768]{1,0:T(8,128)(2,1)S(1)} %get-tuple-element.60.wl_ref, ...), custom_call_target="tpu_custom_call" | custom-call | tf_op jit(solution)/shard_map/pallas_call | solution.py:349
  22.0 1.6 %shard_map.116 = (f32[192,1024]{1,0:T(8,128)S(1)}, f32[192,1024]{1,0:T(8,128)S(1)}, f32[192,1024]{1,0:T(8,128)S(1)}, f32[48,512]{1,0:T(8,128)S(1)}, f32[48,512]{...) custom-call(f32[192,1024]{1,0:T(8,128)S(1)} %shard_map.115.part_ref, ...), custom_call_target="tpu_custom_call" | custom-call | tf_op jit(solution)/shard_map/pallas_call | solution.py:349
  25.9 1.8 %shard_map.117.part_ref = f32[192,1024]{1,0:T(8,128)S(1)} custom-call(f32[192,1024]{1,0:T(8,128)S(1)} %get-tuple-element.66.d_ref, f32[8,128]{1,0:T(8,128)S(1)} %bitcast.38, s32[48,128]{1,0:T(8,128)S(1)} %bitcast.23, bf16[192,768]{1,0:T(8,128)(2,1)S(1)} %get-tuple-element.59.wh_ref, bf16[192,768]{1,0:T(8,128)(2,1)S(1)} %get-tuple-element.60.wl_ref, ...), custom_call_target="tpu_custom_call" | custom-call | tf_op jit(solution)/shard_map/pallas_call | solution.py:349
  28.7 1.9 %collective-permute-done.7.gy_out = f32[48,256]{1,0:T(8,128)S(1)} collective-permute-done((f32[48,256]{1,0:T(8,128)S(1)}, f32[48,256]{1,0:T(8,128)S(1)}, u32[]{:S(2)}, u32[]{:S(2)}) %collective-permute-start.7) | collective-permute-done | bytes 49184 | tf_op jit(solution)/shard_map/ppermute | solution.py:366
  32.7 2.3 %collective-permute-start.9 = (f32[48,512]{1,0:T(8,128)S(1)}, f32[48,512]{1,0:T(8,128)S(1)}, u32[]{:S(2)}, u32[]{:S(2)}) collective-permute-start(f32[48,512]{1,0:T(8,128)S(1)} %get-tuple-element.77), channel_id=1, source_target_pairs={{0,124},{4,8},{8,4},{12,16},{16,12},{20,24},{24,20},{28,32},{32,28... | collective-permute-start | bytes 294920 | tf_op jit(solution)/shard_map/ppermute | solution.py:366
  38.1 1.8 %shard_map.119.part_ref = f32[192,1024]{1,0:T(8,128)S(1)} custom-call(f32[192,1024]{1,0:T(8,128)S(1)} %get-tuple-element.73.d_ref, f32[8,128]{1,0:T(8,128)S(1)} %bitcast.40, s32[48,128]{1,0:T(8,128)S(1)} %bitcast.25, bf16[192,768]{1,0:T(8,128)(2,1)S(1)} %get-tuple-element.59.wh_ref, bf16[192,768]{1,0:T(8,128)(2,1)S(1)} %get-tuple-element.60.wl_ref, ...), custom_call_target="tpu_custom_call" | custom-call | tf_op jit(solution)/shard_map/pallas_call | solution.py:349
  40.5 2.5 %shard_map.120 = (f32[192,1024]{1,0:T(8,128)S(1)}, f32[192,1024]{1,0:T(8,128)}, f32[192,1024]{1,0:T(8,128)}, f32[48,512]{1,0:T(8,128)}, f32[48,512]{1,0:T(8,128)}, /*index=5*/f32[48,256]{1,0:T(8,128)}, f32[48,256]{1,0:T(8,128)}) custom-call(f32[192,1024]{1,0:T(8,128)S(1)} %shard_map.119.part_ref, f32[192,1024]{1,0:T(8,128)S(1)} %get-tuple-element.74.r_ref, ...), custom_call_target="tpu_custom_call" | custom-call | tf_op jit(solution)/shard_map/pallas_call | solution.py:349
  43.1 2.3 %shard_map.122 = f32[32,8,128]{2,1,0:T(8,128)} custom-call(f32[192,1024]{1,0:T(8,128)S(1)} %get-tuple-element.80.r_ref, bf16[1024,1024]{1,0:T(8,128)(2,1)S(1)} %shard_map.121.hot_ref, bf16[24,192]{1,0:T(8,128)(2,1)S(1)} %get-tuple-element.81.pth_ref, bf16[24,192]{1,0:T(8,128)(2,1)S(1)} %get-tuple-element.82.ptl_ref), custom_call_target="tpu_custom_call" | custom-call | tf_op jit(solution)/shard_map/pallas_call | solution.py:349
  46.3 3.9 %all-to-all-start = ((f32[32,8,128]{2,1,0:T(8,128)}), f32[32,8,128]{2,1,0:T(8,128)S(1)}, u32[]{:S(2)}, u32[]{:S(2)}) async-start(f32[32,8,128]{2,1,0:T(8,128)} %shard_map.122), calls=%async_computation | async-start | bytes 262144 | tf_op jit(solution)/shard_map/all_to_all | solution.py:464
  50.2 3.7 %copy-done.5 = f32[1,32,32,24,24]{2,4,3,1,0:T(8,128)S(1)} copy-done((f32[1,32,32,24,24]{2,4,3,1,0:T(8,128)S(1)}, f32[1,32,32,24,24]{2,4,3,1,0:T(8,128)}, u32[]{:S(2)}) %copy-start.5) | copy-done | bytes 2359320
  53.8 5.2 %shard_map.123.inv_ref = f32[32,24,8,128]{3,2,1,0:T(8,128)S(1)} custom-call(f32[32,24,24,32]{3,2,1,0:T(8,128)S(1)} %bitcast.20), custom_call_target="tpu_custom_call" | custom-call | tf_op jit(solution)/shard_map/pallas_call | solution.py:465
  59.0 1.6 %copy-done.3 = f32[32,24,8,128]{3,2,1,0:T(8,128)} copy-done((f32[32,24,8,128]{3,2,1,0:T(8,128)}, f32[32,24,8,128]{3,2,1,0:T(8,128)S(1)}, u32[]{:S(2)}) %copy-start.3) | copy-done | bytes 3145752
  60.6 1.9 %copy-done.4 = f32[32,24,8,128]{3,2,1,0:T(8,128)S(1)} copy-done((f32[32,24,8,128]{3,2,1,0:T(8,128)S(1)}, f32[32,24,8,128]{3,2,1,0:T(8,128)}, u32[]{:S(2)}) %copy-start.4) | copy-done | bytes 3145752
  63.0 15.1 %all_to_all.10.sol_in = f32[32,8,128]{2,1,0:T(8,128)S(1)} all-to-all(f32[32,8,128]{2,1,0:T(8,128)S(1)} %shard_map.124), channel_id=1, replica_groups=mesh['gx'=32,'gy'=4] {'gx'}, dimensions={0} | all-to-all | bytes 262144 | tf_op jit(solution)/shard_map/all_to_all | solution.py:476
  78.1 1.9 %shard_map.125 = (f32[192,1024]{1,0:T(8,128)S(1)}, f32[192,1024]{1,0:T(8,128)S(1)}, f32[48,512]{1,0:T(8,128)S(1)}, f32[48,512]{1,0:T(8,128)S(1)}, f32[48,256]{1,0:T(8,128)S(1)}, /*index=5*/f32[48,256]{1,0:T(8,128)S(1)}) custom-call(f32[32,8,128]{2,1,0:T(8,128)S(1)} %all_to_all.10.sol_in, f32[192,1024]{1,0:T(8,128)S(1)} %copy-done.9, f32[8,128]{1,0:T(8,128)S(1)} %bitcast.42, ...), custom_call_target="tpu_custom_call" | custom-call | tf_op jit(solution)/shard_map/pallas_call | solution.py:349
  80.2 1.9 %collective-permute-start.13 = (f32[48,512]{1,0:T(8,128)S(1)}, f32[48,512]{1,0:T(8,128)S(1)}, u32[]{:S(2)}, u32[]{:S(2)}) collective-permute-start(f32[48,512]{1,0:T(8,128)S(1)} %get-tuple-element.88), channel_id=1, source_target_pairs={{0,124},{4,8},{8,4},{12,16},{16,12},{20,24},{24,20},{28,32},{32,28... | collective-permute-start | bytes 294920 | tf_op jit(solution)/shard_map/ppermute | solution.py:366
  82.8 2.0 %collective-permute-start.15 = (f32[48,256]{1,0:T(8,128)S(1)}, f32[48,256]{1,0:T(8,128)S(1)}, u32[]{:S(2)}, u32[]{:S(2)}) collective-permute-start(f32[48,256]{1,0:T(8,128)S(1)} %get-tuple-element.90), channel_id=1, source_target_pairs={{0,3},{1,2},{2,1},{3,0},{4,7},{5,6},{6,5},{7,4},{8,11},{9,10},{10,... | collective-permute-start | bytes 147464 | tf_op jit(solution)/shard_map/ppermute | solution.py:366
  84.8 1.8 %shard_map.126.part_ref = f32[192,1024]{1,0:T(8,128)S(1)} custom-call(f32[192,1024]{1,0:T(8,128)S(1)} %get-tuple-element.85.d_ref, f32[8,128]{1,0:T(8,128)S(1)} %bitcast.43, s32[48,128]{1,0:T(8,128)S(1)} %bitcast.27, bf16[192,768]{1,0:T(8,128)(2,1)S(1)} %get-tuple-element.59.wh_ref, bf16[192,768]{1,0:T(8,128)(2,1)S(1)} %get-tuple-element.60.wl_ref, ...), custom_call_target="tpu_custom_call" | custom-call | tf_op jit(solution)/shard_map/pallas_call | solution.py:349
  89.7 1.9 %collective-permute-start.17 = (f32[48,512]{1,0:T(8,128)S(1)}, f32[48,512]{1,0:T(8,128)S(1)}, u32[]{:S(2)}, u32[]{:S(2)}) collective-permute-start(f32[48,512]{1,0:T(8,128)S(1)} %get-tuple-element.95), channel_id=1, source_target_pairs={{0,124},{4,8},{8,4},{12,16},{16,12},{20,24},{24,20},{28,32},{32,28... | collective-permute-start | bytes 294920 | tf_op jit(solution)/shard_map/ppermute | solution.py:366
  91.9 2.0 %collective-permute-start.19 = (f32[48,256]{1,0:T(8,128)S(1)}, f32[48,256]{1,0:T(8,128)S(1)}, u32[]{:S(2)}, u32[]{:S(2)}) collective-permute-start(f32[48,256]{1,0:T(8,128)S(1)} %get-tuple-element.97), channel_id=1, source_target_pairs={{0,3},{1,2},{2,1},{3,0},{4,7},{5,6},{6,5},{7,4},{8,11},{9,10},{10,... | collective-permute-start | bytes 147464 | tf_op jit(solution)/shard_map/ppermute | solution.py:366
  93.8 1.8 %shard_map.128.part_ref = f32[192,1024]{1,0:T(8,128)S(1)} custom-call(f32[192,1024]{1,0:T(8,128)S(1)} %get-tuple-element.91.d_ref, f32[8,128]{1,0:T(8,128)S(1)} %bitcast.45, s32[48,128]{1,0:T(8,128)S(1)} %bitcast.29, bf16[192,768]{1,0:T(8,128)(2,1)S(1)} %get-tuple-element.59.wh_ref, bf16[192,768]{1,0:T(8,128)(2,1)S(1)} %get-tuple-element.60.wl_ref, ...), custom_call_target="tpu_custom_call" | custom-call | tf_op jit(solution)/shard_map/pallas_call | solution.py:349
  98.8 2.0 %collective-permute-start.21 = (f32[48,512]{1,0:T(8,128)S(1)}, f32[48,512]{1,0:T(8,128)S(1)}, u32[]{:S(2)}, u32[]{:S(2)}) collective-permute-start(f32[48,512]{1,0:T(8,128)S(1)} %get-tuple-element.102), channel_id=1, source_target_pairs={{0,124},{4,8},{8,4},{12,16},{16,12},{20,24},{24,20},{28,32},{32,28... | collective-permute-start | bytes 294920 | tf_op jit(solution)/shard_map/ppermute | solution.py:366
  101.3 2.0 %collective-permute-start.23 = (f32[48,256]{1,0:T(8,128)S(1)}, f32[48,256]{1,0:T(8,128)S(1)}, u32[]{:S(2)}, u32[]{:S(2)}) collective-permute-start(f32[48,256]{1,0:T(8,128)S(1)} %get-tuple-element.104), channel_id=1, source_target_pairs={{0,3},{1,2},{2,1},{3,0},{4,7},{5,6},{6,5},{7,4},{8,11},{9,10},{10,... | collective-permute-start | bytes 147464 | tf_op jit(solution)/shard_map/ppermute | solution.py:366
  103.3 1.8 %shard_map.130.part_ref = f32[192,1024]{1,0:T(8,128)S(1)} custom-call(f32[192,1024]{1,0:T(8,128)S(1)} %get-tuple-element.98.d_ref, f32[8,128]{1,0:T(8,128)S(1)} %bitcast.47, s32[48,128]{1,0:T(8,128)S(1)} %bitcast.31, bf16[192,768]{1,0:T(8,128)(2,1)S(1)} %get-tuple-element.59.wh_ref, bf16[192,768]{1,0:T(8,128)(2,1)S(1)} %get-tuple-element.60.wl_ref, ...), custom_call_target="tpu_custom_call" | custom-call | tf_op jit(solution)/shard_map/pallas_call | solution.py:349
  106.6 1.5 %shard_map.131 = (f32[192,1024]{1,0:T(8,128)S(1)}, f32[192,1024]{1,0:T(8,128)S(1)}, f32[192,1024]{1,0:T(8,128)S(1)}, f32[48,512]{1,0:T(8,128)S(1)}, f32[48,512]{...) custom-call(f32[192,1024]{1,0:T(8,128)S(1)} %shard_map.130.part_ref, ...), custom_call_target="tpu_custom_call" | custom-call | tf_op jit(solution)/shard_map/pallas_call | solution.py:349
  108.3 1.9 %collective-permute-start.25 = (f32[48,512]{1,0:T(8,128)S(1)}, f32[48,512]{1,0:T(8,128)S(1)}, u32[]{:S(2)}, u32[]{:S(2)}) collective-permute-start(f32[48,512]{1,0:T(8,128)S(1)} %get-tuple-element.109), channel_id=1, source_target_pairs={{0,124},{4,8},{8,4},{12,16},{16,12},{20,24},{24,20},{28,32},{32,28... | collective-permute-start | bytes 294920 | tf_op jit(solution)/shard_map/ppermute | solution.py:366
  110.4 2.0 %collective-permute-start.27 = (f32[48,256]{1,0:T(8,128)S(1)}, f32[48,256]{1,0:T(8,128)S(1)}, u32[]{:S(2)}, u32[]{:S(2)}) collective-permute-start(f32[48,256]{1,0:T(8,128)S(1)} %get-tuple-element.111), channel_id=1, source_target_pairs={{0,3},{1,2},{2,1},{3,0},{4,7},{5,6},{6,5},{7,4},{8,11},{9,10},{10,... | collective-permute-start | bytes 147464 | tf_op jit(solution)/shard_map/ppermute | solution.py:366
  112.4 1.8 %shard_map.132.part_ref = f32[192,1024]{1,0:T(8,128)S(1)} custom-call(f32[192,1024]{1,0:T(8,128)S(1)} %get-tuple-element.105.d_ref, f32[8,128]{1,0:T(8,128)S(1)} %bitcast.49, s32[48,128]{1,0:T(8,128)S(1)} %bitcast.33, bf16[192,768]{1,0:T(8,128)(2,1)S(1)} %get-tuple-element.59.wh_ref, bf16[192,768]{1,0:T(8,128)(2,1)S(1)} %get-tuple-element.60.wl_ref, ...), custom_call_target="tpu_custom_call" | custom-call | tf_op jit(solution)/shard_map/pallas_call | solution.py:349
  115.7 2.5 %shard_map.133 = (f32[1536,128]{1,0:T(8,128)}, f32[1536,128]{1,0:T(8,128)}) custom-call(f32[192,1024]{1,0:T(8,128)S(1)} %shard_map.132.part_ref, f32[192,1024]{1,0:T(8,128)S(1)} %get-tuple-element.106.r_ref, f32[192,1024]{1,0:T(8,128)S(1)} %get-tuple-element.107.x_ref, s32[48,128]{1,0:T(8,128)S(1)} %bitcast.34, ...), custom_call_target="tpu_custom_call" | custom-call | tf_op jit(solution)/shard_map/pallas_call | solution.py:349
  (91 shorter events, 31.2 us)
Async XLA Ops:
  0.6 21.4 %copy-start.7 = (s32[6,2,4,128]{3,2,1,0:T(4,128)S(1)}, s32[6,2,4,128]{3,2,1,0:T(4,128)}, u32[]{:S(2)}) copy-start(s32[6,2,4,128]{3,2,1,0:T(4,128)} %param.12) | copy-start | bytes 73732
  4.4 17.5 %collective-permute-start = (f32[48,512]{1,0:T(8,128)S(1)}, f32[48,512]{1,0:T(8,128)S(1)}, u32[]{:S(2)}, u32[]{:S(2)}) collective-permute-start(f32[48,512]{1,0:T(8,128)S(1)} %get-tuple-element.62), channel_id=1, source_target_pairs={{0,4},{4,0},{8,12},{12,8},{16,20},{20,16},{24,28},{28,24},{32,36},... | collective-permute-start | bytes 294920 | tf_op jit(solution)/shard_map/ppermute | solution.py:361
  4.5 17.5 %collective-permute-start.1 = (f32[48,512]{1,0:T(8,128)S(1)}, f32[48,512]{1,0:T(8,128)S(1)}, u32[]{:S(2)}, u32[]{:S(2)}) collective-permute-start(f32[48,512]{1,0:T(8,128)S(1)} %get-tuple-element.63), channel_id=1, source_target_pairs={{0,124},{4,8},{8,4},{12,16},{16,12},{20,24},{24,20},{28,32},{32,28... | collective-permute-start | bytes 294920 | tf_op jit(solution)/shard_map/ppermute | solution.py:366
  10.9 11.0 %collective-permute-start.2 = (f32[48,256]{1,0:T(8,128)S(1)}, f32[48,256]{1,0:T(8,128)S(1)}, u32[]{:S(2)}, u32[]{:S(2)}) collective-permute-start(f32[48,256]{1,0:T(8,128)S(1)} %get-tuple-element.64), channel_id=1, source_target_pairs={{0,1},{1,0},{2,3},{3,2},{4,5},{5,4},{6,7},{7,6},{8,9},{9,8},{10,11... | collective-permute-start | bytes 147464 | tf_op jit(solution)/shard_map/ppermute | solution.py:361
  12.5 9.4 %collective-permute-start.3 = (f32[48,256]{1,0:T(8,128)S(1)}, f32[48,256]{1,0:T(8,128)S(1)}, u32[]{:S(2)}, u32[]{:S(2)}) collective-permute-start(f32[48,256]{1,0:T(8,128)S(1)} %get-tuple-element.65), channel_id=1, source_target_pairs={{0,3},{1,2},{2,1},{3,0},{4,7},{5,6},{6,5},{7,4},{8,11},{9,10},{10,... | collective-permute-start | bytes 147464 | tf_op jit(solution)/shard_map/ppermute | solution.py:366
  23.6 7.0 %collective-permute-start.4 = (f32[48,512]{1,0:T(8,128)S(1)}, f32[48,512]{1,0:T(8,128)S(1)}, u32[]{:S(2)}, u32[]{:S(2)}) collective-permute-start(f32[48,512]{1,0:T(8,128)S(1)} %get-tuple-element.69), channel_id=1, source_target_pairs={{0,4},{4,0},{8,12},{12,8},{16,20},{20,16},{24,28},{28,24},{32,36},... | collective-permute-start | bytes 294920 | tf_op jit(solution)/shard_map/ppermute | solution.py:361
  23.6 7.4 %collective-permute-start.5 = (f32[48,512]{1,0:T(8,128)S(1)}, f32[48,512]{1,0:T(8,128)S(1)}, u32[]{:S(2)}, u32[]{:S(2)}) collective-permute-start(f32[48,512]{1,0:T(8,128)S(1)} %get-tuple-element.70), channel_id=1, source_target_pairs={{0,124},{4,8},{8,4},{12,16},{16,12},{20,24},{24,20},{28,32},{32,28... | collective-permute-start | bytes 294920 | tf_op jit(solution)/shard_map/ppermute | solution.py:366
  24.6 4.1 %collective-permute-start.6 = (f32[48,256]{1,0:T(8,128)S(1)}, f32[48,256]{1,0:T(8,128)S(1)}, u32[]{:S(2)}, u32[]{:S(2)}) collective-permute-start(f32[48,256]{1,0:T(8,128)S(1)} %get-tuple-element.71), channel_id=1, source_target_pairs={{0,1},{1,0},{2,3},{3,2},{4,5},{5,4},{6,7},{7,6},{8,9},{9,8},{10,11... | collective-permute-start | bytes 147464 | tf_op jit(solution)/shard_map/ppermute | solution.py:361
  25.3 5.3 %collective-permute-start.7 = (f32[48,256]{1,0:T(8,128)S(1)}, f32[48,256]{1,0:T(8,128)S(1)}, u32[]{:S(2)}, u32[]{:S(2)}) collective-permute-start(f32[48,256]{1,0:T(8,128)S(1)} %get-tuple-element.72), channel_id=1, source_target_pairs={{0,3},{1,2},{2,1},{3,0},{4,7},{5,6},{6,5},{7,4},{8,11},{9,10},{10,... | collective-permute-start | bytes 147464 | tf_op jit(solution)/shard_map/ppermute | solution.py:366
  32.7 7.9 %collective-permute-start.8 = (f32[48,512]{1,0:T(8,128)S(1)}, f32[48,512]{1,0:T(8,128)S(1)}, u32[]{:S(2)}, u32[]{:S(2)}) collective-permute-start(f32[48,512]{1,0:T(8,128)S(1)} %get-tuple-element.76), channel_id=1, source_target_pairs={{0,4},{4,0},{8,12},{12,8},{16,20},{20,16},{24,28},{28,24},{32,36},... | collective-permute-start | bytes 294920 | tf_op jit(solution)/shard_map/ppermute | solution.py:361
  32.7 7.8 %collective-permute-start.9 = (f32[48,512]{1,0:T(8,128)S(1)}, f32[48,512]{1,0:T(8,128)S(1)}, u32[]{:S(2)}, u32[]{:S(2)}) collective-permute-start(f32[48,512]{1,0:T(8,128)S(1)} %get-tuple-element.77), channel_id=1, source_target_pairs={{0,124},{4,8},{8,4},{12,16},{16,12},{20,24},{24,20},{28,32},{32,28... | collective-permute-start | bytes 294920 | tf_op jit(solution)/shard_map/ppermute | solution.py:366
  35.1 4.8 %collective-permute-start.10 = (f32[48,256]{1,0:T(8,128)S(1)}, f32[48,256]{1,0:T(8,128)S(1)}, u32[]{:S(2)}, u32[]{:S(2)}) collective-permute-start(f32[48,256]{1,0:T(8,128)S(1)} %get-tuple-element.78), channel_id=1, source_target_pairs={{0,1},{1,0},{2,3},{3,2},{4,5},{5,4},{6,7},{7,6},{8,9},{9,8},{10,11... | collective-permute-start | bytes 147464 | tf_op jit(solution)/shard_map/ppermute | solution.py:361
  35.2 5.3 %collective-permute-start.11 = (f32[48,256]{1,0:T(8,128)S(1)}, f32[48,256]{1,0:T(8,128)S(1)}, u32[]{:S(2)}, u32[]{:S(2)}) collective-permute-start(f32[48,256]{1,0:T(8,128)S(1)} %get-tuple-element.79), channel_id=1, source_target_pairs={{0,3},{1,2},{2,1},{3,0},{4,7},{5,6},{6,5},{7,4},{8,11},{9,10},{10,... | collective-permute-start | bytes 147464 | tf_op jit(solution)/shard_map/ppermute | solution.py:366
  46.3 14.3 %all-to-all-start = ((f32[32,8,128]{2,1,0:T(8,128)}), f32[32,8,128]{2,1,0:T(8,128)S(1)}, u32[]{:S(2)}, u32[]{:S(2)}) async-start(f32[32,8,128]{2,1,0:T(8,128)} %shard_map.122), calls=%async_computation | async-start | bytes 262144 | tf_op jit(solution)/shard_map/all_to_all | solution.py:464
  62.5 15.6 %copy-start.9 = (f32[192,1024]{1,0:T(8,128)S(1)}, f32[192,1024]{1,0:T(8,128)}, u32[]{:S(2)}) copy-start(f32[192,1024]{1,0:T(8,128)} %copy-done.8) | copy-start | bytes 2359300
  63.0 25.1 %copy-start.11 = (f32[192,1024]{1,0:T(8,128)S(1)}, f32[192,1024]{1,0:T(8,128)}, u32[]{:S(2)}) copy-start(f32[192,1024]{1,0:T(8,128)} %copy-done.10) | copy-start | bytes 2359300
  80.0 8.0 %collective-permute-start.12 = (f32[48,512]{1,0:T(8,128)S(1)}, f32[48,512]{1,0:T(8,128)S(1)}, u32[]{:S(2)}, u32[]{:S(2)}) collective-permute-start(f32[48,512]{1,0:T(8,128)S(1)} %get-tuple-element.87), channel_id=1, source_target_pairs={{0,4},{4,0},{8,12},{12,8},{16,20},{20,16},{24,28},{28,24},{32,36},... | collective-permute-start | bytes 294920 | tf_op jit(solution)/shard_map/ppermute | solution.py:361
  80.2 7.9 %collective-permute-start.13 = (f32[48,512]{1,0:T(8,128)S(1)}, f32[48,512]{1,0:T(8,128)S(1)}, u32[]{:S(2)}, u32[]{:S(2)}) collective-permute-start(f32[48,512]{1,0:T(8,128)S(1)} %get-tuple-element.88), channel_id=1, source_target_pairs={{0,124},{4,8},{8,4},{12,16},{16,12},{20,24},{24,20},{28,32},{32,28... | collective-permute-start | bytes 294920 | tf_op jit(solution)/shard_map/ppermute | solution.py:366
  82.1 4.4 %collective-permute-start.14 = (f32[48,256]{1,0:T(8,128)S(1)}, f32[48,256]{1,0:T(8,128)S(1)}, u32[]{:S(2)}, u32[]{:S(2)}) collective-permute-start(f32[48,256]{1,0:T(8,128)S(1)} %get-tuple-element.89), channel_id=1, source_target_pairs={{0,1},{1,0},{2,3},{3,2},{4,5},{5,4},{6,7},{7,6},{8,9},{9,8},{10,11... | collective-permute-start | bytes 147464 | tf_op jit(solution)/shard_map/ppermute | solution.py:361
  82.8 5.3 %collective-permute-start.15 = (f32[48,256]{1,0:T(8,128)S(1)}, f32[48,256]{1,0:T(8,128)S(1)}, u32[]{:S(2)}, u32[]{:S(2)}) collective-permute-start(f32[48,256]{1,0:T(8,128)S(1)} %get-tuple-element.90), channel_id=1, source_target_pairs={{0,3},{1,2},{2,1},{3,0},{4,7},{5,6},{6,5},{7,4},{8,11},{9,10},{10,... | collective-permute-start | bytes 147464 | tf_op jit(solution)/shard_map/ppermute | solution.py:366
  89.6 7.5 %collective-permute-start.16 = (f32[48,512]{1,0:T(8,128)S(1)}, f32[48,512]{1,0:T(8,128)S(1)}, u32[]{:S(2)}, u32[]{:S(2)}) collective-permute-start(f32[48,512]{1,0:T(8,128)S(1)} %get-tuple-element.94), channel_id=1, source_target_pairs={{0,4},{4,0},{8,12},{12,8},{16,20},{20,16},{24,28},{28,24},{32,36},... | collective-permute-start | bytes 294920 | tf_op jit(solution)/shard_map/ppermute | solution.py:361
  89.7 7.4 %collective-permute-start.17 = (f32[48,512]{1,0:T(8,128)S(1)}, f32[48,512]{1,0:T(8,128)S(1)}, u32[]{:S(2)}, u32[]{:S(2)}) collective-permute-start(f32[48,512]{1,0:T(8,128)S(1)} %get-tuple-element.95), channel_id=1, source_target_pairs={{0,124},{4,8},{8,4},{12,16},{16,12},{20,24},{24,20},{28,32},{32,28... | collective-permute-start | bytes 294920 | tf_op jit(solution)/shard_map/ppermute | solution.py:366
  91.6 4.1 %collective-permute-start.18 = (f32[48,256]{1,0:T(8,128)S(1)}, f32[48,256]{1,0:T(8,128)S(1)}, u32[]{:S(2)}, u32[]{:S(2)}) collective-permute-start(f32[48,256]{1,0:T(8,128)S(1)} %get-tuple-element.96), channel_id=1, source_target_pairs={{0,1},{1,0},{2,3},{3,2},{4,5},{5,4},{6,7},{7,6},{8,9},{9,8},{10,11... | collective-permute-start | bytes 147464 | tf_op jit(solution)/shard_map/ppermute | solution.py:361
  91.9 5.3 %collective-permute-start.19 = (f32[48,256]{1,0:T(8,128)S(1)}, f32[48,256]{1,0:T(8,128)S(1)}, u32[]{:S(2)}, u32[]{:S(2)}) collective-permute-start(f32[48,256]{1,0:T(8,128)S(1)} %get-tuple-element.97), channel_id=1, source_target_pairs={{0,3},{1,2},{2,1},{3,0},{4,7},{5,6},{6,5},{7,4},{8,11},{9,10},{10,... | collective-permute-start | bytes 147464 | tf_op jit(solution)/shard_map/ppermute | solution.py:366
  98.7 7.9 %collective-permute-start.20 = (f32[48,512]{1,0:T(8,128)S(1)}, f32[48,512]{1,0:T(8,128)S(1)}, u32[]{:S(2)}, u32[]{:S(2)}) collective-permute-start(f32[48,512]{1,0:T(8,128)S(1)} %get-tuple-element.101), channel_id=1, source_target_pairs={{0,4},{4,0},{8,12},{12,8},{16,20},{20,16},{24,28},{28,24},{32,36},... | collective-permute-start | bytes 294920 | tf_op jit(solution)/shard_map/ppermute | solution.py:361
  98.8 7.8 %collective-permute-start.21 = (f32[48,512]{1,0:T(8,128)S(1)}, f32[48,512]{1,0:T(8,128)S(1)}, u32[]{:S(2)}, u32[]{:S(2)}) collective-permute-start(f32[48,512]{1,0:T(8,128)S(1)} %get-tuple-element.102), channel_id=1, source_target_pairs={{0,124},{4,8},{8,4},{12,16},{16,12},{20,24},{24,20},{28,32},{32,28... | collective-permute-start | bytes 294920 | tf_op jit(solution)/shard_map/ppermute | solution.py:366
  100.8 4.3 %collective-permute-start.22 = (f32[48,256]{1,0:T(8,128)S(1)}, f32[48,256]{1,0:T(8,128)S(1)}, u32[]{:S(2)}, u32[]{:S(2)}) collective-permute-start(f32[48,256]{1,0:T(8,128)S(1)} %get-tuple-element.103), channel_id=1, source_target_pairs={{0,1},{1,0},{2,3},{3,2},{4,5},{5,4},{6,7},{7,6},{8,9},{9,8},{10,11... | collective-permute-start | bytes 147464 | tf_op jit(solution)/shard_map/ppermute | solution.py:361
  101.3 5.3 %collective-permute-start.23 = (f32[48,256]{1,0:T(8,128)S(1)}, f32[48,256]{1,0:T(8,128)S(1)}, u32[]{:S(2)}, u32[]{:S(2)}) collective-permute-start(f32[48,256]{1,0:T(8,128)S(1)} %get-tuple-element.104), channel_id=1, source_target_pairs={{0,3},{1,2},{2,1},{3,0},{4,7},{5,6},{6,5},{7,4},{8,11},{9,10},{10,... | collective-permute-start | bytes 147464 | tf_op jit(solution)/shard_map/ppermute | solution.py:366
  108.2 7.5 %collective-permute-start.24 = (f32[48,512]{1,0:T(8,128)S(1)}, f32[48,512]{1,0:T(8,128)S(1)}, u32[]{:S(2)}, u32[]{:S(2)}) collective-permute-start(f32[48,512]{1,0:T(8,128)S(1)} %get-tuple-element.108), channel_id=1, source_target_pairs={{0,4},{4,0},{8,12},{12,8},{16,20},{20,16},{24,28},{28,24},{32,36},... | collective-permute-start | bytes 294920 | tf_op jit(solution)/shard_map/ppermute | solution.py:361
  108.3 7.4 %collective-permute-start.25 = (f32[48,512]{1,0:T(8,128)S(1)}, f32[48,512]{1,0:T(8,128)S(1)}, u32[]{:S(2)}, u32[]{:S(2)}) collective-permute-start(f32[48,512]{1,0:T(8,128)S(1)} %get-tuple-element.109), channel_id=1, source_target_pairs={{0,124},{4,8},{8,4},{12,16},{16,12},{20,24},{24,20},{28,32},{32,28... | collective-permute-start | bytes 294920 | tf_op jit(solution)/shard_map/ppermute | solution.py:366
  110.1 4.1 %collective-permute-start.26 = (f32[48,256]{1,0:T(8,128)S(1)}, f32[48,256]{1,0:T(8,128)S(1)}, u32[]{:S(2)}, u32[]{:S(2)}) collective-permute-start(f32[48,256]{1,0:T(8,128)S(1)} %get-tuple-element.110), channel_id=1, source_target_pairs={{0,1},{1,0},{2,3},{3,2},{4,5},{5,4},{6,7},{7,6},{8,9},{9,8},{10,11... | collective-permute-start | bytes 147464 | tf_op jit(solution)/shard_map/ppermute | solution.py:361
  110.4 5.3 %collective-permute-start.27 = (f32[48,256]{1,0:T(8,128)S(1)}, f32[48,256]{1,0:T(8,128)S(1)}, u32[]{:S(2)}, u32[]{:S(2)}) collective-permute-start(f32[48,256]{1,0:T(8,128)S(1)} %get-tuple-element.111), channel_id=1, source_target_pairs={{0,3},{1,2},{2,1},{3,0},{4,7},{5,6},{6,5},{7,4},{8,11},{9,10},{10,... | collective-permute-start | bytes 147464 | tf_op jit(solution)/shard_map/ppermute | solution.py:366
  (18 other events, 68.3 us)

commit v3 on v2

--- a/solution.py
+++ b/solution.py
@@ -78,10 +78,15 @@
     return coef_ref[col : col + 1, :]
 
 
-def emit_traces(w_of, sel_ref, par_ref, sends):
+def sides(place_ref):
+    at_x, at_y = place_ref[0], place_ref[1]
+    last_x, last_y = place_ref[2], place_ref[3]
+    return at_x % 2 == 0, at_y % 2 == 0, (at_x > 0, at_x < last_x, at_y > 0, at_y < last_y)
+
+
+def emit_traces(w_of, sel_ref, place_ref, sends):
     sx_in, sx_out, sy_in, sy_out = sends
-    even_x = par_ref[0] == 0
-    even_y = par_ref[1] == 0
+    even_x, even_y, _ = sides(place_ref)
     for y in range(4):
         low = face_rows(w_of(y), 0)
         high = face_rows(w_of(4 + y), 3)
@@ -97,24 +102,45 @@
         sy_out[:, lanes(x)] = jnp.where(even_y, ends[0], ends[1])
 
 
-def first_kernel(rs_ref, coef_ref, sel_ref, par_ref, r_ref, d_ref, *sends):
+def fetch(pairs, sems):
+    copies = [pltpu.make_async_copy(a, b, sems.at[n]) for n, (a, b) in enumerate(pairs)]
+    for copy in copies:
+        copy.start()
+    return copies
+
+
+def first_kernel(
+    rs_hbm, coef_hbm, ori_hbm, sel_hbm, place_ref,
+    r_ref, d_ref, coef_ref, ori_ref, sel_ref, sx_in, sx_out, sy_in, sy_out, rs_ref, sems,
+):
+    copies = fetch(
+        ((rs_hbm, rs_ref), (coef_hbm, coef_ref), (sel_hbm, sel_ref), (ori_hbm, ori_ref)), sems
+    )
+    for copy in copies[:3]:
+        copy.wait()
     for col in range(COLS):
         v = rs_ref[pl.ds(col, BLOCK, stride=COLS), :]
         r_ref[:, lanes(col)] = v
         d_ref[:, lanes(col)] = v * (1.0 / THETA)
     emit_traces(
-        lambda col: d_ref[:, lanes(col)] * tile_coef(coef_ref, col), sel_ref, par_ref, sends
-    )
-
-
-def weights_kernel(stiff_ref, faces_ref, pt_ref, wh_ref, wl_ref, pth_ref, ptl_ref, ph_ref, pl_ref):
+        lambda col: d_ref[:, lanes(col)] * tile_coef(coef_ref, col),
+        sel_ref,
+        place_ref,
+        (sx_in, sx_out, sy_in, sy_out),
+    )
+    copies[3].wait()
+
+
+def weights_kernel(
+    stiff_hbm, faces_hbm, pt_hbm, wh_ref, wl_ref, pth_ref, ptl_ref, ph_ref, pl_ref,
+    stiff_ref, faces_ref, pt_ref, sems,
+):
+    copies = fetch(((stiff_hbm, stiff_ref), (pt_hbm, pt_ref), (faces_hbm, faces_ref)), sems)
+    copies[0].wait()
     high, low = split(stiff_ref[...])
     wh_ref[:, 0:BLOCK] = high
     wl_ref[:, 0:BLOCK] = low
-    for piece in range(3):
-        high, low = split(faces_ref[192 * piece : 192 * (piece + 1), :].T)
-        wh_ref[:, 192 * (piece + 1) : 192 * (piece + 2)] = high
-        wl_ref[:, 192 * (piece + 1) : 192 * (piece + 2)] = low
+    copies[1].wait()
     pt = pt_ref[...]
     high, low = split(pt)
     pth_ref[...] = high
@@ -122,6 +148,11 @@
     high, low = split(pt.T)
     ph_ref[...] = high
     pl_ref[...] = low
+    copies[2].wait()
+    for piece in range(3):
+        high, low = split(faces_ref[192 * piece : 192 * (piece + 1), :].T)
+        wh_ref[:, 192 * (piece + 1) : 192 * (piece + 2)] = high
+        wl_ref[:, 192 * (piece + 1) : 192 * (piece + 2)] = low
 
 
 def interior_kernel(d_ref, coef_ref, ori_ref, wh_ref, wl_ref, sel_ref, out_ref, xh_ref, xl_ref, t_ref):
@@ -182,40 +213,39 @@
     )
 
 
-def halo_sum(part_ref, ori_ref, wh_ref, wl_ref, par_ref, gets, ad_ref):
+def halo_sum(part_ref, ori_ref, wh_ref, wl_ref, place_ref, gets, ad_ref):
     gx_in, gx_out, gy_in, gy_out = gets
-    even_x = par_ref[0] == 0
-    even_y = par_ref[1] == 0
-
-    def lower(inside, outside, even, there):
+    even_x, even_y, there = sides(place_ref)
+
+    def lower(inside, outside, even, found):
         return lambda n: jnp.where(
-            there, jnp.where(even, outside[:, lanes(n)], inside[:, lanes(n)]), 0.0
+            found, jnp.where(even, outside[:, lanes(n)], inside[:, lanes(n)]), 0.0
         )
 
-    def upper(inside, outside, even, there):
+    def upper(inside, outside, even, found):
         return lambda n: jnp.where(
-            there, jnp.where(even, inside[:, lanes(n)], outside[:, lanes(n)]), 0.0
+            found, jnp.where(even, inside[:, lanes(n)], outside[:, lanes(n)]), 0.0
         )
 
     weights = (ori_ref, wh_ref, wl_ref)
     ad_ref[:, 0:512] = part_ref[:, 0:512] + halo_product(
-        lower(gx_in, gx_out, even_x, par_ref[2] == 1), (0, 1, 2, 3), 0, *weights
+        lower(gx_in, gx_out, even_x, there[0]), (0, 1, 2, 3), 0, *weights
     )
     ad_ref[:, 512:1024] = part_ref[:, 512:1024] + halo_product(
-        upper(gx_in, gx_out, even_x, par_ref[3] == 1), (4, 5, 6, 7), 1, *weights
+        upper(gx_in, gx_out, even_x, there[1]), (4, 5, 6, 7), 1, *weights
     )
     for cols, direction, pick in (((0, 4), 2, lower), ((3, 7), 3, upper)):
-        there = par_ref[direction + 2] == 1
-        both = halo_product(pick(gy_in, gy_out, even_y, there), cols, direction, *weights)
+        halo = pick(gy_in, gy_out, even_y, there[direction])
+        both = halo_product(halo, cols, direction, *weights)
         for n, col in enumerate(cols):
             ad_ref[:, lanes(col)] += both[:, lanes(n)]
 
 
 def step_kernel(
-    scales, part_ref, r_ref, d_ref, x_ref, coef_ref, ori_ref, wh_ref, wl_ref, sel_ref, par_ref,
+    scales, part_ref, r_ref, d_ref, x_ref, coef_ref, ori_ref, wh_ref, wl_ref, sel_ref, place_ref,
     gx_in, gx_out, gy_in, gy_out, r_out, d_out, x_out, sx_in, sx_out, sy_in, sy_out, ad_ref,
 ):
-    halo_sum(part_ref, ori_ref, wh_ref, wl_ref, par_ref, (gx_in, gx_out, gy_in, gy_out), ad_ref)
+    halo_sum(part_ref, ori_ref, wh_ref, wl_ref, place_ref, (gx_in, gx_out, gy_in, gy_out), ad_ref)
     keep, gain = scales
     for col in range(COLS):
         at = lanes(col)
@@ -229,16 +259,16 @@
     emit_traces(
         lambda col: d_out[:, lanes(col)] * tile_coef(coef_ref, col),
         sel_ref,
-        par_ref,
+        place_ref,
         (sx_in, sx_out, sy_in, sy_out),
     )
 
 
 def last_kernel(
-    part_ref, r_ref, x_ref, ori_ref, wh_ref, wl_ref, par_ref, gx_in, gx_out, gy_in, gy_out,
+    part_ref, r_ref, x_ref, ori_ref, wh_ref, wl_ref, place_ref, gx_in, gx_out, gy_in, gy_out,
     x_out, r_out, ad_ref,
 ):
-    halo_sum(part_ref, ori_ref, wh_ref, wl_ref, par_ref, (gx_in, gx_out, gy_in, gy_out), ad_ref)
+    halo_sum(part_ref, ori_ref, wh_ref, wl_ref, place_ref, (gx_in, gx_out, gy_in, gy_out), ad_ref)
     for col in range(COLS):
         at = lanes(col)
         rows = pl.ds(col, BLOCK, stride=COLS)
@@ -246,15 +276,9 @@
         r_out[rows, :] = r_ref[:, at] - ad_ref[:, at]
 
 
-def pack_kernel(in_ref, out_ref):
-    for s in range(in_ref.shape[0]):
-        for column in range(CW):
-            tiles = [in_ref[s, 8 * q : 8 * q + 8, column, :] for q in range(3)]
-            tiles.append(jnp.zeros((8, CAP), F32))
-            out_ref[s, column] = jnp.concatenate(tiles, axis=-1)
-
-
-def slots_kernel(agg_ref, owner_ref, hot_ref):
+def slots_kernel(agg_hbm, owner_hbm, hot_ref, agg_ref, owner_ref, sems):
+    for copy in fetch(((agg_hbm, agg_ref), (owner_hbm, owner_ref)), sems):
+        copy.wait()
     owner = owner_ref[...]
     owner_hot = lax.broadcasted_iota(jnp.int32, (OWNERS, AGG), 0) == owner
     before = lax.broadcasted_iota(jnp.int32, (AGG, AGG), 0) < lax.broadcasted_iota(
@@ -273,8 +297,14 @@
         hot_ref[:, at] = hot.astype(BF16)
 
 
-def restrict_kernel(r_ref, hot_ref, pth_ref, ptl_ref, out_ref, rhs_ref):
-    r_high, r_low = split(r_ref[...])
+def restrict_kernel(
+    part_ref, r_ref, ori_ref, wh_ref, wl_ref, hot_ref, pth_ref, ptl_ref, place_ref,
+    gx_in, gx_out, gy_in, gy_out, r_out, out_ref, ad_ref, rhs_ref,
+):
+    halo_sum(part_ref, ori_ref, wh_ref, wl_ref, place_ref, (gx_in, gx_out, gy_in, gy_out), ad_ref)
+    resid = r_ref[...] - ad_ref[...]
+    r_out[...] = resid
+    r_high, r_low = split(resid)
     proj = dot3(pth_ref[...], ptl_ref[...], r_high, r_low)
     p_high, p_low = split(proj)
     rhs_ref[...] = dot_nt(p_high, hot_ref[...]) + dot_nt(p_low, hot_ref[...])
@@ -289,23 +319,17 @@
         out_ref[o] = total
 
 
-def solve_kernel(rhs_ref, inv_ref, out_ref, wide_ref):
-    group = lax.broadcasted_iota(jnp.int32, (8, LANES), 1) >> 5
+def solve_kernel(rhs_ref, inv_ref, out_ref):
+    pad = jnp.zeros((8, CAP), F32)
     for s in range(OWNERS):
         tile = rhs_ref[s]
-        for q in range(3):
-            part = jnp.where(group == q, tile, 0.0)
-            part = part + pltpu.roll(part, 32, 1)
-            wide_ref[s, 8 * q : 8 * q + 8, :] = part + pltpu.roll(part, 64, 1)
-        total = None
-        for b in range(CW):
-            term = inv_ref[s, b] * wide_ref[s, b : b + 1, :]
-            total = term if total is None else total + term
-        out_ref[s] = total
+        rhs = jnp.concatenate([tile[:, CAP * q : CAP * (q + 1)] for q in range(3)], axis=0)
+        rows = [jnp.sum(inv_ref[s, 8 * q : 8 * q + 8] * rhs[None], axis=1) for q in range(3)]
+        out_ref[s] = jnp.concatenate([*rows, pad], axis=1)
 
 
 def lift_kernel(
-    sol_in, x_ref, coef_ref, hot_ref, ph_ref, pl_ref, sel_ref, par_ref,
+    sol_in, x_ref, coef_ref, hot_ref, ph_ref, pl_ref, sel_ref, place_ref,
     d_out, x_out, sx_in, sx_out, sy_in, sy_out, sol_ref,
 ):
     group = lax.broadcasted_iota(jnp.int32, (8, LANES), 1) >> 5
@@ -329,7 +353,7 @@
     emit_traces(
         lambda col: d_out[:, lanes(col)] * tile_coef(coef_ref, col),
         sel_ref,
-        par_ref,
+        place_ref,
         (sx_in, sx_out, sy_in, sy_out),
     )
 
@@ -338,19 +362,17 @@
     return pltpu.VMEM(shape, dtype)
 
 
-def call(kernel, outs, args, scratch=(), smem=(), limit=20):
-    vmem = pl.BlockSpec(memory_space=pltpu.VMEM)
-    scalar = pl.BlockSpec(memory_space=pltpu.SMEM)
-    specs = [scalar if n in smem else vmem for n in range(len(args))]
-    placed = [
-        a if n in smem else pltpu.with_memory_space_constraint(a, pltpu.VMEM)
-        for n, a in enumerate(args)
-    ]
+def call(kernel, outs, args, scratch=(), smem=(), hbm=(), limit=20):
+    specs, placed = [], []
+    for n, a in enumerate(args):
+        space = pltpu.SMEM if n in smem else pltpu.HBM if n in hbm else pltpu.VMEM
+        specs.append(pl.BlockSpec(memory_space=space))
+        placed.append(a if n in smem else pltpu.with_memory_space_constraint(a, space))
     return pl.pallas_call(
         kernel,
         out_shape=outs,
         in_specs=specs,
-        out_specs=[vmem] * len(outs),
+        out_specs=[pl.BlockSpec(memory_space=pltpu.VMEM)] * len(outs),
         scratch_shapes=list(scratch),
         compiler_params=pltpu.CompilerParams(vmem_limit_bytes=limit << 20),
     )(*placed)
@@ -392,39 +414,38 @@
     coarse_inverse,
 ):
     shape = right_side.shape
-    at_x, at_y = lax.axis_index("gx"), lax.axis_index("gy")
-    par = jnp.stack(
-        [
-            at_x & 1,
-            at_y & 1,
-            at_x > 0,
-            at_x < lax.axis_size("gx") - 1,
-            at_y > 0,
-            at_y < lax.axis_size("gy") - 1,
-        ]
-    ).astype(jnp.int32)
-    sel = jnp.asarray(selection())
-    coef = coefficient.reshape(COLS, LANES)
-    ori = orientation.reshape(6 * COLS, LANES)
-
+    place = jnp.stack([lax.axis_index("gx"), lax.axis_index("gy")])
+    place = jnp.concatenate(
+        [place, jnp.array([lax.axis_size("gx") - 1, lax.axis_size("gy") - 1], jnp.int32)]
+    )
+    dma = pltpu.SemaphoreType.DMA
     full = field(BLOCK, ELEMS)
-    r, d, *sends = call(
+    rows = (BLOCK * COLS, LANES)
+    r, d, coef, ori, sel, *sends = call(
         first_kernel,
-        [full, full, *SENDS],
-        [right_side.reshape(BLOCK * COLS, LANES), coef, sel, par],
-        smem=(3,),
+        [full, full, field(COLS, LANES), field(6 * COLS, LANES, dtype=jnp.int32),
+         field(BLOCK, BLOCK, dtype=BF16), *SENDS],
+        [right_side.reshape(rows), coefficient.reshape(COLS, LANES),
+         orientation.reshape(6 * COLS, LANES), jnp.asarray(selection()), place],
+        scratch=[field(*rows), dma((4,))],
+        smem=(4,),
+        hbm=(0, 1, 2, 3),
     )
     wide = field(BLOCK, 768, dtype=BF16)
+    down, up = field(CW, BLOCK, dtype=BF16), field(BLOCK, CW, dtype=BF16)
     wh, wl, pth, ptl, ph, plo = call(
         weights_kernel,
-        [wide, wide, field(CW, BLOCK, dtype=BF16), field(CW, BLOCK, dtype=BF16),
-         field(BLOCK, CW, dtype=BF16), field(BLOCK, CW, dtype=BF16)],
+        [wide, wide, down, down, up, up],
         [stiffness, jnp.transpose(face_blocks, (0, 1, 3, 2)).reshape(576, BLOCK), prolong_basis.T],
+        scratch=[field(BLOCK, BLOCK), field(576, BLOCK), field(CW, BLOCK), dma((3,))],
+        hbm=(0, 1, 2),
     )
     hot = call(
         slots_kernel,
         [field(ELEMS, ELEMS, dtype=BF16)],
         [aggregate_map.reshape(COLS, LANES), owner_map.reshape(1, AGG)],
+        scratch=[field(COLS, LANES, dtype=jnp.int32), field(1, AGG, dtype=jnp.int32), dma((2,))],
+        hbm=(0, 1),
     )[0]
 
     def interior(step):
@@ -447,7 +468,7 @@
         return call(
             functools.partial(step_kernel, scales),
             [full, full, full, *SENDS],
-            [part, r, d, x, coef, ori, wh, wl, sel, par, *gets],
+            [part, r, d, x, coef, ori, wh, wl, sel, place, *gets],
             scratch=accumulator,
             smem=(9,),
         )
@@ -456,28 +477,24 @@
     x = d
     for scales in steps:
         r, d, x, *sends = advance(scales, r, d, x, sends)
-    r, _, _, *_ = advance((0.0, 1.0 / THETA), r, d, x, sends)
+    gets = exchange(sends)
+    part = interior(d)
     packets = field(OWNERS, 8, LANES)
-    rhs = call(
-        restrict_kernel, [packets], [r, hot, pth, ptl], scratch=[pltpu.VMEM((CW, ELEMS), F32)]
-    )[0]
+    r, rhs = call(
+        restrict_kernel,
+        [full, packets],
+        [part, r, ori, wh, wl, hot, pth, ptl, place, *gets],
+        scratch=[*accumulator, field(CW, ELEMS)],
+        smem=(8,),
+    )
     rhs = lax.all_to_all(rhs, "gx", split_axis=0, concat_axis=0, tiled=True)
-    inverse = pl.pallas_call(
-        pack_kernel,
-        out_shape=field(OWNERS, CW, 8, LANES),
-        grid=(8,),
-        in_specs=[pl.BlockSpec((4, CW, CW, CAP), lambda s: (s, 0, 0, 0))],
-        out_specs=pl.BlockSpec((4, CW, 8, LANES), lambda s: (s, 0, 0, 0)),
-        compiler_params=pltpu.CompilerParams(vmem_limit_bytes=16 << 20),
-    )(jnp.transpose(coarse_inverse[0], (0, 2, 3, 1)))
-    sol = call(
-        solve_kernel, [packets], [rhs, inverse], scratch=[pltpu.VMEM((OWNERS, CW, LANES), F32)]
-    )[0]
+    inverse = jnp.transpose(coarse_inverse[0], (0, 2, 3, 1))
+    sol = call(solve_kernel, [packets], [rhs, inverse])[0]
     sol = lax.all_to_all(sol, "gx", split_axis=0, concat_axis=0, tiled=True)
     d, x, *sends = call(
         lift_kernel,
         [full, full, *SENDS],
-        [sol, x, coef, hot, ph, plo, sel, par],
+        [sol, x, coef, hot, ph, plo, sel, place],
         scratch=[pltpu.VMEM((CW, ELEMS), F32)],
         smem=(7,),
     )
@@ -489,7 +506,7 @@
     x, r = call(
         last_kernel,
         [jax.ShapeDtypeStruct((BLOCK * COLS, LANES), F32)] * 2,
-        [part, r, x, ori, wh, wl, par, *gets],
+        [part, r, x, ori, wh, wl, place, *gets],
         scratch=accumulator,
         smem=(6,),
     )

time: 119 us -> 105 us (0.88)
  local copies, waits for them, and re-layouts: 15.9 us -> 0.01 us
  blocking collectives: 15.1 us -> 22.9 us
  starting transfers between devices: 37.9 us -> 34.3 us
  Pallas kernels: 37.9 us -> 35.1 us
    unnamed x42 -> x6, local copies, waits for them, and re-layouts: 15.9 us -> 0.01 us
    all_to_all x0 -> x1, blocking collectives: none -> 11.7 us  [shards(): rhs = lax.all_to_all(rhs, 'gx', split_axis=0, concat_axis=0, tiled=True)]
    all_to_all x1 -> x0, starting transfers between devices: 3.86 us -> none  [shards(): rhs = lax.all_to_all(rhs, 'gx', split_axis=0, concat_axis=0, tiled=True)]
    all_to_all x1, blocking collectives: 15.1 us -> 11.3 us  [shards(): sol = lax.all_to_all(sol, 'gx', split_axis=0, concat_axis=0, tiled=True)]
    pallas_call x21 -> x19, Pallas kernels: 37.9 us -> 35.1 us  [call(): pl.pallas_call(kernel, out_shape=outs, in_specs=specs, out_specs=[pl.Bloc...]
  transfers between devices with their start and end apart: 29 -> 28, of which waited for: 10 -> 9; matrix products, arithmetic and copies ran while one was open for 0% -> 0% of each run, Pallas kernels for 17% -> 16%
where the time goes in v3:
time: 105 us; the launch traced here: 104 us
  Pallas kernels  35.1 us (33%)
  starting transfers between devices  34.3 us (33%)
  blocking collectives  22.9 us (22%)
  waiting for transfers between devices  10.4 us (10%)
    pallas_call x19, Pallas kernels, call(): pl.pallas_call(kernel, out_shape=outs, in_specs=specs, out_specs=[pl.Bloc...  35.1 us
    ppermute x14, starting transfers between devices, swap_odd(): lax.ppermute(v, axis, [(i, (i + 1 if i % 2 else i - 1) % count) for i in...  28.8 us
    all_to_all x1, blocking collectives, shards(): rhs = lax.all_to_all(rhs, 'gx', split_axis=0, concat_axis=0, tiled=True)  11.7 us
    all_to_all x1, blocking collectives, shards(): sol = lax.all_to_all(sol, 'gx', split_axis=0, concat_axis=0, tiled=True)  11.3 us
    ppermute x14, waiting for transfers between devices, swap_odd(): lax.ppermute(v, axis, [(i, (i + 1 if i % 2 else i - 1) % count) for i in...  8.56 us
    ppermute x14, starting transfers between devices, swap_even(): return lax.ppermute(v, axis, [(i, i ^ 1) for i in range(count)])  5.56 us
  transfers between devices with their start and end apart: 28, of which 9 were waited for; matrix products, arithmetic and copies ran while one was open for 0% of the time, Pallas kernels for 16%

profile of v3, /device:TPU:0, one launch (start us, length us, event | category | flops | bytes accessed | tf_op | source)
XLA Modules:
  0.0 104.5 jit_solution(12762917107678532844)
XLA Ops:
  1.4 2.1 %shard_map.122 = (f32[192,1024]{1,0:T(8,128)S(1)}, f32[192,1024]{1,0:T(8,128)S(1)}, f32[8,128]{1,0:T(8,128)S(1)}, s32[48,128]{1,0:T(8,128)S(1)}, bf16[192,192]{1...) custom-call(f32[1536,128]{1,0:T(8,128)} %bitcast.19, ...), custom_call_target="tpu_custom_call" | custom-call | tf_op jit(solution)/shard_map/pallas_call | solution.py:371
  3.6 6.4 %collective-permute-start.1 = (f32[48,512]{1,0:T(8,128)S(1)}, f32[48,512]{1,0:T(8,128)S(1)}, u32[]{:S(2)}, u32[]{:S(2)}) collective-permute-start(f32[48,512]{1,0:T(8,128)S(1)} %get-tuple-element.70), channel_id=1, source_target_pairs={{0,124},{4,8},{8,4},{12,16},{16,12},{20,24},{24,20},{28,32},{32,28... | collective-permute-start | bytes 294920 | tf_op jit(solution)/shard_map/ppermute | solution.py:388
  10.0 1.6 %collective-permute-start.2 = (f32[48,256]{1,0:T(8,128)S(1)}, f32[48,256]{1,0:T(8,128)S(1)}, u32[]{:S(2)}, u32[]{:S(2)}) collective-permute-start(f32[48,256]{1,0:T(8,128)S(1)} %get-tuple-element.71), channel_id=1, source_target_pairs={{0,1},{1,0},{2,3},{3,2},{4,5},{5,4},{6,7},{7,6},{8,9},{9,8},{10,11... | collective-permute-start | bytes 147464 | tf_op jit(solution)/shard_map/ppermute | solution.py:383
  11.6 2.2 %collective-permute-start.3 = (f32[48,256]{1,0:T(8,128)S(1)}, f32[48,256]{1,0:T(8,128)S(1)}, u32[]{:S(2)}, u32[]{:S(2)}) collective-permute-start(f32[48,256]{1,0:T(8,128)S(1)} %get-tuple-element.72), channel_id=1, source_target_pairs={{0,3},{1,2},{2,1},{3,0},{4,7},{5,6},{6,5},{7,4},{8,11},{9,10},{10,... | collective-permute-start | bytes 147464 | tf_op jit(solution)/shard_map/ppermute | solution.py:388
  13.8 1.6 %shard_map.123 = (bf16[192,768]{1,0:T(8,128)(2,1)S(1)}, bf16[192,768]{1,0:T(8,128)(2,1)S(1)}, bf16[24,192]{1,0:T(8,128)(2,1)S(1)}, bf16[24,192]{1,0:T(8,128)(2,1...) custom-call(f32[192,192]{1,0:T(8,128)} %stiff_hbm.1, f32[576,192]{1,0:T(8,128)} %bitcast.20, ...), custom_call_target="tpu_custom_call" | custom-call | tf_op jit(solution)/shard_map/pallas_call | solution.py:371
  15.4 1.8 %shard_map.124.part_ref = f32[192,1024]{1,0:T(8,128)S(1)} custom-call(f32[192,1024]{1,0:T(8,128)S(1)} %get-tuple-element.62.d_ref.x_ref, f32[8,128]{1,0:T(8,128)S(1)} %get-tuple-element.63.coef_ref, s32[48,128]{1,0:T(8,128)S(1)} %get-tuple-element.64.ori_ref, bf16[192,768]{1,0:T(8,128)(2,1)S(1)} %get-tuple-element.65.wh_ref, ...), custom_call_target="tpu_custom_call" | custom-call | tf_op jit(solution)/shard_map/pallas_call | solution.py:371
  17.2 1.6 %shard_map.125 = (f32[192,1024]{1,0:T(8,128)S(1)}, f32[192,1024]{1,0:T(8,128)S(1)}, f32[192,1024]{1,0:T(8,128)S(1)}, f32[48,512]{1,0:T(8,128)S(1)}, f32[48,512]{...) custom-call(f32[192,1024]{1,0:T(8,128)S(1)} %shard_map.124.part_ref, ...), custom_call_target="tpu_custom_call" | custom-call | tf_op jit(solution)/shard_map/pallas_call | solution.py:371
  20.7 2.2 %collective-permute-start.7 = (f32[48,256]{1,0:T(8,128)S(1)}, f32[48,256]{1,0:T(8,128)S(1)}, u32[]{:S(2)}, u32[]{:S(2)}) collective-permute-start(f32[48,256]{1,0:T(8,128)S(1)} %get-tuple-element.79), channel_id=1, source_target_pairs={{0,3},{1,2},{2,1},{3,0},{4,7},{5,6},{6,5},{7,4},{8,11},{9,10},{10,... | collective-permute-start | bytes 147464 | tf_op jit(solution)/shard_map/ppermute | solution.py:388
  22.9 1.8 %shard_map.126.part_ref = f32[192,1024]{1,0:T(8,128)S(1)} custom-call(f32[192,1024]{1,0:T(8,128)S(1)} %get-tuple-element.73.d_ref, f32[8,128]{1,0:T(8,128)S(1)} %get-tuple-element.63.coef_ref, s32[48,128]{1,0:T(8,128)S(1)} %get-tuple-element.64.ori_ref, bf16[192,768]{1,0:T(8,128)(2,1)S(1)} %get-tuple-element.65.wh_ref, ...), custom_call_target="tpu_custom_call" | custom-call | tf_op jit(solution)/shard_map/pallas_call | solution.py:371
  26.3 1.5 %shard_map.127 = (f32[192,1024]{1,0:T(8,128)S(1)}, f32[192,1024]{1,0:T(8,128)S(1)}, f32[192,1024]{1,0:T(8,128)S(1)}, f32[48,512]{1,0:T(8,128)S(1)}, f32[48,512]{...) custom-call(f32[192,1024]{1,0:T(8,128)S(1)} %shard_map.126.part_ref, ...), custom_call_target="tpu_custom_call" | custom-call | tf_op jit(solution)/shard_map/pallas_call | solution.py:371
  28.0 2.3 %collective-permute-start.9 = (f32[48,512]{1,0:T(8,128)S(1)}, f32[48,512]{1,0:T(8,128)S(1)}, u32[]{:S(2)}, u32[]{:S(2)}) collective-permute-start(f32[48,512]{1,0:T(8,128)S(1)} %get-tuple-element.85), channel_id=1, source_target_pairs={{0,124},{4,8},{8,4},{12,16},{16,12},{20,24},{24,20},{28,32},{32,28... | collective-permute-start | bytes 294920 | tf_op jit(solution)/shard_map/ppermute | solution.py:388
  30.5 1.9 %collective-permute-start.11 = (f32[48,256]{1,0:T(8,128)S(1)}, f32[48,256]{1,0:T(8,128)S(1)}, u32[]{:S(2)}, u32[]{:S(2)}) collective-permute-start(f32[48,256]{1,0:T(8,128)S(1)} %get-tuple-element.87), channel_id=1, source_target_pairs={{0,3},{1,2},{2,1},{3,0},{4,7},{5,6},{6,5},{7,4},{8,11},{9,10},{10,... | collective-permute-start | bytes 147464 | tf_op jit(solution)/shard_map/ppermute | solution.py:388
  32.3 2.4 %shard_map.129.hot_ref = bf16[1024,1024]{1,0:T(8,128)(2,1)S(1)} custom-call(s32[8,128]{1,0:T(8,128)} %bitcast.24, s32[1,512]{1,0:T(1,128)} %bitcast.25), custom_call_target="tpu_custom_call" | custom-call | tf_op jit(solution)/shard_map/pallas_call | solution.py:371
  34.7 1.8 %shard_map.128.part_ref = f32[192,1024]{1,0:T(8,128)S(1)} custom-call(f32[192,1024]{1,0:T(8,128)S(1)} %get-tuple-element.80.d_ref, f32[8,128]{1,0:T(8,128)S(1)} %get-tuple-element.63.coef_ref, s32[48,128]{1,0:T(8,128)S(1)} %get-tuple-element.64.ori_ref, bf16[192,768]{1,0:T(8,128)(2,1)S(1)} %get-tuple-element.65.wh_ref, ...), custom_call_target="tpu_custom_call" | custom-call | tf_op jit(solution)/shard_map/pallas_call | solution.py:371
  36.5 2.9 %shard_map.130 = (f32[192,1024]{1,0:T(8,128)S(1)}, f32[32,8,128]{2,1,0:T(8,128)S(1)}) custom-call(f32[192,1024]{1,0:T(8,128)S(1)} %shard_map.128.part_ref, f32[192,1024]{1,0:T(8,128)S(1)} %get-tuple-element.81.r_ref, s32[48,128]{1,0:T(8,128)S(1)} %get-tuple-element.64.ori_ref, bf16[192,768]{1,0:T(8,128)(2,1)S(1)} %get-tuple-element.65.wh_ref, ...), custom_call_target="tpu_custom_call" | custom-call | tf_op jit(solution)/shard_map/pallas_call | solution.py:371
  39.4 11.7 %all_to_all.10.rhs_ref = f32[32,8,128]{2,1,0:T(8,128)S(1)} all-to-all(f32[32,8,128]{2,1,0:T(8,128)S(1)} %get-tuple-element.88), channel_id=1, replica_groups=mesh['gx'=32,'gy'=4] {'gx'}, dimensions={0} | all-to-all | bytes 262144 | tf_op jit(solution)/shard_map/all_to_all | solution.py:490
  51.1 1.6 %shard_map.131 = f32[32,8,128]{2,1,0:T(8,128)S(1)} custom-call(f32[32,8,128]{2,1,0:T(8,128)S(1)} %all_to_all.10.rhs_ref, f32[32,24,24,32]{3,2,1,0:T(8,128)S(1)} %bitcast.18), custom_call_target="tpu_custom_call" | custom-call | tf_op jit(solution)/shard_map/pallas_call | solution.py:371
  52.7 11.3 %all_to_all.11.sol_in = f32[32,8,128]{2,1,0:T(8,128)S(1)} all-to-all(f32[32,8,128]{2,1,0:T(8,128)S(1)} %shard_map.131), channel_id=1, replica_groups=mesh['gx'=32,'gy'=4] {'gx'}, dimensions={0} | all-to-all | bytes 262144 | tf_op jit(solution)/shard_map/all_to_all | solution.py:493
  63.9 1.9 %shard_map.132 = (f32[192,1024]{1,0:T(8,128)S(1)}, f32[192,1024]{1,0:T(8,128)S(1)}, f32[48,512]{1,0:T(8,128)S(1)}, f32[48,512]{1,0:T(8,128)S(1)}, f32[48,256]{1,0:T(8,128)S(1)}, /*index=5*/f32[48,256]{1,0:T(8,128)S(1)}) custom-call(f32[32,8,128]{2,1,0:T(8,128)S(1)} %all_to_all.11.sol_in, f32[192,1024]{1,0:T(8,128)S(1)} %get-tuple-element.89.x_ref, ...), custom_call_target="tpu_custom_call" | custom-call | tf_op jit(solution)/shard_map/pallas_call | solution.py:371
  66.1 1.9 %collective-permute-start.13 = (f32[48,512]{1,0:T(8,128)S(1)}, f32[48,512]{1,0:T(8,128)S(1)}, u32[]{:S(2)}, u32[]{:S(2)}) collective-permute-start(f32[48,512]{1,0:T(8,128)S(1)} %get-tuple-element.96), channel_id=1, source_target_pairs={{0,124},{4,8},{8,4},{12,16},{16,12},{20,24},{24,20},{28,32},{32,28... | collective-permute-start | bytes 294920 | tf_op jit(solution)/shard_map/ppermute | solution.py:388
  70.4 1.8 %shard_map.133.part_ref = f32[192,1024]{1,0:T(8,128)S(1)} custom-call(f32[192,1024]{1,0:T(8,128)S(1)} %get-tuple-element.92.d_ref, f32[8,128]{1,0:T(8,128)S(1)} %get-tuple-element.63.coef_ref, s32[48,128]{1,0:T(8,128)S(1)} %get-tuple-element.64.ori_ref, bf16[192,768]{1,0:T(8,128)(2,1)S(1)} %get-tuple-element.65.wh_ref, ...), custom_call_target="tpu_custom_call" | custom-call | tf_op jit(solution)/shard_map/pallas_call | solution.py:371
  72.2 2.2 %collective-permute-done.15.gy_out = f32[48,256]{1,0:T(8,128)S(1)} collective-permute-done((f32[48,256]{1,0:T(8,128)S(1)}, f32[48,256]{1,0:T(8,128)S(1)}, u32[]{:S(2)}, u32[]{:S(2)}) %collective-permute-start.15) | collective-permute-done | bytes 49184 | tf_op jit(solution)/shard_map/ppermute | solution.py:388
  76.0 1.9 %collective-permute-start.17 = (f32[48,512]{1,0:T(8,128)S(1)}, f32[48,512]{1,0:T(8,128)S(1)}, u32[]{:S(2)}, u32[]{:S(2)}) collective-permute-start(f32[48,512]{1,0:T(8,128)S(1)} %get-tuple-element.103), channel_id=1, source_target_pairs={{0,124},{4,8},{8,4},{12,16},{16,12},{20,24},{24,20},{28,32},{32,28... | collective-permute-start | bytes 294920 | tf_op jit(solution)/shard_map/ppermute | solution.py:388
  79.5 1.8 %shard_map.135.part_ref = f32[192,1024]{1,0:T(8,128)S(1)} custom-call(f32[192,1024]{1,0:T(8,128)S(1)} %get-tuple-element.99.d_ref, f32[8,128]{1,0:T(8,128)S(1)} %get-tuple-element.63.coef_ref, s32[48,128]{1,0:T(8,128)S(1)} %get-tuple-element.64.ori_ref, bf16[192,768]{1,0:T(8,128)(2,1)S(1)} %get-tuple-element.65.wh_ref, ...), custom_call_target="tpu_custom_call" | custom-call | tf_op jit(solution)/shard_map/pallas_call | solution.py:371
  83.5 1.5 %shard_map.136 = (f32[192,1024]{1,0:T(8,128)S(1)}, f32[192,1024]{1,0:T(8,128)S(1)}, f32[192,1024]{1,0:T(8,128)S(1)}, f32[48,512]{1,0:T(8,128)S(1)}, f32[48,512]{...) custom-call(f32[192,1024]{1,0:T(8,128)S(1)} %shard_map.135.part_ref, ...), custom_call_target="tpu_custom_call" | custom-call | tf_op jit(solution)/shard_map/pallas_call | solution.py:371
  85.1 1.9 %collective-permute-start.21 = (f32[48,512]{1,0:T(8,128)S(1)}, f32[48,512]{1,0:T(8,128)S(1)}, u32[]{:S(2)}, u32[]{:S(2)}) collective-permute-start(f32[48,512]{1,0:T(8,128)S(1)} %get-tuple-element.110), channel_id=1, source_target_pairs={{0,124},{4,8},{8,4},{12,16},{16,12},{20,24},{24,20},{28,32},{32,28... | collective-permute-start | bytes 294920 | tf_op jit(solution)/shard_map/ppermute | solution.py:388
  88.9 1.8 %shard_map.137.part_ref = f32[192,1024]{1,0:T(8,128)S(1)} custom-call(f32[192,1024]{1,0:T(8,128)S(1)} %get-tuple-element.106.d_ref, f32[8,128]{1,0:T(8,128)S(1)} %get-tuple-element.63.coef_ref, s32[48,128]{1,0:T(8,128)S(1)} %get-tuple-element.64.ori_ref, bf16[192,768]{1,0:T(8,128)(2,1)S(1)} %get-tuple-element.65.wh_ref, ...), custom_call_target="tpu_custom_call" | custom-call | tf_op jit(solution)/shard_map/pallas_call | solution.py:371
  91.2 1.7 %collective-permute-done.23.gy_out = f32[48,256]{1,0:T(8,128)S(1)} collective-permute-done((f32[48,256]{1,0:T(8,128)S(1)}, f32[48,256]{1,0:T(8,128)S(1)}, u32[]{:S(2)}, u32[]{:S(2)}) %collective-permute-start.23) | collective-permute-done | bytes 49184 | tf_op jit(solution)/shard_map/ppermute | solution.py:388
  92.9 1.6 %shard_map.138 = (f32[192,1024]{1,0:T(8,128)S(1)}, f32[192,1024]{1,0:T(8,128)S(1)}, f32[192,1024]{1,0:T(8,128)S(1)}, f32[48,512]{1,0:T(8,128)S(1)}, f32[48,512]{...) custom-call(f32[192,1024]{1,0:T(8,128)S(1)} %shard_map.137.part_ref, ...), custom_call_target="tpu_custom_call" | custom-call | tf_op jit(solution)/shard_map/pallas_call | solution.py:371
  94.6 1.9 %collective-permute-start.25 = (f32[48,512]{1,0:T(8,128)S(1)}, f32[48,512]{1,0:T(8,128)S(1)}, u32[]{:S(2)}, u32[]{:S(2)}) collective-permute-start(f32[48,512]{1,0:T(8,128)S(1)} %get-tuple-element.117), channel_id=1, source_target_pairs={{0,124},{4,8},{8,4},{12,16},{16,12},{20,24},{24,20},{28,32},{32,28... | collective-permute-start | bytes 294920 | tf_op jit(solution)/shard_map/ppermute | solution.py:388
  98.0 1.8 %shard_map.139.part_ref = f32[192,1024]{1,0:T(8,128)S(1)} custom-call(f32[192,1024]{1,0:T(8,128)S(1)} %get-tuple-element.113.d_ref, f32[8,128]{1,0:T(8,128)S(1)} %get-tuple-element.63.coef_ref, s32[48,128]{1,0:T(8,128)S(1)} %get-tuple-element.64.ori_ref, bf16[192,768]{1,0:T(8,128)(2,1)S(1)} %get-tuple-element.65.wh_ref, ...), custom_call_target="tpu_custom_call" | custom-call | tf_op jit(solution)/shard_map/pallas_call | solution.py:371
  102.0 2.4 %shard_map.140 = (f32[1536,128]{1,0:T(8,128)}, f32[1536,128]{1,0:T(8,128)}) custom-call(f32[192,1024]{1,0:T(8,128)S(1)} %shard_map.139.part_ref, f32[192,1024]{1,0:T(8,128)S(1)} %get-tuple-element.114.r_ref, f32[192,1024]{1,0:T(8,128)S(1)} %get-tuple-element.115.x_ref, s32[48,128]{1,0:T(8,128)S(1)} %get-tuple-element.64.ori_ref, ...), custom_call_target="tpu_custom_call" | custom-call | tf_op jit(solution)/shard_map/pallas_call | solution.py:371
  (53 shorter events, 19.0 us)
Async XLA Ops:
  3.5 13.7 %collective-permute-start = (f32[48,512]{1,0:T(8,128)S(1)}, f32[48,512]{1,0:T(8,128)S(1)}, u32[]{:S(2)}, u32[]{:S(2)}) collective-permute-start(f32[48,512]{1,0:T(8,128)S(1)} %get-tuple-element.69), channel_id=1, source_target_pairs={{0,4},{4,0},{8,12},{12,8},{16,20},{20,16},{24,28},{28,24},{32,36},... | collective-permute-start | bytes 294920 | tf_op jit(solution)/shard_map/ppermute | solution.py:383
  3.6 13.6 %collective-permute-start.1 = (f32[48,512]{1,0:T(8,128)S(1)}, f32[48,512]{1,0:T(8,128)S(1)}, u32[]{:S(2)}, u32[]{:S(2)}) collective-permute-start(f32[48,512]{1,0:T(8,128)S(1)} %get-tuple-element.70), channel_id=1, source_target_pairs={{0,124},{4,8},{8,4},{12,16},{16,12},{20,24},{24,20},{28,32},{32,28... | collective-permute-start | bytes 294920 | tf_op jit(solution)/shard_map/ppermute | solution.py:388
  10.0 7.1 %collective-permute-start.2 = (f32[48,256]{1,0:T(8,128)S(1)}, f32[48,256]{1,0:T(8,128)S(1)}, u32[]{:S(2)}, u32[]{:S(2)}) collective-permute-start(f32[48,256]{1,0:T(8,128)S(1)} %get-tuple-element.71), channel_id=1, source_target_pairs={{0,1},{1,0},{2,3},{3,2},{4,5},{5,4},{6,7},{7,6},{8,9},{9,8},{10,11... | collective-permute-start | bytes 147464 | tf_op jit(solution)/shard_map/ppermute | solution.py:383
  11.6 5.6 %collective-permute-start.3 = (f32[48,256]{1,0:T(8,128)S(1)}, f32[48,256]{1,0:T(8,128)S(1)}, u32[]{:S(2)}, u32[]{:S(2)}) collective-permute-start(f32[48,256]{1,0:T(8,128)S(1)} %get-tuple-element.72), channel_id=1, source_target_pairs={{0,3},{1,2},{2,1},{3,0},{4,7},{5,6},{6,5},{7,4},{8,11},{9,10},{10,... | collective-permute-start | bytes 147464 | tf_op jit(solution)/shard_map/ppermute | solution.py:388
  15.4 35.7 %slice-start = ((s8[9437184]{0:T(1024)(128)(4,1)}), s8[4194304]{0:T(1024)(128)(4,1)S(1)}, s32[]{:S(2)}) async-start(s8[9437184]{0:T(1024)(128)(4,1)} %bitcast.16), calls=%async_computation.2 | async-start | bytes 8388608
  18.8 7.2 %collective-permute-start.4 = (f32[48,512]{1,0:T(8,128)S(1)}, f32[48,512]{1,0:T(8,128)S(1)}, u32[]{:S(2)}, u32[]{:S(2)}) collective-permute-start(f32[48,512]{1,0:T(8,128)S(1)} %get-tuple-element.76), channel_id=1, source_target_pairs={{0,4},{4,0},{8,12},{12,8},{16,20},{20,16},{24,28},{28,24},{32,36},... | collective-permute-start | bytes 294920 | tf_op jit(solution)/shard_map/ppermute | solution.py:383
  18.9 7.4 %collective-permute-start.5 = (f32[48,512]{1,0:T(8,128)S(1)}, f32[48,512]{1,0:T(8,128)S(1)}, u32[]{:S(2)}, u32[]{:S(2)}) collective-permute-start(f32[48,512]{1,0:T(8,128)S(1)} %get-tuple-element.77), channel_id=1, source_target_pairs={{0,124},{4,8},{8,4},{12,16},{16,12},{20,24},{24,20},{28,32},{32,28... | collective-permute-start | bytes 294920 | tf_op jit(solution)/shard_map/ppermute | solution.py:388
  19.8 4.9 %collective-permute-start.6 = (f32[48,256]{1,0:T(8,128)S(1)}, f32[48,256]{1,0:T(8,128)S(1)}, u32[]{:S(2)}, u32[]{:S(2)}) collective-permute-start(f32[48,256]{1,0:T(8,128)S(1)} %get-tuple-element.78), channel_id=1, source_target_pairs={{0,1},{1,0},{2,3},{3,2},{4,5},{5,4},{6,7},{7,6},{8,9},{9,8},{10,11... | collective-permute-start | bytes 147464 | tf_op jit(solution)/shard_map/ppermute | solution.py:383
  20.7 5.3 %collective-permute-start.7 = (f32[48,256]{1,0:T(8,128)S(1)}, f32[48,256]{1,0:T(8,128)S(1)}, u32[]{:S(2)}, u32[]{:S(2)}) collective-permute-start(f32[48,256]{1,0:T(8,128)S(1)} %get-tuple-element.79), channel_id=1, source_target_pairs={{0,3},{1,2},{2,1},{3,0},{4,7},{5,6},{6,5},{7,4},{8,11},{9,10},{10,... | collective-permute-start | bytes 147464 | tf_op jit(solution)/shard_map/ppermute | solution.py:388
  22.9 28.2 %slice-start.1 = ((s8[9437184]{0:T(1024)(128)(4,1)}), s8[4194304]{0:T(1024)(128)(4,1)S(1)}, s32[]{:S(2)}) async-start(s8[9437184]{0:T(1024)(128)(4,1)} %bitcast.16), calls=%async_computation.3 | async-start | bytes 8388608
  27.9 8.6 %collective-permute-start.8 = (f32[48,512]{1,0:T(8,128)S(1)}, f32[48,512]{1,0:T(8,128)S(1)}, u32[]{:S(2)}, u32[]{:S(2)}) collective-permute-start(f32[48,512]{1,0:T(8,128)S(1)} %get-tuple-element.84), channel_id=1, source_target_pairs={{0,4},{4,0},{8,12},{12,8},{16,20},{20,16},{24,28},{28,24},{32,36},... | collective-permute-start | bytes 294920 | tf_op jit(solution)/shard_map/ppermute | solution.py:383
  28.0 8.5 %collective-permute-start.9 = (f32[48,512]{1,0:T(8,128)S(1)}, f32[48,512]{1,0:T(8,128)S(1)}, u32[]{:S(2)}, u32[]{:S(2)}) collective-permute-start(f32[48,512]{1,0:T(8,128)S(1)} %get-tuple-element.85), channel_id=1, source_target_pairs={{0,124},{4,8},{8,4},{12,16},{16,12},{20,24},{24,20},{28,32},{32,28... | collective-permute-start | bytes 294920 | tf_op jit(solution)/shard_map/ppermute | solution.py:388
  30.3 6.2 %collective-permute-start.10 = (f32[48,256]{1,0:T(8,128)S(1)}, f32[48,256]{1,0:T(8,128)S(1)}, u32[]{:S(2)}, u32[]{:S(2)}) collective-permute-start(f32[48,256]{1,0:T(8,128)S(1)} %get-tuple-element.86), channel_id=1, source_target_pairs={{0,1},{1,0},{2,3},{3,2},{4,5},{5,4},{6,7},{7,6},{8,9},{9,8},{10,11... | collective-permute-start | bytes 147464 | tf_op jit(solution)/shard_map/ppermute | solution.py:383
  30.5 6.0 %collective-permute-start.11 = (f32[48,256]{1,0:T(8,128)S(1)}, f32[48,256]{1,0:T(8,128)S(1)}, u32[]{:S(2)}, u32[]{:S(2)}) collective-permute-start(f32[48,256]{1,0:T(8,128)S(1)} %get-tuple-element.87), channel_id=1, source_target_pairs={{0,3},{1,2},{2,1},{3,0},{4,7},{5,6},{6,5},{7,4},{8,11},{9,10},{10,... | collective-permute-start | bytes 147464 | tf_op jit(solution)/shard_map/ppermute | solution.py:388
  32.3 18.7 %slice-start.2 = ((s8[9437184]{0:T(1024)(128)(4,1)}), s8[1048576]{0:T(1024)(128)(4,1)S(1)}, s32[]{:S(2)}) async-start(s8[9437184]{0:T(1024)(128)(4,1)} %bitcast.16), calls=%async_computation.4 | async-start | bytes 2097152
  65.9 8.5 %collective-permute-start.12 = (f32[48,512]{1,0:T(8,128)S(1)}, f32[48,512]{1,0:T(8,128)S(1)}, u32[]{:S(2)}, u32[]{:S(2)}) collective-permute-start(f32[48,512]{1,0:T(8,128)S(1)} %get-tuple-element.95), channel_id=1, source_target_pairs={{0,4},{4,0},{8,12},{12,8},{16,20},{20,16},{24,28},{28,24},{32,36},... | collective-permute-start | bytes 294920 | tf_op jit(solution)/shard_map/ppermute | solution.py:383
  66.1 8.3 %collective-permute-start.13 = (f32[48,512]{1,0:T(8,128)S(1)}, f32[48,512]{1,0:T(8,128)S(1)}, u32[]{:S(2)}, u32[]{:S(2)}) collective-permute-start(f32[48,512]{1,0:T(8,128)S(1)} %get-tuple-element.96), channel_id=1, source_target_pairs={{0,124},{4,8},{8,4},{12,16},{16,12},{20,24},{24,20},{28,32},{32,28... | collective-permute-start | bytes 294920 | tf_op jit(solution)/shard_map/ppermute | solution.py:388
  67.9 4.3 %collective-permute-start.14 = (f32[48,256]{1,0:T(8,128)S(1)}, f32[48,256]{1,0:T(8,128)S(1)}, u32[]{:S(2)}, u32[]{:S(2)}) collective-permute-start(f32[48,256]{1,0:T(8,128)S(1)} %get-tuple-element.97), channel_id=1, source_target_pairs={{0,1},{1,0},{2,3},{3,2},{4,5},{5,4},{6,7},{7,6},{8,9},{9,8},{10,11... | collective-permute-start | bytes 147464 | tf_op jit(solution)/shard_map/ppermute | solution.py:383
  69.1 5.3 %collective-permute-start.15 = (f32[48,256]{1,0:T(8,128)S(1)}, f32[48,256]{1,0:T(8,128)S(1)}, u32[]{:S(2)}, u32[]{:S(2)}) collective-permute-start(f32[48,256]{1,0:T(8,128)S(1)} %get-tuple-element.98), channel_id=1, source_target_pairs={{0,3},{1,2},{2,1},{3,0},{4,7},{5,6},{6,5},{7,4},{8,11},{9,10},{10,... | collective-permute-start | bytes 147464 | tf_op jit(solution)/shard_map/ppermute | solution.py:388
  75.9 7.5 %collective-permute-start.16 = (f32[48,512]{1,0:T(8,128)S(1)}, f32[48,512]{1,0:T(8,128)S(1)}, u32[]{:S(2)}, u32[]{:S(2)}) collective-permute-start(f32[48,512]{1,0:T(8,128)S(1)} %get-tuple-element.102), channel_id=1, source_target_pairs={{0,4},{4,0},{8,12},{12,8},{16,20},{20,16},{24,28},{28,24},{32,36},... | collective-permute-start | bytes 294920 | tf_op jit(solution)/shard_map/ppermute | solution.py:383
  76.0 7.4 %collective-permute-start.17 = (f32[48,512]{1,0:T(8,128)S(1)}, f32[48,512]{1,0:T(8,128)S(1)}, u32[]{:S(2)}, u32[]{:S(2)}) collective-permute-start(f32[48,512]{1,0:T(8,128)S(1)} %get-tuple-element.103), channel_id=1, source_target_pairs={{0,124},{4,8},{8,4},{12,16},{16,12},{20,24},{24,20},{28,32},{32,28... | collective-permute-start | bytes 294920 | tf_op jit(solution)/shard_map/ppermute | solution.py:388
  77.9 4.1 %collective-permute-start.18 = (f32[48,256]{1,0:T(8,128)S(1)}, f32[48,256]{1,0:T(8,128)S(1)}, u32[]{:S(2)}, u32[]{:S(2)}) collective-permute-start(f32[48,256]{1,0:T(8,128)S(1)} %get-tuple-element.104), channel_id=1, source_target_pairs={{0,1},{1,0},{2,3},{3,2},{4,5},{5,4},{6,7},{7,6},{8,9},{9,8},{10,11... | collective-permute-start | bytes 147464 | tf_op jit(solution)/shard_map/ppermute | solution.py:383
  78.2 5.3 %collective-permute-start.19 = (f32[48,256]{1,0:T(8,128)S(1)}, f32[48,256]{1,0:T(8,128)S(1)}, u32[]{:S(2)}, u32[]{:S(2)}) collective-permute-start(f32[48,256]{1,0:T(8,128)S(1)} %get-tuple-element.105), channel_id=1, source_target_pairs={{0,3},{1,2},{2,1},{3,0},{4,7},{5,6},{6,5},{7,4},{8,11},{9,10},{10,... | collective-permute-start | bytes 147464 | tf_op jit(solution)/shard_map/ppermute | solution.py:388
  85.0 7.9 %collective-permute-start.20 = (f32[48,512]{1,0:T(8,128)S(1)}, f32[48,512]{1,0:T(8,128)S(1)}, u32[]{:S(2)}, u32[]{:S(2)}) collective-permute-start(f32[48,512]{1,0:T(8,128)S(1)} %get-tuple-element.109), channel_id=1, source_target_pairs={{0,4},{4,0},{8,12},{12,8},{16,20},{20,16},{24,28},{28,24},{32,36},... | collective-permute-start | bytes 294920 | tf_op jit(solution)/shard_map/ppermute | solution.py:383
  85.1 7.8 %collective-permute-start.21 = (f32[48,512]{1,0:T(8,128)S(1)}, f32[48,512]{1,0:T(8,128)S(1)}, u32[]{:S(2)}, u32[]{:S(2)}) collective-permute-start(f32[48,512]{1,0:T(8,128)S(1)} %get-tuple-element.110), channel_id=1, source_target_pairs={{0,124},{4,8},{8,4},{12,16},{16,12},{20,24},{24,20},{28,32},{32,28... | collective-permute-start | bytes 294920 | tf_op jit(solution)/shard_map/ppermute | solution.py:388
  87.1 4.1 %collective-permute-start.22 = (f32[48,256]{1,0:T(8,128)S(1)}, f32[48,256]{1,0:T(8,128)S(1)}, u32[]{:S(2)}, u32[]{:S(2)}) collective-permute-start(f32[48,256]{1,0:T(8,128)S(1)} %get-tuple-element.111), channel_id=1, source_target_pairs={{0,1},{1,0},{2,3},{3,2},{4,5},{5,4},{6,7},{7,6},{8,9},{9,8},{10,11... | collective-permute-start | bytes 147464 | tf_op jit(solution)/shard_map/ppermute | solution.py:383
  87.6 5.3 %collective-permute-start.23 = (f32[48,256]{1,0:T(8,128)S(1)}, f32[48,256]{1,0:T(8,128)S(1)}, u32[]{:S(2)}, u32[]{:S(2)}) collective-permute-start(f32[48,256]{1,0:T(8,128)S(1)} %get-tuple-element.112), channel_id=1, source_target_pairs={{0,3},{1,2},{2,1},{3,0},{4,7},{5,6},{6,5},{7,4},{8,11},{9,10},{10,... | collective-permute-start | bytes 147464 | tf_op jit(solution)/shard_map/ppermute | solution.py:388
  94.5 7.5 %collective-permute-start.24 = (f32[48,512]{1,0:T(8,128)S(1)}, f32[48,512]{1,0:T(8,128)S(1)}, u32[]{:S(2)}, u32[]{:S(2)}) collective-permute-start(f32[48,512]{1,0:T(8,128)S(1)} %get-tuple-element.116), channel_id=1, source_target_pairs={{0,4},{4,0},{8,12},{12,8},{16,20},{20,16},{24,28},{28,24},{32,36},... | collective-permute-start | bytes 294920 | tf_op jit(solution)/shard_map/ppermute | solution.py:383
  94.6 7.4 %collective-permute-start.25 = (f32[48,512]{1,0:T(8,128)S(1)}, f32[48,512]{1,0:T(8,128)S(1)}, u32[]{:S(2)}, u32[]{:S(2)}) collective-permute-start(f32[48,512]{1,0:T(8,128)S(1)} %get-tuple-element.117), channel_id=1, source_target_pairs={{0,124},{4,8},{8,4},{12,16},{16,12},{20,24},{24,20},{28,32},{32,28... | collective-permute-start | bytes 294920 | tf_op jit(solution)/shard_map/ppermute | solution.py:388
  96.4 4.1 %collective-permute-start.26 = (f32[48,256]{1,0:T(8,128)S(1)}, f32[48,256]{1,0:T(8,128)S(1)}, u32[]{:S(2)}, u32[]{:S(2)}) collective-permute-start(f32[48,256]{1,0:T(8,128)S(1)} %get-tuple-element.118), channel_id=1, source_target_pairs={{0,1},{1,0},{2,3},{3,2},{4,5},{5,4},{6,7},{7,6},{8,9},{9,8},{10,11... | collective-permute-start | bytes 147464 | tf_op jit(solution)/shard_map/ppermute | solution.py:383
  96.7 5.3 %collective-permute-start.27 = (f32[48,256]{1,0:T(8,128)S(1)}, f32[48,256]{1,0:T(8,128)S(1)}, u32[]{:S(2)}, u32[]{:S(2)}) collective-permute-start(f32[48,256]{1,0:T(8,128)S(1)} %get-tuple-element.119), channel_id=1, source_target_pairs={{0,3},{1,2},{2,1},{3,0},{4,7},{5,6},{6,5},{7,4},{8,11},{9,10},{10,... | collective-permute-start | bytes 147464 | tf_op jit(solution)/shard_map/ppermute | solution.py:388

commit v4 on v3

v4 whole, which is shorter than its diff:
```python
import functools

import jax
import jax.numpy as jnp
import ml_dtypes
import numpy as np
from jax import lax
from jax.experimental import pallas as pl
from jax.experimental.pallas import tpu as pltpu
from jax.sharding import PartitionSpec as P

BLOCK = 192
TRACE = 48
CW = 24
DEGREE = 3
COLS = 8
LANES = 128
ELEMS = COLS * LANES
OWNERS = 32
CAP = 32
AGG = 512

F32 = jnp.float32
BF16 = jnp.bfloat16

THETA = 0.5 * (4.0 + 0.25)
DELTA = 0.5 * (4.0 - 0.25)
SIGMA = THETA / DELTA


def chebyshev():
    rho = 1.0 / SIGMA
    steps = []
    for _ in range(DEGREE - 1):
        rho_new = 1.0 / (2.0 * SIGMA - rho)
        steps.append((rho_new * rho, 2.0 * rho_new / DELTA))
        rho = rho_new
    return steps


def selection():
    sel = np.zeros((192, 192), np.float32)
    t = np.arange(48)
    for group, rows in enumerate(
        (16 * (t // 4) + t % 4, 16 * (t // 4) + t % 4 + 12, 4 * t, 4 * t + 3)
    ):
        sel[48 * group + t, rows] = 1.0
    return sel.astype(ml_dtypes.bfloat16)


def dot(a, b):
    return jnp.dot(a, b, preferred_element_type=F32)


def dot_nt(a, b):
    return lax.dot_general(a, b, (((1,), (1,)), ((), ())), preferred_element_type=F32)


def split(v):
    high = v.astype(BF16)
    return high, (v - high.astype(F32)).astype(BF16)


def dot3(a_high, a_low, b_high, b_low):
    return dot(a_high, b_high) + dot(a_high, b_low) + dot(a_low, b_high)


def lanes(col):
    return slice(LANES * col, LANES * (col + 1))


def face_rows(v, node):
    at = 16 * node
    return jnp.concatenate([v[64 * c + at : 64 * c + at + 16] for c in range(3)], axis=0)


def tile_coef(coef_ref, col):
    return coef_ref[col : col + 1, :]


def sides():
    at_x, at_y = lax.axis_index("gx"), lax.axis_index("gy")
    last_x, last_y = lax.axis_size("gx") - 1, lax.axis_size("gy") - 1
    return at_x % 2 == 0, at_y % 2 == 0, (at_x > 0, at_x < last_x, at_y > 0, at_y < last_y)


def y_traces(w_of, sel_ref):
    ends = []
    for y, rows in ((0, slice(0, 48)), (3, slice(48, 96))):
        high, low = split(jnp.concatenate([w_of(y), w_of(4 + y)], axis=1))
        pick = sel_ref[rows, :]
        ends.append(dot(pick, high) + dot(pick, low))
    return ends


def post(lower_x, upper_x, lower_y, upper_y, sends):
    sx_in, sx_out, sy_in, sy_out = sends
    even_x, even_y, _ = sides()
    sx_in[...] = jnp.where(even_x, upper_x, lower_x)
    sx_out[...] = jnp.where(even_x, lower_x, upper_x)
    sy_in[...] = jnp.where(even_y, upper_y, lower_y)
    sy_out[...] = jnp.where(even_y, lower_y, upper_y)


def edge_traces(w_of, sel_ref):
    lower_x = jnp.concatenate([face_rows(w_of(y), 0) for y in range(4)], axis=1)
    upper_x = jnp.concatenate([face_rows(w_of(4 + y), 3) for y in range(4)], axis=1)
    return (lower_x, upper_x, *y_traces(w_of, sel_ref))


def fetch(pairs, sems):
    copies = [pltpu.make_async_copy(a, b, sems.at[n]) for n, (a, b) in enumerate(pairs)]
    for copy in copies:
        copy.start()
    return copies


def first_kernel(
    rs_hbm, coef_hbm, ori_hbm, sel_hbm, agg_hbm, owner_hbm,
    r_ref, d_ref, coef_ref, ori_ref, sel_ref, agg_ref, owner_ref, sx_in, sx_out, sy_in, sy_out,
    rs_ref, sems,
):
    copies = fetch(
        (
            (rs_hbm, rs_ref),
            (coef_hbm, coef_ref),
            (sel_hbm, sel_ref),
            (ori_hbm, ori_ref),
            (agg_hbm, agg_ref),
            (owner_hbm, owner_ref),
        ),
        sems,
    )
    for copy in copies[:3]:
        copy.wait()
    for col in range(COLS):
        v = rs_ref[pl.ds(col, BLOCK, stride=COLS), :]
        r_ref[:, lanes(col)] = v
        d_ref[:, lanes(col)] = v * (1.0 / THETA)
    post(
        *edge_traces(lambda col: d_ref[:, lanes(col)] * tile_coef(coef_ref, col), sel_ref),
        (sx_in, sx_out, sy_in, sy_out),
    )
    for copy in copies[3:]:
        copy.wait()


def weights_kernel(
    stiff_hbm, faces_hbm, pt_hbm, sel_ref,
    wh_ref, wl_ref, halo_ref, rim_ref, pth_ref, ptl_ref, ph_ref, pl_ref,
    stiff_ref, faces_ref, pt_ref, sems,
):
    copies = fetch(((stiff_hbm, stiff_ref), (pt_hbm, pt_ref), (faces_hbm, faces_ref)), sems)
    copies[0].wait()
    high, low = split(stiff_ref[...])
    wh_ref[:, 0:BLOCK] = high
    wl_ref[:, 0:BLOCK] = low
    copies[1].wait()
    pt = pt_ref[...]
    high, low = split(pt)
    pth_ref[...] = high
    ptl_ref[...] = low
    high, low = split(pt.T)
    ph_ref[...] = high
    pl_ref[...] = low
    copies[2].wait()
    for piece in range(3):
        high, low = split(faces_ref[192 * piece : 192 * (piece + 1), :].T)
        wh_ref[:, 192 * (piece + 1) : 192 * (piece + 2)] = high
        wl_ref[:, 192 * (piece + 1) : 192 * (piece + 2)] = low
    for direction in range(4):
        at = BLOCK + 96 * direction
        high, low = wh_ref[:, at : at + 96], wl_ref[:, at : at + 96]
        stack = jnp.concatenate([high, high, low], axis=1)
        halo_ref[direction] = stack
        if direction < 2:
            near, far = face_rows(stack, 3 * direction), sel_ref[0:96, :]
            rim_ref[direction, 0:48, :] = near
            rim_ref[direction, 48:144, :] = dot(far, stack).astype(BF16)
        else:
            rim_ref[direction, 0:48, :] = face_rows(stack, 0)
            rim_ref[direction, 48:96, :] = face_rows(stack, 3)
            pick = sel_ref[48 * (direction - 2) : 48 * (direction - 1), :]
            rim_ref[direction, 96:144, :] = dot(pick, stack).astype(BF16)


def interior(d_ref, coef_ref, ori_ref, wh_ref, wl_ref, sel_ref, out_ref, xh_ref, xl_ref, t_ref):
    for col in range(COLS):
        high, low = split(d_ref[:, lanes(col)] * tile_coef(coef_ref, col))
        xh_ref[0:BLOCK, lanes(col)] = high
        xl_ref[0:BLOCK, lanes(col)] = low
    lane = lax.broadcasted_iota(jnp.int32, (48, LANES), 1)
    for x_ref in (xh_ref, xl_ref):
        t_ref[...] = dot(sel_ref[...], x_ref[0:BLOCK, :])
        for col in range(COLS):
            x, y = col // 4, col % 4
            for direction in range(6):
                trace = None
                if direction == 0 and x == 1:
                    trace = face_rows(x_ref[0:BLOCK, lanes(col - 4)], 3).astype(F32)
                elif direction == 1 and x == 0:
                    trace = face_rows(x_ref[0:BLOCK, lanes(col + 4)], 0).astype(F32)
                elif direction == 2 and y > 0:
                    trace = t_ref[48:96, lanes(col - 1)]
                elif direction == 3 and y < 3:
                    trace = t_ref[0:48, lanes(col + 1)]
                elif direction == 4:
                    trace = jnp.where(lane == 0, 0.0, pltpu.roll(t_ref[144:192, lanes(col)], 1, 1))
                elif direction == 5:
                    trace = jnp.where(
                        lane == LANES - 1, 0.0, pltpu.roll(t_ref[96:144, lanes(col)], LANES - 1, 1)
                    )
                at = BLOCK + 96 * direction
                if trace is None:
                    x_ref[at : at + 96, lanes(col)] = jnp.zeros((96, LANES), BF16)
                    continue
                row = COLS * direction + col
                picked = ori_ref[row : row + 1, :] == 1
                x_ref[at : at + 48, lanes(col)] = jnp.where(picked, 0.0, trace).astype(BF16)
                x_ref[at + 48 : at + 96, lanes(col)] = jnp.where(picked, trace, 0.0).astype(BF16)
    for half in range(2):
        span = slice(512 * half, 512 * (half + 1))
        out_ref[:, span] = dot3(wh_ref[...], wl_ref[...], xh_ref[:, span], xl_ref[:, span])


def ahead(scales, r_ref, d_ref, part_ref, coef_ref, sel_ref, pres):
    keep, gain = scales

    def w_of(col):
        at = lanes(col)
        step = gain * (r_ref[:, at] - part_ref[:, at])
        if keep:
            step = keep * d_ref[:, at] + step
        return step * tile_coef(coef_ref, col)

    for pre, value in zip(pres, edge_traces(w_of, sel_ref)):
        pre[...] = value


def start_kernel(
    scales, r_ref, d_ref, coef_ref, ori_ref, wh_ref, wl_ref, sel_ref, *rest,
):
    part_ref, *pres, xh_ref, xl_ref, t_ref = rest
    interior(d_ref, coef_ref, ori_ref, wh_ref, wl_ref, sel_ref, part_ref, xh_ref, xl_ref, t_ref)
    ahead(scales, r_ref, d_ref, part_ref, coef_ref, sel_ref, pres)


def halo_stacks(ori_ref, gets):
    gx_in, gx_out, gy_in, gy_out = gets
    even_x, even_y, found = sides()
    stacks = []
    for direction, cols in enumerate(((0, 1, 2, 3), (4, 5, 6, 7), (0, 4), (3, 7))):
        inside, outside, even = (gx_in, gx_out, even_x) if direction < 2 else (gy_in, gy_out, even_y)
        from_outside = even if direction % 2 == 0 else jnp.logical_not(even)
        parts = []
        for n, col in enumerate(cols):
            trace = jnp.where(from_outside, outside[:, lanes(n)], inside[:, lanes(n)])
            trace = jnp.where(found[direction], trace, 0.0)
            row = COLS * direction + col
            picked = ori_ref[row : row + 1, :] == 1
            both = jnp.concatenate(
                [jnp.where(picked, 0.0, trace), jnp.where(picked, trace, 0.0)], axis=0
            )
            high, low = split(both)
            parts.append(jnp.concatenate([high, low, high], axis=0))
        stacks.append(jnp.concatenate(parts, axis=1))
    return stacks


def send_kernel(gain, coef_ref, ori_ref, rim_ref, *rest):
    gets, pres, sends, stacks = rest[0:4], rest[4:8], rest[8:12], rest[12:16]
    values = halo_stacks(ori_ref, gets)
    for stack, value in zip(stacks, values):
        stack[...] = value
    from_x = [dot(rim_ref[n], values[n]) for n in range(2)]
    from_y = [dot(rim_ref[n], values[n]) for n in range(2, 4)]
    lower_x, upper_x, lower_y, upper_y = pres
    xs = []
    for x, pre in enumerate((lower_x, upper_x)):
        cols = []
        for y in range(4):
            halo = from_x[x][0:48, lanes(y)]
            if y in (0, 3):
                halo = halo + from_y[y // 3][48 * x : 48 * x + 48, lanes(x)]
            cols.append(pre[:, lanes(y)] - halo * (gain * tile_coef(coef_ref, 4 * x + y)))
        xs.append(jnp.concatenate(cols, axis=1))
    ys = []
    for end, pre in enumerate((lower_y, upper_y)):
        cols = []
        for x in range(2):
            halo = from_y[end][96:144, lanes(x)]
            halo = halo + from_x[x][48 + 48 * end : 96 + 48 * end, lanes(3 * end)]
            cols.append(pre[:, lanes(x)] - halo * (gain * tile_coef(coef_ref, 4 * x + 3 * end)))
        ys.append(jnp.concatenate(cols, axis=1))
    post(*xs, *ys, sends)


def add_halo(ad_ref, part_ref, halo_ref, values):
    ad_ref[:, 0:512] = part_ref[:, 0:512] + dot(halo_ref[0], values[0])
    ad_ref[:, 512:1024] = part_ref[:, 512:1024] + dot(halo_ref[1], values[1])
    for end in range(2):
        both = dot(halo_ref[2 + end], values[2 + end])
        for x in range(2):
            ad_ref[:, lanes(4 * x + 3 * end)] += both[:, lanes(x)]


def step_kernel(
    scales, onward, closing, part_ref, r_ref, d_ref, x_ref, coef_ref, ori_ref, wh_ref, wl_ref, sel_ref,
    halo_ref, lx_ref, ux_ref, ly_ref, uy_ref, r_out, d_out, x_out, part_out, *rest,
):
    *pres, xh_ref, xl_ref, t_ref, ad_ref = rest
    add_halo(ad_ref, part_ref, halo_ref, [v[...] for v in (lx_ref, ux_ref, ly_ref, uy_ref)])
    keep, gain = scales
    for col in range(COLS):
        at = lanes(col)
        resid = r_ref[:, at] - ad_ref[:, at]
        step = gain * resid
        if keep:
            step = keep * d_ref[:, at] + step
        r_out[:, at] = resid
        d_out[:, at] = step
        total = x_ref[:, at] + step
        if closing:
            x_out[pl.ds(col, BLOCK, stride=COLS), :] = total
        else:
            x_out[:, at] = total
    interior(d_out, coef_ref, ori_ref, wh_ref, wl_ref, sel_ref, part_out, xh_ref, xl_ref, t_ref)
    if onward is not None:
        ahead(onward, r_out, d_out, part_out, coef_ref, sel_ref, pres)


def last_kernel(part_ref, r_ref, ori_ref, halo_ref, gx_in, gx_out, gy_in, gy_out, r_out, ad_ref):
    add_halo(ad_ref, part_ref, halo_ref, halo_stacks(ori_ref, (gx_in, gx_out, gy_in, gy_out)))
    for col in range(COLS):
        at = lanes(col)
        r_out[pl.ds(col, BLOCK, stride=COLS), :] = r_ref[:, at] - ad_ref[:, at]


def slots_kernel(agg_ref, owner_ref, hot_ref):
    owner = owner_ref[...]
    owner_hot = lax.broadcasted_iota(jnp.int32, (OWNERS, AGG), 0) == owner
    before = lax.broadcasted_iota(jnp.int32, (AGG, AGG), 0) < lax.broadcasted_iota(
        jnp.int32, (AGG, AGG), 1
    )
    counts = dot(owner_hot.astype(BF16), before.astype(BF16))
    slot = jnp.sum(jnp.where(owner_hot, counts, 0.0), axis=0, keepdims=True)
    first = lax.broadcasted_iota(jnp.int32, (8, AGG), 0) == 0
    table = jnp.where(first, owner.astype(F32), slot).astype(BF16)
    for col in range(COLS):
        at = lanes(col)
        member = lax.broadcasted_iota(jnp.int32, (AGG, LANES), 0) == agg_ref[col : col + 1, :]
        found = dot(table, member.astype(BF16))
        target = (found[0:1] * float(CAP) + found[1:2]).astype(jnp.int32)
        hot = lax.broadcasted_iota(jnp.int32, (OWNERS * CAP, LANES), 0) == target
        hot_ref[:, at] = hot.astype(BF16)


def restrict_kernel(
    part_ref, r_ref, ori_ref, halo_ref, hot_ref, pth_ref, ptl_ref,
    gx_in, gx_out, gy_in, gy_out, r_out, out_ref, ad_ref, rhs_ref,
):
    add_halo(ad_ref, part_ref, halo_ref, halo_stacks(ori_ref, (gx_in, gx_out, gy_in, gy_out)))
    resid = r_ref[...] - ad_ref[...]
    r_out[...] = resid
    r_high, r_low = split(resid)
    proj = dot3(pth_ref[...], ptl_ref[...], r_high, r_low)
    p_high, p_low = split(proj)
    rhs_ref[...] = dot_nt(p_high, hot_ref[...]) + dot_nt(p_low, hot_ref[...])
    group = lax.broadcasted_iota(jnp.int32, (8, LANES), 1) >> 5
    for o in range(OWNERS):
        total = jnp.zeros((8, LANES), F32)
        for q in range(3):
            moved = rhs_ref[8 * q : 8 * q + 8, lanes(o // 4)]
            if q != o % 4:
                moved = pltpu.roll(moved, 32 * ((q - o) % 4), 1)
            total = jnp.where(group == q, moved, total)
        out_ref[o] = total


def solve_kernel(rhs_ref, inv_ref, out_ref):
    pad = jnp.zeros((8, CAP), F32)
    for s in range(OWNERS):
        tile = rhs_ref[s]
        rhs = jnp.concatenate([tile[:, CAP * q : CAP * (q + 1)] for q in range(3)], axis=0)
        rows = [jnp.sum(inv_ref[s, 8 * q : 8 * q + 8] * rhs[None], axis=1) for q in range(3)]
        out_ref[s] = jnp.concatenate([*rows, pad], axis=1)


def lift_kernel(
    sol_in, x_ref, coef_ref, hot_ref, ph_ref, pl_ref, sel_ref,
    d_out, x_out, sx_in, sx_out, sy_in, sy_out, sol_ref,
):
    group = lax.broadcasted_iota(jnp.int32, (8, LANES), 1) >> 5
    for q in range(3):
        for j in range(8):
            total = jnp.zeros((8, LANES), F32)
            for g in range(4):
                moved = sol_in[4 * j + g]
                if g != q:
                    moved = pltpu.roll(moved, 32 * ((g - q) % 4), 1)
                total = jnp.where(group == g, moved, total)
            sol_ref[8 * q : 8 * q + 8, lanes(j)] = total
    s_high, s_low = split(sol_ref[...])
    each = dot(s_high, hot_ref[...]) + dot(s_low, hot_ref[...])
    e_high, e_low = split(each)
    for half in range(2):
        span = slice(512 * half, 512 * (half + 1))
        lift = dot3(ph_ref[...], pl_ref[...], e_high[:, span], e_low[:, span])
        d_out[:, span] = lift
        x_out[:, span] = x_ref[:, span] + lift
    post(
        *edge_traces(lambda col: d_out[:, lanes(col)] * tile_coef(coef_ref, col), sel_ref),
        (sx_in, sx_out, sy_in, sy_out),
    )


def field(*shape, dtype=F32):
    return pltpu.VMEM(shape, dtype)


def call(kernel, outs, args, scratch=(), hbm=(), limit=20):
    specs, placed = [], []
    for n, a in enumerate(args):
        space = pltpu.HBM if n in hbm else pltpu.VMEM
        specs.append(pl.BlockSpec(memory_space=space))
        placed.append(pltpu.with_memory_space_constraint(a, space))
    return pl.pallas_call(
        kernel,
        out_shape=outs,
        in_specs=specs,
        out_specs=[pl.BlockSpec(memory_space=pltpu.VMEM)] * len(outs),
        scratch_shapes=list(scratch),
        compiler_params=pltpu.CompilerParams(vmem_limit_bytes=limit << 20),
    )(*placed)


def swap_even(v, axis):
    count = lax.axis_size(axis)
    return lax.ppermute(v, axis, [(i, i ^ 1) for i in range(count)])


def swap_odd(v, axis):
    count = lax.axis_size(axis)
    return lax.ppermute(
        v, axis, [(i, (i + 1 if i % 2 else i - 1) % count) for i in range(count)]
    )


def exchange(sends):
    return (
        swap_even(sends[0], "gx"),
        swap_odd(sends[1], "gx"),
        swap_even(sends[2], "gy"),
        swap_odd(sends[3], "gy"),
    )


SENDS = [field(48, 512), field(48, 512), field(48, 256), field(48, 256)]


def shards(
    right_side,
    coefficient,
    orientation,
    aggregate_map,
    owner_map,
    stiffness,
    face_blocks,
    prolong_basis,
    coarse_inverse,
):
    shape = right_side.shape
    dma = pltpu.SemaphoreType.DMA
    ints = functools.partial(field, dtype=jnp.int32)
    halves = functools.partial(field, dtype=BF16)
    full = field(BLOCK, ELEMS)
    rows = (BLOCK * COLS, LANES)
    r, d, coef, ori, sel, agg, owner, *sends = call(
        first_kernel,
        [full, full, field(COLS, LANES), ints(6 * COLS, LANES), halves(BLOCK, BLOCK),
         ints(COLS, LANES), ints(1, AGG), *SENDS],
        [right_side.reshape(rows), coefficient.reshape(COLS, LANES),
         orientation.reshape(6 * COLS, LANES), jnp.asarray(selection()),
         aggregate_map.reshape(COLS, LANES), owner_map.reshape(1, AGG)],
        scratch=[field(*rows), dma((6,))],
        hbm=(0, 1, 2, 3, 4, 5),
    )
    wide, down, up = halves(BLOCK, 768), halves(CW, BLOCK), halves(BLOCK, CW)
    wh, wl, halo, rim, pth, ptl, ph, plo = call(
        weights_kernel,
        [wide, wide, halves(4, BLOCK, 288), halves(4, 144, 288), down, down, up, up],
        [stiffness, jnp.transpose(face_blocks, (0, 1, 3, 2)).reshape(576, BLOCK), prolong_basis.T,
         sel],
        scratch=[field(BLOCK, BLOCK), field(576, BLOCK), field(CW, BLOCK), dma((3,))],
        hbm=(0, 1, 2),
    )
    hot = call(slots_kernel, [halves(ELEMS, ELEMS)], [agg, owner])[0]

    products = [halves(768, ELEMS), halves(768, ELEMS), full]
    stacks = [halves(288, 512), halves(288, 512), halves(288, 256), halves(288, 256)]
    tables = [coef, ori, wh, wl, sel]

    def start(scales, r, d):
        return call(functools.partial(start_kernel, scales), [full, *SENDS], [r, d, *tables], products)

    def step(scales, onward, part, r, d, x, gets, pres, closing=False):
        *sends, lx, ux, ly, uy = call(
            functools.partial(send_kernel, scales[1]),
            [*SENDS, *stacks],
            [coef, ori, rim, *gets, *pres],
        )
        gets = exchange(sends)
        x_out = jax.ShapeDtypeStruct(rows, F32) if closing else full
        outs = [full, full, x_out, full] + ([] if onward is None else SENDS)
        r, d, x, part, *pres = call(
            functools.partial(step_kernel, scales, onward, closing),
            outs,
            [part, r, d, x, *tables, halo, lx, ux, ly, uy],
            [*products, full],
        )
        return part, r, d, x, gets, pres

    second, third = chebyshev()
    opening = (0.0, 1.0 / THETA)
    gets = exchange(sends)
    part, *pres = start(second, r, d)
    part, r, d, x, gets, pres = step(second, third, part, r, d, d, gets, pres)
    part, r, d, x, gets, _ = step(third, None, part, r, d, x, gets, pres)
    packets = field(OWNERS, 8, LANES)
    r, rhs = call(
        restrict_kernel,
        [full, packets],
        [part, r, ori, halo, hot, pth, ptl, *gets],
        [full, field(CW, ELEMS)],
    )
    rhs = lax.all_to_all(rhs, "gx", split_axis=0, concat_axis=0, tiled=True)
    inverse = jnp.transpose(coarse_inverse[0], (0, 2, 3, 1))
    sol = call(solve_kernel, [packets], [rhs, inverse])[0]
    sol = lax.all_to_all(sol, "gx", split_axis=0, concat_axis=0, tiled=True)
    d, x, *sends = call(
        lift_kernel,
        [full, full, *SENDS],
        [sol, x, coef, hot, ph, plo, sel],
        [field(CW, ELEMS)],
    )
    gets = exchange(sends)
    part, *pres = start(opening, r, d)
    part, r, d, x, gets, pres = step(opening, second, part, r, d, x, gets, pres)
    part, r, d, x, gets, pres = step(second, third, part, r, d, x, gets, pres)
    part, r, _, x, gets, _ = step(third, None, part, r, d, x, gets, pres, closing=True)
    r = call(
        last_kernel,
        [jax.ShapeDtypeStruct(rows, F32)],
        [part, r, ori, halo, *gets],
        [full],
    )[0]
    return x.reshape(shape), r.reshape(shape)


def solution(mesh):
    in_specs = (
        P(None, "gx", "gy", None),
        P("gx", "gy", None),
        P(None, "gx", "gy", None),
        P("gx", "gy", None),
        P(("gx", "gy"), None),
        P(),
        P(),
        P(),
        P(("gx", "gy"), None, None, None, None),
    )
    out_specs = (P(None, "gx", "gy", None), P(None, "gx", "gy", None))
    return jax.shard_map(shards, mesh=mesh, in_specs=in_specs, out_specs=out_specs, check_vma=False)
```

time: 105 us -> 96.4 us (0.918)
  Pallas kernels: 35.1 us -> 30 us
  waiting for transfers between devices: 10.4 us -> 7.16 us
  starting transfers between devices: 34.3 us -> 35.7 us
    pallas_call x19, Pallas kernels: 35.1 us -> 30 us  [call(): pl.pallas_call(kernel, out_shape=outs, in_specs=specs, out_specs=[pl.Bloc...]
    ppermute x14, waiting for transfers between devices: 1.87 us -> 0.04 us  [swap_even(): return lax.ppermute(v, axis, [(i, i ^ 1) for i in range(count)])]
    ppermute x14, waiting for transfers between devices: 8.56 us -> 7.12 us  [swap_odd(): lax.ppermute(v, axis, [(i, (i + 1 if i % 2 else i - 1) % count) for i in...]
  transfers between devices with their start and end apart: 28 -> 28, of which waited for: 9 -> 6; matrix products, arithmetic and copies ran while one was open for 0% -> 0% of each run, Pallas kernels for 16% -> 20%
where the time goes in v4:
time: 96.4 us; the launch traced here: 96.1 us
  starting transfers between devices  35.7 us (37%)
  Pallas kernels  30 us (31%)
  blocking collectives  22.3 us (23%)
  waiting for transfers between devices  7.16 us (7%)
    pallas_call x19, Pallas kernels, call(): pl.pallas_call(kernel, out_shape=outs, in_specs=specs, out_specs=[pl.Bloc...  30 us
    ppermute x14, starting transfers between devices, swap_odd(): lax.ppermute(v, axis, [(i, (i + 1 if i % 2 else i - 1) % count) for i in...  29.2 us
    all_to_all x1, blocking collectives, shards(): sol = lax.all_to_all(sol, 'gx', split_axis=0, concat_axis=0, tiled=True)  11.3 us
    all_to_all x1, blocking collectives, shards(): rhs = lax.all_to_all(rhs, 'gx', split_axis=0, concat_axis=0, tiled=True)  11.1 us
    ppermute x14, waiting for transfers between devices, swap_odd(): lax.ppermute(v, axis, [(i, (i + 1 if i % 2 else i - 1) % count) for i in...  7.12 us
    ppermute x14, starting transfers between devices, swap_even(): return lax.ppermute(v, axis, [(i, i ^ 1) for i in range(count)])  6.42 us
  transfers between devices with their start and end apart: 28, of which 6 were waited for; matrix products, arithmetic and copies ran while one was open for 0% of the time, Pallas kernels for 20%

profile of v4, /device:TPU:0, one launch (start us, length us, event | category | flops | bytes accessed | tf_op | source)
XLA Modules:
  0.0 96.1 jit_solution(2208585802618844769)
XLA Ops:
  0.6 1.6 %shard_map.113 = (f32[192,1024]{1,0:T(8,128)S(1)}, f32[192,1024]{1,0:T(8,128)S(1)}, f32[8,128]{1,0:T(8,128)S(1)}, s32[48,128]{1,0:T(8,128)S(1)}, bf16[192,192]{1...) custom-call(f32[1536,128]{1,0:T(8,128)} %bitcast.17, ...), custom_call_target="tpu_custom_call" | custom-call | tf_op jit(solution)/shard_map/pallas_call | solution.py:427
  2.3 6.4 %collective-permute-start.1 = (f32[48,512]{1,0:T(8,128)S(1)}, f32[48,512]{1,0:T(8,128)S(1)}, u32[]{:S(2)}, u32[]{:S(2)}) collective-permute-start(f32[48,512]{1,0:T(8,128)S(1)} %get-tuple-element.120), channel_id=1, source_target_pairs={{0,124},{4,8},{8,4},{12,16},{16,12},{20,24},{24,20},{28,32},{32,28... | collective-permute-start | bytes 294920 | tf_op jit(solution)/shard_map/ppermute | solution.py:444
  8.7 1.6 %collective-permute-start.2 = (f32[48,256]{1,0:T(8,128)S(1)}, f32[48,256]{1,0:T(8,128)S(1)}, u32[]{:S(2)}, u32[]{:S(2)}) collective-permute-start(f32[48,256]{1,0:T(8,128)S(1)} %get-tuple-element.121), channel_id=1, source_target_pairs={{0,1},{1,0},{2,3},{3,2},{4,5},{5,4},{6,7},{7,6},{8,9},{9,8},{10,11... | collective-permute-start | bytes 147464 | tf_op jit(solution)/shard_map/ppermute | solution.py:439
  10.3 2.2 %collective-permute-start.3 = (f32[48,256]{1,0:T(8,128)S(1)}, f32[48,256]{1,0:T(8,128)S(1)}, u32[]{:S(2)}, u32[]{:S(2)}) collective-permute-start(f32[48,256]{1,0:T(8,128)S(1)} %get-tuple-element.122), channel_id=1, source_target_pairs={{0,3},{1,2},{2,1},{3,0},{4,7},{5,6},{6,5},{7,4},{8,11},{9,10},{10,... | collective-permute-start | bytes 147464 | tf_op jit(solution)/shard_map/ppermute | solution.py:444
  12.5 2.0 %shard_map.114 = (bf16[192,768]{1,0:T(8,128)(2,1)S(1)}, bf16[192,768]{1,0:T(8,128)(2,1)S(1)}, bf16[4,192,288]{2,1,0:T(8,128)(2,1)S(1)}, bf16[4,144,288]{2,1,0:T(...) custom-call(f32[192,192]{1,0:T(8,128)} %stiff_hbm.1, ...), custom_call_target="tpu_custom_call" | custom-call | tf_op jit(solution)/shard_map/pallas_call | solution.py:427
  14.5 2.0 %shard_map.115 = (f32[192,1024]{1,0:T(8,128)S(1)}, f32[48,512]{1,0:T(8,128)S(1)}, f32[48,512]{1,0:T(8,128)S(1)}, f32[48,256]{1,0:T(8,128)S(1)}, f32[48,256]{1,0:T(8,128)S(1)}) custom-call(f32[192,1024]{1,0:T(8,128)S(1)} %get-tuple-element.109.r_ref, f32[192,1024]{1,0:T(8,128)S(1)} %get-tuple-element.110.d_ref.x_ref, ...), custom_call_target="tpu_custom_call" | custom-call | tf_op jit(solution)/shard_map/pallas_call | solution.py:427
  18.7 1.8 %collective-permute-start.7 = (f32[48,256]{1,0:T(8,128)S(1)}, f32[48,256]{1,0:T(8,128)S(1)}, u32[]{:S(2)}, u32[]{:S(2)}) collective-permute-start(f32[48,256]{1,0:T(8,128)S(1)} %get-tuple-element.138), channel_id=1, source_target_pairs={{0,3},{1,2},{2,1},{3,0},{4,7},{5,6},{6,5},{7,4},{8,11},{9,10},{10,... | collective-permute-start | bytes 147464 | tf_op jit(solution)/shard_map/ppermute | solution.py:444
  20.5 2.4 %shard_map.117 = (f32[192,1024]{1,0:T(8,128)S(1)}, f32[192,1024]{1,0:T(8,128)S(1)}, f32[192,1024]{1,0:T(8,128)S(1)}, f32[192,1024]{1,0:T(8,128)S(1)}, f32[48,512...) custom-call(f32[192,1024]{1,0:T(8,128)S(1)} %get-tuple-element.116.part_ref, ...), custom_call_target="tpu_custom_call" | custom-call | tf_op jit(solution)/shard_map/pallas_call | solution.py:427
  25.1 2.3 %collective-permute-start.9 = (f32[48,512]{1,0:T(8,128)S(1)}, f32[48,512]{1,0:T(8,128)S(1)}, u32[]{:S(2)}, u32[]{:S(2)}) collective-permute-start(f32[48,512]{1,0:T(8,128)S(1)} %get-tuple-element.154), channel_id=1, source_target_pairs={{0,124},{4,8},{8,4},{12,16},{16,12},{20,24},{24,20},{28,32},{32,28... | collective-permute-start | bytes 294920 | tf_op jit(solution)/shard_map/ppermute | solution.py:444
  27.6 1.8 %collective-permute-start.11 = (f32[48,256]{1,0:T(8,128)S(1)}, f32[48,256]{1,0:T(8,128)S(1)}, u32[]{:S(2)}, u32[]{:S(2)}) collective-permute-start(f32[48,256]{1,0:T(8,128)S(1)} %get-tuple-element.156), channel_id=1, source_target_pairs={{0,3},{1,2},{2,1},{3,0},{4,7},{5,6},{6,5},{7,4},{8,11},{9,10},{10,... | collective-permute-start | bytes 147464 | tf_op jit(solution)/shard_map/ppermute | solution.py:444
  29.4 1.5 %shard_map.120.hot_ref = bf16[1024,1024]{1,0:T(8,128)(2,1)S(1)} custom-call(s32[8,128]{1,0:T(8,128)S(1)} %get-tuple-element.149.agg_ref, s32[1,512]{1,0:T(1,128)S(1)} %get-tuple-element.150.owner_ref), custom_call_target="tpu_custom_call" | custom-call | tf_op jit(solution)/shard_map/pallas_call | solution.py:427
  31.0 2.8 %shard_map.119 = (f32[192,1024]{1,0:T(8,128)S(1)}, f32[192,1024]{1,0:T(8,128)}, f32[192,1024]{1,0:T(8,128)S(1)}, f32[192,1024]{1,0:T(8,128)S(1)}) custom-call(f32[192,1024]{1,0:T(8,128)S(1)} %get-tuple-element.131.part_ref, f32[192,1024]{1,0:T(8,128)S(1)} %get-tuple-element.132.r_ref, f32[192,1024]{1,0:T(8,128)S(1)} %get-tuple-element.133.d_ref, ...), custom_call_target="tpu_custom_call" | custom-call | tf_op jit(solution)/shard_map/pallas_call | solution.py:427
  33.8 2.2 %shard_map.121 = (f32[192,1024]{1,0:T(8,128)S(1)}, f32[32,8,128]{2,1,0:T(8,128)S(1)}) custom-call(f32[192,1024]{1,0:T(8,128)S(1)} %get-tuple-element.147.part_ref, f32[192,1024]{1,0:T(8,128)S(1)} %get-tuple-element.148.r_ref, s32[48,128]{1,0:T(8,128)S(1)} %get-tuple-element.112.ori_ref, bf16[4,192,288]{2,1,0:T(8,128)(2,1)S(1)} %get-tuple-element.117.halo_ref, ...), custom_call_target="tpu_custom_call" | custom-call | tf_op jit(solution)/shard_map/pallas_call | solution.py:427
  36.0 11.1 %all_to_all.10.rhs_ref = f32[32,8,128]{2,1,0:T(8,128)S(1)} all-to-all(f32[32,8,128]{2,1,0:T(8,128)S(1)} %get-tuple-element.158), channel_id=1, replica_groups=mesh['gx'=32,'gy'=4] {'gx'}, dimensions={0} | all-to-all | bytes 262144 | tf_op jit(solution)/shard_map/all_to_all | solution.py:536
  47.1 1.6 %shard_map.122 = f32[32,8,128]{2,1,0:T(8,128)S(1)} custom-call(f32[32,8,128]{2,1,0:T(8,128)S(1)} %all_to_all.10.rhs_ref, f32[32,24,24,32]{3,2,1,0:T(8,128)S(1)} %bitcast.16), custom_call_target="tpu_custom_call" | custom-call | tf_op jit(solution)/shard_map/pallas_call | solution.py:427
  48.6 11.3 %all_to_all.11.sol_in = f32[32,8,128]{2,1,0:T(8,128)S(1)} all-to-all(f32[32,8,128]{2,1,0:T(8,128)S(1)} %shard_map.122), channel_id=1, replica_groups=mesh['gx'=32,'gy'=4] {'gx'}, dimensions={0} | all-to-all | bytes 262144 | tf_op jit(solution)/shard_map/all_to_all | solution.py:539
  59.9 1.4 %shard_map.123 = (f32[192,1024]{1,0:T(8,128)S(1)}, f32[192,1024]{1,0:T(8,128)S(1)}, f32[48,512]{1,0:T(8,128)S(1)}, f32[48,512]{1,0:T(8,128)S(1)}, f32[48,256]{1,0:T(8,128)S(1)}, /*index=5*/f32[48,256]{1,0:T(8,128)S(1)}) custom-call(f32[32,8,128]{2,1,0:T(8,128)S(1)} %all_to_all.11.sol_in, f32[192,1024]{1,0:T(8,128)S(1)} %get-tuple-element.159.x_ref, ...), custom_call_target="tpu_custom_call" | custom-call | tf_op jit(solution)/shard_map/pallas_call | solution.py:427
  61.5 1.9 %collective-permute-start.13 = (f32[48,512]{1,0:T(8,128)S(1)}, f32[48,512]{1,0:T(8,128)S(1)}, u32[]{:S(2)}, u32[]{:S(2)}) collective-permute-start(f32[48,512]{1,0:T(8,128)S(1)} %get-tuple-element.166), channel_id=1, source_target_pairs={{0,124},{4,8},{8,4},{12,16},{16,12},{20,24},{24,20},{28,32},{32,28... | collective-permute-start | bytes 294920 | tf_op jit(solution)/shard_map/ppermute | solution.py:444
  64.5 2.0 %collective-permute-start.15 = (f32[48,256]{1,0:T(8,128)S(1)}, f32[48,256]{1,0:T(8,128)S(1)}, u32[]{:S(2)}, u32[]{:S(2)}) collective-permute-start(f32[48,256]{1,0:T(8,128)S(1)} %get-tuple-element.168), channel_id=1, source_target_pairs={{0,3},{1,2},{2,1},{3,0},{4,7},{5,6},{6,5},{7,4},{8,11},{9,10},{10,... | collective-permute-start | bytes 147464 | tf_op jit(solution)/shard_map/ppermute | solution.py:444
  66.5 1.9 %shard_map.124 = (f32[192,1024]{1,0:T(8,128)S(1)}, f32[48,512]{1,0:T(8,128)S(1)}, f32[48,512]{1,0:T(8,128)S(1)}, f32[48,256]{1,0:T(8,128)S(1)}, f32[48,256]{1,0:T(8,128)S(1)}) custom-call(f32[192,1024]{1,0:T(8,128)S(1)} %get-tuple-element.157.r_ref, f32[192,1024]{1,0:T(8,128)S(1)} %get-tuple-element.162.d_ref, f32[8,128]{1,0:T(8,128)S(1)} %get-tuple-element.111.coef_ref, ...), custom_call_target="tpu_custom_call" | custom-call | tf_op jit(solution)/shard_map/pallas_call | solution.py:427
  68.4 1.4 %collective-permute-done.15.rest_3_ = f32[48,256]{1,0:T(8,128)S(1)} collective-permute-done((f32[48,256]{1,0:T(8,128)S(1)}, f32[48,256]{1,0:T(8,128)S(1)}, u32[]{:S(2)}, u32[]{:S(2)}) %collective-permute-start.15) | collective-permute-done | bytes 49184 | tf_op jit(solution)/shard_map/ppermute | solution.py:444
  70.4 1.8 %collective-permute-start.17 = (f32[48,512]{1,0:T(8,128)S(1)}, f32[48,512]{1,0:T(8,128)S(1)}, u32[]{:S(2)}, u32[]{:S(2)}) collective-permute-start(f32[48,512]{1,0:T(8,128)S(1)} %get-tuple-element.182), channel_id=1, source_target_pairs={{0,124},{4,8},{8,4},{12,16},{16,12},{20,24},{24,20},{28,32},{32,28... | collective-permute-start | bytes 294920 | tf_op jit(solution)/shard_map/ppermute | solution.py:444
  72.5 2.0 %collective-permute-start.19 = (f32[48,256]{1,0:T(8,128)S(1)}, f32[48,256]{1,0:T(8,128)S(1)}, u32[]{:S(2)}, u32[]{:S(2)}) collective-permute-start(f32[48,256]{1,0:T(8,128)S(1)} %get-tuple-element.184), channel_id=1, source_target_pairs={{0,3},{1,2},{2,1},{3,0},{4,7},{5,6},{6,5},{7,4},{8,11},{9,10},{10,... | collective-permute-start | bytes 147464 | tf_op jit(solution)/shard_map/ppermute | solution.py:444
  74.5 2.3 %shard_map.126 = (f32[192,1024]{1,0:T(8,128)S(1)}, f32[192,1024]{1,0:T(8,128)S(1)}, f32[192,1024]{1,0:T(8,128)S(1)}, f32[192,1024]{1,0:T(8,128)S(1)}, f32[48,512...) custom-call(f32[192,1024]{1,0:T(8,128)S(1)} %get-tuple-element.163.part_ref, ...), custom_call_target="tpu_custom_call" | custom-call | tf_op jit(solution)/shard_map/pallas_call | solution.py:427
  78.4 1.9 %collective-permute-start.21 = (f32[48,512]{1,0:T(8,128)S(1)}, f32[48,512]{1,0:T(8,128)S(1)}, u32[]{:S(2)}, u32[]{:S(2)}) collective-permute-start(f32[48,512]{1,0:T(8,128)S(1)} %get-tuple-element.198), channel_id=1, source_target_pairs={{0,124},{4,8},{8,4},{12,16},{16,12},{20,24},{24,20},{28,32},{32,28... | collective-permute-start | bytes 294920 | tf_op jit(solution)/shard_map/ppermute | solution.py:444
  81.3 1.5 %collective-permute-start.23 = (f32[48,256]{1,0:T(8,128)S(1)}, f32[48,256]{1,0:T(8,128)S(1)}, u32[]{:S(2)}, u32[]{:S(2)}) collective-permute-start(f32[48,256]{1,0:T(8,128)S(1)} %get-tuple-element.200), channel_id=1, source_target_pairs={{0,3},{1,2},{2,1},{3,0},{4,7},{5,6},{6,5},{7,4},{8,11},{9,10},{10,... | collective-permute-start | bytes 147464 | tf_op jit(solution)/shard_map/ppermute | solution.py:444
  82.8 2.4 %shard_map.128 = (f32[192,1024]{1,0:T(8,128)S(1)}, f32[192,1024]{1,0:T(8,128)S(1)}, f32[192,1024]{1,0:T(8,128)S(1)}, f32[192,1024]{1,0:T(8,128)S(1)}, f32[48,512...) custom-call(f32[192,1024]{1,0:T(8,128)S(1)} %get-tuple-element.177.part_ref, ...), custom_call_target="tpu_custom_call" | custom-call | tf_op jit(solution)/shard_map/pallas_call | solution.py:427
  85.2 1.5 %collective-permute-done.23.rest_3_ = f32[48,256]{1,0:T(8,128)S(1)} collective-permute-done((f32[48,256]{1,0:T(8,128)S(1)}, f32[48,256]{1,0:T(8,128)S(1)}, u32[]{:S(2)}, u32[]{:S(2)}) %collective-permute-start.23) | collective-permute-done | bytes 49184 | tf_op jit(solution)/shard_map/ppermute | solution.py:444
  89.4 1.4 %collective-permute-start.27 = (f32[48,256]{1,0:T(8,128)S(1)}, f32[48,256]{1,0:T(8,128)S(1)}, u32[]{:S(2)}, u32[]{:S(2)}) collective-permute-start(f32[48,256]{1,0:T(8,128)S(1)} %get-tuple-element.215), channel_id=1, source_target_pairs={{0,3},{1,2},{2,1},{3,0},{4,7},{5,6},{6,5},{7,4},{8,11},{9,10},{10,... | collective-permute-start | bytes 147464 | tf_op jit(solution)/shard_map/ppermute | solution.py:444
  90.8 2.3 %shard_map.130 = (f32[192,1024]{1,0:T(8,128)S(1)}, f32[192,1024]{1,0:T(8,128)}, f32[1536,128]{1,0:T(8,128)}, f32[192,1024]{1,0:T(8,128)S(1)}) custom-call(f32[192,1024]{1,0:T(8,128)S(1)} %get-tuple-element.193.part_ref, f32[192,1024]{1,0:T(8,128)S(1)} %get-tuple-element.194.r_ref, f32[192,1024]{1,0:T(8,128)S(1)} %get-tuple-element.195.d_ref, ...), custom_call_target="tpu_custom_call" | custom-call | tf_op jit(solution)/shard_map/pallas_call | solution.py:427
  93.1 1.6 %collective-permute-done.27.gy_out = f32[48,256]{1,0:T(8,128)S(1)} collective-permute-done((f32[48,256]{1,0:T(8,128)S(1)}, f32[48,256]{1,0:T(8,128)S(1)}, u32[]{:S(2)}, u32[]{:S(2)}) %collective-permute-start.27) | collective-permute-done | bytes 49184 | tf_op jit(solution)/shard_map/ppermute | solution.py:444
  94.7 1.4 %shard_map.131 = f32[1536,128]{1,0:T(8,128)} custom-call(f32[192,1024]{1,0:T(8,128)S(1)} %get-tuple-element.210.part_ref, f32[192,1024]{1,0:T(8,128)S(1)} %get-tuple-element.211.r_ref, s32[48,128]{1,0:T(8,128)S(1)} %get-tuple-element.112.ori_ref, bf16[4,192,288]{2,1,0:T(8,128)(2,1)S(1)} %get-tuple-element.117.halo_ref, ...), custom_call_target="tpu_custom_call" | custom-call | tf_op jit(solution)/shard_map/pallas_call | solution.py:427
  (52 shorter events, 12.1 us)
Async XLA Ops:
  2.2 14.3 %collective-permute-start = (f32[48,512]{1,0:T(8,128)S(1)}, f32[48,512]{1,0:T(8,128)S(1)}, u32[]{:S(2)}, u32[]{:S(2)}) collective-permute-start(f32[48,512]{1,0:T(8,128)S(1)} %get-tuple-element.119), channel_id=1, source_target_pairs={{0,4},{4,0},{8,12},{12,8},{16,20},{20,16},{24,28},{28,24},{32,36},... | collective-permute-start | bytes 294920 | tf_op jit(solution)/shard_map/ppermute | solution.py:439
  2.3 14.2 %collective-permute-start.1 = (f32[48,512]{1,0:T(8,128)S(1)}, f32[48,512]{1,0:T(8,128)S(1)}, u32[]{:S(2)}, u32[]{:S(2)}) collective-permute-start(f32[48,512]{1,0:T(8,128)S(1)} %get-tuple-element.120), channel_id=1, source_target_pairs={{0,124},{4,8},{8,4},{12,16},{16,12},{20,24},{24,20},{28,32},{32,28... | collective-permute-start | bytes 294920 | tf_op jit(solution)/shard_map/ppermute | solution.py:444
  8.7 7.8 %collective-permute-start.2 = (f32[48,256]{1,0:T(8,128)S(1)}, f32[48,256]{1,0:T(8,128)S(1)}, u32[]{:S(2)}, u32[]{:S(2)}) collective-permute-start(f32[48,256]{1,0:T(8,128)S(1)} %get-tuple-element.121), channel_id=1, source_target_pairs={{0,1},{1,0},{2,3},{3,2},{4,5},{5,4},{6,7},{7,6},{8,9},{9,8},{10,11... | collective-permute-start | bytes 147464 | tf_op jit(solution)/shard_map/ppermute | solution.py:439
  10.3 6.2 %collective-permute-start.3 = (f32[48,256]{1,0:T(8,128)S(1)}, f32[48,256]{1,0:T(8,128)S(1)}, u32[]{:S(2)}, u32[]{:S(2)}) collective-permute-start(f32[48,256]{1,0:T(8,128)S(1)} %get-tuple-element.122), channel_id=1, source_target_pairs={{0,3},{1,2},{2,1},{3,0},{4,7},{5,6},{6,5},{7,4},{8,11},{9,10},{10,... | collective-permute-start | bytes 147464 | tf_op jit(solution)/shard_map/ppermute | solution.py:444
  14.5 32.5 %slice-start = ((s8[9437184]{0:T(1024)(128)(4,1)}), s8[4194304]{0:T(1024)(128)(4,1)S(1)}, s32[]{:S(2)}) async-start(s8[9437184]{0:T(1024)(128)(4,1)} %bitcast.14), calls=%async_computation.2 | async-start | bytes 8388608
  17.0 7.0 %collective-permute-start.4 = (f32[48,512]{1,0:T(8,128)S(1)}, f32[48,512]{1,0:T(8,128)S(1)}, u32[]{:S(2)}, u32[]{:S(2)}) collective-permute-start(f32[48,512]{1,0:T(8,128)S(1)} %get-tuple-element.135), channel_id=1, source_target_pairs={{0,4},{4,0},{8,12},{12,8},{16,20},{20,16},{24,28},{28,24},{32,36},... | collective-permute-start | bytes 294920 | tf_op jit(solution)/shard_map/ppermute | solution.py:439
  17.1 7.4 %collective-permute-start.5 = (f32[48,512]{1,0:T(8,128)S(1)}, f32[48,512]{1,0:T(8,128)S(1)}, u32[]{:S(2)}, u32[]{:S(2)}) collective-permute-start(f32[48,512]{1,0:T(8,128)S(1)} %get-tuple-element.136), channel_id=1, source_target_pairs={{0,124},{4,8},{8,4},{12,16},{16,12},{20,24},{24,20},{28,32},{32,28... | collective-permute-start | bytes 294920 | tf_op jit(solution)/shard_map/ppermute | solution.py:444
  18.0 4.9 %collective-permute-start.6 = (f32[48,256]{1,0:T(8,128)S(1)}, f32[48,256]{1,0:T(8,128)S(1)}, u32[]{:S(2)}, u32[]{:S(2)}) collective-permute-start(f32[48,256]{1,0:T(8,128)S(1)} %get-tuple-element.137), channel_id=1, source_target_pairs={{0,1},{1,0},{2,3},{3,2},{4,5},{5,4},{6,7},{7,6},{8,9},{9,8},{10,11... | collective-permute-start | bytes 147464 | tf_op jit(solution)/shard_map/ppermute | solution.py:439
  18.7 5.3 %collective-permute-start.7 = (f32[48,256]{1,0:T(8,128)S(1)}, f32[48,256]{1,0:T(8,128)S(1)}, u32[]{:S(2)}, u32[]{:S(2)}) collective-permute-start(f32[48,256]{1,0:T(8,128)S(1)} %get-tuple-element.138), channel_id=1, source_target_pairs={{0,3},{1,2},{2,1},{3,0},{4,7},{5,6},{6,5},{7,4},{8,11},{9,10},{10,... | collective-permute-start | bytes 147464 | tf_op jit(solution)/shard_map/ppermute | solution.py:444
  20.5 26.5 %slice-start.1 = ((s8[9437184]{0:T(1024)(128)(4,1)}), s8[4194304]{0:T(1024)(128)(4,1)S(1)}, s32[]{:S(2)}) async-start(s8[9437184]{0:T(1024)(128)(4,1)} %bitcast.14), calls=%async_computation.3 | async-start | bytes 8388608
  25.0 8.8 %collective-permute-start.8 = (f32[48,512]{1,0:T(8,128)S(1)}, f32[48,512]{1,0:T(8,128)S(1)}, u32[]{:S(2)}, u32[]{:S(2)}) collective-permute-start(f32[48,512]{1,0:T(8,128)S(1)} %get-tuple-element.153), channel_id=1, source_target_pairs={{0,4},{4,0},{8,12},{12,8},{16,20},{20,16},{24,28},{28,24},{32,36},... | collective-permute-start | bytes 294920 | tf_op jit(solution)/shard_map/ppermute | solution.py:439
  25.1 8.7 %collective-permute-start.9 = (f32[48,512]{1,0:T(8,128)S(1)}, f32[48,512]{1,0:T(8,128)S(1)}, u32[]{:S(2)}, u32[]{:S(2)}) collective-permute-start(f32[48,512]{1,0:T(8,128)S(1)} %get-tuple-element.154), channel_id=1, source_target_pairs={{0,124},{4,8},{8,4},{12,16},{16,12},{20,24},{24,20},{28,32},{32,28... | collective-permute-start | bytes 294920 | tf_op jit(solution)/shard_map/ppermute | solution.py:444
  27.4 6.4 %collective-permute-start.10 = (f32[48,256]{1,0:T(8,128)S(1)}, f32[48,256]{1,0:T(8,128)S(1)}, u32[]{:S(2)}, u32[]{:S(2)}) collective-permute-start(f32[48,256]{1,0:T(8,128)S(1)} %get-tuple-element.155), channel_id=1, source_target_pairs={{0,1},{1,0},{2,3},{3,2},{4,5},{5,4},{6,7},{7,6},{8,9},{9,8},{10,11... | collective-permute-start | bytes 147464 | tf_op jit(solution)/shard_map/ppermute | solution.py:439
  27.6 6.2 %collective-permute-start.11 = (f32[48,256]{1,0:T(8,128)S(1)}, f32[48,256]{1,0:T(8,128)S(1)}, u32[]{:S(2)}, u32[]{:S(2)}) collective-permute-start(f32[48,256]{1,0:T(8,128)S(1)} %get-tuple-element.156), channel_id=1, source_target_pairs={{0,3},{1,2},{2,1},{3,0},{4,7},{5,6},{6,5},{7,4},{8,11},{9,10},{10,... | collective-permute-start | bytes 147464 | tf_op jit(solution)/shard_map/ppermute | solution.py:444
  31.0 16.1 %slice-start.2 = ((s8[9437184]{0:T(1024)(128)(4,1)}), s8[1048576]{0:T(1024)(128)(4,1)S(1)}, s32[]{:S(2)}) async-start(s8[9437184]{0:T(1024)(128)(4,1)} %bitcast.14), calls=%async_computation.4 | async-start | bytes 2097152
  61.3 8.5 %collective-permute-start.12 = (f32[48,512]{1,0:T(8,128)S(1)}, f32[48,512]{1,0:T(8,128)S(1)}, u32[]{:S(2)}, u32[]{:S(2)}) collective-permute-start(f32[48,512]{1,0:T(8,128)S(1)} %get-tuple-element.165), channel_id=1, source_target_pairs={{0,4},{4,0},{8,12},{12,8},{16,20},{20,16},{24,28},{28,24},{32,36},... | collective-permute-start | bytes 294920 | tf_op jit(solution)/shard_map/ppermute | solution.py:439
  61.5 8.3 %collective-permute-start.13 = (f32[48,512]{1,0:T(8,128)S(1)}, f32[48,512]{1,0:T(8,128)S(1)}, u32[]{:S(2)}, u32[]{:S(2)}) collective-permute-start(f32[48,512]{1,0:T(8,128)S(1)} %get-tuple-element.166), channel_id=1, source_target_pairs={{0,124},{4,8},{8,4},{12,16},{16,12},{20,24},{24,20},{28,32},{32,28... | collective-permute-start | bytes 294920 | tf_op jit(solution)/shard_map/ppermute | solution.py:444
  63.4 5.1 %collective-permute-start.14 = (f32[48,256]{1,0:T(8,128)S(1)}, f32[48,256]{1,0:T(8,128)S(1)}, u32[]{:S(2)}, u32[]{:S(2)}) collective-permute-start(f32[48,256]{1,0:T(8,128)S(1)} %get-tuple-element.167), channel_id=1, source_target_pairs={{0,1},{1,0},{2,3},{3,2},{4,5},{5,4},{6,7},{7,6},{8,9},{9,8},{10,11... | collective-permute-start | bytes 147464 | tf_op jit(solution)/shard_map/ppermute | solution.py:439
  64.5 5.3 %collective-permute-start.15 = (f32[48,256]{1,0:T(8,128)S(1)}, f32[48,256]{1,0:T(8,128)S(1)}, u32[]{:S(2)}, u32[]{:S(2)}) collective-permute-start(f32[48,256]{1,0:T(8,128)S(1)} %get-tuple-element.168), channel_id=1, source_target_pairs={{0,3},{1,2},{2,1},{3,0},{4,7},{5,6},{6,5},{7,4},{8,11},{9,10},{10,... | collective-permute-start | bytes 147464 | tf_op jit(solution)/shard_map/ppermute | solution.py:444
  70.3 7.5 %collective-permute-start.16 = (f32[48,512]{1,0:T(8,128)S(1)}, f32[48,512]{1,0:T(8,128)S(1)}, u32[]{:S(2)}, u32[]{:S(2)}) collective-permute-start(f32[48,512]{1,0:T(8,128)S(1)} %get-tuple-element.181), channel_id=1, source_target_pairs={{0,4},{4,0},{8,12},{12,8},{16,20},{20,16},{24,28},{28,24},{32,36},... | collective-permute-start | bytes 294920 | tf_op jit(solution)/shard_map/ppermute | solution.py:439
  70.4 7.4 %collective-permute-start.17 = (f32[48,512]{1,0:T(8,128)S(1)}, f32[48,512]{1,0:T(8,128)S(1)}, u32[]{:S(2)}, u32[]{:S(2)}) collective-permute-start(f32[48,512]{1,0:T(8,128)S(1)} %get-tuple-element.182), channel_id=1, source_target_pairs={{0,124},{4,8},{8,4},{12,16},{16,12},{20,24},{24,20},{28,32},{32,28... | collective-permute-start | bytes 294920 | tf_op jit(solution)/shard_map/ppermute | solution.py:444
  72.2 4.6 %collective-permute-start.18 = (f32[48,256]{1,0:T(8,128)S(1)}, f32[48,256]{1,0:T(8,128)S(1)}, u32[]{:S(2)}, u32[]{:S(2)}) collective-permute-start(f32[48,256]{1,0:T(8,128)S(1)} %get-tuple-element.183), channel_id=1, source_target_pairs={{0,1},{1,0},{2,3},{3,2},{4,5},{5,4},{6,7},{7,6},{8,9},{9,8},{10,11... | collective-permute-start | bytes 147464 | tf_op jit(solution)/shard_map/ppermute | solution.py:439
  72.5 5.3 %collective-permute-start.19 = (f32[48,256]{1,0:T(8,128)S(1)}, f32[48,256]{1,0:T(8,128)S(1)}, u32[]{:S(2)}, u32[]{:S(2)}) collective-permute-start(f32[48,256]{1,0:T(8,128)S(1)} %get-tuple-element.184), channel_id=1, source_target_pairs={{0,3},{1,2},{2,1},{3,0},{4,7},{5,6},{6,5},{7,4},{8,11},{9,10},{10,... | collective-permute-start | bytes 147464 | tf_op jit(solution)/shard_map/ppermute | solution.py:444
  78.3 8.4 %collective-permute-start.20 = (f32[48,512]{1,0:T(8,128)S(1)}, f32[48,512]{1,0:T(8,128)S(1)}, u32[]{:S(2)}, u32[]{:S(2)}) collective-permute-start(f32[48,512]{1,0:T(8,128)S(1)} %get-tuple-element.197), channel_id=1, source_target_pairs={{0,4},{4,0},{8,12},{12,8},{16,20},{20,16},{24,28},{28,24},{32,36},... | collective-permute-start | bytes 294920 | tf_op jit(solution)/shard_map/ppermute | solution.py:439
  78.4 8.3 %collective-permute-start.21 = (f32[48,512]{1,0:T(8,128)S(1)}, f32[48,512]{1,0:T(8,128)S(1)}, u32[]{:S(2)}, u32[]{:S(2)}) collective-permute-start(f32[48,512]{1,0:T(8,128)S(1)} %get-tuple-element.198), channel_id=1, source_target_pairs={{0,124},{4,8},{8,4},{12,16},{16,12},{20,24},{24,20},{28,32},{32,28... | collective-permute-start | bytes 294920 | tf_op jit(solution)/shard_map/ppermute | solution.py:444
  80.3 4.9 %collective-permute-start.22 = (f32[48,256]{1,0:T(8,128)S(1)}, f32[48,256]{1,0:T(8,128)S(1)}, u32[]{:S(2)}, u32[]{:S(2)}) collective-permute-start(f32[48,256]{1,0:T(8,128)S(1)} %get-tuple-element.199), channel_id=1, source_target_pairs={{0,1},{1,0},{2,3},{3,2},{4,5},{5,4},{6,7},{7,6},{8,9},{9,8},{10,11... | collective-permute-start | bytes 147464 | tf_op jit(solution)/shard_map/ppermute | solution.py:439
  81.3 5.3 %collective-permute-start.23 = (f32[48,256]{1,0:T(8,128)S(1)}, f32[48,256]{1,0:T(8,128)S(1)}, u32[]{:S(2)}, u32[]{:S(2)}) collective-permute-start(f32[48,256]{1,0:T(8,128)S(1)} %get-tuple-element.200), channel_id=1, source_target_pairs={{0,3},{1,2},{2,1},{3,0},{4,7},{5,6},{6,5},{7,4},{8,11},{9,10},{10,... | collective-permute-start | bytes 147464 | tf_op jit(solution)/shard_map/ppermute | solution.py:444
  87.1 7.6 %collective-permute-start.24 = (f32[48,512]{1,0:T(8,128)S(1)}, f32[48,512]{1,0:T(8,128)S(1)}, u32[]{:S(2)}, u32[]{:S(2)}) collective-permute-start(f32[48,512]{1,0:T(8,128)S(1)} %get-tuple-element.212), channel_id=1, source_target_pairs={{0,4},{4,0},{8,12},{12,8},{16,20},{20,16},{24,28},{28,24},{32,36},... | collective-permute-start | bytes 294920 | tf_op jit(solution)/shard_map/ppermute | solution.py:439
  87.2 7.5 %collective-permute-start.25 = (f32[48,512]{1,0:T(8,128)S(1)}, f32[48,512]{1,0:T(8,128)S(1)}, u32[]{:S(2)}, u32[]{:S(2)}) collective-permute-start(f32[48,512]{1,0:T(8,128)S(1)} %get-tuple-element.213), channel_id=1, source_target_pairs={{0,124},{4,8},{8,4},{12,16},{16,12},{20,24},{24,20},{28,32},{32,28... | collective-permute-start | bytes 294920 | tf_op jit(solution)/shard_map/ppermute | solution.py:444
  88.5 4.5 %collective-permute-start.26 = (f32[48,256]{1,0:T(8,128)S(1)}, f32[48,256]{1,0:T(8,128)S(1)}, u32[]{:S(2)}, u32[]{:S(2)}) collective-permute-start(f32[48,256]{1,0:T(8,128)S(1)} %get-tuple-element.214), channel_id=1, source_target_pairs={{0,1},{1,0},{2,3},{3,2},{4,5},{5,4},{6,7},{7,6},{8,9},{9,8},{10,11... | collective-permute-start | bytes 147464 | tf_op jit(solution)/shard_map/ppermute | solution.py:439
  89.4 5.3 %collective-permute-start.27 = (f32[48,256]{1,0:T(8,128)S(1)}, f32[48,256]{1,0:T(8,128)S(1)}, u32[]{:S(2)}, u32[]{:S(2)}) collective-permute-start(f32[48,256]{1,0:T(8,128)S(1)} %get-tuple-element.215), channel_id=1, source_target_pairs={{0,3},{1,2},{2,1},{3,0},{4,7},{5,6},{6,5},{7,4},{8,11},{9,10},{10,... | collective-permute-start | bytes 147464 | tf_op jit(solution)/shard_map/ppermute | solution.py:444

commit v5 on v4

--- a/solution.py
+++ b/solution.py
@@ -145,38 +145,82 @@
         copy.wait()
 
 
+def stacked(v):
+    high = v.astype(BF16).astype(F32)
+    return jnp.concatenate([high, v - high], axis=0).astype(BF16)
+
+
+def stacked3(v):
+    high = v.astype(BF16).astype(F32)
+    return jnp.concatenate([high, v - high, high], axis=0).astype(BF16)
+
+
+def beside(v):
+    high, low = split(v)
+    return jnp.concatenate([high, high, low], axis=1)
+
+
+def slot_table(agg_ref, owner_ref, te_ref):
+    owner = owner_ref[...]
+    owner_hot = lax.broadcasted_iota(jnp.int32, (OWNERS, AGG), 0) == owner
+    before = lax.broadcasted_iota(jnp.int32, (AGG, AGG), 0) < lax.broadcasted_iota(
+        jnp.int32, (AGG, AGG), 1
+    )
+    counts = dot(owner_hot.astype(BF16), before.astype(BF16))
+    slot = jnp.sum(jnp.where(owner_hot, counts, 0.0), axis=0, keepdims=True)
+    first = lax.broadcasted_iota(jnp.int32, (8, AGG), 0) == 0
+    table = jnp.where(first, owner.astype(F32), slot).astype(BF16)
+    for col in range(COLS):
+        member = lax.broadcasted_iota(jnp.int32, (AGG, LANES), 0) == agg_ref[col : col + 1, :]
+        found = dot(table, member.astype(BF16))
+        te_ref[col : col + 1, :] = (found[0:1] * float(CAP) + found[1:2]).astype(jnp.int32)
+
+
+def one_hots(te_ref, hot_ref, tall_ref):
+    for col in range(COLS):
+        te = te_ref[col : col + 1, :]
+        hot = lax.broadcasted_iota(jnp.int32, (OWNERS * CAP, LANES), 0) == te
+        hot_ref[:, lanes(col)] = hot.astype(BF16)
+        te_down = jnp.broadcast_to(te, (LANES, LANES)).astype(F32).T.astype(jnp.int32)
+        lane = lax.broadcasted_iota(jnp.int32, (LANES, LANES), 1)
+        for tile in range(8):
+            tall_ref[lanes(col), lanes(tile)] = (te_down == lane + LANES * tile).astype(BF16)
+
+
 def weights_kernel(
-    stiff_hbm, faces_hbm, pt_hbm, sel_ref,
-    wh_ref, wl_ref, halo_ref, rim_ref, pth_ref, ptl_ref, ph_ref, pl_ref,
-    stiff_ref, faces_ref, pt_ref, sems,
-):
-    copies = fetch(((stiff_hbm, stiff_ref), (pt_hbm, pt_ref), (faces_hbm, faces_ref)), sems)
+    stiff_hbm, faces_hbm, pt_hbm, sel_ref, agg_ref, owner_ref,
+    wh_ref, wl_ref, halo_ref, rim_ref, pf_ref, pt_ref, lift_ref, edge_ref, te_ref,
+    stiff_ref, faces_ref, basis_ref, sems,
+):
+    copies = fetch(((stiff_hbm, stiff_ref), (pt_hbm, basis_ref), (faces_hbm, faces_ref)), sems)
+    slot_table(agg_ref, owner_ref, te_ref)
     copies[0].wait()
     high, low = split(stiff_ref[...])
     wh_ref[:, 0:BLOCK] = high
     wl_ref[:, 0:BLOCK] = low
     copies[1].wait()
-    pt = pt_ref[...]
-    high, low = split(pt)
-    pth_ref[...] = high
-    ptl_ref[...] = low
-    high, low = split(pt.T)
-    ph_ref[...] = high
-    pl_ref[...] = low
+    pt = basis_ref[...]
+    pt_ref[...] = stacked(pt)
+    lift = beside(pt.T)
+    lift_ref[...] = lift
+    edge_ref[0:48, :] = face_rows(lift, 0)
+    edge_ref[48:96, :] = face_rows(lift, 3)
+    edge_ref[96:192, :] = dot(sel_ref[0:96, :], lift).astype(BF16)
     copies[2].wait()
     for piece in range(3):
         high, low = split(faces_ref[192 * piece : 192 * (piece + 1), :].T)
         wh_ref[:, 192 * (piece + 1) : 192 * (piece + 2)] = high
         wl_ref[:, 192 * (piece + 1) : 192 * (piece + 2)] = low
+    pt_high, pt_low = split(pt)
     for direction in range(4):
         at = BLOCK + 96 * direction
         high, low = wh_ref[:, at : at + 96], wl_ref[:, at : at + 96]
         stack = jnp.concatenate([high, high, low], axis=1)
         halo_ref[direction] = stack
+        pf_ref[direction] = beside(dot3(pt_high, pt_low, high, low))
         if direction < 2:
-            near, far = face_rows(stack, 3 * direction), sel_ref[0:96, :]
-            rim_ref[direction, 0:48, :] = near
-            rim_ref[direction, 48:144, :] = dot(far, stack).astype(BF16)
+            rim_ref[direction, 0:48, :] = face_rows(stack, 3 * direction)
+            rim_ref[direction, 48:144, :] = dot(sel_ref[0:96, :], stack).astype(BF16)
         else:
             rim_ref[direction, 0:48, :] = face_rows(stack, 0)
             rim_ref[direction, 48:96, :] = face_rows(stack, 3)
@@ -245,6 +289,20 @@
     ahead(scales, r_ref, d_ref, part_ref, coef_ref, sel_ref, pres)
 
 
+def lifted_kernel(
+    scales, part_ref, r_ref, x_ref, each_ref, coef_ref, ori_ref, wh_ref, wl_ref, sel_ref,
+    halo_ref, lift_ref, lx_ref, ux_ref, ly_ref, uy_ref, r_out, x_out, part_out, *rest,
+):
+    *pres, xh_ref, xl_ref, t_ref, d_ref = rest
+    add_halo(d_ref, part_ref, halo_ref, [v[...] for v in (lx_ref, ux_ref, ly_ref, uy_ref)])
+    r_out[...] = r_ref[...] - d_ref[...]
+    lift = dot(lift_ref[...], stacked3(each_ref[...]))
+    d_ref[...] = lift
+    x_out[...] = x_ref[...] + lift
+    interior(d_ref, coef_ref, ori_ref, wh_ref, wl_ref, sel_ref, part_out, xh_ref, xl_ref, t_ref)
+    ahead(scales, r_out, d_ref, part_out, coef_ref, sel_ref, pres)
+
+
 def halo_stacks(ori_ref, gets):
     gx_in, gx_out, gy_in, gy_out = gets
     even_x, even_y, found = sides()
@@ -305,10 +363,14 @@
 
 
 def step_kernel(
-    scales, onward, closing, part_ref, r_ref, d_ref, x_ref, coef_ref, ori_ref, wh_ref, wl_ref, sel_ref,
-    halo_ref, lx_ref, ux_ref, ly_ref, uy_ref, r_out, d_out, x_out, part_out, *rest,
-):
-    *pres, xh_ref, xl_ref, t_ref, ad_ref = rest
+    scales, onward, then, part_ref, r_ref, d_ref, x_ref, coef_ref, ori_ref, wh_ref, wl_ref, sel_ref,
+    halo_ref, lx_ref, ux_ref, ly_ref, uy_ref, *rest,
+):
+    if then == "hots":
+        te_ref, *rest = rest
+    elif then == "restrict":
+        pt_ref, tall_ref, *rest = rest
+    r_out, d_out, x_out, part_out, *outs, xh_ref, xl_ref, t_ref, ad_ref = rest
     add_halo(ad_ref, part_ref, halo_ref, [v[...] for v in (lx_ref, ux_ref, ly_ref, uy_ref)])
     keep, gain = scales
     for col in range(COLS):
@@ -320,52 +382,60 @@
         r_out[:, at] = resid
         d_out[:, at] = step
         total = x_ref[:, at] + step
-        if closing:
+        if then == "close":
             x_out[pl.ds(col, BLOCK, stride=COLS), :] = total
         else:
             x_out[:, at] = total
     interior(d_out, coef_ref, ori_ref, wh_ref, wl_ref, sel_ref, part_out, xh_ref, xl_ref, t_ref)
     if onward is not None:
-        ahead(onward, r_out, d_out, part_out, coef_ref, sel_ref, pres)
-
-
-def last_kernel(part_ref, r_ref, ori_ref, halo_ref, gx_in, gx_out, gy_in, gy_out, r_out, ad_ref):
+        ahead(onward, r_out, d_out, part_out, coef_ref, sel_ref, outs[0:4])
+    if then == "hots":
+        one_hots(te_ref, *outs[4:6])
+    elif then == "restrict":
+        high, low = split(r_out[...] - part_out[...])
+        both = dot(pt_ref[...], high)
+        proj = both[0:CW] + both[CW:] + dot(pt_ref[0:CW, :], low)
+        outs[0][...] = routed(proj, tall_ref)
+
+
+def routed(v, one_hot_ref):
+    both = dot(stacked(v), one_hot_ref[...])
+    return both[0:CW] + both[CW:]
+
+
+def last_kernel(
+    part_ref, r_ref, ori_ref, halo_ref, gx_in, gx_out, gy_in, gy_out, r_hbm, ad_ref, out_ref, sems
+):
     add_halo(ad_ref, part_ref, halo_ref, halo_stacks(ori_ref, (gx_in, gx_out, gy_in, gy_out)))
+    copies = []
+    for piece in range(3):
+        rows = slice(64 * piece, 64 * (piece + 1))
+        for col in range(COLS):
+            at = lanes(col)
+            out_ref[pl.ds(512 * piece + col, 64, stride=COLS), :] = r_ref[rows, at] - ad_ref[rows, at]
+        span = pl.ds(512 * piece, 512)
+        copies.append(pltpu.make_async_copy(out_ref.at[span], r_hbm.at[span], sems.at[piece]))
+        copies[-1].start()
+    for copy in copies:
+        copy.wait()
+
+
+def restrict_kernel(
+    pre_ref, ori_ref, pf_ref, tall_ref, gx_in, gx_out, gy_in, gy_out,
+    out_ref, lx_ref, ux_ref, ly_ref, uy_ref, rhs_ref,
+):
+    values = halo_stacks(ori_ref, (gx_in, gx_out, gy_in, gy_out))
+    for stack, value in zip((lx_ref, ux_ref, ly_ref, uy_ref), values):
+        stack[...] = value
+    parts = [dot(pf_ref[n], value) for n, value in enumerate(values)]
+    cols = []
     for col in range(COLS):
-        at = lanes(col)
-        r_out[pl.ds(col, BLOCK, stride=COLS), :] = r_ref[:, at] - ad_ref[:, at]
-
-
-def slots_kernel(agg_ref, owner_ref, hot_ref):
-    owner = owner_ref[...]
-    owner_hot = lax.broadcasted_iota(jnp.int32, (OWNERS, AGG), 0) == owner
-    before = lax.broadcasted_iota(jnp.int32, (AGG, AGG), 0) < lax.broadcasted_iota(
-        jnp.int32, (AGG, AGG), 1
-    )
-    counts = dot(owner_hot.astype(BF16), before.astype(BF16))
-    slot = jnp.sum(jnp.where(owner_hot, counts, 0.0), axis=0, keepdims=True)
-    first = lax.broadcasted_iota(jnp.int32, (8, AGG), 0) == 0
-    table = jnp.where(first, owner.astype(F32), slot).astype(BF16)
-    for col in range(COLS):
-        at = lanes(col)
-        member = lax.broadcasted_iota(jnp.int32, (AGG, LANES), 0) == agg_ref[col : col + 1, :]
-        found = dot(table, member.astype(BF16))
-        target = (found[0:1] * float(CAP) + found[1:2]).astype(jnp.int32)
-        hot = lax.broadcasted_iota(jnp.int32, (OWNERS * CAP, LANES), 0) == target
-        hot_ref[:, at] = hot.astype(BF16)
-
-
-def restrict_kernel(
-    part_ref, r_ref, ori_ref, halo_ref, hot_ref, pth_ref, ptl_ref,
-    gx_in, gx_out, gy_in, gy_out, r_out, out_ref, ad_ref, rhs_ref,
-):
-    add_halo(ad_ref, part_ref, halo_ref, halo_stacks(ori_ref, (gx_in, gx_out, gy_in, gy_out)))
-    resid = r_ref[...] - ad_ref[...]
-    r_out[...] = resid
-    r_high, r_low = split(resid)
-    proj = dot3(pth_ref[...], ptl_ref[...], r_high, r_low)
-    p_high, p_low = split(proj)
-    rhs_ref[...] = dot_nt(p_high, hot_ref[...]) + dot_nt(p_low, hot_ref[...])
+        x, y = col // 4, col % 4
+        part = parts[x][:, lanes(y)]
+        if y in (0, 3):
+            part = part + parts[2 + y // 3][:, lanes(x)]
+        cols.append(part)
+    rhs_ref[...] = pre_ref[...] - routed(jnp.concatenate(cols, axis=1), tall_ref)
     group = lax.broadcasted_iota(jnp.int32, (8, LANES), 1) >> 5
     for o in range(OWNERS):
         total = jnp.zeros((8, LANES), F32)
@@ -387,8 +457,7 @@
 
 
 def lift_kernel(
-    sol_in, x_ref, coef_ref, hot_ref, ph_ref, pl_ref, sel_ref,
-    d_out, x_out, sx_in, sx_out, sy_in, sy_out, sol_ref,
+    sol_in, coef_ref, hot_ref, edge_ref, each_ref, sx_in, sx_out, sy_in, sy_out, sol_ref
 ):
     group = lax.broadcasted_iota(jnp.int32, (8, LANES), 1) >> 5
     for q in range(3):
@@ -400,25 +469,23 @@
                     moved = pltpu.roll(moved, 32 * ((g - q) % 4), 1)
                 total = jnp.where(group == g, moved, total)
             sol_ref[8 * q : 8 * q + 8, lanes(j)] = total
-    s_high, s_low = split(sol_ref[...])
-    each = dot(s_high, hot_ref[...]) + dot(s_low, hot_ref[...])
-    e_high, e_low = split(each)
-    for half in range(2):
-        span = slice(512 * half, 512 * (half + 1))
-        lift = dot3(ph_ref[...], pl_ref[...], e_high[:, span], e_low[:, span])
-        d_out[:, span] = lift
-        x_out[:, span] = x_ref[:, span] + lift
-    post(
-        *edge_traces(lambda col: d_out[:, lanes(col)] * tile_coef(coef_ref, col), sel_ref),
-        (sx_in, sx_out, sy_in, sy_out),
-    )
+    each = routed(sol_ref[...], hot_ref)
+    each_ref[...] = each
+    stack = stacked3(each)
+    sides_of = []
+    for n, cols in enumerate(((0, 1, 2, 3), (4, 5, 6, 7), (0, 4), (3, 7))):
+        values = jnp.concatenate([stack[:, lanes(col)] for col in cols], axis=1)
+        traces = dot(edge_ref[48 * n : 48 * n + 48, :], values)
+        scale = jnp.concatenate([tile_coef(coef_ref, col) for col in cols], axis=1)
+        sides_of.append(traces * scale)
+    post(*sides_of, (sx_in, sx_out, sy_in, sy_out))
 
 
 def field(*shape, dtype=F32):
     return pltpu.VMEM(shape, dtype)
 
 
-def call(kernel, outs, args, scratch=(), hbm=(), limit=20):
+def call(kernel, outs, args, scratch=(), hbm=(), limit=20, out_space=pltpu.VMEM):
     specs, placed = [], []
     for n, a in enumerate(args):
         space = pltpu.HBM if n in hbm else pltpu.VMEM
@@ -428,7 +495,7 @@
         kernel,
         out_shape=outs,
         in_specs=specs,
-        out_specs=[pl.BlockSpec(memory_space=pltpu.VMEM)] * len(outs),
+        out_specs=[pl.BlockSpec(memory_space=out_space)] * len(outs),
         scratch_shapes=list(scratch),
         compiler_params=pltpu.CompilerParams(vmem_limit_bytes=limit << 20),
     )(*placed)
@@ -485,74 +552,75 @@
         scratch=[field(*rows), dma((6,))],
         hbm=(0, 1, 2, 3, 4, 5),
     )
-    wide, down, up = halves(BLOCK, 768), halves(CW, BLOCK), halves(BLOCK, CW)
-    wh, wl, halo, rim, pth, ptl, ph, plo = call(
+    wide, hots = halves(BLOCK, 768), halves(ELEMS, ELEMS)
+    wh, wl, halo, rim, pf, pt, lift, edge, te = call(
         weights_kernel,
-        [wide, wide, halves(4, BLOCK, 288), halves(4, 144, 288), down, down, up, up],
+        [wide, wide, halves(4, BLOCK, 288), halves(4, 144, 288), halves(4, CW, 288),
+         halves(2 * CW, BLOCK), halves(BLOCK, 3 * CW), halves(BLOCK, 3 * CW), ints(COLS, LANES)],
         [stiffness, jnp.transpose(face_blocks, (0, 1, 3, 2)).reshape(576, BLOCK), prolong_basis.T,
-         sel],
+         sel, agg, owner],
         scratch=[field(BLOCK, BLOCK), field(576, BLOCK), field(CW, BLOCK), dma((3,))],
         hbm=(0, 1, 2),
     )
-    hot = call(slots_kernel, [halves(ELEMS, ELEMS)], [agg, owner])[0]
 
     products = [halves(768, ELEMS), halves(768, ELEMS), full]
     stacks = [halves(288, 512), halves(288, 512), halves(288, 256), halves(288, 256)]
     tables = [coef, ori, wh, wl, sel]
 
-    def start(scales, r, d):
-        return call(functools.partial(start_kernel, scales), [full, *SENDS], [r, d, *tables], products)
-
-    def step(scales, onward, part, r, d, x, gets, pres, closing=False):
+    def step(scales, onward, part, r, d, x, gets, pres, then=None, extra=(), extra_outs=()):
         *sends, lx, ux, ly, uy = call(
             functools.partial(send_kernel, scales[1]),
             [*SENDS, *stacks],
             [coef, ori, rim, *gets, *pres],
         )
         gets = exchange(sends)
-        x_out = jax.ShapeDtypeStruct(rows, F32) if closing else full
-        outs = [full, full, x_out, full] + ([] if onward is None else SENDS)
-        r, d, x, part, *pres = call(
-            functools.partial(step_kernel, scales, onward, closing),
-            outs,
-            [part, r, d, x, *tables, halo, lx, ux, ly, uy],
+        x_out = jax.ShapeDtypeStruct(rows, F32) if then == "close" else full
+        r, d, x, part, *outs = call(
+            functools.partial(step_kernel, scales, onward, then),
+            [full, full, x_out, full, *([] if onward is None else SENDS), *extra_outs],
+            [part, r, d, x, *tables, halo, lx, ux, ly, uy, *extra],
             [*products, full],
         )
-        return part, r, d, x, gets, pres
+        return part, r, d, x, gets, outs
 
     second, third = chebyshev()
     opening = (0.0, 1.0 / THETA)
     gets = exchange(sends)
-    part, *pres = start(second, r, d)
-    part, r, d, x, gets, pres = step(second, third, part, r, d, d, gets, pres)
-    part, r, d, x, gets, _ = step(third, None, part, r, d, x, gets, pres)
+    part, *pres = call(
+        functools.partial(start_kernel, second), [full, *SENDS], [r, d, *tables], products
+    )
+    part, r, d, x, gets, (*pres, hot, tall) = step(
+        second, third, part, r, d, d, gets, pres, "hots", [te], [hots, hots]
+    )
+    coarse = field(CW, ELEMS)
+    part, r, d, x, gets, (pre,) = step(
+        third, None, part, r, d, x, gets, pres, "restrict", [pt, tall], [coarse]
+    )
     packets = field(OWNERS, 8, LANES)
-    r, rhs = call(
-        restrict_kernel,
-        [full, packets],
-        [part, r, ori, halo, hot, pth, ptl, *gets],
-        [full, field(CW, ELEMS)],
+    rhs, *near = call(
+        restrict_kernel, [packets, *stacks], [pre, ori, pf, tall, *gets], [coarse]
     )
     rhs = lax.all_to_all(rhs, "gx", split_axis=0, concat_axis=0, tiled=True)
     inverse = jnp.transpose(coarse_inverse[0], (0, 2, 3, 1))
     sol = call(solve_kernel, [packets], [rhs, inverse])[0]
     sol = lax.all_to_all(sol, "gx", split_axis=0, concat_axis=0, tiled=True)
-    d, x, *sends = call(
-        lift_kernel,
-        [full, full, *SENDS],
-        [sol, x, coef, hot, ph, plo, sel],
-        [field(CW, ELEMS)],
-    )
+    each, *sends = call(lift_kernel, [coarse, *SENDS], [sol, coef, hot, edge], [coarse])
     gets = exchange(sends)
-    part, *pres = start(opening, r, d)
-    part, r, d, x, gets, pres = step(opening, second, part, r, d, x, gets, pres)
+    r, x, part, *pres = call(
+        functools.partial(lifted_kernel, opening),
+        [full, full, full, *SENDS],
+        [part, r, x, each, *tables, halo, lift, *near],
+        [*products, full],
+    )
+    part, r, d, x, gets, pres = step(opening, second, part, r, r, x, gets, pres)
     part, r, d, x, gets, pres = step(second, third, part, r, d, x, gets, pres)
-    part, r, _, x, gets, _ = step(third, None, part, r, d, x, gets, pres, closing=True)
+    part, r, _, x, gets, _ = step(third, None, part, r, d, x, gets, pres, "close")
     r = call(
         last_kernel,
         [jax.ShapeDtypeStruct(rows, F32)],
         [part, r, ori, halo, *gets],
-        [full],
+        [full, field(*rows), dma((3,))],
+        out_space=pltpu.HBM,
     )[0]
     return x.reshape(shape), r.reshape(shape)
 

time: 96.4 us -> 94.5 us (0.980)
  waiting for transfers between devices: 7.16 us -> 5.73 us
    ppermute x14, waiting for transfers between devices: 7.12 us -> 5.69 us  [swap_odd(): lax.ppermute(v, axis, [(i, (i + 1 if i % 2 else i - 1) % count) for i in...]
    pallas_call x19 -> x18, Pallas kernels: 30 us -> 29.4 us  [call(): pl.pallas_call(kernel, out_shape=outs, in_specs=specs, out_specs=[pl.Bloc...]
  transfers between devices with their start and end apart: 28 -> 28, of which waited for: 6 -> 5; matrix products, arithmetic and copies ran while one was open for 0% -> 0% of each run, Pallas kernels for 20% -> 22%
where the time goes in v5:
time: 94.5 us; the launch traced here: 94.3 us
  starting transfers between devices  35.9 us (38%)
  Pallas kernels  29.4 us (31%)
  blocking collectives  22 us (23%)
  waiting for transfers between devices  5.73 us (6%)
  between operations  1.12 us (1%)
    ppermute x14, starting transfers between devices, swap_odd(): lax.ppermute(v, axis, [(i, (i + 1 if i % 2 else i - 1) % count) for i in...  29.5 us
    pallas_call x18, Pallas kernels, call(): pl.pallas_call(kernel, out_shape=outs, in_specs=specs, out_specs=[pl.Bloc...  29.4 us
    all_to_all x1, blocking collectives, shards(): sol = lax.all_to_all(sol, 'gx', split_axis=0, concat_axis=0, tiled=True)  11.3 us
    all_to_all x1, blocking collectives, shards(): rhs = lax.all_to_all(rhs, 'gx', split_axis=0, concat_axis=0, tiled=True)  10.8 us
    ppermute x14, starting transfers between devices, swap_even(): return lax.ppermute(v, axis, [(i, i ^ 1) for i in range(count)])  6.44 us
    ppermute x14, waiting for transfers between devices, swap_odd(): lax.ppermute(v, axis, [(i, (i + 1 if i % 2 else i - 1) % count) for i in...  5.69 us
  transfers between devices with their start and end apart: 28, of which 5 were waited for; matrix products, arithmetic and copies ran while one was open for 0% of the time, Pallas kernels for 22%

profile of v5, /device:TPU:0, one launch (start us, length us, event | category | flops | bytes accessed | tf_op | source)
XLA Modules:
  0.0 94.3 jit_solution(7527783616061491522)
XLA Ops:
  0.6 1.6 %shard_map.113 = (f32[192,1024]{1,0:T(8,128)S(1)}, f32[192,1024]{1,0:T(8,128)S(1)}, f32[8,128]{1,0:T(8,128)S(1)}, s32[48,128]{1,0:T(8,128)S(1)}, bf16[192,192]{1...) custom-call(f32[1536,128]{1,0:T(8,128)} %bitcast.17, ...), custom_call_target="tpu_custom_call" | custom-call | tf_op jit(solution)/shard_map/pallas_call | solution.py:494
  2.3 6.4 %collective-permute-start.1 = (f32[48,512]{1,0:T(8,128)S(1)}, f32[48,512]{1,0:T(8,128)S(1)}, u32[]{:S(2)}, u32[]{:S(2)}) collective-permute-start(f32[48,512]{1,0:T(8,128)S(1)} %get-tuple-element.130), channel_id=1, source_target_pairs={{0,124},{4,8},{8,4},{12,16},{16,12},{20,24},{24,20},{28,32},{32,28... | collective-permute-start | bytes 294920 | tf_op jit(solution)/shard_map/ppermute | solution.py:511
  8.7 1.6 %collective-permute-start.2 = (f32[48,256]{1,0:T(8,128)S(1)}, f32[48,256]{1,0:T(8,128)S(1)}, u32[]{:S(2)}, u32[]{:S(2)}) collective-permute-start(f32[48,256]{1,0:T(8,128)S(1)} %get-tuple-element.131), channel_id=1, source_target_pairs={{0,1},{1,0},{2,3},{3,2},{4,5},{5,4},{6,7},{7,6},{8,9},{9,8},{10,11... | collective-permute-start | bytes 147464 | tf_op jit(solution)/shard_map/ppermute | solution.py:506
  10.3 2.2 %collective-permute-start.3 = (f32[48,256]{1,0:T(8,128)S(1)}, f32[48,256]{1,0:T(8,128)S(1)}, u32[]{:S(2)}, u32[]{:S(2)}) collective-permute-start(f32[48,256]{1,0:T(8,128)S(1)} %get-tuple-element.132), channel_id=1, source_target_pairs={{0,3},{1,2},{2,1},{3,0},{4,7},{5,6},{6,5},{7,4},{8,11},{9,10},{10,... | collective-permute-start | bytes 147464 | tf_op jit(solution)/shard_map/ppermute | solution.py:511
  12.5 2.3 %shard_map.114 = (bf16[192,768]{1,0:T(8,128)(2,1)S(1)}, bf16[192,768]{1,0:T(8,128)(2,1)S(1)}, bf16[4,192,288]{2,1,0:T(8,128)(2,1)S(1)}, bf16[4,144,288]{2,1,0:T(...) custom-call(f32[192,192]{1,0:T(8,128)} %stiff_hbm.1, ...), custom_call_target="tpu_custom_call" | custom-call | tf_op jit(solution)/shard_map/pallas_call | solution.py:494
  14.8 2.0 %shard_map.115 = (f32[192,1024]{1,0:T(8,128)S(1)}, f32[48,512]{1,0:T(8,128)S(1)}, f32[48,512]{1,0:T(8,128)S(1)}, f32[48,256]{1,0:T(8,128)S(1)}, f32[48,256]{1,0:T(8,128)S(1)}) custom-call(f32[192,1024]{1,0:T(8,128)S(1)} %get-tuple-element.117.r_ref, f32[192,1024]{1,0:T(8,128)S(1)} %get-tuple-element.118.d_ref.x_ref, ...), custom_call_target="tpu_custom_call" | custom-call | tf_op jit(solution)/shard_map/pallas_call | solution.py:494
  19.0 1.5 %collective-permute-start.7 = (f32[48,256]{1,0:T(8,128)S(1)}, f32[48,256]{1,0:T(8,128)S(1)}, u32[]{:S(2)}, u32[]{:S(2)}) collective-permute-start(f32[48,256]{1,0:T(8,128)S(1)} %get-tuple-element.149), channel_id=1, source_target_pairs={{0,3},{1,2},{2,1},{3,0},{4,7},{5,6},{6,5},{7,4},{8,11},{9,10},{10,... | collective-permute-start | bytes 147464 | tf_op jit(solution)/shard_map/ppermute | solution.py:511
  20.5 4.0 %shard_map.117 = (f32[192,1024]{1,0:T(8,128)S(1)}, f32[192,1024]{1,0:T(8,128)S(1)}, f32[192,1024]{1,0:T(8,128)S(1)}, f32[192,1024]{1,0:T(8,128)S(1)}, f32[48,512...) custom-call(f32[192,1024]{1,0:T(8,128)S(1)} %get-tuple-element.126.p, ...), custom_call_target="tpu_custom_call" | custom-call | tf_op jit(solution)/shard_map/pallas_call | solution.py:494
  25.4 2.6 %collective-permute-start.9 = (f32[48,512]{1,0:T(8,128)S(1)}, f32[48,512]{1,0:T(8,128)S(1)}, u32[]{:S(2)}, u32[]{:S(2)}) collective-permute-start(f32[48,512]{1,0:T(8,128)S(1)} %get-tuple-element.166), channel_id=1, source_target_pairs={{0,124},{4,8},{8,4},{12,16},{16,12},{20,24},{24,20},{28,32},{32,28... | collective-permute-start | bytes 294920 | tf_op jit(solution)/shard_map/ppermute | solution.py:511
  28.0 1.1 %collective-permute-start.10 = (f32[48,256]{1,0:T(8,128)S(1)}, f32[48,256]{1,0:T(8,128)S(1)}, u32[]{:S(2)}, u32[]{:S(2)}) collective-permute-start(f32[48,256]{1,0:T(8,128)S(1)} %get-tuple-element.167), channel_id=1, source_target_pairs={{0,1},{1,0},{2,3},{3,2},{4,5},{5,4},{6,7},{7,6},{8,9},{9,8},{10,11... | collective-permute-start | bytes 147464 | tf_op jit(solution)/shard_map/ppermute | solution.py:506
  29.1 2.2 %collective-permute-start.11 = (f32[48,256]{1,0:T(8,128)S(1)}, f32[48,256]{1,0:T(8,128)S(1)}, u32[]{:S(2)}, u32[]{:S(2)}) collective-permute-start(f32[48,256]{1,0:T(8,128)S(1)} %get-tuple-element.168), channel_id=1, source_target_pairs={{0,3},{1,2},{2,1},{3,0},{4,7},{5,6},{6,5},{7,4},{8,11},{9,10},{10,... | collective-permute-start | bytes 147464 | tf_op jit(solution)/shard_map/ppermute | solution.py:511
  31.3 3.5 %shard_map.119 = (f32[192,1024]{1,0:T(8,128)S(1)}, f32[192,1024]{1,0:T(8,128)}, f32[192,1024]{1,0:T(8,128)S(1)}, f32[192,1024]{1,0:T(8,128)S(1)}, f32[24,1024]{1,0:T(8,128)S(1)}) custom-call(f32[192,1024]{1,0:T(8,128)S(1)} %get-tuple-element.142.part_ref, f32[192,1024]{1,0:T(8,128)S(1)} %get-tuple-element.143.r_ref, ...), custom_call_target="tpu_custom_call" | custom-call | tf_op jit(solution)/shard_map/pallas_call | solution.py:494
  35.7 10.8 %all_to_all.10.rhs_ref = f32[32,8,128]{2,1,0:T(8,128)S(1)} all-to-all(f32[32,8,128]{2,1,0:T(8,128)S(1)} %get-tuple-element.169), channel_id=1, replica_groups=mesh['gx'=32,'gy'=4] {'gx'}, dimensions={0} | all-to-all | bytes 262144 | tf_op jit(solution)/shard_map/all_to_all | solution.py:603
  46.5 1.6 %shard_map.121 = f32[32,8,128]{2,1,0:T(8,128)S(1)} custom-call(f32[32,8,128]{2,1,0:T(8,128)S(1)} %all_to_all.10.rhs_ref, f32[32,24,24,32]{3,2,1,0:T(8,128)S(1)} %bitcast.16), custom_call_target="tpu_custom_call" | custom-call | tf_op jit(solution)/shard_map/pallas_call | solution.py:494
  48.1 11.3 %all_to_all.11.sol_in = f32[32,8,128]{2,1,0:T(8,128)S(1)} all-to-all(f32[32,8,128]{2,1,0:T(8,128)S(1)} %shard_map.121), channel_id=1, replica_groups=mesh['gx'=32,'gy'=4] {'gx'}, dimensions={0} | all-to-all | bytes 262144 | tf_op jit(solution)/shard_map/all_to_all | solution.py:606
  60.2 1.9 %collective-permute-start.13 = (f32[48,512]{1,0:T(8,128)S(1)}, f32[48,512]{1,0:T(8,128)S(1)}, u32[]{:S(2)}, u32[]{:S(2)}) collective-permute-start(f32[48,512]{1,0:T(8,128)S(1)} %get-tuple-element.182), channel_id=1, source_target_pairs={{0,124},{4,8},{8,4},{12,16},{16,12},{20,24},{24,20},{28,32},{32,28... | collective-permute-start | bytes 294920 | tf_op jit(solution)/shard_map/ppermute | solution.py:511
  62.8 1.6 %collective-permute-start.15 = (f32[48,256]{1,0:T(8,128)S(1)}, f32[48,256]{1,0:T(8,128)S(1)}, u32[]{:S(2)}, u32[]{:S(2)}) collective-permute-start(f32[48,256]{1,0:T(8,128)S(1)} %get-tuple-element.184), channel_id=1, source_target_pairs={{0,3},{1,2},{2,1},{3,0},{4,7},{5,6},{6,5},{7,4},{8,11},{9,10},{10,... | collective-permute-start | bytes 147464 | tf_op jit(solution)/shard_map/ppermute | solution.py:511
  64.4 2.3 %shard_map.123 = (f32[192,1024]{1,0:T(8,128)S(1)}, f32[192,1024]{1,0:T(8,128)S(1)}, f32[192,1024]{1,0:T(8,128)S(1)}, f32[48,512]{1,0:T(8,128)S(1)}, f32[48,512]{...) custom-call(f32[192,1024]{1,0:T(8,128)S(1)} %get-tuple-element.160.part_ref, ...), custom_call_target="tpu_custom_call" | custom-call | tf_op jit(solution)/shard_map/pallas_call | solution.py:494
  66.8 1.3 %collective-permute-done.15.rest_3_ = f32[48,256]{1,0:T(8,128)S(1)} collective-permute-done((f32[48,256]{1,0:T(8,128)S(1)}, f32[48,256]{1,0:T(8,128)S(1)}, u32[]{:S(2)}, u32[]{:S(2)}) %collective-permute-start.15) | collective-permute-done | bytes 49184 | tf_op jit(solution)/shard_map/ppermute | solution.py:511
  68.7 1.8 %collective-permute-start.17 = (f32[48,512]{1,0:T(8,128)S(1)}, f32[48,512]{1,0:T(8,128)S(1)}, u32[]{:S(2)}, u32[]{:S(2)}) collective-permute-start(f32[48,512]{1,0:T(8,128)S(1)} %get-tuple-element.198), channel_id=1, source_target_pairs={{0,124},{4,8},{8,4},{12,16},{16,12},{20,24},{24,20},{28,32},{32,28... | collective-permute-start | bytes 294920 | tf_op jit(solution)/shard_map/ppermute | solution.py:511
  71.0 1.5 %collective-permute-start.19 = (f32[48,256]{1,0:T(8,128)S(1)}, f32[48,256]{1,0:T(8,128)S(1)}, u32[]{:S(2)}, u32[]{:S(2)}) collective-permute-start(f32[48,256]{1,0:T(8,128)S(1)} %get-tuple-element.200), channel_id=1, source_target_pairs={{0,3},{1,2},{2,1},{3,0},{4,7},{5,6},{6,5},{7,4},{8,11},{9,10},{10,... | collective-permute-start | bytes 147464 | tf_op jit(solution)/shard_map/ppermute | solution.py:511
  72.4 2.3 %shard_map.125 = (f32[192,1024]{1,0:T(8,128)S(1)}, f32[192,1024]{1,0:T(8,128)S(1)}, f32[192,1024]{1,0:T(8,128)S(1)}, f32[192,1024]{1,0:T(8,128)S(1)}, f32[48,512...) custom-call(f32[192,1024]{1,0:T(8,128)S(1)} %get-tuple-element.178.part_ref, ...), custom_call_target="tpu_custom_call" | custom-call | tf_op jit(solution)/shard_map/pallas_call | solution.py:494
  74.8 1.5 %collective-permute-done.19.rest_3_ = f32[48,256]{1,0:T(8,128)S(1)} collective-permute-done((f32[48,256]{1,0:T(8,128)S(1)}, f32[48,256]{1,0:T(8,128)S(1)}, u32[]{:S(2)}, u32[]{:S(2)}) %collective-permute-start.19) | collective-permute-done | bytes 49184 | tf_op jit(solution)/shard_map/ppermute | solution.py:511
  76.8 1.8 %collective-permute-start.21 = (f32[48,512]{1,0:T(8,128)S(1)}, f32[48,512]{1,0:T(8,128)S(1)}, u32[]{:S(2)}, u32[]{:S(2)}) collective-permute-start(f32[48,512]{1,0:T(8,128)S(1)} %get-tuple-element.214), channel_id=1, source_target_pairs={{0,124},{4,8},{8,4},{12,16},{16,12},{20,24},{24,20},{28,32},{32,28... | collective-permute-start | bytes 294920 | tf_op jit(solution)/shard_map/ppermute | solution.py:511
  79.3 1.6 %collective-permute-start.23 = (f32[48,256]{1,0:T(8,128)S(1)}, f32[48,256]{1,0:T(8,128)S(1)}, u32[]{:S(2)}, u32[]{:S(2)}) collective-permute-start(f32[48,256]{1,0:T(8,128)S(1)} %get-tuple-element.216), channel_id=1, source_target_pairs={{0,3},{1,2},{2,1},{3,0},{4,7},{5,6},{6,5},{7,4},{8,11},{9,10},{10,... | collective-permute-start | bytes 147464 | tf_op jit(solution)/shard_map/ppermute | solution.py:511
  80.9 2.4 %shard_map.127 = (f32[192,1024]{1,0:T(8,128)S(1)}, f32[192,1024]{1,0:T(8,128)S(1)}, f32[192,1024]{1,0:T(8,128)S(1)}, f32[192,1024]{1,0:T(8,128)S(1)}, f32[48,512...) custom-call(f32[192,1024]{1,0:T(8,128)S(1)} %get-tuple-element.193.part_ref, ...), custom_call_target="tpu_custom_call" | custom-call | tf_op jit(solution)/shard_map/pallas_call | solution.py:494
  83.3 1.3 %collective-permute-done.23.rest_3_ = f32[48,256]{1,0:T(8,128)S(1)} collective-permute-done((f32[48,256]{1,0:T(8,128)S(1)}, f32[48,256]{1,0:T(8,128)S(1)}, u32[]{:S(2)}, u32[]{:S(2)}) %collective-permute-start.23) | collective-permute-done | bytes 49184 | tf_op jit(solution)/shard_map/ppermute | solution.py:511
  85.1 1.7 %collective-permute-start.25 = (f32[48,512]{1,0:T(8,128)S(1)}, f32[48,512]{1,0:T(8,128)S(1)}, u32[]{:S(2)}, u32[]{:S(2)}) collective-permute-start(f32[48,512]{1,0:T(8,128)S(1)} %get-tuple-element.229), channel_id=1, source_target_pairs={{0,124},{4,8},{8,4},{12,16},{16,12},{20,24},{24,20},{28,32},{32,28... | collective-permute-start | bytes 294920 | tf_op jit(solution)/shard_map/ppermute | solution.py:511
  87.4 1.7 %collective-permute-start.27 = (f32[48,256]{1,0:T(8,128)S(1)}, f32[48,256]{1,0:T(8,128)S(1)}, u32[]{:S(2)}, u32[]{:S(2)}) collective-permute-start(f32[48,256]{1,0:T(8,128)S(1)} %get-tuple-element.231), channel_id=1, source_target_pairs={{0,3},{1,2},{2,1},{3,0},{4,7},{5,6},{6,5},{7,4},{8,11},{9,10},{10,... | collective-permute-start | bytes 147464 | tf_op jit(solution)/shard_map/ppermute | solution.py:511
  89.1 2.3 %shard_map.129 = (f32[192,1024]{1,0:T(8,128)S(1)}, f32[192,1024]{1,0:T(8,128)}, f32[1536,128]{1,0:T(8,128)}, f32[192,1024]{1,0:T(8,128)S(1)}) custom-call(f32[192,1024]{1,0:T(8,128)S(1)} %get-tuple-element.209.part_ref, f32[192,1024]{1,0:T(8,128)S(1)} %get-tuple-element.210.r_ref, f32[192,1024]{1,0:T(8,128)S(1)} %get-tuple-element.211.d_ref, ...), custom_call_target="tpu_custom_call" | custom-call | tf_op jit(solution)/shard_map/pallas_call | solution.py:494
  91.4 1.3 %collective-permute-done.27.gy_out = f32[48,256]{1,0:T(8,128)S(1)} collective-permute-done((f32[48,256]{1,0:T(8,128)S(1)}, f32[48,256]{1,0:T(8,128)S(1)}, u32[]{:S(2)}, u32[]{:S(2)}) %collective-permute-start.27) | collective-permute-done | bytes 49184 | tf_op jit(solution)/shard_map/ppermute | solution.py:511
  92.7 1.4 %shard_map.130 = f32[1536,128]{1,0:T(8,128)} custom-call(f32[192,1024]{1,0:T(8,128)S(1)} %get-tuple-element.226.part_ref, f32[192,1024]{1,0:T(8,128)S(1)} %get-tuple-element.227.r_ref, s32[48,128]{1,0:T(8,128)S(1)} %get-tuple-element.120.ori_ref, bf16[4,192,288]{2,1,0:T(8,128)(2,1)S(1)} %get-tuple-element.127.halo_ref, ...), custom_call_target="tpu_custom_call" | custom-call | tf_op jit(solution)/shard_map/pallas_call | solution.py:494
  (51 shorter events, 8.8 us)
Async XLA Ops:
  2.2 14.6 %collective-permute-start = (f32[48,512]{1,0:T(8,128)S(1)}, f32[48,512]{1,0:T(8,128)S(1)}, u32[]{:S(2)}, u32[]{:S(2)}) collective-permute-start(f32[48,512]{1,0:T(8,128)S(1)} %get-tuple-element.129), channel_id=1, source_target_pairs={{0,4},{4,0},{8,12},{12,8},{16,20},{20,16},{24,28},{28,24},{32,36},... | collective-permute-start | bytes 294920 | tf_op jit(solution)/shard_map/ppermute | solution.py:506
  2.3 14.5 %collective-permute-start.1 = (f32[48,512]{1,0:T(8,128)S(1)}, f32[48,512]{1,0:T(8,128)S(1)}, u32[]{:S(2)}, u32[]{:S(2)}) collective-permute-start(f32[48,512]{1,0:T(8,128)S(1)} %get-tuple-element.130), channel_id=1, source_target_pairs={{0,124},{4,8},{8,4},{12,16},{16,12},{20,24},{24,20},{28,32},{32,28... | collective-permute-start | bytes 294920 | tf_op jit(solution)/shard_map/ppermute | solution.py:511
  8.7 8.0 %collective-permute-start.2 = (f32[48,256]{1,0:T(8,128)S(1)}, f32[48,256]{1,0:T(8,128)S(1)}, u32[]{:S(2)}, u32[]{:S(2)}) collective-permute-start(f32[48,256]{1,0:T(8,128)S(1)} %get-tuple-element.131), channel_id=1, source_target_pairs={{0,1},{1,0},{2,3},{3,2},{4,5},{5,4},{6,7},{7,6},{8,9},{9,8},{10,11... | collective-permute-start | bytes 147464 | tf_op jit(solution)/shard_map/ppermute | solution.py:506
  10.3 6.5 %collective-permute-start.3 = (f32[48,256]{1,0:T(8,128)S(1)}, f32[48,256]{1,0:T(8,128)S(1)}, u32[]{:S(2)}, u32[]{:S(2)}) collective-permute-start(f32[48,256]{1,0:T(8,128)S(1)} %get-tuple-element.132), channel_id=1, source_target_pairs={{0,3},{1,2},{2,1},{3,0},{4,7},{5,6},{6,5},{7,4},{8,11},{9,10},{10,... | collective-permute-start | bytes 147464 | tf_op jit(solution)/shard_map/ppermute | solution.py:511
  16.8 29.7 %slice-start = ((s8[9437184]{0:T(1024)(128)(4,1)}), s8[4194304]{0:T(1024)(128)(4,1)S(1)}, s32[]{:S(2)}) async-start(s8[9437184]{0:T(1024)(128)(4,1)} %bitcast.14), calls=%async_computation.2 | async-start | bytes 8388608
  17.3 7.2 %collective-permute-start.4 = (f32[48,512]{1,0:T(8,128)S(1)}, f32[48,512]{1,0:T(8,128)S(1)}, u32[]{:S(2)}, u32[]{:S(2)}) collective-permute-start(f32[48,512]{1,0:T(8,128)S(1)} %get-tuple-element.146), channel_id=1, source_target_pairs={{0,4},{4,0},{8,12},{12,8},{16,20},{20,16},{24,28},{28,24},{32,36},... | collective-permute-start | bytes 294920 | tf_op jit(solution)/shard_map/ppermute | solution.py:506
  17.4 7.4 %collective-permute-start.5 = (f32[48,512]{1,0:T(8,128)S(1)}, f32[48,512]{1,0:T(8,128)S(1)}, u32[]{:S(2)}, u32[]{:S(2)}) collective-permute-start(f32[48,512]{1,0:T(8,128)S(1)} %get-tuple-element.147), channel_id=1, source_target_pairs={{0,124},{4,8},{8,4},{12,16},{16,12},{20,24},{24,20},{28,32},{32,28... | collective-permute-start | bytes 294920 | tf_op jit(solution)/shard_map/ppermute | solution.py:511
  18.3 6.2 %collective-permute-start.6 = (f32[48,256]{1,0:T(8,128)S(1)}, f32[48,256]{1,0:T(8,128)S(1)}, u32[]{:S(2)}, u32[]{:S(2)}) collective-permute-start(f32[48,256]{1,0:T(8,128)S(1)} %get-tuple-element.148), channel_id=1, source_target_pairs={{0,1},{1,0},{2,3},{3,2},{4,5},{5,4},{6,7},{7,6},{8,9},{9,8},{10,11... | collective-permute-start | bytes 147464 | tf_op jit(solution)/shard_map/ppermute | solution.py:506
  19.0 5.5 %collective-permute-start.7 = (f32[48,256]{1,0:T(8,128)S(1)}, f32[48,256]{1,0:T(8,128)S(1)}, u32[]{:S(2)}, u32[]{:S(2)}) collective-permute-start(f32[48,256]{1,0:T(8,128)S(1)} %get-tuple-element.149), channel_id=1, source_target_pairs={{0,3},{1,2},{2,1},{3,0},{4,7},{5,6},{6,5},{7,4},{8,11},{9,10},{10,... | collective-permute-start | bytes 147464 | tf_op jit(solution)/shard_map/ppermute | solution.py:511
  20.5 26.0 %slice-start.1 = ((s8[9437184]{0:T(1024)(128)(4,1)}), s8[4194304]{0:T(1024)(128)(4,1)S(1)}, s32[]{:S(2)}) async-start(s8[9437184]{0:T(1024)(128)(4,1)} %bitcast.14), calls=%async_computation.3 | async-start | bytes 8388608
  25.3 9.6 %collective-permute-start.8 = (f32[48,512]{1,0:T(8,128)S(1)}, f32[48,512]{1,0:T(8,128)S(1)}, u32[]{:S(2)}, u32[]{:S(2)}) collective-permute-start(f32[48,512]{1,0:T(8,128)S(1)} %get-tuple-element.165), channel_id=1, source_target_pairs={{0,4},{4,0},{8,12},{12,8},{16,20},{20,16},{24,28},{28,24},{32,36},... | collective-permute-start | bytes 294920 | tf_op jit(solution)/shard_map/ppermute | solution.py:506
  25.4 9.5 %collective-permute-start.9 = (f32[48,512]{1,0:T(8,128)S(1)}, f32[48,512]{1,0:T(8,128)S(1)}, u32[]{:S(2)}, u32[]{:S(2)}) collective-permute-start(f32[48,512]{1,0:T(8,128)S(1)} %get-tuple-element.166), channel_id=1, source_target_pairs={{0,124},{4,8},{8,4},{12,16},{16,12},{20,24},{24,20},{28,32},{32,28... | collective-permute-start | bytes 294920 | tf_op jit(solution)/shard_map/ppermute | solution.py:511
  28.0 6.8 %collective-permute-start.10 = (f32[48,256]{1,0:T(8,128)S(1)}, f32[48,256]{1,0:T(8,128)S(1)}, u32[]{:S(2)}, u32[]{:S(2)}) collective-permute-start(f32[48,256]{1,0:T(8,128)S(1)} %get-tuple-element.167), channel_id=1, source_target_pairs={{0,1},{1,0},{2,3},{3,2},{4,5},{5,4},{6,7},{7,6},{8,9},{9,8},{10,11... | collective-permute-start | bytes 147464 | tf_op jit(solution)/shard_map/ppermute | solution.py:506
  29.1 5.7 %collective-permute-start.11 = (f32[48,256]{1,0:T(8,128)S(1)}, f32[48,256]{1,0:T(8,128)S(1)}, u32[]{:S(2)}, u32[]{:S(2)}) collective-permute-start(f32[48,256]{1,0:T(8,128)S(1)} %get-tuple-element.168), channel_id=1, source_target_pairs={{0,3},{1,2},{2,1},{3,0},{4,7},{5,6},{6,5},{7,4},{8,11},{9,10},{10,... | collective-permute-start | bytes 147464 | tf_op jit(solution)/shard_map/ppermute | solution.py:511
  31.3 15.2 %slice-start.2 = ((s8[9437184]{0:T(1024)(128)(4,1)}), s8[1048576]{0:T(1024)(128)(4,1)S(1)}, s32[]{:S(2)}) async-start(s8[9437184]{0:T(1024)(128)(4,1)} %bitcast.14), calls=%async_computation.4 | async-start | bytes 2097152
  60.1 8.1 %collective-permute-start.12 = (f32[48,512]{1,0:T(8,128)S(1)}, f32[48,512]{1,0:T(8,128)S(1)}, u32[]{:S(2)}, u32[]{:S(2)}) collective-permute-start(f32[48,512]{1,0:T(8,128)S(1)} %get-tuple-element.181), channel_id=1, source_target_pairs={{0,4},{4,0},{8,12},{12,8},{16,20},{20,16},{24,28},{28,24},{32,36},... | collective-permute-start | bytes 294920 | tf_op jit(solution)/shard_map/ppermute | solution.py:506
  60.2 7.9 %collective-permute-start.13 = (f32[48,512]{1,0:T(8,128)S(1)}, f32[48,512]{1,0:T(8,128)S(1)}, u32[]{:S(2)}, u32[]{:S(2)}) collective-permute-start(f32[48,512]{1,0:T(8,128)S(1)} %get-tuple-element.182), channel_id=1, source_target_pairs={{0,124},{4,8},{8,4},{12,16},{16,12},{20,24},{24,20},{28,32},{32,28... | collective-permute-start | bytes 294920 | tf_op jit(solution)/shard_map/ppermute | solution.py:511
  62.1 4.7 %collective-permute-start.14 = (f32[48,256]{1,0:T(8,128)S(1)}, f32[48,256]{1,0:T(8,128)S(1)}, u32[]{:S(2)}, u32[]{:S(2)}) collective-permute-start(f32[48,256]{1,0:T(8,128)S(1)} %get-tuple-element.183), channel_id=1, source_target_pairs={{0,1},{1,0},{2,3},{3,2},{4,5},{5,4},{6,7},{7,6},{8,9},{9,8},{10,11... | collective-permute-start | bytes 147464 | tf_op jit(solution)/shard_map/ppermute | solution.py:506
  62.8 5.3 %collective-permute-start.15 = (f32[48,256]{1,0:T(8,128)S(1)}, f32[48,256]{1,0:T(8,128)S(1)}, u32[]{:S(2)}, u32[]{:S(2)}) collective-permute-start(f32[48,256]{1,0:T(8,128)S(1)} %get-tuple-element.184), channel_id=1, source_target_pairs={{0,3},{1,2},{2,1},{3,0},{4,7},{5,6},{6,5},{7,4},{8,11},{9,10},{10,... | collective-permute-start | bytes 147464 | tf_op jit(solution)/shard_map/ppermute | solution.py:511
  68.6 7.7 %collective-permute-start.16 = (f32[48,512]{1,0:T(8,128)S(1)}, f32[48,512]{1,0:T(8,128)S(1)}, u32[]{:S(2)}, u32[]{:S(2)}) collective-permute-start(f32[48,512]{1,0:T(8,128)S(1)} %get-tuple-element.197), channel_id=1, source_target_pairs={{0,4},{4,0},{8,12},{12,8},{16,20},{20,16},{24,28},{28,24},{32,36},... | collective-permute-start | bytes 294920 | tf_op jit(solution)/shard_map/ppermute | solution.py:506
  68.7 7.6 %collective-permute-start.17 = (f32[48,512]{1,0:T(8,128)S(1)}, f32[48,512]{1,0:T(8,128)S(1)}, u32[]{:S(2)}, u32[]{:S(2)}) collective-permute-start(f32[48,512]{1,0:T(8,128)S(1)} %get-tuple-element.198), channel_id=1, source_target_pairs={{0,124},{4,8},{8,4},{12,16},{16,12},{20,24},{24,20},{28,32},{32,28... | collective-permute-start | bytes 294920 | tf_op jit(solution)/shard_map/ppermute | solution.py:511
  70.5 4.3 %collective-permute-start.18 = (f32[48,256]{1,0:T(8,128)S(1)}, f32[48,256]{1,0:T(8,128)S(1)}, u32[]{:S(2)}, u32[]{:S(2)}) collective-permute-start(f32[48,256]{1,0:T(8,128)S(1)} %get-tuple-element.199), channel_id=1, source_target_pairs={{0,1},{1,0},{2,3},{3,2},{4,5},{5,4},{6,7},{7,6},{8,9},{9,8},{10,11... | collective-permute-start | bytes 147464 | tf_op jit(solution)/shard_map/ppermute | solution.py:506
  71.0 5.3 %collective-permute-start.19 = (f32[48,256]{1,0:T(8,128)S(1)}, f32[48,256]{1,0:T(8,128)S(1)}, u32[]{:S(2)}, u32[]{:S(2)}) collective-permute-start(f32[48,256]{1,0:T(8,128)S(1)} %get-tuple-element.200), channel_id=1, source_target_pairs={{0,3},{1,2},{2,1},{3,0},{4,7},{5,6},{6,5},{7,4},{8,11},{9,10},{10,... | collective-permute-start | bytes 147464 | tf_op jit(solution)/shard_map/ppermute | solution.py:511
  76.7 7.9 %collective-permute-start.20 = (f32[48,512]{1,0:T(8,128)S(1)}, f32[48,512]{1,0:T(8,128)S(1)}, u32[]{:S(2)}, u32[]{:S(2)}) collective-permute-start(f32[48,512]{1,0:T(8,128)S(1)} %get-tuple-element.213), channel_id=1, source_target_pairs={{0,4},{4,0},{8,12},{12,8},{16,20},{20,16},{24,28},{28,24},{32,36},... | collective-permute-start | bytes 294920 | tf_op jit(solution)/shard_map/ppermute | solution.py:506
  76.8 7.8 %collective-permute-start.21 = (f32[48,512]{1,0:T(8,128)S(1)}, f32[48,512]{1,0:T(8,128)S(1)}, u32[]{:S(2)}, u32[]{:S(2)}) collective-permute-start(f32[48,512]{1,0:T(8,128)S(1)} %get-tuple-element.214), channel_id=1, source_target_pairs={{0,124},{4,8},{8,4},{12,16},{16,12},{20,24},{24,20},{28,32},{32,28... | collective-permute-start | bytes 294920 | tf_op jit(solution)/shard_map/ppermute | solution.py:511
  78.6 4.7 %collective-permute-start.22 = (f32[48,256]{1,0:T(8,128)S(1)}, f32[48,256]{1,0:T(8,128)S(1)}, u32[]{:S(2)}, u32[]{:S(2)}) collective-permute-start(f32[48,256]{1,0:T(8,128)S(1)} %get-tuple-element.215), channel_id=1, source_target_pairs={{0,1},{1,0},{2,3},{3,2},{4,5},{5,4},{6,7},{7,6},{8,9},{9,8},{10,11... | collective-permute-start | bytes 147464 | tf_op jit(solution)/shard_map/ppermute | solution.py:506
  79.3 5.3 %collective-permute-start.23 = (f32[48,256]{1,0:T(8,128)S(1)}, f32[48,256]{1,0:T(8,128)S(1)}, u32[]{:S(2)}, u32[]{:S(2)}) collective-permute-start(f32[48,256]{1,0:T(8,128)S(1)} %get-tuple-element.216), channel_id=1, source_target_pairs={{0,3},{1,2},{2,1},{3,0},{4,7},{5,6},{6,5},{7,4},{8,11},{9,10},{10,... | collective-permute-start | bytes 147464 | tf_op jit(solution)/shard_map/ppermute | solution.py:511
  85.0 7.6 %collective-permute-start.24 = (f32[48,512]{1,0:T(8,128)S(1)}, f32[48,512]{1,0:T(8,128)S(1)}, u32[]{:S(2)}, u32[]{:S(2)}) collective-permute-start(f32[48,512]{1,0:T(8,128)S(1)} %get-tuple-element.228), channel_id=1, source_target_pairs={{0,4},{4,0},{8,12},{12,8},{16,20},{20,16},{24,28},{28,24},{32,36},... | collective-permute-start | bytes 294920 | tf_op jit(solution)/shard_map/ppermute | solution.py:506
  85.1 7.5 %collective-permute-start.25 = (f32[48,512]{1,0:T(8,128)S(1)}, f32[48,512]{1,0:T(8,128)S(1)}, u32[]{:S(2)}, u32[]{:S(2)}) collective-permute-start(f32[48,512]{1,0:T(8,128)S(1)} %get-tuple-element.229), channel_id=1, source_target_pairs={{0,124},{4,8},{8,4},{12,16},{16,12},{20,24},{24,20},{28,32},{32,28... | collective-permute-start | bytes 294920 | tf_op jit(solution)/shard_map/ppermute | solution.py:511
  86.8 4.6 %collective-permute-start.26 = (f32[48,256]{1,0:T(8,128)S(1)}, f32[48,256]{1,0:T(8,128)S(1)}, u32[]{:S(2)}, u32[]{:S(2)}) collective-permute-start(f32[48,256]{1,0:T(8,128)S(1)} %get-tuple-element.230), channel_id=1, source_target_pairs={{0,1},{1,0},{2,3},{3,2},{4,5},{5,4},{6,7},{7,6},{8,9},{9,8},{10,11... | collective-permute-start | bytes 147464 | tf_op jit(solution)/shard_map/ppermute | solution.py:506
  87.4 5.3 %collective-permute-start.27 = (f32[48,256]{1,0:T(8,128)S(1)}, f32[48,256]{1,0:T(8,128)S(1)}, u32[]{:S(2)}, u32[]{:S(2)}) collective-permute-start(f32[48,256]{1,0:T(8,128)S(1)} %get-tuple-element.231), channel_id=1, source_target_pairs={{0,3},{1,2},{2,1},{3,0},{4,7},{5,6},{6,5},{7,4},{8,11},{9,10},{10,... | collective-permute-start | bytes 147464 | tf_op jit(solution)/shard_map/ppermute | solution.py:511

commit v6 on v5

--- a/solution.py
+++ b/solution.py
@@ -116,32 +116,39 @@
 
 
 def first_kernel(
-    rs_hbm, coef_hbm, ori_hbm, sel_hbm, agg_hbm, owner_hbm,
-    r_ref, d_ref, coef_ref, ori_ref, sel_ref, agg_ref, owner_ref, sx_in, sx_out, sy_in, sy_out,
-    rs_ref, sems,
-):
+    rs_hbm, coef_hbm, ori_hbm, sel_hbm, agg_hbm, owner_hbm, stiff_hbm, faces_hbm, pt_hbm,
+    r_ref, d_ref, coef_ref, ori_ref, sel_ref, agg_ref, owner_ref, stiff_ref, faces_ref, pt_ref,
+    sx_in, sx_out, sy_in, sy_out, rs_ref, sems,
+):
+    pieces = [pl.ds(512 * c, 512) for c in range(3)]
     copies = fetch(
-        (
-            (rs_hbm, rs_ref),
+        [(rs_hbm.at[piece], rs_ref.at[piece]) for piece in pieces]
+        + [
             (coef_hbm, coef_ref),
             (sel_hbm, sel_ref),
-            (ori_hbm, ori_ref),
             (agg_hbm, agg_ref),
             (owner_hbm, owner_ref),
-        ),
+            (ori_hbm, ori_ref),
+            (stiff_hbm, stiff_ref),
+            (pt_hbm, pt_ref),
+            (faces_hbm, faces_ref),
+        ],
         sems,
     )
-    for copy in copies[:3]:
+    for c in range(3):
+        copies[c].wait()
+        rows = slice(64 * c, 64 * (c + 1))
+        for col in range(COLS):
+            v = rs_ref[pl.ds(512 * c + col, 64, stride=COLS), :]
+            r_ref[rows, lanes(col)] = v
+            d_ref[rows, lanes(col)] = v * (1.0 / THETA)
+    for copy in copies[3:5]:
         copy.wait()
-    for col in range(COLS):
-        v = rs_ref[pl.ds(col, BLOCK, stride=COLS), :]
-        r_ref[:, lanes(col)] = v
-        d_ref[:, lanes(col)] = v * (1.0 / THETA)
     post(
         *edge_traces(lambda col: d_ref[:, lanes(col)] * tile_coef(coef_ref, col), sel_ref),
         (sx_in, sx_out, sy_in, sy_out),
     )
-    for copy in copies[3:]:
+    for copy in copies[5:]:
         copy.wait()
 
 
@@ -180,25 +187,19 @@
     for col in range(COLS):
         te = te_ref[col : col + 1, :]
         hot = lax.broadcasted_iota(jnp.int32, (OWNERS * CAP, LANES), 0) == te
-        hot_ref[:, lanes(col)] = hot.astype(BF16)
-        te_down = jnp.broadcast_to(te, (LANES, LANES)).astype(F32).T.astype(jnp.int32)
-        lane = lax.broadcasted_iota(jnp.int32, (LANES, LANES), 1)
-        for tile in range(8):
-            tall_ref[lanes(col), lanes(tile)] = (te_down == lane + LANES * tile).astype(BF16)
+        hot = hot.astype(F32).astype(BF16)
+        hot_ref[:, lanes(col)] = hot
+        tall_ref[lanes(col), :] = hot.T
 
 
 def weights_kernel(
-    stiff_hbm, faces_hbm, pt_hbm, sel_ref, agg_ref, owner_ref,
+    stiff_ref, faces_ref, basis_ref, sel_ref, agg_ref, owner_ref,
     wh_ref, wl_ref, halo_ref, rim_ref, pf_ref, pt_ref, lift_ref, edge_ref, te_ref,
-    stiff_ref, faces_ref, basis_ref, sems,
-):
-    copies = fetch(((stiff_hbm, stiff_ref), (pt_hbm, basis_ref), (faces_hbm, faces_ref)), sems)
+):
     slot_table(agg_ref, owner_ref, te_ref)
-    copies[0].wait()
     high, low = split(stiff_ref[...])
     wh_ref[:, 0:BLOCK] = high
     wl_ref[:, 0:BLOCK] = low
-    copies[1].wait()
     pt = basis_ref[...]
     pt_ref[...] = stacked(pt)
     lift = beside(pt.T)
@@ -206,7 +207,6 @@
     edge_ref[0:48, :] = face_rows(lift, 0)
     edge_ref[48:96, :] = face_rows(lift, 3)
     edge_ref[96:192, :] = dot(sel_ref[0:96, :], lift).astype(BF16)
-    copies[2].wait()
     for piece in range(3):
         high, low = split(faces_ref[192 * piece : 192 * (piece + 1), :].T)
         wh_ref[:, 192 * (piece + 1) : 192 * (piece + 2)] = high
@@ -447,12 +447,33 @@
         out_ref[o] = total
 
 
+def row_sums(tiles):
+    row = lax.broadcasted_iota(jnp.int32, tiles[0].shape, 0)
+    low = row < 4
+    tiles = [
+        jnp.where(low, p, q) + pltpu.roll(jnp.where(low, q, p), 4, 0)
+        for p, q in zip(tiles[:4], tiles[4:])
+    ]
+    for bit in (2, 1):
+        tiles = [
+            jnp.where((row & bit) == 0, p + pltpu.roll(p, 8 - bit, 0), q + pltpu.roll(q, bit, 0))
+            for p, q in zip(tiles[:bit], tiles[bit:])
+        ]
+    return tiles[0]
+
+
 def solve_kernel(rhs_ref, inv_ref, out_ref):
     pad = jnp.zeros((8, CAP), F32)
     for s in range(OWNERS):
         tile = rhs_ref[s]
-        rhs = jnp.concatenate([tile[:, CAP * q : CAP * (q + 1)] for q in range(3)], axis=0)
-        rows = [jnp.sum(inv_ref[s, 8 * q : 8 * q + 8] * rhs[None], axis=1) for q in range(3)]
+        parts = [tile[:, CAP * q : CAP * (q + 1)] for q in range(3)]
+        rows = []
+        for q in range(3):
+            tiles = []
+            for a in range(8 * q, 8 * q + 8):
+                terms = [inv_ref[s, a, 8 * b : 8 * b + 8, :] * parts[b] for b in range(3)]
+                tiles.append(terms[0] + terms[1] + terms[2])
+            rows.append(row_sums(tiles))
         out_ref[s] = jnp.concatenate([*rows, pad], axis=1)
 
 
@@ -542,25 +563,24 @@
     halves = functools.partial(field, dtype=BF16)
     full = field(BLOCK, ELEMS)
     rows = (BLOCK * COLS, LANES)
-    r, d, coef, ori, sel, agg, owner, *sends = call(
+    r, d, coef, ori, sel, agg, owner, stiff, faces, basis, *sends = call(
         first_kernel,
         [full, full, field(COLS, LANES), ints(6 * COLS, LANES), halves(BLOCK, BLOCK),
-         ints(COLS, LANES), ints(1, AGG), *SENDS],
+         ints(COLS, LANES), ints(1, AGG), field(BLOCK, BLOCK), field(576, BLOCK),
+         field(CW, BLOCK), *SENDS],
         [right_side.reshape(rows), coefficient.reshape(COLS, LANES),
          orientation.reshape(6 * COLS, LANES), jnp.asarray(selection()),
-         aggregate_map.reshape(COLS, LANES), owner_map.reshape(1, AGG)],
-        scratch=[field(*rows), dma((6,))],
-        hbm=(0, 1, 2, 3, 4, 5),
+         aggregate_map.reshape(COLS, LANES), owner_map.reshape(1, AGG), stiffness,
+         jnp.transpose(face_blocks, (0, 1, 3, 2)).reshape(576, BLOCK), prolong_basis.T],
+        scratch=[field(*rows), dma((11,))],
+        hbm=tuple(range(9)),
     )
     wide, hots = halves(BLOCK, 768), halves(ELEMS, ELEMS)
     wh, wl, halo, rim, pf, pt, lift, edge, te = call(
         weights_kernel,
         [wide, wide, halves(4, BLOCK, 288), halves(4, 144, 288), halves(4, CW, 288),
          halves(2 * CW, BLOCK), halves(BLOCK, 3 * CW), halves(BLOCK, 3 * CW), ints(COLS, LANES)],
-        [stiffness, jnp.transpose(face_blocks, (0, 1, 3, 2)).reshape(576, BLOCK), prolong_basis.T,
-         sel, agg, owner],
-        scratch=[field(BLOCK, BLOCK), field(576, BLOCK), field(CW, BLOCK), dma((3,))],
-        hbm=(0, 1, 2),
+        [stiff, faces, basis, sel, agg, owner],
     )
 
     products = [halves(768, ELEMS), halves(768, ELEMS), full]

time: 94.5 us -> 92.7 us (0.981)
  Pallas kernels: 29.4 us -> 26.4 us
  waiting for transfers between devices: 5.73 us -> 7.05 us
    pallas_call x18, Pallas kernels: 29.4 us -> 26.4 us  [call(): pl.pallas_call(kernel, out_shape=outs, in_specs=specs, out_specs=[pl.Bloc...]
    ppermute x14, waiting for transfers between devices: 5.69 us -> 6.74 us  [swap_odd(): lax.ppermute(v, axis, [(i, (i + 1 if i % 2 else i - 1) % count) for i in...]
  transfers between devices with their start and end apart: 28 -> 28, of which waited for: 5 -> 8; matrix products, arithmetic and copies ran while one was open for 0% -> 0% of each run, Pallas kernels for 22% -> 20%
where the time goes in v6:
time: 92.7 us; the launch traced here: 92.5 us
  starting transfers between devices  35.7 us (39%)
  Pallas kernels  26.4 us (28%)
  blocking collectives  22.2 us (24%)
  waiting for transfers between devices  7.05 us (8%)
  between operations  1.08 us (1%)
    ppermute x14, starting transfers between devices, swap_odd(): lax.ppermute(v, axis, [(i, (i + 1 if i % 2 else i - 1) % count) for i in...  28.7 us
    pallas_call x18, Pallas kernels, call(): pl.pallas_call(kernel, out_shape=outs, in_specs=specs, out_specs=[pl.Bloc...  26.4 us
    all_to_all x1, blocking collectives, shards(): sol = lax.all_to_all(sol, 'gx', split_axis=0, concat_axis=0, tiled=True)  11.3 us
    all_to_all x1, blocking collectives, shards(): rhs = lax.all_to_all(rhs, 'gx', split_axis=0, concat_axis=0, tiled=True)  11 us
    ppermute x14, starting transfers between devices, swap_even(): return lax.ppermute(v, axis, [(i, i ^ 1) for i in range(count)])  7.01 us
    ppermute x14, waiting for transfers between devices, swap_odd(): lax.ppermute(v, axis, [(i, (i + 1 if i % 2 else i - 1) % count) for i in...  6.74 us
  transfers between devices with their start and end apart: 28, of which 8 were waited for; matrix products, arithmetic and copies ran while one was open for 0% of the time, Pallas kernels for 20%

profile of v6, /device:TPU:0, one launch (start us, length us, event | category | flops | bytes accessed | tf_op | source)
XLA Modules:
  0.0 92.5 jit_solution(4623396600135920459)
XLA Ops:
  0.6 1.6 %shard_map.113 = (f32[192,1024]{1,0:T(8,128)S(1)}, f32[192,1024]{1,0:T(8,128)S(1)}, f32[8,128]{1,0:T(8,128)S(1)}, s32[48,128]{1,0:T(8,128)S(1)}, bf16[192,192]{1...) custom-call(f32[1536,128]{1,0:T(8,128)} %bitcast.17, ...), custom_call_target="tpu_custom_call" | custom-call | tf_op jit(solution)/shard_map/pallas_call | solution.py:515
  2.3 6.4 %collective-permute-start.1 = (f32[48,512]{1,0:T(8,128)S(1)}, f32[48,512]{1,0:T(8,128)S(1)}, u32[]{:S(2)}, u32[]{:S(2)}) collective-permute-start(f32[48,512]{1,0:T(8,128)S(1)} %get-tuple-element.136), channel_id=1, source_target_pairs={{0,124},{4,8},{8,4},{12,16},{16,12},{20,24},{24,20},{28,32},{32,28... | collective-permute-start | bytes 294920 | tf_op jit(solution)/shard_map/ppermute | solution.py:532
  8.7 1.6 %collective-permute-start.2 = (f32[48,256]{1,0:T(8,128)S(1)}, f32[48,256]{1,0:T(8,128)S(1)}, u32[]{:S(2)}, u32[]{:S(2)}) collective-permute-start(f32[48,256]{1,0:T(8,128)S(1)} %get-tuple-element.137), channel_id=1, source_target_pairs={{0,1},{1,0},{2,3},{3,2},{4,5},{5,4},{6,7},{7,6},{8,9},{9,8},{10,11... | collective-permute-start | bytes 147464 | tf_op jit(solution)/shard_map/ppermute | solution.py:527
  10.3 2.2 %collective-permute-start.3 = (f32[48,256]{1,0:T(8,128)S(1)}, f32[48,256]{1,0:T(8,128)S(1)}, u32[]{:S(2)}, u32[]{:S(2)}) collective-permute-start(f32[48,256]{1,0:T(8,128)S(1)} %get-tuple-element.138), channel_id=1, source_target_pairs={{0,3},{1,2},{2,1},{3,0},{4,7},{5,6},{6,5},{7,4},{8,11},{9,10},{10,... | collective-permute-start | bytes 147464 | tf_op jit(solution)/shard_map/ppermute | solution.py:532
  12.5 1.2 %shard_map.114 = (bf16[192,768]{1,0:T(8,128)(2,1)S(1)}, bf16[192,768]{1,0:T(8,128)(2,1)S(1)}, bf16[4,192,288]{2,1,0:T(8,128)(2,1)S(1)}, bf16[4,144,288]{2,1,0:T(...) custom-call(f32[192,192]{1,0:T(8,128)S(1)} %get-tuple-element.124.st, ...), custom_call_target="tpu_custom_call" | custom-call | tf_op jit(solution)/shard_map/pallas_call | solution.py:515
  13.7 2.0 %shard_map.115 = (f32[192,1024]{1,0:T(8,128)S(1)}, f32[48,512]{1,0:T(8,128)S(1)}, f32[48,512]{1,0:T(8,128)S(1)}, f32[48,256]{1,0:T(8,128)S(1)}, f32[48,256]{1,0:T(8,128)S(1)}) custom-call(f32[192,1024]{1,0:T(8,128)S(1)} %get-tuple-element.120.r_ref, f32[192,1024]{1,0:T(8,128)S(1)} %get-tuple-element.121.d_ref.x_ref, ...), custom_call_target="tpu_custom_call" | custom-call | tf_op jit(solution)/shard_map/pallas_call | solution.py:515
  18.3 2.2 %collective-permute-start.7 = (f32[48,256]{1,0:T(8,128)S(1)}, f32[48,256]{1,0:T(8,128)S(1)}, u32[]{:S(2)}, u32[]{:S(2)}) collective-permute-start(f32[48,256]{1,0:T(8,128)S(1)} %get-tuple-element.155), channel_id=1, source_target_pairs={{0,3},{1,2},{2,1},{3,0},{4,7},{5,6},{6,5},{7,4},{8,11},{9,10},{10,... | collective-permute-start | bytes 147464 | tf_op jit(solution)/shard_map/ppermute | solution.py:532
  20.5 2.7 %shard_map.117 = (f32[192,1024]{1,0:T(8,128)S(1)}, f32[192,1024]{1,0:T(8,128)S(1)}, f32[192,1024]{1,0:T(8,128)S(1)}, f32[192,1024]{1,0:T(8,128)S(1)}, f32[48,512...) custom-call(f32[192,1024]{1,0:T(8,128)S(1)} %get-tuple-element.132.p, ...), custom_call_target="tpu_custom_call" | custom-call | tf_op jit(solution)/shard_map/pallas_call | solution.py:515
  24.2 2.4 %collective-permute-start.9 = (f32[48,512]{1,0:T(8,128)S(1)}, f32[48,512]{1,0:T(8,128)S(1)}, u32[]{:S(2)}, u32[]{:S(2)}) collective-permute-start(f32[48,512]{1,0:T(8,128)S(1)} %get-tuple-element.172), channel_id=1, source_target_pairs={{0,124},{4,8},{8,4},{12,16},{16,12},{20,24},{24,20},{28,32},{32,28... | collective-permute-start | bytes 294920 | tf_op jit(solution)/shard_map/ppermute | solution.py:532
  26.6 1.1 %collective-permute-start.10 = (f32[48,256]{1,0:T(8,128)S(1)}, f32[48,256]{1,0:T(8,128)S(1)}, u32[]{:S(2)}, u32[]{:S(2)}) collective-permute-start(f32[48,256]{1,0:T(8,128)S(1)} %get-tuple-element.173), channel_id=1, source_target_pairs={{0,1},{1,0},{2,3},{3,2},{4,5},{5,4},{6,7},{7,6},{8,9},{9,8},{10,11... | collective-permute-start | bytes 147464 | tf_op jit(solution)/shard_map/ppermute | solution.py:527
  27.7 1.1 %collective-permute-start.11 = (f32[48,256]{1,0:T(8,128)S(1)}, f32[48,256]{1,0:T(8,128)S(1)}, u32[]{:S(2)}, u32[]{:S(2)}) collective-permute-start(f32[48,256]{1,0:T(8,128)S(1)} %get-tuple-element.174), channel_id=1, source_target_pairs={{0,3},{1,2},{2,1},{3,0},{4,7},{5,6},{6,5},{7,4},{8,11},{9,10},{10,... | collective-permute-start | bytes 147464 | tf_op jit(solution)/shard_map/ppermute | solution.py:532
  28.9 3.5 %shard_map.119 = (f32[192,1024]{1,0:T(8,128)S(1)}, f32[192,1024]{1,0:T(8,128)}, f32[192,1024]{1,0:T(8,128)S(1)}, f32[192,1024]{1,0:T(8,128)S(1)}, f32[24,1024]{1,0:T(8,128)S(1)}) custom-call(f32[192,1024]{1,0:T(8,128)S(1)} %get-tuple-element.148.part_ref, f32[192,1024]{1,0:T(8,128)S(1)} %get-tuple-element.149.r_ref, ...), custom_call_target="tpu_custom_call" | custom-call | tf_op jit(solution)/shard_map/pallas_call | solution.py:515
  33.9 11.0 %all_to_all.10.rhs_ref = f32[32,8,128]{2,1,0:T(8,128)S(1)} all-to-all(f32[32,8,128]{2,1,0:T(8,128)S(1)} %get-tuple-element.175), channel_id=1, replica_groups=mesh['gx'=32,'gy'=4] {'gx'}, dimensions={0} | all-to-all | bytes 262144 | tf_op jit(solution)/shard_map/all_to_all | solution.py:623
  45.9 11.3 %all_to_all.11.sol_in = f32[32,8,128]{2,1,0:T(8,128)S(1)} all-to-all(f32[32,8,128]{2,1,0:T(8,128)S(1)} %shard_map.121), channel_id=1, replica_groups=mesh['gx'=32,'gy'=4] {'gx'}, dimensions={0} | all-to-all | bytes 262144 | tf_op jit(solution)/shard_map/all_to_all | solution.py:626
  58.0 1.9 %collective-permute-start.13 = (f32[48,512]{1,0:T(8,128)S(1)}, f32[48,512]{1,0:T(8,128)S(1)}, u32[]{:S(2)}, u32[]{:S(2)}) collective-permute-start(f32[48,512]{1,0:T(8,128)S(1)} %get-tuple-element.188), channel_id=1, source_target_pairs={{0,124},{4,8},{8,4},{12,16},{16,12},{20,24},{24,20},{28,32},{32,28... | collective-permute-start | bytes 294920 | tf_op jit(solution)/shard_map/ppermute | solution.py:532
  59.9 1.1 %collective-permute-start.14 = (f32[48,256]{1,0:T(8,128)S(1)}, f32[48,256]{1,0:T(8,128)S(1)}, u32[]{:S(2)}, u32[]{:S(2)}) collective-permute-start(f32[48,256]{1,0:T(8,128)S(1)} %get-tuple-element.189), channel_id=1, source_target_pairs={{0,1},{1,0},{2,3},{3,2},{4,5},{5,4},{6,7},{7,6},{8,9},{9,8},{10,11... | collective-permute-start | bytes 147464 | tf_op jit(solution)/shard_map/ppermute | solution.py:527
  61.1 1.1 %collective-permute-start.15 = (f32[48,256]{1,0:T(8,128)S(1)}, f32[48,256]{1,0:T(8,128)S(1)}, u32[]{:S(2)}, u32[]{:S(2)}) collective-permute-start(f32[48,256]{1,0:T(8,128)S(1)} %get-tuple-element.190), channel_id=1, source_target_pairs={{0,3},{1,2},{2,1},{3,0},{4,7},{5,6},{6,5},{7,4},{8,11},{9,10},{10,... | collective-permute-start | bytes 147464 | tf_op jit(solution)/shard_map/ppermute | solution.py:532
  62.2 2.4 %shard_map.123 = (f32[192,1024]{1,0:T(8,128)S(1)}, f32[192,1024]{1,0:T(8,128)S(1)}, f32[192,1024]{1,0:T(8,128)S(1)}, f32[48,512]{1,0:T(8,128)S(1)}, f32[48,512]{...) custom-call(f32[192,1024]{1,0:T(8,128)S(1)} %get-tuple-element.166.part_ref, ...), custom_call_target="tpu_custom_call" | custom-call | tf_op jit(solution)/shard_map/pallas_call | solution.py:515
  64.6 1.8 %collective-permute-done.15.rest_3_ = f32[48,256]{1,0:T(8,128)S(1)} collective-permute-done((f32[48,256]{1,0:T(8,128)S(1)}, f32[48,256]{1,0:T(8,128)S(1)}, u32[]{:S(2)}, u32[]{:S(2)}) %collective-permute-start.15) | collective-permute-done | bytes 49184 | tf_op jit(solution)/shard_map/ppermute | solution.py:532
  66.9 1.8 %collective-permute-start.17 = (f32[48,512]{1,0:T(8,128)S(1)}, f32[48,512]{1,0:T(8,128)S(1)}, u32[]{:S(2)}, u32[]{:S(2)}) collective-permute-start(f32[48,512]{1,0:T(8,128)S(1)} %get-tuple-element.204), channel_id=1, source_target_pairs={{0,124},{4,8},{8,4},{12,16},{16,12},{20,24},{24,20},{28,32},{32,28... | collective-permute-start | bytes 294920 | tf_op jit(solution)/shard_map/ppermute | solution.py:532
  69.0 1.2 %collective-permute-start.19 = (f32[48,256]{1,0:T(8,128)S(1)}, f32[48,256]{1,0:T(8,128)S(1)}, u32[]{:S(2)}, u32[]{:S(2)}) collective-permute-start(f32[48,256]{1,0:T(8,128)S(1)} %get-tuple-element.206), channel_id=1, source_target_pairs={{0,3},{1,2},{2,1},{3,0},{4,7},{5,6},{6,5},{7,4},{8,11},{9,10},{10,... | collective-permute-start | bytes 147464 | tf_op jit(solution)/shard_map/ppermute | solution.py:532
  70.2 2.3 %shard_map.125 = (f32[192,1024]{1,0:T(8,128)S(1)}, f32[192,1024]{1,0:T(8,128)S(1)}, f32[192,1024]{1,0:T(8,128)S(1)}, f32[192,1024]{1,0:T(8,128)S(1)}, f32[48,512...) custom-call(f32[192,1024]{1,0:T(8,128)S(1)} %get-tuple-element.184.part_ref, ...), custom_call_target="tpu_custom_call" | custom-call | tf_op jit(solution)/shard_map/pallas_call | solution.py:515
  72.8 1.5 %collective-permute-done.19.rest_3_ = f32[48,256]{1,0:T(8,128)S(1)} collective-permute-done((f32[48,256]{1,0:T(8,128)S(1)}, f32[48,256]{1,0:T(8,128)S(1)}, u32[]{:S(2)}, u32[]{:S(2)}) %collective-permute-start.19) | collective-permute-done | bytes 49184 | tf_op jit(solution)/shard_map/ppermute | solution.py:532
  75.1 1.9 %collective-permute-start.21 = (f32[48,512]{1,0:T(8,128)S(1)}, f32[48,512]{1,0:T(8,128)S(1)}, u32[]{:S(2)}, u32[]{:S(2)}) collective-permute-start(f32[48,512]{1,0:T(8,128)S(1)} %get-tuple-element.220), channel_id=1, source_target_pairs={{0,124},{4,8},{8,4},{12,16},{16,12},{20,24},{24,20},{28,32},{32,28... | collective-permute-start | bytes 294920 | tf_op jit(solution)/shard_map/ppermute | solution.py:532
  77.6 1.8 %collective-permute-start.23 = (f32[48,256]{1,0:T(8,128)S(1)}, f32[48,256]{1,0:T(8,128)S(1)}, u32[]{:S(2)}, u32[]{:S(2)}) collective-permute-start(f32[48,256]{1,0:T(8,128)S(1)} %get-tuple-element.222), channel_id=1, source_target_pairs={{0,3},{1,2},{2,1},{3,0},{4,7},{5,6},{6,5},{7,4},{8,11},{9,10},{10,... | collective-permute-start | bytes 147464 | tf_op jit(solution)/shard_map/ppermute | solution.py:532
  79.4 2.4 %shard_map.127 = (f32[192,1024]{1,0:T(8,128)S(1)}, f32[192,1024]{1,0:T(8,128)S(1)}, f32[192,1024]{1,0:T(8,128)S(1)}, f32[192,1024]{1,0:T(8,128)S(1)}, f32[48,512...) custom-call(f32[192,1024]{1,0:T(8,128)S(1)} %get-tuple-element.199.part_ref, ...), custom_call_target="tpu_custom_call" | custom-call | tf_op jit(solution)/shard_map/pallas_call | solution.py:515
  81.8 1.1 %collective-permute-done.23.rest_3_ = f32[48,256]{1,0:T(8,128)S(1)} collective-permute-done((f32[48,256]{1,0:T(8,128)S(1)}, f32[48,256]{1,0:T(8,128)S(1)}, u32[]{:S(2)}, u32[]{:S(2)}) %collective-permute-start.23) | collective-permute-done | bytes 49184 | tf_op jit(solution)/shard_map/ppermute | solution.py:532
  83.4 1.8 %collective-permute-start.25 = (f32[48,512]{1,0:T(8,128)S(1)}, f32[48,512]{1,0:T(8,128)S(1)}, u32[]{:S(2)}, u32[]{:S(2)}) collective-permute-start(f32[48,512]{1,0:T(8,128)S(1)} %get-tuple-element.235), channel_id=1, source_target_pairs={{0,124},{4,8},{8,4},{12,16},{16,12},{20,24},{24,20},{28,32},{32,28... | collective-permute-start | bytes 294920 | tf_op jit(solution)/shard_map/ppermute | solution.py:532
  85.6 1.8 %collective-permute-start.27 = (f32[48,256]{1,0:T(8,128)S(1)}, f32[48,256]{1,0:T(8,128)S(1)}, u32[]{:S(2)}, u32[]{:S(2)}) collective-permute-start(f32[48,256]{1,0:T(8,128)S(1)} %get-tuple-element.237), channel_id=1, source_target_pairs={{0,3},{1,2},{2,1},{3,0},{4,7},{5,6},{6,5},{7,4},{8,11},{9,10},{10,... | collective-permute-start | bytes 147464 | tf_op jit(solution)/shard_map/ppermute | solution.py:532
  87.4 2.3 %shard_map.129 = (f32[192,1024]{1,0:T(8,128)S(1)}, f32[192,1024]{1,0:T(8,128)}, f32[1536,128]{1,0:T(8,128)}, f32[192,1024]{1,0:T(8,128)S(1)}) custom-call(f32[192,1024]{1,0:T(8,128)S(1)} %get-tuple-element.215.part_ref, f32[192,1024]{1,0:T(8,128)S(1)} %get-tuple-element.216.r_ref, f32[192,1024]{1,0:T(8,128)S(1)} %get-tuple-element.217.d_ref, ...), custom_call_target="tpu_custom_call" | custom-call | tf_op jit(solution)/shard_map/pallas_call | solution.py:515
  89.7 1.2 %collective-permute-done.27.gy_out = f32[48,256]{1,0:T(8,128)S(1)} collective-permute-done((f32[48,256]{1,0:T(8,128)S(1)}, f32[48,256]{1,0:T(8,128)S(1)}, u32[]{:S(2)}, u32[]{:S(2)}) %collective-permute-start.27) | collective-permute-done | bytes 49184 | tf_op jit(solution)/shard_map/ppermute | solution.py:532
  90.9 1.4 %shard_map.130 = f32[1536,128]{1,0:T(8,128)} custom-call(f32[192,1024]{1,0:T(8,128)S(1)} %get-tuple-element.232.part_ref, f32[192,1024]{1,0:T(8,128)S(1)} %get-tuple-element.233.r_ref, s32[48,128]{1,0:T(8,128)S(1)} %get-tuple-element.123.ori_ref, bf16[4,192,288]{2,1,0:T(8,128)(2,1)S(1)} %get-tuple-element.133.halo_ref, ...), custom_call_target="tpu_custom_call" | custom-call | tf_op jit(solution)/shard_map/pallas_call | solution.py:515
  (51 shorter events, 10.3 us)
Async XLA Ops:
  2.2 13.4 %collective-permute-start = (f32[48,512]{1,0:T(8,128)S(1)}, f32[48,512]{1,0:T(8,128)S(1)}, u32[]{:S(2)}, u32[]{:S(2)}) collective-permute-start(f32[48,512]{1,0:T(8,128)S(1)} %get-tuple-element.135), channel_id=1, source_target_pairs={{0,4},{4,0},{8,12},{12,8},{16,20},{20,16},{24,28},{28,24},{32,36},... | collective-permute-start | bytes 294920 | tf_op jit(solution)/shard_map/ppermute | solution.py:527
  2.3 13.4 %collective-permute-start.1 = (f32[48,512]{1,0:T(8,128)S(1)}, f32[48,512]{1,0:T(8,128)S(1)}, u32[]{:S(2)}, u32[]{:S(2)}) collective-permute-start(f32[48,512]{1,0:T(8,128)S(1)} %get-tuple-element.136), channel_id=1, source_target_pairs={{0,124},{4,8},{8,4},{12,16},{16,12},{20,24},{24,20},{28,32},{32,28... | collective-permute-start | bytes 294920 | tf_op jit(solution)/shard_map/ppermute | solution.py:532
  8.7 6.9 %collective-permute-start.2 = (f32[48,256]{1,0:T(8,128)S(1)}, f32[48,256]{1,0:T(8,128)S(1)}, u32[]{:S(2)}, u32[]{:S(2)}) collective-permute-start(f32[48,256]{1,0:T(8,128)S(1)} %get-tuple-element.137), channel_id=1, source_target_pairs={{0,1},{1,0},{2,3},{3,2},{4,5},{5,4},{6,7},{7,6},{8,9},{9,8},{10,11... | collective-permute-start | bytes 147464 | tf_op jit(solution)/shard_map/ppermute | solution.py:527
  10.3 5.3 %collective-permute-start.3 = (f32[48,256]{1,0:T(8,128)S(1)}, f32[48,256]{1,0:T(8,128)S(1)}, u32[]{:S(2)}, u32[]{:S(2)}) collective-permute-start(f32[48,256]{1,0:T(8,128)S(1)} %get-tuple-element.138), channel_id=1, source_target_pairs={{0,3},{1,2},{2,1},{3,0},{4,7},{5,6},{6,5},{7,4},{8,11},{9,10},{10,... | collective-permute-start | bytes 147464 | tf_op jit(solution)/shard_map/ppermute | solution.py:532
  15.7 29.2 %slice-start = ((s8[9437184]{0:T(1024)(128)(4,1)}), s8[4194304]{0:T(1024)(128)(4,1)S(1)}, s32[]{:S(2)}) async-start(s8[9437184]{0:T(1024)(128)(4,1)} %bitcast.14), calls=%async_computation.2 | async-start | bytes 8388608
  16.2 7.4 %collective-permute-start.4 = (f32[48,512]{1,0:T(8,128)S(1)}, f32[48,512]{1,0:T(8,128)S(1)}, u32[]{:S(2)}, u32[]{:S(2)}) collective-permute-start(f32[48,512]{1,0:T(8,128)S(1)} %get-tuple-element.152), channel_id=1, source_target_pairs={{0,4},{4,0},{8,12},{12,8},{16,20},{20,16},{24,28},{28,24},{32,36},... | collective-permute-start | bytes 294920 | tf_op jit(solution)/shard_map/ppermute | solution.py:527
  16.2 7.4 %collective-permute-start.5 = (f32[48,512]{1,0:T(8,128)S(1)}, f32[48,512]{1,0:T(8,128)S(1)}, u32[]{:S(2)}, u32[]{:S(2)}) collective-permute-start(f32[48,512]{1,0:T(8,128)S(1)} %get-tuple-element.153), channel_id=1, source_target_pairs={{0,124},{4,8},{8,4},{12,16},{16,12},{20,24},{24,20},{28,32},{32,28... | collective-permute-start | bytes 294920 | tf_op jit(solution)/shard_map/ppermute | solution.py:532
  17.2 6.0 %collective-permute-start.6 = (f32[48,256]{1,0:T(8,128)S(1)}, f32[48,256]{1,0:T(8,128)S(1)}, u32[]{:S(2)}, u32[]{:S(2)}) collective-permute-start(f32[48,256]{1,0:T(8,128)S(1)} %get-tuple-element.154), channel_id=1, source_target_pairs={{0,1},{1,0},{2,3},{3,2},{4,5},{5,4},{6,7},{7,6},{8,9},{9,8},{10,11... | collective-permute-start | bytes 147464 | tf_op jit(solution)/shard_map/ppermute | solution.py:527
  18.3 5.3 %collective-permute-start.7 = (f32[48,256]{1,0:T(8,128)S(1)}, f32[48,256]{1,0:T(8,128)S(1)}, u32[]{:S(2)}, u32[]{:S(2)}) collective-permute-start(f32[48,256]{1,0:T(8,128)S(1)} %get-tuple-element.155), channel_id=1, source_target_pairs={{0,3},{1,2},{2,1},{3,0},{4,7},{5,6},{6,5},{7,4},{8,11},{9,10},{10,... | collective-permute-start | bytes 147464 | tf_op jit(solution)/shard_map/ppermute | solution.py:532
  20.5 24.4 %slice-start.1 = ((s8[9437184]{0:T(1024)(128)(4,1)}), s8[4194304]{0:T(1024)(128)(4,1)S(1)}, s32[]{:S(2)}) async-start(s8[9437184]{0:T(1024)(128)(4,1)} %bitcast.14), calls=%async_computation.3 | async-start | bytes 8388608
  24.1 8.9 %collective-permute-start.8 = (f32[48,512]{1,0:T(8,128)S(1)}, f32[48,512]{1,0:T(8,128)S(1)}, u32[]{:S(2)}, u32[]{:S(2)}) collective-permute-start(f32[48,512]{1,0:T(8,128)S(1)} %get-tuple-element.171), channel_id=1, source_target_pairs={{0,4},{4,0},{8,12},{12,8},{16,20},{20,16},{24,28},{28,24},{32,36},... | collective-permute-start | bytes 294920 | tf_op jit(solution)/shard_map/ppermute | solution.py:527
  24.2 8.8 %collective-permute-start.9 = (f32[48,512]{1,0:T(8,128)S(1)}, f32[48,512]{1,0:T(8,128)S(1)}, u32[]{:S(2)}, u32[]{:S(2)}) collective-permute-start(f32[48,512]{1,0:T(8,128)S(1)} %get-tuple-element.172), channel_id=1, source_target_pairs={{0,124},{4,8},{8,4},{12,16},{16,12},{20,24},{24,20},{28,32},{32,28... | collective-permute-start | bytes 294920 | tf_op jit(solution)/shard_map/ppermute | solution.py:532
  26.6 5.8 %collective-permute-start.10 = (f32[48,256]{1,0:T(8,128)S(1)}, f32[48,256]{1,0:T(8,128)S(1)}, u32[]{:S(2)}, u32[]{:S(2)}) collective-permute-start(f32[48,256]{1,0:T(8,128)S(1)} %get-tuple-element.173), channel_id=1, source_target_pairs={{0,1},{1,0},{2,3},{3,2},{4,5},{5,4},{6,7},{7,6},{8,9},{9,8},{10,11... | collective-permute-start | bytes 147464 | tf_op jit(solution)/shard_map/ppermute | solution.py:527
  27.7 5.3 %collective-permute-start.11 = (f32[48,256]{1,0:T(8,128)S(1)}, f32[48,256]{1,0:T(8,128)S(1)}, u32[]{:S(2)}, u32[]{:S(2)}) collective-permute-start(f32[48,256]{1,0:T(8,128)S(1)} %get-tuple-element.174), channel_id=1, source_target_pairs={{0,3},{1,2},{2,1},{3,0},{4,7},{5,6},{6,5},{7,4},{8,11},{9,10},{10,... | collective-permute-start | bytes 147464 | tf_op jit(solution)/shard_map/ppermute | solution.py:532
  28.9 16.0 %slice-start.2 = ((s8[9437184]{0:T(1024)(128)(4,1)}), s8[1048576]{0:T(1024)(128)(4,1)S(1)}, s32[]{:S(2)}) async-start(s8[9437184]{0:T(1024)(128)(4,1)} %bitcast.14), calls=%async_computation.4 | async-start | bytes 2097152
  57.8 8.5 %collective-permute-start.12 = (f32[48,512]{1,0:T(8,128)S(1)}, f32[48,512]{1,0:T(8,128)S(1)}, u32[]{:S(2)}, u32[]{:S(2)}) collective-permute-start(f32[48,512]{1,0:T(8,128)S(1)} %get-tuple-element.187), channel_id=1, source_target_pairs={{0,4},{4,0},{8,12},{12,8},{16,20},{20,16},{24,28},{28,24},{32,36},... | collective-permute-start | bytes 294920 | tf_op jit(solution)/shard_map/ppermute | solution.py:527
  58.0 8.3 %collective-permute-start.13 = (f32[48,512]{1,0:T(8,128)S(1)}, f32[48,512]{1,0:T(8,128)S(1)}, u32[]{:S(2)}, u32[]{:S(2)}) collective-permute-start(f32[48,512]{1,0:T(8,128)S(1)} %get-tuple-element.188), channel_id=1, source_target_pairs={{0,124},{4,8},{8,4},{12,16},{16,12},{20,24},{24,20},{28,32},{32,28... | collective-permute-start | bytes 294920 | tf_op jit(solution)/shard_map/ppermute | solution.py:532
  59.9 4.6 %collective-permute-start.14 = (f32[48,256]{1,0:T(8,128)S(1)}, f32[48,256]{1,0:T(8,128)S(1)}, u32[]{:S(2)}, u32[]{:S(2)}) collective-permute-start(f32[48,256]{1,0:T(8,128)S(1)} %get-tuple-element.189), channel_id=1, source_target_pairs={{0,1},{1,0},{2,3},{3,2},{4,5},{5,4},{6,7},{7,6},{8,9},{9,8},{10,11... | collective-permute-start | bytes 147464 | tf_op jit(solution)/shard_map/ppermute | solution.py:527
  61.1 5.3 %collective-permute-start.15 = (f32[48,256]{1,0:T(8,128)S(1)}, f32[48,256]{1,0:T(8,128)S(1)}, u32[]{:S(2)}, u32[]{:S(2)}) collective-permute-start(f32[48,256]{1,0:T(8,128)S(1)} %get-tuple-element.190), channel_id=1, source_target_pairs={{0,3},{1,2},{2,1},{3,0},{4,7},{5,6},{6,5},{7,4},{8,11},{9,10},{10,... | collective-permute-start | bytes 147464 | tf_op jit(solution)/shard_map/ppermute | solution.py:532
  66.8 7.5 %collective-permute-start.16 = (f32[48,512]{1,0:T(8,128)S(1)}, f32[48,512]{1,0:T(8,128)S(1)}, u32[]{:S(2)}, u32[]{:S(2)}) collective-permute-start(f32[48,512]{1,0:T(8,128)S(1)} %get-tuple-element.203), channel_id=1, source_target_pairs={{0,4},{4,0},{8,12},{12,8},{16,20},{20,16},{24,28},{28,24},{32,36},... | collective-permute-start | bytes 294920 | tf_op jit(solution)/shard_map/ppermute | solution.py:527
  66.9 7.4 %collective-permute-start.17 = (f32[48,512]{1,0:T(8,128)S(1)}, f32[48,512]{1,0:T(8,128)S(1)}, u32[]{:S(2)}, u32[]{:S(2)}) collective-permute-start(f32[48,512]{1,0:T(8,128)S(1)} %get-tuple-element.204), channel_id=1, source_target_pairs={{0,124},{4,8},{8,4},{12,16},{16,12},{20,24},{24,20},{28,32},{32,28... | collective-permute-start | bytes 294920 | tf_op jit(solution)/shard_map/ppermute | solution.py:532
  68.7 4.1 %collective-permute-start.18 = (f32[48,256]{1,0:T(8,128)S(1)}, f32[48,256]{1,0:T(8,128)S(1)}, u32[]{:S(2)}, u32[]{:S(2)}) collective-permute-start(f32[48,256]{1,0:T(8,128)S(1)} %get-tuple-element.205), channel_id=1, source_target_pairs={{0,1},{1,0},{2,3},{3,2},{4,5},{5,4},{6,7},{7,6},{8,9},{9,8},{10,11... | collective-permute-start | bytes 147464 | tf_op jit(solution)/shard_map/ppermute | solution.py:527
  69.0 5.3 %collective-permute-start.19 = (f32[48,256]{1,0:T(8,128)S(1)}, f32[48,256]{1,0:T(8,128)S(1)}, u32[]{:S(2)}, u32[]{:S(2)}) collective-permute-start(f32[48,256]{1,0:T(8,128)S(1)} %get-tuple-element.206), channel_id=1, source_target_pairs={{0,3},{1,2},{2,1},{3,0},{4,7},{5,6},{6,5},{7,4},{8,11},{9,10},{10,... | collective-permute-start | bytes 147464 | tf_op jit(solution)/shard_map/ppermute | solution.py:532
  74.8 8.1 %collective-permute-start.20 = (f32[48,512]{1,0:T(8,128)S(1)}, f32[48,512]{1,0:T(8,128)S(1)}, u32[]{:S(2)}, u32[]{:S(2)}) collective-permute-start(f32[48,512]{1,0:T(8,128)S(1)} %get-tuple-element.219), channel_id=1, source_target_pairs={{0,4},{4,0},{8,12},{12,8},{16,20},{20,16},{24,28},{28,24},{32,36},... | collective-permute-start | bytes 294920 | tf_op jit(solution)/shard_map/ppermute | solution.py:527
  75.1 7.8 %collective-permute-start.21 = (f32[48,512]{1,0:T(8,128)S(1)}, f32[48,512]{1,0:T(8,128)S(1)}, u32[]{:S(2)}, u32[]{:S(2)}) collective-permute-start(f32[48,512]{1,0:T(8,128)S(1)} %get-tuple-element.220), channel_id=1, source_target_pairs={{0,124},{4,8},{8,4},{12,16},{16,12},{20,24},{24,20},{28,32},{32,28... | collective-permute-start | bytes 294920 | tf_op jit(solution)/shard_map/ppermute | solution.py:532
  77.1 4.7 %collective-permute-start.22 = (f32[48,256]{1,0:T(8,128)S(1)}, f32[48,256]{1,0:T(8,128)S(1)}, u32[]{:S(2)}, u32[]{:S(2)}) collective-permute-start(f32[48,256]{1,0:T(8,128)S(1)} %get-tuple-element.221), channel_id=1, source_target_pairs={{0,1},{1,0},{2,3},{3,2},{4,5},{5,4},{6,7},{7,6},{8,9},{9,8},{10,11... | collective-permute-start | bytes 147464 | tf_op jit(solution)/shard_map/ppermute | solution.py:527
  77.6 5.3 %collective-permute-start.23 = (f32[48,256]{1,0:T(8,128)S(1)}, f32[48,256]{1,0:T(8,128)S(1)}, u32[]{:S(2)}, u32[]{:S(2)}) collective-permute-start(f32[48,256]{1,0:T(8,128)S(1)} %get-tuple-element.222), channel_id=1, source_target_pairs={{0,3},{1,2},{2,1},{3,0},{4,7},{5,6},{6,5},{7,4},{8,11},{9,10},{10,... | collective-permute-start | bytes 147464 | tf_op jit(solution)/shard_map/ppermute | solution.py:532
  83.4 7.5 %collective-permute-start.24 = (f32[48,512]{1,0:T(8,128)S(1)}, f32[48,512]{1,0:T(8,128)S(1)}, u32[]{:S(2)}, u32[]{:S(2)}) collective-permute-start(f32[48,512]{1,0:T(8,128)S(1)} %get-tuple-element.234), channel_id=1, source_target_pairs={{0,4},{4,0},{8,12},{12,8},{16,20},{20,16},{24,28},{28,24},{32,36},... | collective-permute-start | bytes 294920 | tf_op jit(solution)/shard_map/ppermute | solution.py:527
  83.4 7.4 %collective-permute-start.25 = (f32[48,512]{1,0:T(8,128)S(1)}, f32[48,512]{1,0:T(8,128)S(1)}, u32[]{:S(2)}, u32[]{:S(2)}) collective-permute-start(f32[48,512]{1,0:T(8,128)S(1)} %get-tuple-element.235), channel_id=1, source_target_pairs={{0,124},{4,8},{8,4},{12,16},{16,12},{20,24},{24,20},{28,32},{32,28... | collective-permute-start | bytes 294920 | tf_op jit(solution)/shard_map/ppermute | solution.py:532
  85.3 4.4 %collective-permute-start.26 = (f32[48,256]{1,0:T(8,128)S(1)}, f32[48,256]{1,0:T(8,128)S(1)}, u32[]{:S(2)}, u32[]{:S(2)}) collective-permute-start(f32[48,256]{1,0:T(8,128)S(1)} %get-tuple-element.236), channel_id=1, source_target_pairs={{0,1},{1,0},{2,3},{3,2},{4,5},{5,4},{6,7},{7,6},{8,9},{9,8},{10,11... | collective-permute-start | bytes 147464 | tf_op jit(solution)/shard_map/ppermute | solution.py:527
  85.6 5.3 %collective-permute-start.27 = (f32[48,256]{1,0:T(8,128)S(1)}, f32[48,256]{1,0:T(8,128)S(1)}, u32[]{:S(2)}, u32[]{:S(2)}) collective-permute-start(f32[48,256]{1,0:T(8,128)S(1)} %get-tuple-element.237), channel_id=1, source_target_pairs={{0,3},{1,2},{2,1},{3,0},{4,7},{5,6},{6,5},{7,4},{8,11},{9,10},{10,... | collective-permute-start | bytes 147464 | tf_op jit(solution)/shard_map/ppermute | solution.py:532

commit v7 on v6

--- a/solution.py
+++ b/solution.py
@@ -282,18 +282,21 @@
 
 
 def start_kernel(
-    scales, r_ref, d_ref, coef_ref, ori_ref, wh_ref, wl_ref, sel_ref, *rest,
-):
-    part_ref, *pres, xh_ref, xl_ref, t_ref = rest
+    scales, r_ref, d_ref, coef_ref, ori_ref, wh_ref, wl_ref, sel_ref, inner_ref, *rest,
+):
+    part_ref, inner_out, *pres, xh_ref, xl_ref, t_ref = rest
+    inner_out[...] = inner_ref[...]
     interior(d_ref, coef_ref, ori_ref, wh_ref, wl_ref, sel_ref, part_ref, xh_ref, xl_ref, t_ref)
     ahead(scales, r_ref, d_ref, part_ref, coef_ref, sel_ref, pres)
 
 
 def lifted_kernel(
     scales, part_ref, r_ref, x_ref, each_ref, coef_ref, ori_ref, wh_ref, wl_ref, sel_ref,
-    halo_ref, lift_ref, lx_ref, ux_ref, ly_ref, uy_ref, r_out, x_out, part_out, *rest,
+    halo_ref, lift_ref, lx_ref, ux_ref, ly_ref, uy_ref, inner_ref,
+    r_out, x_out, part_out, inner_out, *rest,
 ):
     *pres, xh_ref, xl_ref, t_ref, d_ref = rest
+    inner_out[...] = inner_ref[...]
     add_halo(d_ref, part_ref, halo_ref, [v[...] for v in (lx_ref, ux_ref, ly_ref, uy_ref)])
     r_out[...] = r_ref[...] - d_ref[...]
     lift = dot(lift_ref[...], stacked3(each_ref[...]))
@@ -364,13 +367,14 @@
 
 def step_kernel(
     scales, onward, then, part_ref, r_ref, d_ref, x_ref, coef_ref, ori_ref, wh_ref, wl_ref, sel_ref,
-    halo_ref, lx_ref, ux_ref, ly_ref, uy_ref, *rest,
+    halo_ref, lx_ref, ux_ref, ly_ref, uy_ref, inner_ref, *rest,
 ):
     if then == "hots":
         te_ref, *rest = rest
     elif then == "restrict":
         pt_ref, tall_ref, *rest = rest
-    r_out, d_out, x_out, part_out, *outs, xh_ref, xl_ref, t_ref, ad_ref = rest
+    r_out, d_out, x_out, part_out, inner_out, *outs, xh_ref, xl_ref, t_ref, ad_ref = rest
+    inner_out[...] = inner_ref[...]
     add_halo(ad_ref, part_ref, halo_ref, [v[...] for v in (lx_ref, ux_ref, ly_ref, uy_ref)])
     keep, gain = scales
     for col in range(COLS):
@@ -534,15 +538,15 @@
     )
 
 
-def exchange(sends):
-    return (
-        swap_even(sends[0], "gx"),
-        swap_odd(sends[1], "gx"),
-        swap_even(sends[2], "gy"),
-        swap_odd(sends[3], "gy"),
-    )
-
-
+def outward(sends):
+    return swap_odd(sends[1], "gx"), swap_even(sends[2], "gy"), swap_odd(sends[3], "gy")
+
+
+def inward(inner):
+    return swap_even(inner, "gx")
+
+
+INNER = pltpu.VMEM((48, 512), F32)
 SENDS = [field(48, 512), field(48, 512), field(48, 256), field(48, 256)]
 
 
@@ -593,22 +597,26 @@
             [*SENDS, *stacks],
             [coef, ori, rim, *gets, *pres],
         )
-        gets = exchange(sends)
+        gets = outward(sends)
         x_out = jax.ShapeDtypeStruct(rows, F32) if then == "close" else full
-        r, d, x, part, *outs = call(
+        r, d, x, part, inner, *outs = call(
             functools.partial(step_kernel, scales, onward, then),
-            [full, full, x_out, full, *([] if onward is None else SENDS), *extra_outs],
-            [part, r, d, x, *tables, halo, lx, ux, ly, uy, *extra],
+            [full, full, x_out, full, INNER, *([] if onward is None else SENDS), *extra_outs],
+            [part, r, d, x, *tables, halo, lx, ux, ly, uy, sends[0], *extra],
             [*products, full],
         )
-        return part, r, d, x, gets, outs
+        return part, r, d, x, (inward(inner), *gets), outs
 
     second, third = chebyshev()
     opening = (0.0, 1.0 / THETA)
-    gets = exchange(sends)
-    part, *pres = call(
-        functools.partial(start_kernel, second), [full, *SENDS], [r, d, *tables], products
-    )
+    gets = outward(sends)
+    part, inner, *pres = call(
+        functools.partial(start_kernel, second),
+        [full, INNER, *SENDS],
+        [r, d, *tables, sends[0]],
+        products,
+    )
+    gets = (inward(inner), *gets)
     part, r, d, x, gets, (*pres, hot, tall) = step(
         second, third, part, r, d, d, gets, pres, "hots", [te], [hots, hots]
     )
@@ -625,13 +633,14 @@
     sol = call(solve_kernel, [packets], [rhs, inverse])[0]
     sol = lax.all_to_all(sol, "gx", split_axis=0, concat_axis=0, tiled=True)
     each, *sends = call(lift_kernel, [coarse, *SENDS], [sol, coef, hot, edge], [coarse])
-    gets = exchange(sends)
-    r, x, part, *pres = call(
+    gets = outward(sends)
+    r, x, part, inner, *pres = call(
         functools.partial(lifted_kernel, opening),
-        [full, full, full, *SENDS],
-        [part, r, x, each, *tables, halo, lift, *near],
+        [full, full, full, INNER, *SENDS],
+        [part, r, x, each, *tables, halo, lift, *near, sends[0]],
         [*products, full],
     )
+    gets = (inward(inner), *gets)
     part, r, d, x, gets, pres = step(opening, second, part, r, r, x, gets, pres)
     part, r, d, x, gets, pres = step(second, third, part, r, d, x, gets, pres)
     part, r, _, x, gets, _ = step(third, None, part, r, d, x, gets, pres, "close")

time: 92.7 us -> 112 us (1.21)
  waiting for transfers between devices: 7.05 us -> 21.9 us
  starting transfers between devices: 35.7 us -> 40.7 us
    ppermute x14, waiting for transfers between devices: 0.31 us -> 9.05 us  [swap_even(): return lax.ppermute(v, axis, [(i, i ^ 1) for i in range(count)])]
    ppermute x14, starting transfers between devices: 28.7 us -> 35.6 us  [swap_odd(): lax.ppermute(v, axis, [(i, (i + 1 if i % 2 else i - 1) % count) for i in...]
    ppermute x14, waiting for transfers between devices: 6.74 us -> 12.9 us  [swap_odd(): lax.ppermute(v, axis, [(i, (i + 1 if i % 2 else i - 1) % count) for i in...]
    ppermute x14, starting transfers between devices: 7.01 us -> 5.16 us  [swap_even(): return lax.ppermute(v, axis, [(i, i ^ 1) for i in range(count)])]
  transfers between devices with their start and end apart: 28 -> 28, of which waited for: 8 -> 14; matrix products, arithmetic and copies ran while one was open for 0% -> 0% of each run, Pallas kernels for 20% -> 7%
where the time goes in v7:
time: 112 us
  starting transfers between devices  40.7 us (36%)
  Pallas kernels  26.5 us (24%)
  blocking collectives  22 us (20%)
  waiting for transfers between devices  21.9 us (20%)
    ppermute x14, starting transfers between devices, swap_odd(): lax.ppermute(v, axis, [(i, (i + 1 if i % 2 else i - 1) % count) for i in...  35.6 us
    pallas_call x18, Pallas kernels, call(): pl.pallas_call(kernel, out_shape=outs, in_specs=specs, out_specs=[pl.Bloc...  26.5 us
    ppermute x14, waiting for transfers between devices, swap_odd(): lax.ppermute(v, axis, [(i, (i + 1 if i % 2 else i - 1) % count) for i in...  12.9 us
    all_to_all x1, blocking collectives, shards(): sol = lax.all_to_all(sol, 'gx', split_axis=0, concat_axis=0, tiled=True)  11.3 us
    all_to_all x1, blocking collectives, shards(): rhs = lax.all_to_all(rhs, 'gx', split_axis=0, concat_axis=0, tiled=True)  10.8 us
    ppermute x14, waiting for transfers between devices, swap_even(): return lax.ppermute(v, axis, [(i, i ^ 1) for i in range(count)])  9.05 us
    ppermute x14, starting transfers between devices, swap_even(): return lax.ppermute(v, axis, [(i, i ^ 1) for i in range(count)])  5.16 us
  transfers between devices with their start and end apart: 28, of which 14 were waited for; matrix products, arithmetic and copies ran while one was open for 0% of the time, Pallas kernels for 7%

profile of v7, /device:TPU:0, one launch (start us, length us, event | category | flops | bytes accessed | tf_op | source)
XLA Modules:
  0.0 112.3 jit_solution(11274225584495499423)
XLA Ops:
  0.6 1.6 %shard_map.113 = (f32[192,1024]{1,0:T(8,128)S(1)}, f32[192,1024]{1,0:T(8,128)S(1)}, f32[8,128]{1,0:T(8,128)S(1)}, s32[48,128]{1,0:T(8,128)S(1)}, bf16[192,192]{1...) custom-call(f32[1536,128]{1,0:T(8,128)} %bitcast.17, ...), custom_call_target="tpu_custom_call" | custom-call | tf_op jit(solution)/shard_map/pallas_call | solution.py:519
  2.2 5.8 %collective-permute-start.1 = (f32[48,512]{1,0:T(8,128)S(1)}, f32[48,512]{1,0:T(8,128)S(1)}, u32[]{:S(2)}, u32[]{:S(2)}) collective-permute-start(f32[48,512]{1,0:T(8,128)S(1)} %get-tuple-element.144), channel_id=1, source_target_pairs={{0,124},{4,8},{8,4},{12,16},{16,12},{20,24},{24,20},{28,32},{32,28... | collective-permute-start | bytes 294920 | tf_op jit(solution)/shard_map/ppermute | solution.py:536
  9.2 2.0 %shard_map.115 = (f32[192,1024]{1,0:T(8,128)S(1)}, f32[48,512]{1,0:T(8,128)S(1)}, f32[48,512]{1,0:T(8,128)S(1)}, f32[48,512]{1,0:T(8,128)S(1)}, f32[48,256]{1,0:T(8,128)S(1)}, /*index=5*/f32[48,256]{1,0:T(8,128)S(1)}) custom-call(f32[192,1024]{1,0:T(8,128)S(1)} %get-tuple-element.127.r_ref, f32[192,1024]{1,0:T(8,128)S(1)} %get-tuple-element.128.d_ref.x_ref, ...), custom_call_target="tpu_custom_call" | custom-call | tf_op jit(solution)/shard_map/pallas_call | solution.py:519
  11.3 1.7 %collective-permute-start.2 = (f32[48,256]{1,0:T(8,128)S(1)}, f32[48,256]{1,0:T(8,128)S(1)}, u32[]{:S(2)}, u32[]{:S(2)}) collective-permute-start(f32[48,256]{1,0:T(8,128)S(1)} %get-tuple-element.145), channel_id=1, source_target_pairs={{0,1},{1,0},{2,3},{3,2},{4,5},{5,4},{6,7},{7,6},{8,9},{9,8},{10,11... | collective-permute-start | bytes 147464 | tf_op jit(solution)/shard_map/ppermute | solution.py:531
  13.0 2.2 %collective-permute-start.3 = (f32[48,256]{1,0:T(8,128)S(1)}, f32[48,256]{1,0:T(8,128)S(1)}, u32[]{:S(2)}, u32[]{:S(2)}) collective-permute-start(f32[48,256]{1,0:T(8,128)S(1)} %get-tuple-element.146), channel_id=1, source_target_pairs={{0,3},{1,2},{2,1},{3,0},{4,7},{5,6},{6,5},{7,4},{8,11},{9,10},{10,... | collective-permute-start | bytes 147464 | tf_op jit(solution)/shard_map/ppermute | solution.py:536
  15.5 2.8 %collective-permute-done.3.rest_3_ = f32[48,256]{1,0:T(8,128)S(1)} collective-permute-done((f32[48,256]{1,0:T(8,128)S(1)}, f32[48,256]{1,0:T(8,128)S(1)}, u32[]{:S(2)}, u32[]{:S(2)}) %collective-permute-start.3) | collective-permute-done | bytes 49184 | tf_op jit(solution)/shard_map/ppermute | solution.py:536
  18.8 2.7 %shard_map.117 = (f32[192,1024]{1,0:T(8,128)S(1)}, f32[192,1024]{1,0:T(8,128)S(1)}, f32[192,1024]{1,0:T(8,128)S(1)}, f32[192,1024]{1,0:T(8,128)S(1)}, f32[48,512...) custom-call(f32[192,1024]{1,0:T(8,128)S(1)} %get-tuple-element.140.p, ...), custom_call_target="tpu_custom_call" | custom-call | tf_op jit(solution)/shard_map/pallas_call | solution.py:519
  21.7 2.3 %collective-permute-start.7 = (f32[48,256]{1,0:T(8,128)S(1)}, f32[48,256]{1,0:T(8,128)S(1)}, u32[]{:S(2)}, u32[]{:S(2)}) collective-permute-start(f32[48,256]{1,0:T(8,128)S(1)} %get-tuple-element.164), channel_id=1, source_target_pairs={{0,3},{1,2},{2,1},{3,0},{4,7},{5,6},{6,5},{7,4},{8,11},{9,10},{10,... | collective-permute-start | bytes 147464 | tf_op jit(solution)/shard_map/ppermute | solution.py:536
  24.0 1.8 %collective-permute-done.6.rest_2_ = f32[48,256]{1,0:T(8,128)S(1)} collective-permute-done((f32[48,256]{1,0:T(8,128)S(1)}, f32[48,256]{1,0:T(8,128)S(1)}, u32[]{:S(2)}, u32[]{:S(2)}) %collective-permute-start.6) | collective-permute-done | bytes 49184 | tf_op jit(solution)/shard_map/ppermute | solution.py:531
  27.6 3.5 %shard_map.119 = (f32[192,1024]{1,0:T(8,128)S(1)}, f32[192,1024]{1,0:T(8,128)}, f32[192,1024]{1,0:T(8,128)S(1)}, f32[192,1024]{1,0:T(8,128)S(1)}, f32[48,512]{1,0:T(8,128)S(1)}, /*index=5*/f32[24,1024]{1,0:T(8,128)S(1)}) custom-call(f32[192,1024]{1,0:T(8,128)S(1)} %get-tuple-element.157.part_ref, f32[192,1024]{1,0:T(8,128)S(1)} %get-tuple-element.158.r_ref, ...), custom_call_target="tpu_custom_call" | custom-call | tf_op jit(solution)/shard_map/pallas_call | solution.py:519
  31.2 5.4 %collective-permute-start.9 = (f32[48,512]{1,0:T(8,128)S(1)}, f32[48,512]{1,0:T(8,128)S(1)}, u32[]{:S(2)}, u32[]{:S(2)}) collective-permute-start(f32[48,512]{1,0:T(8,128)S(1)} %get-tuple-element.182), channel_id=1, source_target_pairs={{0,124},{4,8},{8,4},{12,16},{16,12},{20,24},{24,20},{28,32},{32,28... | collective-permute-start | bytes 294920 | tf_op jit(solution)/shard_map/ppermute | solution.py:536
  37.3 2.2 %collective-permute-start.11 = (f32[48,256]{1,0:T(8,128)S(1)}, f32[48,256]{1,0:T(8,128)S(1)}, u32[]{:S(2)}, u32[]{:S(2)}) collective-permute-start(f32[48,256]{1,0:T(8,128)S(1)} %get-tuple-element.184), channel_id=1, source_target_pairs={{0,3},{1,2},{2,1},{3,0},{4,7},{5,6},{6,5},{7,4},{8,11},{9,10},{10,... | collective-permute-start | bytes 147464 | tf_op jit(solution)/shard_map/ppermute | solution.py:536
  40.6 2.0 %collective-permute-done.11.gy_out = f32[48,256]{1,0:T(8,128)S(1)} collective-permute-done((f32[48,256]{1,0:T(8,128)S(1)}, f32[48,256]{1,0:T(8,128)S(1)}, u32[]{:S(2)}, u32[]{:S(2)}) %collective-permute-start.11) | collective-permute-done | bytes 49184 | tf_op jit(solution)/shard_map/ppermute | solution.py:536
  43.5 10.8 %all_to_all.10.rhs_ref = f32[32,8,128]{2,1,0:T(8,128)S(1)} all-to-all(f32[32,8,128]{2,1,0:T(8,128)S(1)} %get-tuple-element.185), channel_id=1, replica_groups=mesh['gx'=32,'gy'=4] {'gx'}, dimensions={0} | all-to-all | bytes 262144 | tf_op jit(solution)/shard_map/all_to_all | solution.py:631
  55.3 11.3 %all_to_all.11.sol_in = f32[32,8,128]{2,1,0:T(8,128)S(1)} all-to-all(f32[32,8,128]{2,1,0:T(8,128)S(1)} %shard_map.121), channel_id=1, replica_groups=mesh['gx'=32,'gy'=4] {'gx'}, dimensions={0} | all-to-all | bytes 262144 | tf_op jit(solution)/shard_map/all_to_all | solution.py:634
  67.2 2.4 %shard_map.123 = (f32[192,1024]{1,0:T(8,128)S(1)}, f32[192,1024]{1,0:T(8,128)S(1)}, f32[192,1024]{1,0:T(8,128)S(1)}, f32[48,512]{1,0:T(8,128)S(1)}, f32[48,512]{...) custom-call(f32[192,1024]{1,0:T(8,128)S(1)} %get-tuple-element.176.part_ref, ...), custom_call_target="tpu_custom_call" | custom-call | tf_op jit(solution)/shard_map/pallas_call | solution.py:519
  69.8 1.9 %collective-permute-start.13 = (f32[48,512]{1,0:T(8,128)S(1)}, f32[48,512]{1,0:T(8,128)S(1)}, u32[]{:S(2)}, u32[]{:S(2)}) collective-permute-start(f32[48,512]{1,0:T(8,128)S(1)} %get-tuple-element.199), channel_id=1, source_target_pairs={{0,124},{4,8},{8,4},{12,16},{16,12},{20,24},{24,20},{28,32},{32,28... | collective-permute-start | bytes 294920 | tf_op jit(solution)/shard_map/ppermute | solution.py:536
  72.2 2.2 %collective-permute-start.15 = (f32[48,256]{1,0:T(8,128)S(1)}, f32[48,256]{1,0:T(8,128)S(1)}, u32[]{:S(2)}, u32[]{:S(2)}) collective-permute-start(f32[48,256]{1,0:T(8,128)S(1)} %get-tuple-element.201), channel_id=1, source_target_pairs={{0,3},{1,2},{2,1},{3,0},{4,7},{5,6},{6,5},{7,4},{8,11},{9,10},{10,... | collective-permute-start | bytes 147464 | tf_op jit(solution)/shard_map/ppermute | solution.py:536
  75.8 1.8 %collective-permute-done.15.rest_3_ = f32[48,256]{1,0:T(8,128)S(1)} collective-permute-done((f32[48,256]{1,0:T(8,128)S(1)}, f32[48,256]{1,0:T(8,128)S(1)}, u32[]{:S(2)}, u32[]{:S(2)}) %collective-permute-start.15) | collective-permute-done | bytes 49184 | tf_op jit(solution)/shard_map/ppermute | solution.py:536
  78.0 1.8 %collective-permute-start.17 = (f32[48,512]{1,0:T(8,128)S(1)}, f32[48,512]{1,0:T(8,128)S(1)}, u32[]{:S(2)}, u32[]{:S(2)}) collective-permute-start(f32[48,512]{1,0:T(8,128)S(1)} %get-tuple-element.216), channel_id=1, source_target_pairs={{0,124},{4,8},{8,4},{12,16},{16,12},{20,24},{24,20},{28,32},{32,28... | collective-permute-start | bytes 294920 | tf_op jit(solution)/shard_map/ppermute | solution.py:536
  79.8 2.3 %shard_map.125 = (f32[192,1024]{1,0:T(8,128)S(1)}, f32[192,1024]{1,0:T(8,128)S(1)}, f32[192,1024]{1,0:T(8,128)S(1)}, f32[192,1024]{1,0:T(8,128)S(1)}, f32[48,512...) custom-call(f32[192,1024]{1,0:T(8,128)S(1)} %get-tuple-element.195.p, ...), custom_call_target="tpu_custom_call" | custom-call | tf_op jit(solution)/shard_map/pallas_call | solution.py:519
  82.6 2.2 %collective-permute-start.19 = (f32[48,256]{1,0:T(8,128)S(1)}, f32[48,256]{1,0:T(8,128)S(1)}, u32[]{:S(2)}, u32[]{:S(2)}) collective-permute-start(f32[48,256]{1,0:T(8,128)S(1)} %get-tuple-element.218), channel_id=1, source_target_pairs={{0,3},{1,2},{2,1},{3,0},{4,7},{5,6},{6,5},{7,4},{8,11},{9,10},{10,... | collective-permute-start | bytes 147464 | tf_op jit(solution)/shard_map/ppermute | solution.py:536
  84.8 1.6 %collective-permute-done.18.rest_2_ = f32[48,256]{1,0:T(8,128)S(1)} collective-permute-done((f32[48,256]{1,0:T(8,128)S(1)}, f32[48,256]{1,0:T(8,128)S(1)}, u32[]{:S(2)}, u32[]{:S(2)}) %collective-permute-start.18) | collective-permute-done | bytes 49184 | tf_op jit(solution)/shard_map/ppermute | solution.py:531
  86.4 1.5 %collective-permute-done.19.rest_3_ = f32[48,256]{1,0:T(8,128)S(1)} collective-permute-done((f32[48,256]{1,0:T(8,128)S(1)}, f32[48,256]{1,0:T(8,128)S(1)}, u32[]{:S(2)}, u32[]{:S(2)}) %collective-permute-start.19) | collective-permute-done | bytes 49184 | tf_op jit(solution)/shard_map/ppermute | solution.py:536
  88.4 2.4 %shard_map.127 = (f32[192,1024]{1,0:T(8,128)S(1)}, f32[192,1024]{1,0:T(8,128)S(1)}, f32[192,1024]{1,0:T(8,128)S(1)}, f32[192,1024]{1,0:T(8,128)S(1)}, f32[48,512...) custom-call(f32[192,1024]{1,0:T(8,128)S(1)} %get-tuple-element.211.p, ...), custom_call_target="tpu_custom_call" | custom-call | tf_op jit(solution)/shard_map/pallas_call | solution.py:519
  90.9 3.7 %collective-permute-start.21 = (f32[48,512]{1,0:T(8,128)S(1)}, f32[48,512]{1,0:T(8,128)S(1)}, u32[]{:S(2)}, u32[]{:S(2)}) collective-permute-start(f32[48,512]{1,0:T(8,128)S(1)} %get-tuple-element.233), channel_id=1, source_target_pairs={{0,124},{4,8},{8,4},{12,16},{16,12},{20,24},{24,20},{28,32},{32,28... | collective-permute-start | bytes 294920 | tf_op jit(solution)/shard_map/ppermute | solution.py:536
  95.1 2.2 %collective-permute-start.23 = (f32[48,256]{1,0:T(8,128)S(1)}, f32[48,256]{1,0:T(8,128)S(1)}, u32[]{:S(2)}, u32[]{:S(2)}) collective-permute-start(f32[48,256]{1,0:T(8,128)S(1)} %get-tuple-element.235), channel_id=1, source_target_pairs={{0,3},{1,2},{2,1},{3,0},{4,7},{5,6},{6,5},{7,4},{8,11},{9,10},{10,... | collective-permute-start | bytes 147464 | tf_op jit(solution)/shard_map/ppermute | solution.py:536
  98.7 1.7 %collective-permute-done.23.rest_3_ = f32[48,256]{1,0:T(8,128)S(1)} collective-permute-done((f32[48,256]{1,0:T(8,128)S(1)}, f32[48,256]{1,0:T(8,128)S(1)}, u32[]{:S(2)}, u32[]{:S(2)}) %collective-permute-start.23) | collective-permute-done | bytes 49184 | tf_op jit(solution)/shard_map/ppermute | solution.py:536
  100.9 2.3 %shard_map.129 = (f32[192,1024]{1,0:T(8,128)S(1)}, f32[192,1024]{1,0:T(8,128)}, f32[1536,128]{1,0:T(8,128)}, f32[192,1024]{1,0:T(8,128)S(1)}, f32[48,512]{1,0:T(8,128)S(1)}) custom-call(f32[192,1024]{1,0:T(8,128)S(1)} %get-tuple-element.228.part_ref, f32[192,1024]{1,0:T(8,128)S(1)} %get-tuple-element.229.r_ref, f32[192,1024]{1,0:T(8,128)S(1)} %get-tuple-element.230.d_ref, ...), custom_call_target="tpu_custom_call" | custom-call | tf_op jit(solution)/shard_map/pallas_call | solution.py:519
  103.3 1.6 %collective-permute-start.25 = (f32[48,512]{1,0:T(8,128)S(1)}, f32[48,512]{1,0:T(8,128)S(1)}, u32[]{:S(2)}, u32[]{:S(2)}) collective-permute-start(f32[48,512]{1,0:T(8,128)S(1)} %get-tuple-element.249), channel_id=1, source_target_pairs={{0,124},{4,8},{8,4},{12,16},{16,12},{20,24},{24,20},{28,32},{32,28... | collective-permute-start | bytes 294920 | tf_op jit(solution)/shard_map/ppermute | solution.py:536
  105.4 2.2 %collective-permute-start.27 = (f32[48,256]{1,0:T(8,128)S(1)}, f32[48,256]{1,0:T(8,128)S(1)}, u32[]{:S(2)}, u32[]{:S(2)}) collective-permute-start(f32[48,256]{1,0:T(8,128)S(1)} %get-tuple-element.251), channel_id=1, source_target_pairs={{0,3},{1,2},{2,1},{3,0},{4,7},{5,6},{6,5},{7,4},{8,11},{9,10},{10,... | collective-permute-start | bytes 147464 | tf_op jit(solution)/shard_map/ppermute | solution.py:536
  109.0 1.7 %collective-permute-done.27.gy_out = f32[48,256]{1,0:T(8,128)S(1)} collective-permute-done((f32[48,256]{1,0:T(8,128)S(1)}, f32[48,256]{1,0:T(8,128)S(1)}, u32[]{:S(2)}, u32[]{:S(2)}) %collective-permute-start.27) | collective-permute-done | bytes 49184 | tf_op jit(solution)/shard_map/ppermute | solution.py:536
  (51 shorter events, 17.9 us)
Async XLA Ops:
  2.2 16.0 %collective-permute-start.1 = (f32[48,512]{1,0:T(8,128)S(1)}, f32[48,512]{1,0:T(8,128)S(1)}, u32[]{:S(2)}, u32[]{:S(2)}) collective-permute-start(f32[48,512]{1,0:T(8,128)S(1)} %get-tuple-element.144), channel_id=1, source_target_pairs={{0,124},{4,8},{8,4},{12,16},{16,12},{20,24},{24,20},{28,32},{32,28... | collective-permute-start | bytes 294920 | tf_op jit(solution)/shard_map/ppermute | solution.py:536
  11.2 7.1 %collective-permute-start = (f32[48,512]{1,0:T(8,128)S(1)}, f32[48,512]{1,0:T(8,128)S(1)}, u32[]{:S(2)}, u32[]{:S(2)}) collective-permute-start(f32[48,512]{1,0:T(8,128)S(1)} %get-tuple-element.143), channel_id=1, source_target_pairs={{0,4},{4,0},{8,12},{12,8},{16,20},{20,16},{24,28},{28,24},{32,36},... | collective-permute-start | bytes 294920 | tf_op jit(solution)/shard_map/ppermute | solution.py:531
  11.3 4.2 %collective-permute-start.2 = (f32[48,256]{1,0:T(8,128)S(1)}, f32[48,256]{1,0:T(8,128)S(1)}, u32[]{:S(2)}, u32[]{:S(2)}) collective-permute-start(f32[48,256]{1,0:T(8,128)S(1)} %get-tuple-element.145), channel_id=1, source_target_pairs={{0,1},{1,0},{2,3},{3,2},{4,5},{5,4},{6,7},{7,6},{8,9},{9,8},{10,11... | collective-permute-start | bytes 147464 | tf_op jit(solution)/shard_map/ppermute | solution.py:531
  13.0 5.3 %collective-permute-start.3 = (f32[48,256]{1,0:T(8,128)S(1)}, f32[48,256]{1,0:T(8,128)S(1)}, u32[]{:S(2)}, u32[]{:S(2)}) collective-permute-start(f32[48,256]{1,0:T(8,128)S(1)} %get-tuple-element.146), channel_id=1, source_target_pairs={{0,3},{1,2},{2,1},{3,0},{4,7},{5,6},{6,5},{7,4},{8,11},{9,10},{10,... | collective-permute-start | bytes 147464 | tf_op jit(solution)/shard_map/ppermute | solution.py:536
  18.3 36.0 %slice-start = ((s8[9437184]{0:T(1024)(128)(4,1)}), s8[4194304]{0:T(1024)(128)(4,1)S(1)}, s32[]{:S(2)}) async-start(s8[9437184]{0:T(1024)(128)(4,1)} %bitcast.14), calls=%async_computation.2 | async-start | bytes 8388608
  18.7 8.4 %collective-permute-start.5 = (f32[48,512]{1,0:T(8,128)S(1)}, f32[48,512]{1,0:T(8,128)S(1)}, u32[]{:S(2)}, u32[]{:S(2)}) collective-permute-start(f32[48,512]{1,0:T(8,128)S(1)} %get-tuple-element.162), channel_id=1, source_target_pairs={{0,124},{4,8},{8,4},{12,16},{16,12},{20,24},{24,20},{28,32},{32,28... | collective-permute-start | bytes 294920 | tf_op jit(solution)/shard_map/ppermute | solution.py:536
  18.8 35.4 %slice-start.1 = ((s8[9437184]{0:T(1024)(128)(4,1)}), s8[4194304]{0:T(1024)(128)(4,1)S(1)}, s32[]{:S(2)}) async-start(s8[9437184]{0:T(1024)(128)(4,1)} %bitcast.14), calls=%async_computation.3 | async-start | bytes 8388608
  21.6 5.6 %collective-permute-start.4 = (f32[48,512]{1,0:T(8,128)S(1)}, f32[48,512]{1,0:T(8,128)S(1)}, u32[]{:S(2)}, u32[]{:S(2)}) collective-permute-start(f32[48,512]{1,0:T(8,128)S(1)} %get-tuple-element.161), channel_id=1, source_target_pairs={{0,4},{4,0},{8,12},{12,8},{16,20},{20,16},{24,28},{28,24},{32,36},... | collective-permute-start | bytes 294920 | tf_op jit(solution)/shard_map/ppermute | solution.py:531
  21.7 4.2 %collective-permute-start.6 = (f32[48,256]{1,0:T(8,128)S(1)}, f32[48,256]{1,0:T(8,128)S(1)}, u32[]{:S(2)}, u32[]{:S(2)}) collective-permute-start(f32[48,256]{1,0:T(8,128)S(1)} %get-tuple-element.163), channel_id=1, source_target_pairs={{0,1},{1,0},{2,3},{3,2},{4,5},{5,4},{6,7},{7,6},{8,9},{9,8},{10,11... | collective-permute-start | bytes 147464 | tf_op jit(solution)/shard_map/ppermute | solution.py:531
  21.7 5.4 %collective-permute-start.7 = (f32[48,256]{1,0:T(8,128)S(1)}, f32[48,256]{1,0:T(8,128)S(1)}, u32[]{:S(2)}, u32[]{:S(2)}) collective-permute-start(f32[48,256]{1,0:T(8,128)S(1)} %get-tuple-element.164), channel_id=1, source_target_pairs={{0,3},{1,2},{2,1},{3,0},{4,7},{5,6},{6,5},{7,4},{8,11},{9,10},{10,... | collective-permute-start | bytes 147464 | tf_op jit(solution)/shard_map/ppermute | solution.py:536
  27.6 26.7 %slice-start.2 = ((s8[9437184]{0:T(1024)(128)(4,1)}), s8[1048576]{0:T(1024)(128)(4,1)S(1)}, s32[]{:S(2)}) async-start(s8[9437184]{0:T(1024)(128)(4,1)} %bitcast.14), calls=%async_computation.4 | async-start | bytes 2097152
  31.1 11.5 %collective-permute-start.8 = (f32[48,512]{1,0:T(8,128)S(1)}, f32[48,512]{1,0:T(8,128)S(1)}, u32[]{:S(2)}, u32[]{:S(2)}) collective-permute-start(f32[48,512]{1,0:T(8,128)S(1)} %get-tuple-element.181), channel_id=1, source_target_pairs={{0,4},{4,0},{8,12},{12,8},{16,20},{20,16},{24,28},{28,24},{32,36},... | collective-permute-start | bytes 294920 | tf_op jit(solution)/shard_map/ppermute | solution.py:531
  31.2 11.5 %collective-permute-start.9 = (f32[48,512]{1,0:T(8,128)S(1)}, f32[48,512]{1,0:T(8,128)S(1)}, u32[]{:S(2)}, u32[]{:S(2)}) collective-permute-start(f32[48,512]{1,0:T(8,128)S(1)} %get-tuple-element.182), channel_id=1, source_target_pairs={{0,124},{4,8},{8,4},{12,16},{16,12},{20,24},{24,20},{28,32},{32,28... | collective-permute-start | bytes 294920 | tf_op jit(solution)/shard_map/ppermute | solution.py:536
  36.5 4.1 %collective-permute-start.10 = (f32[48,256]{1,0:T(8,128)S(1)}, f32[48,256]{1,0:T(8,128)S(1)}, u32[]{:S(2)}, u32[]{:S(2)}) collective-permute-start(f32[48,256]{1,0:T(8,128)S(1)} %get-tuple-element.183), channel_id=1, source_target_pairs={{0,1},{1,0},{2,3},{3,2},{4,5},{5,4},{6,7},{7,6},{8,9},{9,8},{10,11... | collective-permute-start | bytes 147464 | tf_op jit(solution)/shard_map/ppermute | solution.py:531
  37.3 5.3 %collective-permute-start.11 = (f32[48,256]{1,0:T(8,128)S(1)}, f32[48,256]{1,0:T(8,128)S(1)}, u32[]{:S(2)}, u32[]{:S(2)}) collective-permute-start(f32[48,256]{1,0:T(8,128)S(1)} %get-tuple-element.184), channel_id=1, source_target_pairs={{0,3},{1,2},{2,1},{3,0},{4,7},{5,6},{6,5},{7,4},{8,11},{9,10},{10,... | collective-permute-start | bytes 147464 | tf_op jit(solution)/shard_map/ppermute | solution.py:536
  69.6 7.9 %collective-permute-start.12 = (f32[48,512]{1,0:T(8,128)S(1)}, f32[48,512]{1,0:T(8,128)S(1)}, u32[]{:S(2)}, u32[]{:S(2)}) collective-permute-start(f32[48,512]{1,0:T(8,128)S(1)} %get-tuple-element.198), channel_id=1, source_target_pairs={{0,4},{4,0},{8,12},{12,8},{16,20},{20,16},{24,28},{28,24},{32,36},... | collective-permute-start | bytes 294920 | tf_op jit(solution)/shard_map/ppermute | solution.py:531
  69.8 7.7 %collective-permute-start.13 = (f32[48,512]{1,0:T(8,128)S(1)}, f32[48,512]{1,0:T(8,128)S(1)}, u32[]{:S(2)}, u32[]{:S(2)}) collective-permute-start(f32[48,512]{1,0:T(8,128)S(1)} %get-tuple-element.199), channel_id=1, source_target_pairs={{0,124},{4,8},{8,4},{12,16},{16,12},{20,24},{24,20},{28,32},{32,28... | collective-permute-start | bytes 294920 | tf_op jit(solution)/shard_map/ppermute | solution.py:536
  71.7 4.1 %collective-permute-start.14 = (f32[48,256]{1,0:T(8,128)S(1)}, f32[48,256]{1,0:T(8,128)S(1)}, u32[]{:S(2)}, u32[]{:S(2)}) collective-permute-start(f32[48,256]{1,0:T(8,128)S(1)} %get-tuple-element.200), channel_id=1, source_target_pairs={{0,1},{1,0},{2,3},{3,2},{4,5},{5,4},{6,7},{7,6},{8,9},{9,8},{10,11... | collective-permute-start | bytes 147464 | tf_op jit(solution)/shard_map/ppermute | solution.py:531
  72.2 5.3 %collective-permute-start.15 = (f32[48,256]{1,0:T(8,128)S(1)}, f32[48,256]{1,0:T(8,128)S(1)}, u32[]{:S(2)}, u32[]{:S(2)}) collective-permute-start(f32[48,256]{1,0:T(8,128)S(1)} %get-tuple-element.201), channel_id=1, source_target_pairs={{0,3},{1,2},{2,1},{3,0},{4,7},{5,6},{6,5},{7,4},{8,11},{9,10},{10,... | collective-permute-start | bytes 147464 | tf_op jit(solution)/shard_map/ppermute | solution.py:536
  78.0 9.9 %collective-permute-start.17 = (f32[48,512]{1,0:T(8,128)S(1)}, f32[48,512]{1,0:T(8,128)S(1)}, u32[]{:S(2)}, u32[]{:S(2)}) collective-permute-start(f32[48,512]{1,0:T(8,128)S(1)} %get-tuple-element.216), channel_id=1, source_target_pairs={{0,124},{4,8},{8,4},{12,16},{16,12},{20,24},{24,20},{28,32},{32,28... | collective-permute-start | bytes 294920 | tf_op jit(solution)/shard_map/ppermute | solution.py:536
  82.1 5.8 %collective-permute-start.16 = (f32[48,512]{1,0:T(8,128)S(1)}, f32[48,512]{1,0:T(8,128)S(1)}, u32[]{:S(2)}, u32[]{:S(2)}) collective-permute-start(f32[48,512]{1,0:T(8,128)S(1)} %get-tuple-element.215), channel_id=1, source_target_pairs={{0,4},{4,0},{8,12},{12,8},{16,20},{20,16},{24,28},{28,24},{32,36},... | collective-permute-start | bytes 294920 | tf_op jit(solution)/shard_map/ppermute | solution.py:531
  82.2 4.2 %collective-permute-start.18 = (f32[48,256]{1,0:T(8,128)S(1)}, f32[48,256]{1,0:T(8,128)S(1)}, u32[]{:S(2)}, u32[]{:S(2)}) collective-permute-start(f32[48,256]{1,0:T(8,128)S(1)} %get-tuple-element.217), channel_id=1, source_target_pairs={{0,1},{1,0},{2,3},{3,2},{4,5},{5,4},{6,7},{7,6},{8,9},{9,8},{10,11... | collective-permute-start | bytes 147464 | tf_op jit(solution)/shard_map/ppermute | solution.py:531
  82.6 5.3 %collective-permute-start.19 = (f32[48,256]{1,0:T(8,128)S(1)}, f32[48,256]{1,0:T(8,128)S(1)}, u32[]{:S(2)}, u32[]{:S(2)}) collective-permute-start(f32[48,256]{1,0:T(8,128)S(1)} %get-tuple-element.218), channel_id=1, source_target_pairs={{0,3},{1,2},{2,1},{3,0},{4,7},{5,6},{6,5},{7,4},{8,11},{9,10},{10,... | collective-permute-start | bytes 147464 | tf_op jit(solution)/shard_map/ppermute | solution.py:536
  90.8 9.6 %collective-permute-start.20 = (f32[48,512]{1,0:T(8,128)S(1)}, f32[48,512]{1,0:T(8,128)S(1)}, u32[]{:S(2)}, u32[]{:S(2)}) collective-permute-start(f32[48,512]{1,0:T(8,128)S(1)} %get-tuple-element.232), channel_id=1, source_target_pairs={{0,4},{4,0},{8,12},{12,8},{16,20},{20,16},{24,28},{28,24},{32,36},... | collective-permute-start | bytes 294920 | tf_op jit(solution)/shard_map/ppermute | solution.py:531
  90.9 9.5 %collective-permute-start.21 = (f32[48,512]{1,0:T(8,128)S(1)}, f32[48,512]{1,0:T(8,128)S(1)}, u32[]{:S(2)}, u32[]{:S(2)}) collective-permute-start(f32[48,512]{1,0:T(8,128)S(1)} %get-tuple-element.233), channel_id=1, source_target_pairs={{0,124},{4,8},{8,4},{12,16},{16,12},{20,24},{24,20},{28,32},{32,28... | collective-permute-start | bytes 294920 | tf_op jit(solution)/shard_map/ppermute | solution.py:536
  94.6 4.1 %collective-permute-start.22 = (f32[48,256]{1,0:T(8,128)S(1)}, f32[48,256]{1,0:T(8,128)S(1)}, u32[]{:S(2)}, u32[]{:S(2)}) collective-permute-start(f32[48,256]{1,0:T(8,128)S(1)} %get-tuple-element.234), channel_id=1, source_target_pairs={{0,1},{1,0},{2,3},{3,2},{4,5},{5,4},{6,7},{7,6},{8,9},{9,8},{10,11... | collective-permute-start | bytes 147464 | tf_op jit(solution)/shard_map/ppermute | solution.py:531
  95.1 5.3 %collective-permute-start.23 = (f32[48,256]{1,0:T(8,128)S(1)}, f32[48,256]{1,0:T(8,128)S(1)}, u32[]{:S(2)}, u32[]{:S(2)}) collective-permute-start(f32[48,256]{1,0:T(8,128)S(1)} %get-tuple-element.235), channel_id=1, source_target_pairs={{0,3},{1,2},{2,1},{3,0},{4,7},{5,6},{6,5},{7,4},{8,11},{9,10},{10,... | collective-permute-start | bytes 147464 | tf_op jit(solution)/shard_map/ppermute | solution.py:536
  103.2 7.5 %collective-permute-start.24 = (f32[48,512]{1,0:T(8,128)S(1)}, f32[48,512]{1,0:T(8,128)S(1)}, u32[]{:S(2)}, u32[]{:S(2)}) collective-permute-start(f32[48,512]{1,0:T(8,128)S(1)} %get-tuple-element.248), channel_id=1, source_target_pairs={{0,4},{4,0},{8,12},{12,8},{16,20},{20,16},{24,28},{28,24},{32,36},... | collective-permute-start | bytes 294920 | tf_op jit(solution)/shard_map/ppermute | solution.py:531
  103.3 7.5 %collective-permute-start.25 = (f32[48,512]{1,0:T(8,128)S(1)}, f32[48,512]{1,0:T(8,128)S(1)}, u32[]{:S(2)}, u32[]{:S(2)}) collective-permute-start(f32[48,512]{1,0:T(8,128)S(1)} %get-tuple-element.249), channel_id=1, source_target_pairs={{0,124},{4,8},{8,4},{12,16},{16,12},{20,24},{24,20},{28,32},{32,28... | collective-permute-start | bytes 294920 | tf_op jit(solution)/shard_map/ppermute | solution.py:536
  104.9 4.1 %collective-permute-start.26 = (f32[48,256]{1,0:T(8,128)S(1)}, f32[48,256]{1,0:T(8,128)S(1)}, u32[]{:S(2)}, u32[]{:S(2)}) collective-permute-start(f32[48,256]{1,0:T(8,128)S(1)} %get-tuple-element.250), channel_id=1, source_target_pairs={{0,1},{1,0},{2,3},{3,2},{4,5},{5,4},{6,7},{7,6},{8,9},{9,8},{10,11... | collective-permute-start | bytes 147464 | tf_op jit(solution)/shard_map/ppermute | solution.py:531
  105.4 5.3 %collective-permute-start.27 = (f32[48,256]{1,0:T(8,128)S(1)}, f32[48,256]{1,0:T(8,128)S(1)}, u32[]{:S(2)}, u32[]{:S(2)}) collective-permute-start(f32[48,256]{1,0:T(8,128)S(1)} %get-tuple-element.251), channel_id=1, source_target_pairs={{0,3},{1,2},{2,1},{3,0},{4,7},{5,6},{6,5},{7,4},{8,11},{9,10},{10,... | collective-permute-start | bytes 147464 | tf_op jit(solution)/shard_map/ppermute | solution.py:536

commit v8 on v6

--- a/solution.py
+++ b/solution.py
@@ -116,8 +116,8 @@
 
 
 def first_kernel(
-    rs_hbm, coef_hbm, ori_hbm, sel_hbm, agg_hbm, owner_hbm, stiff_hbm, faces_hbm, pt_hbm,
-    r_ref, d_ref, coef_ref, ori_ref, sel_ref, agg_ref, owner_ref, stiff_ref, faces_ref, pt_ref,
+    rs_hbm, coef_hbm, ori_hbm, sel_hbm, agg_hbm, owner_hbm, stiff_hbm, pt_hbm,
+    r_ref, d_ref, coef_ref, ori_ref, sel_ref, agg_ref, owner_ref, stiff_ref, pt_ref,
     sx_in, sx_out, sy_in, sy_out, rs_ref, sems,
 ):
     pieces = [pl.ds(512 * c, 512) for c in range(3)]
@@ -131,7 +131,6 @@
             (ori_hbm, ori_ref),
             (stiff_hbm, stiff_ref),
             (pt_hbm, pt_ref),
-            (faces_hbm, faces_ref),
         ],
         sems,
     )
@@ -193,9 +192,11 @@
 
 
 def weights_kernel(
-    stiff_ref, faces_ref, basis_ref, sel_ref, agg_ref, owner_ref,
-    wh_ref, wl_ref, halo_ref, rim_ref, pf_ref, pt_ref, lift_ref, edge_ref, te_ref,
-):
+    stiff_ref, faces_hbm, basis_ref, sel_ref, agg_ref, owner_ref,
+    wh_ref, wl_ref, halo_ref, rim_ref, pf_ref, pt_ref, lift_ref, edge_ref, te_ref, faces_ref, sems,
+):
+    halves = [pl.ds(0, 384), pl.ds(384, 192)]
+    copies = fetch([(faces_hbm.at[half], faces_ref.at[half]) for half in halves], sems)
     slot_table(agg_ref, owner_ref, te_ref)
     high, low = split(stiff_ref[...])
     wh_ref[:, 0:BLOCK] = high
@@ -208,6 +209,8 @@
     edge_ref[48:96, :] = face_rows(lift, 3)
     edge_ref[96:192, :] = dot(sel_ref[0:96, :], lift).astype(BF16)
     for piece in range(3):
+        if piece != 1:
+            copies[piece // 2].wait()
         high, low = split(faces_ref[192 * piece : 192 * (piece + 1), :].T)
         wh_ref[:, 192 * (piece + 1) : 192 * (piece + 2)] = high
         wl_ref[:, 192 * (piece + 1) : 192 * (piece + 2)] = low
@@ -369,7 +372,7 @@
     if then == "hots":
         te_ref, *rest = rest
     elif then == "restrict":
-        pt_ref, tall_ref, *rest = rest
+        pt_ref, *rest = rest
     r_out, d_out, x_out, part_out, *outs, xh_ref, xl_ref, t_ref, ad_ref = rest
     add_halo(ad_ref, part_ref, halo_ref, [v[...] for v in (lx_ref, ux_ref, ly_ref, uy_ref)])
     keep, gain = scales
@@ -394,8 +397,7 @@
     elif then == "restrict":
         high, low = split(r_out[...] - part_out[...])
         both = dot(pt_ref[...], high)
-        proj = both[0:CW] + both[CW:] + dot(pt_ref[0:CW, :], low)
-        outs[0][...] = routed(proj, tall_ref)
+        outs[0][...] = both[0:CW] + both[CW:] + dot(pt_ref[0:CW, :], low)
 
 
 def routed(v, one_hot_ref):
@@ -435,7 +437,7 @@
         if y in (0, 3):
             part = part + parts[2 + y // 3][:, lanes(x)]
         cols.append(part)
-    rhs_ref[...] = pre_ref[...] - routed(jnp.concatenate(cols, axis=1), tall_ref)
+    rhs_ref[...] = routed(pre_ref[...] - jnp.concatenate(cols, axis=1), tall_ref)
     group = lax.broadcasted_iota(jnp.int32, (8, LANES), 1) >> 5
     for o in range(OWNERS):
         total = jnp.zeros((8, LANES), F32)
@@ -563,24 +565,25 @@
     halves = functools.partial(field, dtype=BF16)
     full = field(BLOCK, ELEMS)
     rows = (BLOCK * COLS, LANES)
-    r, d, coef, ori, sel, agg, owner, stiff, faces, basis, *sends = call(
+    r, d, coef, ori, sel, agg, owner, stiff, basis, *sends = call(
         first_kernel,
         [full, full, field(COLS, LANES), ints(6 * COLS, LANES), halves(BLOCK, BLOCK),
-         ints(COLS, LANES), ints(1, AGG), field(BLOCK, BLOCK), field(576, BLOCK),
-         field(CW, BLOCK), *SENDS],
+         ints(COLS, LANES), ints(1, AGG), field(BLOCK, BLOCK), field(CW, BLOCK), *SENDS],
         [right_side.reshape(rows), coefficient.reshape(COLS, LANES),
          orientation.reshape(6 * COLS, LANES), jnp.asarray(selection()),
          aggregate_map.reshape(COLS, LANES), owner_map.reshape(1, AGG), stiffness,
-         jnp.transpose(face_blocks, (0, 1, 3, 2)).reshape(576, BLOCK), prolong_basis.T],
-        scratch=[field(*rows), dma((11,))],
-        hbm=tuple(range(9)),
+         prolong_basis.T],
+        scratch=[field(*rows), dma((10,))],
+        hbm=tuple(range(8)),
     )
     wide, hots = halves(BLOCK, 768), halves(ELEMS, ELEMS)
     wh, wl, halo, rim, pf, pt, lift, edge, te = call(
         weights_kernel,
         [wide, wide, halves(4, BLOCK, 288), halves(4, 144, 288), halves(4, CW, 288),
          halves(2 * CW, BLOCK), halves(BLOCK, 3 * CW), halves(BLOCK, 3 * CW), ints(COLS, LANES)],
-        [stiff, faces, basis, sel, agg, owner],
+        [stiff, jnp.transpose(face_blocks, (0, 1, 3, 2)).reshape(576, BLOCK), basis, sel, agg, owner],
+        scratch=[field(576, BLOCK), dma((2,))],
+        hbm=(1,),
     )
 
     products = [halves(768, ELEMS), halves(768, ELEMS), full]
@@ -614,7 +617,7 @@
     )
     coarse = field(CW, ELEMS)
     part, r, d, x, gets, (pre,) = step(
-        third, None, part, r, d, x, gets, pres, "restrict", [pt, tall], [coarse]
+        third, None, part, r, d, x, gets, pres, "restrict", [pt], [coarse]
     )
     packets = field(OWNERS, 8, LANES)
     rhs, *near = call(

time: 92.7 us -> 93.1 us (level)
  transfers between devices with their start and end apart: 28 -> 28, of which waited for: 8 -> 6; matrix products, arithmetic and copies ran while one was open for 0% -> 0% of each run, Pallas kernels for 20% -> 21%
where the time goes in v8:
time: 93.1 us; the launch traced here: 92.9 us
  starting transfers between devices  35.7 us (38%)
  Pallas kernels  27.1 us (29%)
  blocking collectives  22.4 us (24%)
  waiting for transfers between devices  6.56 us (7%)
  between operations  1.09 us (1%)
    ppermute x14, starting transfers between devices, swap_odd(): lax.ppermute(v, axis, [(i, (i + 1 if i % 2 else i - 1) % count) for i in...  29.4 us
    pallas_call x18, Pallas kernels, call(): pl.pallas_call(kernel, out_shape=outs, in_specs=specs, out_specs=[pl.Bloc...  27.1 us
    all_to_all x1, blocking collectives, shards(): sol = lax.all_to_all(sol, 'gx', split_axis=0, concat_axis=0, tiled=True)  11.3 us
    all_to_all x1, blocking collectives, shards(): rhs = lax.all_to_all(rhs, 'gx', split_axis=0, concat_axis=0, tiled=True)  11.1 us
    ppermute x14, waiting for transfers between devices, swap_odd(): lax.ppermute(v, axis, [(i, (i + 1 if i % 2 else i - 1) % count) for i in...  6.52 us
    ppermute x14, starting transfers between devices, swap_even(): return lax.ppermute(v, axis, [(i, i ^ 1) for i in range(count)])  6.32 us
  transfers between devices with their start and end apart: 28, of which 6 were waited for; matrix products, arithmetic and copies ran while one was open for 0% of the time, Pallas kernels for 21%

profile of v8, /device:TPU:0, one launch (start us, length us, event | category | flops | bytes accessed | tf_op | source)
XLA Modules:
  0.0 92.9 jit_solution(12640079798202781060)
XLA Ops:
  0.6 1.5 %shard_map.113 = (f32[192,1024]{1,0:T(8,128)S(1)}, f32[192,1024]{1,0:T(8,128)S(1)}, f32[8,128]{1,0:T(8,128)S(1)}, s32[48,128]{1,0:T(8,128)S(1)}, bf16[192,192]{1...) custom-call(f32[1536,128]{1,0:T(8,128)} %bitcast.15, ...), custom_call_target="tpu_custom_call" | custom-call | tf_op jit(solution)/shard_map/pallas_call | solution.py:517
  2.2 6.4 %collective-permute-start.1 = (f32[48,512]{1,0:T(8,128)S(1)}, f32[48,512]{1,0:T(8,128)S(1)}, u32[]{:S(2)}, u32[]{:S(2)}) collective-permute-start(f32[48,512]{1,0:T(8,128)S(1)} %get-tuple-element.134), channel_id=1, source_target_pairs={{0,124},{4,8},{8,4},{12,16},{16,12},{20,24},{24,20},{28,32},{32,28... | collective-permute-start | bytes 294920 | tf_op jit(solution)/shard_map/ppermute | solution.py:534
  8.7 1.6 %collective-permute-start.2 = (f32[48,256]{1,0:T(8,128)S(1)}, f32[48,256]{1,0:T(8,128)S(1)}, u32[]{:S(2)}, u32[]{:S(2)}) collective-permute-start(f32[48,256]{1,0:T(8,128)S(1)} %get-tuple-element.135), channel_id=1, source_target_pairs={{0,1},{1,0},{2,3},{3,2},{4,5},{5,4},{6,7},{7,6},{8,9},{9,8},{10,11... | collective-permute-start | bytes 147464 | tf_op jit(solution)/shard_map/ppermute | solution.py:529
  10.2 2.2 %collective-permute-start.3 = (f32[48,256]{1,0:T(8,128)S(1)}, f32[48,256]{1,0:T(8,128)S(1)}, u32[]{:S(2)}, u32[]{:S(2)}) collective-permute-start(f32[48,256]{1,0:T(8,128)S(1)} %get-tuple-element.136), channel_id=1, source_target_pairs={{0,3},{1,2},{2,1},{3,0},{4,7},{5,6},{6,5},{7,4},{8,11},{9,10},{10,... | collective-permute-start | bytes 147464 | tf_op jit(solution)/shard_map/ppermute | solution.py:534
  12.4 2.3 %shard_map.114 = (bf16[192,768]{1,0:T(8,128)(2,1)S(1)}, bf16[192,768]{1,0:T(8,128)(2,1)S(1)}, bf16[4,192,288]{2,1,0:T(8,128)(2,1)S(1)}, bf16[4,144,288]{2,1,0:T(...) custom-call(f32[192,192]{1,0:T(8,128)S(1)} %get-tuple-element.123.st, ...), custom_call_target="tpu_custom_call" | custom-call | tf_op jit(solution)/shard_map/pallas_call | solution.py:517
  14.7 1.9 %shard_map.115 = (f32[192,1024]{1,0:T(8,128)S(1)}, f32[48,512]{1,0:T(8,128)S(1)}, f32[48,512]{1,0:T(8,128)S(1)}, f32[48,256]{1,0:T(8,128)S(1)}, f32[48,256]{1,0:T(8,128)S(1)}) custom-call(f32[192,1024]{1,0:T(8,128)S(1)} %get-tuple-element.119.r_ref, f32[192,1024]{1,0:T(8,128)S(1)} %get-tuple-element.120.d_ref.x_ref, ...), custom_call_target="tpu_custom_call" | custom-call | tf_op jit(solution)/shard_map/pallas_call | solution.py:517
  18.9 1.6 %collective-permute-start.7 = (f32[48,256]{1,0:T(8,128)S(1)}, f32[48,256]{1,0:T(8,128)S(1)}, u32[]{:S(2)}, u32[]{:S(2)}) collective-permute-start(f32[48,256]{1,0:T(8,128)S(1)} %get-tuple-element.153), channel_id=1, source_target_pairs={{0,3},{1,2},{2,1},{3,0},{4,7},{5,6},{6,5},{7,4},{8,11},{9,10},{10,... | collective-permute-start | bytes 147464 | tf_op jit(solution)/shard_map/ppermute | solution.py:534
  20.4 2.7 %shard_map.117 = (f32[192,1024]{1,0:T(8,128)S(1)}, f32[192,1024]{1,0:T(8,128)S(1)}, f32[192,1024]{1,0:T(8,128)S(1)}, f32[192,1024]{1,0:T(8,128)S(1)}, f32[48,512...) custom-call(f32[192,1024]{1,0:T(8,128)S(1)} %get-tuple-element.130.p, ...), custom_call_target="tpu_custom_call" | custom-call | tf_op jit(solution)/shard_map/pallas_call | solution.py:517
  23.1 1.0 %collective-permute-done.7.rest_3_ = f32[48,256]{1,0:T(8,128)S(1)} collective-permute-done((f32[48,256]{1,0:T(8,128)S(1)}, f32[48,256]{1,0:T(8,128)S(1)}, u32[]{:S(2)}, u32[]{:S(2)}) %collective-permute-start.7) | collective-permute-done | bytes 49184 | tf_op jit(solution)/shard_map/ppermute | solution.py:534
  25.2 2.3 %collective-permute-start.9 = (f32[48,512]{1,0:T(8,128)S(1)}, f32[48,512]{1,0:T(8,128)S(1)}, u32[]{:S(2)}, u32[]{:S(2)}) collective-permute-start(f32[48,512]{1,0:T(8,128)S(1)} %get-tuple-element.170), channel_id=1, source_target_pairs={{0,124},{4,8},{8,4},{12,16},{16,12},{20,24},{24,20},{28,32},{32,28... | collective-permute-start | bytes 294920 | tf_op jit(solution)/shard_map/ppermute | solution.py:534
  27.7 2.1 %collective-permute-start.11 = (f32[48,256]{1,0:T(8,128)S(1)}, f32[48,256]{1,0:T(8,128)S(1)}, u32[]{:S(2)}, u32[]{:S(2)}) collective-permute-start(f32[48,256]{1,0:T(8,128)S(1)} %get-tuple-element.172), channel_id=1, source_target_pairs={{0,3},{1,2},{2,1},{3,0},{4,7},{5,6},{6,5},{7,4},{8,11},{9,10},{10,... | collective-permute-start | bytes 147464 | tf_op jit(solution)/shard_map/ppermute | solution.py:534
  29.9 3.2 %shard_map.119 = (f32[192,1024]{1,0:T(8,128)S(1)}, f32[192,1024]{1,0:T(8,128)}, f32[192,1024]{1,0:T(8,128)S(1)}, f32[192,1024]{1,0:T(8,128)S(1)}, f32[24,1024]{1,0:T(8,128)S(1)}) custom-call(f32[192,1024]{1,0:T(8,128)S(1)} %get-tuple-element.146.part_ref, f32[192,1024]{1,0:T(8,128)S(1)} %get-tuple-element.147.r_ref, ...), custom_call_target="tpu_custom_call" | custom-call | tf_op jit(solution)/shard_map/pallas_call | solution.py:517
  34.0 11.1 %all_to_all.10.rhs_ref = f32[32,8,128]{2,1,0:T(8,128)S(1)} all-to-all(f32[32,8,128]{2,1,0:T(8,128)S(1)} %get-tuple-element.173), channel_id=1, replica_groups=mesh['gx'=32,'gy'=4] {'gx'}, dimensions={0} | all-to-all | bytes 262144 | tf_op jit(solution)/shard_map/all_to_all | solution.py:626
  45.1 1.0 %shard_map.121 = f32[32,8,128]{2,1,0:T(8,128)S(1)} custom-call(f32[32,8,128]{2,1,0:T(8,128)S(1)} %all_to_all.10.rhs_ref, f32[32,24,24,32]{3,2,1,0:T(8,128)S(1)} %bitcast.14), custom_call_target="tpu_custom_call" | custom-call | tf_op jit(solution)/shard_map/pallas_call | solution.py:517
  46.1 11.3 %all_to_all.11.sol_in = f32[32,8,128]{2,1,0:T(8,128)S(1)} all-to-all(f32[32,8,128]{2,1,0:T(8,128)S(1)} %shard_map.121), channel_id=1, replica_groups=mesh['gx'=32,'gy'=4] {'gx'}, dimensions={0} | all-to-all | bytes 262144 | tf_op jit(solution)/shard_map/all_to_all | solution.py:629
  58.2 1.9 %collective-permute-start.13 = (f32[48,512]{1,0:T(8,128)S(1)}, f32[48,512]{1,0:T(8,128)S(1)}, u32[]{:S(2)}, u32[]{:S(2)}) collective-permute-start(f32[48,512]{1,0:T(8,128)S(1)} %get-tuple-element.186), channel_id=1, source_target_pairs={{0,124},{4,8},{8,4},{12,16},{16,12},{20,24},{24,20},{28,32},{32,28... | collective-permute-start | bytes 294920 | tf_op jit(solution)/shard_map/ppermute | solution.py:534
  60.7 2.2 %collective-permute-start.15 = (f32[48,256]{1,0:T(8,128)S(1)}, f32[48,256]{1,0:T(8,128)S(1)}, u32[]{:S(2)}, u32[]{:S(2)}) collective-permute-start(f32[48,256]{1,0:T(8,128)S(1)} %get-tuple-element.188), channel_id=1, source_target_pairs={{0,3},{1,2},{2,1},{3,0},{4,7},{5,6},{6,5},{7,4},{8,11},{9,10},{10,... | collective-permute-start | bytes 147464 | tf_op jit(solution)/shard_map/ppermute | solution.py:534
  62.8 2.3 %shard_map.123 = (f32[192,1024]{1,0:T(8,128)S(1)}, f32[192,1024]{1,0:T(8,128)S(1)}, f32[192,1024]{1,0:T(8,128)S(1)}, f32[48,512]{1,0:T(8,128)S(1)}, f32[48,512]{...) custom-call(f32[192,1024]{1,0:T(8,128)S(1)} %get-tuple-element.163.part_ref, ...), custom_call_target="tpu_custom_call" | custom-call | tf_op jit(solution)/shard_map/pallas_call | solution.py:517
  66.5 2.0 %collective-permute-start.17 = (f32[48,512]{1,0:T(8,128)S(1)}, f32[48,512]{1,0:T(8,128)S(1)}, u32[]{:S(2)}, u32[]{:S(2)}) collective-permute-start(f32[48,512]{1,0:T(8,128)S(1)} %get-tuple-element.202), channel_id=1, source_target_pairs={{0,124},{4,8},{8,4},{12,16},{16,12},{20,24},{24,20},{28,32},{32,28... | collective-permute-start | bytes 294920 | tf_op jit(solution)/shard_map/ppermute | solution.py:534
  69.2 1.7 %collective-permute-start.19 = (f32[48,256]{1,0:T(8,128)S(1)}, f32[48,256]{1,0:T(8,128)S(1)}, u32[]{:S(2)}, u32[]{:S(2)}) collective-permute-start(f32[48,256]{1,0:T(8,128)S(1)} %get-tuple-element.204), channel_id=1, source_target_pairs={{0,3},{1,2},{2,1},{3,0},{4,7},{5,6},{6,5},{7,4},{8,11},{9,10},{10,... | collective-permute-start | bytes 147464 | tf_op jit(solution)/shard_map/ppermute | solution.py:534
  70.8 2.3 %shard_map.125 = (f32[192,1024]{1,0:T(8,128)S(1)}, f32[192,1024]{1,0:T(8,128)S(1)}, f32[192,1024]{1,0:T(8,128)S(1)}, f32[192,1024]{1,0:T(8,128)S(1)}, f32[48,512...) custom-call(f32[192,1024]{1,0:T(8,128)S(1)} %get-tuple-element.182.part_ref, ...), custom_call_target="tpu_custom_call" | custom-call | tf_op jit(solution)/shard_map/pallas_call | solution.py:517
  73.2 1.3 %collective-permute-done.19.rest_3_ = f32[48,256]{1,0:T(8,128)S(1)} collective-permute-done((f32[48,256]{1,0:T(8,128)S(1)}, f32[48,256]{1,0:T(8,128)S(1)}, u32[]{:S(2)}, u32[]{:S(2)}) %collective-permute-start.19) | collective-permute-done | bytes 49184 | tf_op jit(solution)/shard_map/ppermute | solution.py:534
  75.0 1.8 %collective-permute-start.21 = (f32[48,512]{1,0:T(8,128)S(1)}, f32[48,512]{1,0:T(8,128)S(1)}, u32[]{:S(2)}, u32[]{:S(2)}) collective-permute-start(f32[48,512]{1,0:T(8,128)S(1)} %get-tuple-element.218), channel_id=1, source_target_pairs={{0,124},{4,8},{8,4},{12,16},{16,12},{20,24},{24,20},{28,32},{32,28... | collective-permute-start | bytes 294920 | tf_op jit(solution)/shard_map/ppermute | solution.py:534
  76.8 1.1 %collective-permute-start.22 = (f32[48,256]{1,0:T(8,128)S(1)}, f32[48,256]{1,0:T(8,128)S(1)}, u32[]{:S(2)}, u32[]{:S(2)}) collective-permute-start(f32[48,256]{1,0:T(8,128)S(1)} %get-tuple-element.219), channel_id=1, source_target_pairs={{0,1},{1,0},{2,3},{3,2},{4,5},{5,4},{6,7},{7,6},{8,9},{9,8},{10,11... | collective-permute-start | bytes 147464 | tf_op jit(solution)/shard_map/ppermute | solution.py:529
  78.0 1.4 %collective-permute-start.23 = (f32[48,256]{1,0:T(8,128)S(1)}, f32[48,256]{1,0:T(8,128)S(1)}, u32[]{:S(2)}, u32[]{:S(2)}) collective-permute-start(f32[48,256]{1,0:T(8,128)S(1)} %get-tuple-element.220), channel_id=1, source_target_pairs={{0,3},{1,2},{2,1},{3,0},{4,7},{5,6},{6,5},{7,4},{8,11},{9,10},{10,... | collective-permute-start | bytes 147464 | tf_op jit(solution)/shard_map/ppermute | solution.py:534
  79.4 2.4 %shard_map.127 = (f32[192,1024]{1,0:T(8,128)S(1)}, f32[192,1024]{1,0:T(8,128)S(1)}, f32[192,1024]{1,0:T(8,128)S(1)}, f32[192,1024]{1,0:T(8,128)S(1)}, f32[48,512...) custom-call(f32[192,1024]{1,0:T(8,128)S(1)} %get-tuple-element.197.part_ref, ...), custom_call_target="tpu_custom_call" | custom-call | tf_op jit(solution)/shard_map/pallas_call | solution.py:517
  81.8 1.4 %collective-permute-done.23.rest_3_ = f32[48,256]{1,0:T(8,128)S(1)} collective-permute-done((f32[48,256]{1,0:T(8,128)S(1)}, f32[48,256]{1,0:T(8,128)S(1)}, u32[]{:S(2)}, u32[]{:S(2)}) %collective-permute-start.23) | collective-permute-done | bytes 49184 | tf_op jit(solution)/shard_map/ppermute | solution.py:534
  83.8 1.4 %collective-permute-start.25 = (f32[48,512]{1,0:T(8,128)S(1)}, f32[48,512]{1,0:T(8,128)S(1)}, u32[]{:S(2)}, u32[]{:S(2)}) collective-permute-start(f32[48,512]{1,0:T(8,128)S(1)} %get-tuple-element.233), channel_id=1, source_target_pairs={{0,124},{4,8},{8,4},{12,16},{16,12},{20,24},{24,20},{28,32},{32,28... | collective-permute-start | bytes 294920 | tf_op jit(solution)/shard_map/ppermute | solution.py:534
  86.0 1.6 %collective-permute-start.27 = (f32[48,256]{1,0:T(8,128)S(1)}, f32[48,256]{1,0:T(8,128)S(1)}, u32[]{:S(2)}, u32[]{:S(2)}) collective-permute-start(f32[48,256]{1,0:T(8,128)S(1)} %get-tuple-element.235), channel_id=1, source_target_pairs={{0,3},{1,2},{2,1},{3,0},{4,7},{5,6},{6,5},{7,4},{8,11},{9,10},{10,... | collective-permute-start | bytes 147464 | tf_op jit(solution)/shard_map/ppermute | solution.py:534
  87.6 2.3 %shard_map.129 = (f32[192,1024]{1,0:T(8,128)S(1)}, f32[192,1024]{1,0:T(8,128)}, f32[1536,128]{1,0:T(8,128)}, f32[192,1024]{1,0:T(8,128)S(1)}) custom-call(f32[192,1024]{1,0:T(8,128)S(1)} %get-tuple-element.213.part_ref, f32[192,1024]{1,0:T(8,128)S(1)} %get-tuple-element.214.r_ref, f32[192,1024]{1,0:T(8,128)S(1)} %get-tuple-element.215.d_ref, ...), custom_call_target="tpu_custom_call" | custom-call | tf_op jit(solution)/shard_map/pallas_call | solution.py:517
  89.9 1.4 %collective-permute-done.27.gy_out = f32[48,256]{1,0:T(8,128)S(1)} collective-permute-done((f32[48,256]{1,0:T(8,128)S(1)}, f32[48,256]{1,0:T(8,128)S(1)}, u32[]{:S(2)}, u32[]{:S(2)}) %collective-permute-start.27) | collective-permute-done | bytes 49184 | tf_op jit(solution)/shard_map/ppermute | solution.py:534
  91.3 1.4 %shard_map.130 = f32[1536,128]{1,0:T(8,128)} custom-call(f32[192,1024]{1,0:T(8,128)S(1)} %get-tuple-element.230.part_ref, f32[192,1024]{1,0:T(8,128)S(1)} %get-tuple-element.231.r_ref, s32[48,128]{1,0:T(8,128)S(1)} %get-tuple-element.122.ori_ref, bf16[4,192,288]{2,1,0:T(8,128)(2,1)S(1)} %get-tuple-element.131.halo_ref, ...), custom_call_target="tpu_custom_call" | custom-call | tf_op jit(solution)/shard_map/pallas_call | solution.py:517
  (46 shorter events, 9.7 us)
Async XLA Ops:
  2.2 14.5 %collective-permute-start = (f32[48,512]{1,0:T(8,128)S(1)}, f32[48,512]{1,0:T(8,128)S(1)}, u32[]{:S(2)}, u32[]{:S(2)}) collective-permute-start(f32[48,512]{1,0:T(8,128)S(1)} %get-tuple-element.133), channel_id=1, source_target_pairs={{0,4},{4,0},{8,12},{12,8},{16,20},{20,16},{24,28},{28,24},{32,36},... | collective-permute-start | bytes 294920 | tf_op jit(solution)/shard_map/ppermute | solution.py:529
  2.2 14.4 %collective-permute-start.1 = (f32[48,512]{1,0:T(8,128)S(1)}, f32[48,512]{1,0:T(8,128)S(1)}, u32[]{:S(2)}, u32[]{:S(2)}) collective-permute-start(f32[48,512]{1,0:T(8,128)S(1)} %get-tuple-element.134), channel_id=1, source_target_pairs={{0,124},{4,8},{8,4},{12,16},{16,12},{20,24},{24,20},{28,32},{32,28... | collective-permute-start | bytes 294920 | tf_op jit(solution)/shard_map/ppermute | solution.py:534
  8.7 8.0 %collective-permute-start.2 = (f32[48,256]{1,0:T(8,128)S(1)}, f32[48,256]{1,0:T(8,128)S(1)}, u32[]{:S(2)}, u32[]{:S(2)}) collective-permute-start(f32[48,256]{1,0:T(8,128)S(1)} %get-tuple-element.135), channel_id=1, source_target_pairs={{0,1},{1,0},{2,3},{3,2},{4,5},{5,4},{6,7},{7,6},{8,9},{9,8},{10,11... | collective-permute-start | bytes 147464 | tf_op jit(solution)/shard_map/ppermute | solution.py:529
  10.2 6.4 %collective-permute-start.3 = (f32[48,256]{1,0:T(8,128)S(1)}, f32[48,256]{1,0:T(8,128)S(1)}, u32[]{:S(2)}, u32[]{:S(2)}) collective-permute-start(f32[48,256]{1,0:T(8,128)S(1)} %get-tuple-element.136), channel_id=1, source_target_pairs={{0,3},{1,2},{2,1},{3,0},{4,7},{5,6},{6,5},{7,4},{8,11},{9,10},{10,... | collective-permute-start | bytes 147464 | tf_op jit(solution)/shard_map/ppermute | solution.py:534
  17.2 7.0 %collective-permute-start.4 = (f32[48,512]{1,0:T(8,128)S(1)}, f32[48,512]{1,0:T(8,128)S(1)}, u32[]{:S(2)}, u32[]{:S(2)}) collective-permute-start(f32[48,512]{1,0:T(8,128)S(1)} %get-tuple-element.150), channel_id=1, source_target_pairs={{0,4},{4,0},{8,12},{12,8},{16,20},{20,16},{24,28},{28,24},{32,36},... | collective-permute-start | bytes 294920 | tf_op jit(solution)/shard_map/ppermute | solution.py:529
  17.2 7.4 %collective-permute-start.5 = (f32[48,512]{1,0:T(8,128)S(1)}, f32[48,512]{1,0:T(8,128)S(1)}, u32[]{:S(2)}, u32[]{:S(2)}) collective-permute-start(f32[48,512]{1,0:T(8,128)S(1)} %get-tuple-element.151), channel_id=1, source_target_pairs={{0,124},{4,8},{8,4},{12,16},{16,12},{20,24},{24,20},{28,32},{32,28... | collective-permute-start | bytes 294920 | tf_op jit(solution)/shard_map/ppermute | solution.py:534
  18.2 4.9 %collective-permute-start.6 = (f32[48,256]{1,0:T(8,128)S(1)}, f32[48,256]{1,0:T(8,128)S(1)}, u32[]{:S(2)}, u32[]{:S(2)}) collective-permute-start(f32[48,256]{1,0:T(8,128)S(1)} %get-tuple-element.152), channel_id=1, source_target_pairs={{0,1},{1,0},{2,3},{3,2},{4,5},{5,4},{6,7},{7,6},{8,9},{9,8},{10,11... | collective-permute-start | bytes 147464 | tf_op jit(solution)/shard_map/ppermute | solution.py:529
  18.9 5.3 %collective-permute-start.7 = (f32[48,256]{1,0:T(8,128)S(1)}, f32[48,256]{1,0:T(8,128)S(1)}, u32[]{:S(2)}, u32[]{:S(2)}) collective-permute-start(f32[48,256]{1,0:T(8,128)S(1)} %get-tuple-element.153), channel_id=1, source_target_pairs={{0,3},{1,2},{2,1},{3,0},{4,7},{5,6},{6,5},{7,4},{8,11},{9,10},{10,... | collective-permute-start | bytes 147464 | tf_op jit(solution)/shard_map/ppermute | solution.py:534
  20.4 24.7 %copy-start = (f32[1,32,32,24,24]{2,4,3,1,0:T(8,128)S(1)}, f32[1,32,32,24,24]{2,4,3,1,0:T(8,128)}, u32[]{:S(2)}) copy-start(f32[1,32,32,24,24]{2,4,3,1,0:T(8,128)} %param.18) | copy-start | bytes 7077892
  25.1 7.9 %collective-permute-start.8 = (f32[48,512]{1,0:T(8,128)S(1)}, f32[48,512]{1,0:T(8,128)S(1)}, u32[]{:S(2)}, u32[]{:S(2)}) collective-permute-start(f32[48,512]{1,0:T(8,128)S(1)} %get-tuple-element.169), channel_id=1, source_target_pairs={{0,4},{4,0},{8,12},{12,8},{16,20},{20,16},{24,28},{28,24},{32,36},... | collective-permute-start | bytes 294920 | tf_op jit(solution)/shard_map/ppermute | solution.py:529
  25.2 7.8 %collective-permute-start.9 = (f32[48,512]{1,0:T(8,128)S(1)}, f32[48,512]{1,0:T(8,128)S(1)}, u32[]{:S(2)}, u32[]{:S(2)}) collective-permute-start(f32[48,512]{1,0:T(8,128)S(1)} %get-tuple-element.170), channel_id=1, source_target_pairs={{0,124},{4,8},{8,4},{12,16},{16,12},{20,24},{24,20},{28,32},{32,28... | collective-permute-start | bytes 294920 | tf_op jit(solution)/shard_map/ppermute | solution.py:534
  27.6 5.5 %collective-permute-start.10 = (f32[48,256]{1,0:T(8,128)S(1)}, f32[48,256]{1,0:T(8,128)S(1)}, u32[]{:S(2)}, u32[]{:S(2)}) collective-permute-start(f32[48,256]{1,0:T(8,128)S(1)} %get-tuple-element.171), channel_id=1, source_target_pairs={{0,1},{1,0},{2,3},{3,2},{4,5},{5,4},{6,7},{7,6},{8,9},{9,8},{10,11... | collective-permute-start | bytes 147464 | tf_op jit(solution)/shard_map/ppermute | solution.py:529
  27.7 5.4 %collective-permute-start.11 = (f32[48,256]{1,0:T(8,128)S(1)}, f32[48,256]{1,0:T(8,128)S(1)}, u32[]{:S(2)}, u32[]{:S(2)}) collective-permute-start(f32[48,256]{1,0:T(8,128)S(1)} %get-tuple-element.172), channel_id=1, source_target_pairs={{0,3},{1,2},{2,1},{3,0},{4,7},{5,6},{6,5},{7,4},{8,11},{9,10},{10,... | collective-permute-start | bytes 147464 | tf_op jit(solution)/shard_map/ppermute | solution.py:534
  58.0 7.9 %collective-permute-start.12 = (f32[48,512]{1,0:T(8,128)S(1)}, f32[48,512]{1,0:T(8,128)S(1)}, u32[]{:S(2)}, u32[]{:S(2)}) collective-permute-start(f32[48,512]{1,0:T(8,128)S(1)} %get-tuple-element.185), channel_id=1, source_target_pairs={{0,4},{4,0},{8,12},{12,8},{16,20},{20,16},{24,28},{28,24},{32,36},... | collective-permute-start | bytes 294920 | tf_op jit(solution)/shard_map/ppermute | solution.py:529
  58.2 7.8 %collective-permute-start.13 = (f32[48,512]{1,0:T(8,128)S(1)}, f32[48,512]{1,0:T(8,128)S(1)}, u32[]{:S(2)}, u32[]{:S(2)}) collective-permute-start(f32[48,512]{1,0:T(8,128)S(1)} %get-tuple-element.186), channel_id=1, source_target_pairs={{0,124},{4,8},{8,4},{12,16},{16,12},{20,24},{24,20},{28,32},{32,28... | collective-permute-start | bytes 294920 | tf_op jit(solution)/shard_map/ppermute | solution.py:534
  60.1 5.1 %collective-permute-start.14 = (f32[48,256]{1,0:T(8,128)S(1)}, f32[48,256]{1,0:T(8,128)S(1)}, u32[]{:S(2)}, u32[]{:S(2)}) collective-permute-start(f32[48,256]{1,0:T(8,128)S(1)} %get-tuple-element.187), channel_id=1, source_target_pairs={{0,1},{1,0},{2,3},{3,2},{4,5},{5,4},{6,7},{7,6},{8,9},{9,8},{10,11... | collective-permute-start | bytes 147464 | tf_op jit(solution)/shard_map/ppermute | solution.py:529
  60.7 5.3 %collective-permute-start.15 = (f32[48,256]{1,0:T(8,128)S(1)}, f32[48,256]{1,0:T(8,128)S(1)}, u32[]{:S(2)}, u32[]{:S(2)}) collective-permute-start(f32[48,256]{1,0:T(8,128)S(1)} %get-tuple-element.188), channel_id=1, source_target_pairs={{0,3},{1,2},{2,1},{3,0},{4,7},{5,6},{6,5},{7,4},{8,11},{9,10},{10,... | collective-permute-start | bytes 147464 | tf_op jit(solution)/shard_map/ppermute | solution.py:534
  66.4 8.0 %collective-permute-start.16 = (f32[48,512]{1,0:T(8,128)S(1)}, f32[48,512]{1,0:T(8,128)S(1)}, u32[]{:S(2)}, u32[]{:S(2)}) collective-permute-start(f32[48,512]{1,0:T(8,128)S(1)} %get-tuple-element.201), channel_id=1, source_target_pairs={{0,4},{4,0},{8,12},{12,8},{16,20},{20,16},{24,28},{28,24},{32,36},... | collective-permute-start | bytes 294920 | tf_op jit(solution)/shard_map/ppermute | solution.py:529
  66.5 8.0 %collective-permute-start.17 = (f32[48,512]{1,0:T(8,128)S(1)}, f32[48,512]{1,0:T(8,128)S(1)}, u32[]{:S(2)}, u32[]{:S(2)}) collective-permute-start(f32[48,512]{1,0:T(8,128)S(1)} %get-tuple-element.202), channel_id=1, source_target_pairs={{0,124},{4,8},{8,4},{12,16},{16,12},{20,24},{24,20},{28,32},{32,28... | collective-permute-start | bytes 294920 | tf_op jit(solution)/shard_map/ppermute | solution.py:534
  68.5 4.7 %collective-permute-start.18 = (f32[48,256]{1,0:T(8,128)S(1)}, f32[48,256]{1,0:T(8,128)S(1)}, u32[]{:S(2)}, u32[]{:S(2)}) collective-permute-start(f32[48,256]{1,0:T(8,128)S(1)} %get-tuple-element.203), channel_id=1, source_target_pairs={{0,1},{1,0},{2,3},{3,2},{4,5},{5,4},{6,7},{7,6},{8,9},{9,8},{10,11... | collective-permute-start | bytes 147464 | tf_op jit(solution)/shard_map/ppermute | solution.py:529
  69.2 5.3 %collective-permute-start.19 = (f32[48,256]{1,0:T(8,128)S(1)}, f32[48,256]{1,0:T(8,128)S(1)}, u32[]{:S(2)}, u32[]{:S(2)}) collective-permute-start(f32[48,256]{1,0:T(8,128)S(1)} %get-tuple-element.204), channel_id=1, source_target_pairs={{0,3},{1,2},{2,1},{3,0},{4,7},{5,6},{6,5},{7,4},{8,11},{9,10},{10,... | collective-permute-start | bytes 147464 | tf_op jit(solution)/shard_map/ppermute | solution.py:534
  74.9 8.3 %collective-permute-start.20 = (f32[48,512]{1,0:T(8,128)S(1)}, f32[48,512]{1,0:T(8,128)S(1)}, u32[]{:S(2)}, u32[]{:S(2)}) collective-permute-start(f32[48,512]{1,0:T(8,128)S(1)} %get-tuple-element.217), channel_id=1, source_target_pairs={{0,4},{4,0},{8,12},{12,8},{16,20},{20,16},{24,28},{28,24},{32,36},... | collective-permute-start | bytes 294920 | tf_op jit(solution)/shard_map/ppermute | solution.py:529
  75.0 8.2 %collective-permute-start.21 = (f32[48,512]{1,0:T(8,128)S(1)}, f32[48,512]{1,0:T(8,128)S(1)}, u32[]{:S(2)}, u32[]{:S(2)}) collective-permute-start(f32[48,512]{1,0:T(8,128)S(1)} %get-tuple-element.218), channel_id=1, source_target_pairs={{0,124},{4,8},{8,4},{12,16},{16,12},{20,24},{24,20},{28,32},{32,28... | collective-permute-start | bytes 294920 | tf_op jit(solution)/shard_map/ppermute | solution.py:534
  76.8 5.0 %collective-permute-start.22 = (f32[48,256]{1,0:T(8,128)S(1)}, f32[48,256]{1,0:T(8,128)S(1)}, u32[]{:S(2)}, u32[]{:S(2)}) collective-permute-start(f32[48,256]{1,0:T(8,128)S(1)} %get-tuple-element.219), channel_id=1, source_target_pairs={{0,1},{1,0},{2,3},{3,2},{4,5},{5,4},{6,7},{7,6},{8,9},{9,8},{10,11... | collective-permute-start | bytes 147464 | tf_op jit(solution)/shard_map/ppermute | solution.py:529
  78.0 5.3 %collective-permute-start.23 = (f32[48,256]{1,0:T(8,128)S(1)}, f32[48,256]{1,0:T(8,128)S(1)}, u32[]{:S(2)}, u32[]{:S(2)}) collective-permute-start(f32[48,256]{1,0:T(8,128)S(1)} %get-tuple-element.220), channel_id=1, source_target_pairs={{0,3},{1,2},{2,1},{3,0},{4,7},{5,6},{6,5},{7,4},{8,11},{9,10},{10,... | collective-permute-start | bytes 147464 | tf_op jit(solution)/shard_map/ppermute | solution.py:534
  83.7 7.6 %collective-permute-start.24 = (f32[48,512]{1,0:T(8,128)S(1)}, f32[48,512]{1,0:T(8,128)S(1)}, u32[]{:S(2)}, u32[]{:S(2)}) collective-permute-start(f32[48,512]{1,0:T(8,128)S(1)} %get-tuple-element.232), channel_id=1, source_target_pairs={{0,4},{4,0},{8,12},{12,8},{16,20},{20,16},{24,28},{28,24},{32,36},... | collective-permute-start | bytes 294920 | tf_op jit(solution)/shard_map/ppermute | solution.py:529
  83.8 7.5 %collective-permute-start.25 = (f32[48,512]{1,0:T(8,128)S(1)}, f32[48,512]{1,0:T(8,128)S(1)}, u32[]{:S(2)}, u32[]{:S(2)}) collective-permute-start(f32[48,512]{1,0:T(8,128)S(1)} %get-tuple-element.233), channel_id=1, source_target_pairs={{0,124},{4,8},{8,4},{12,16},{16,12},{20,24},{24,20},{28,32},{32,28... | collective-permute-start | bytes 294920 | tf_op jit(solution)/shard_map/ppermute | solution.py:534
  85.2 4.7 %collective-permute-start.26 = (f32[48,256]{1,0:T(8,128)S(1)}, f32[48,256]{1,0:T(8,128)S(1)}, u32[]{:S(2)}, u32[]{:S(2)}) collective-permute-start(f32[48,256]{1,0:T(8,128)S(1)} %get-tuple-element.234), channel_id=1, source_target_pairs={{0,1},{1,0},{2,3},{3,2},{4,5},{5,4},{6,7},{7,6},{8,9},{9,8},{10,11... | collective-permute-start | bytes 147464 | tf_op jit(solution)/shard_map/ppermute | solution.py:529
  86.0 5.3 %collective-permute-start.27 = (f32[48,256]{1,0:T(8,128)S(1)}, f32[48,256]{1,0:T(8,128)S(1)}, u32[]{:S(2)}, u32[]{:S(2)}) collective-permute-start(f32[48,256]{1,0:T(8,128)S(1)} %get-tuple-element.235), channel_id=1, source_target_pairs={{0,3},{1,2},{2,1},{3,0},{4,7},{5,6},{6,5},{7,4},{8,11},{9,10},{10,... | collective-permute-start | bytes 147464 | tf_op jit(solution)/shard_map/ppermute | solution.py:534

commit v9 on v6

--- a/solution.py
+++ b/solution.py
@@ -369,7 +369,7 @@
     if then == "hots":
         te_ref, *rest = rest
     elif then == "restrict":
-        pt_ref, tall_ref, *rest = rest
+        pt_ref, *rest = rest
     r_out, d_out, x_out, part_out, *outs, xh_ref, xl_ref, t_ref, ad_ref = rest
     add_halo(ad_ref, part_ref, halo_ref, [v[...] for v in (lx_ref, ux_ref, ly_ref, uy_ref)])
     keep, gain = scales
@@ -394,8 +394,9 @@
     elif then == "restrict":
         high, low = split(r_out[...] - part_out[...])
         both = dot(pt_ref[...], high)
-        proj = both[0:CW] + both[CW:] + dot(pt_ref[0:CW, :], low)
-        outs[0][...] = routed(proj, tall_ref)
+        outs[0][...] = both[0:CW] + both[CW:] + dot(pt_ref[0:CW, :], low)
+    elif then == "close":
+        r_out[...] = r_out[...] - part_out[...]
 
 
 def routed(v, one_hot_ref):
@@ -404,15 +405,19 @@
 
 
 def last_kernel(
-    part_ref, r_ref, ori_ref, halo_ref, gx_in, gx_out, gy_in, gy_out, r_hbm, ad_ref, out_ref, sems
-):
-    add_halo(ad_ref, part_ref, halo_ref, halo_stacks(ori_ref, (gx_in, gx_out, gy_in, gy_out)))
+    base_ref, ori_ref, halo_ref, gx_in, gx_out, gy_in, gy_out, r_hbm, out_ref, sems
+):
+    values = halo_stacks(ori_ref, (gx_in, gx_out, gy_in, gy_out))
+    parts = [dot(halo_ref[n], value) for n, value in enumerate(values)]
     copies = []
     for piece in range(3):
         rows = slice(64 * piece, 64 * (piece + 1))
         for col in range(COLS):
-            at = lanes(col)
-            out_ref[pl.ds(512 * piece + col, 64, stride=COLS), :] = r_ref[rows, at] - ad_ref[rows, at]
+            x, y = col // 4, col % 4
+            resid = base_ref[rows, lanes(col)] - parts[x][rows, lanes(y)]
+            if y in (0, 3):
+                resid = resid - parts[2 + y // 3][rows, lanes(x)]
+            out_ref[pl.ds(512 * piece + col, 64, stride=COLS), :] = resid
         span = pl.ds(512 * piece, 512)
         copies.append(pltpu.make_async_copy(out_ref.at[span], r_hbm.at[span], sems.at[piece]))
         copies[-1].start()
@@ -435,7 +440,7 @@
         if y in (0, 3):
             part = part + parts[2 + y // 3][:, lanes(x)]
         cols.append(part)
-    rhs_ref[...] = pre_ref[...] - routed(jnp.concatenate(cols, axis=1), tall_ref)
+    rhs_ref[...] = routed(pre_ref[...] - jnp.concatenate(cols, axis=1), tall_ref)
     group = lax.broadcasted_iota(jnp.int32, (8, LANES), 1) >> 5
     for o in range(OWNERS):
         total = jnp.zeros((8, LANES), F32)
@@ -614,7 +619,7 @@
     )
     coarse = field(CW, ELEMS)
     part, r, d, x, gets, (pre,) = step(
-        third, None, part, r, d, x, gets, pres, "restrict", [pt, tall], [coarse]
+        third, None, part, r, d, x, gets, pres, "restrict", [pt], [coarse]
     )
     packets = field(OWNERS, 8, LANES)
     rhs, *near = call(
@@ -638,8 +643,8 @@
     r = call(
         last_kernel,
         [jax.ShapeDtypeStruct(rows, F32)],
-        [part, r, ori, halo, *gets],
-        [full, field(*rows), dma((3,))],
+        [r, ori, halo, *gets],
+        [field(*rows), dma((3,))],
         out_space=pltpu.HBM,
     )[0]
     return x.reshape(shape), r.reshape(shape)

time: 92.7 us -> 92.3 us (level)
  transfers between devices with their start and end apart: 28 -> 28, of which waited for: 8 -> 8; matrix products, arithmetic and copies ran while one was open for 0% -> 0% of each run, Pallas kernels for 20% -> 21%
where the time goes in v9:
time: 92.3 us; the launch traced here: 92.1 us
  starting transfers between devices  35.7 us (39%)
  Pallas kernels  27 us (29%)
  blocking collectives  22 us (24%)
  waiting for transfers between devices  6.32 us (7%)
  between operations  1.05 us (1%)
    ppermute x14, starting transfers between devices, swap_odd(): lax.ppermute(v, axis, [(i, (i + 1 if i % 2 else i - 1) % count) for i in...  29 us
    pallas_call x18, Pallas kernels, call(): pl.pallas_call(kernel, out_shape=outs, in_specs=specs, out_specs=[pl.Bloc...  27 us
    all_to_all x1, blocking collectives, shards(): sol = lax.all_to_all(sol, 'gx', split_axis=0, concat_axis=0, tiled=True)  11.3 us
    all_to_all x1, blocking collectives, shards(): rhs = lax.all_to_all(rhs, 'gx', split_axis=0, concat_axis=0, tiled=True)  10.8 us
    ppermute x14, starting transfers between devices, swap_even(): return lax.ppermute(v, axis, [(i, i ^ 1) for i in range(count)])  6.7 us
    ppermute x14, waiting for transfers between devices, swap_odd(): lax.ppermute(v, axis, [(i, (i + 1 if i % 2 else i - 1) % count) for i in...  6.13 us
  transfers between devices with their start and end apart: 28, of which 8 were waited for; matrix products, arithmetic and copies ran while one was open for 0% of the time, Pallas kernels for 21%

profile of v9, /device:TPU:0, one launch (start us, length us, event | category | flops | bytes accessed | tf_op | source)
XLA Modules:
  0.0 92.1 jit_solution(17836093818118810572)
XLA Ops:
  0.6 1.6 %shard_map.113 = (f32[192,1024]{1,0:T(8,128)S(1)}, f32[192,1024]{1,0:T(8,128)S(1)}, f32[8,128]{1,0:T(8,128)S(1)}, s32[48,128]{1,0:T(8,128)S(1)}, bf16[192,192]{1...) custom-call(f32[1536,128]{1,0:T(8,128)} %bitcast.15, ...), custom_call_target="tpu_custom_call" | custom-call | tf_op jit(solution)/shard_map/pallas_call | solution.py:520
  2.3 6.4 %collective-permute-start.1 = (f32[48,512]{1,0:T(8,128)S(1)}, f32[48,512]{1,0:T(8,128)S(1)}, u32[]{:S(2)}, u32[]{:S(2)}) collective-permute-start(f32[48,512]{1,0:T(8,128)S(1)} %get-tuple-element.135), channel_id=1, source_target_pairs={{0,124},{4,8},{8,4},{12,16},{16,12},{20,24},{24,20},{28,32},{32,28... | collective-permute-start | bytes 294920 | tf_op jit(solution)/shard_map/ppermute | solution.py:537
  8.7 1.6 %collective-permute-start.2 = (f32[48,256]{1,0:T(8,128)S(1)}, f32[48,256]{1,0:T(8,128)S(1)}, u32[]{:S(2)}, u32[]{:S(2)}) collective-permute-start(f32[48,256]{1,0:T(8,128)S(1)} %get-tuple-element.136), channel_id=1, source_target_pairs={{0,1},{1,0},{2,3},{3,2},{4,5},{5,4},{6,7},{7,6},{8,9},{9,8},{10,11... | collective-permute-start | bytes 147464 | tf_op jit(solution)/shard_map/ppermute | solution.py:532
  10.3 2.2 %collective-permute-start.3 = (f32[48,256]{1,0:T(8,128)S(1)}, f32[48,256]{1,0:T(8,128)S(1)}, u32[]{:S(2)}, u32[]{:S(2)}) collective-permute-start(f32[48,256]{1,0:T(8,128)S(1)} %get-tuple-element.137), channel_id=1, source_target_pairs={{0,3},{1,2},{2,1},{3,0},{4,7},{5,6},{6,5},{7,4},{8,11},{9,10},{10,... | collective-permute-start | bytes 147464 | tf_op jit(solution)/shard_map/ppermute | solution.py:537
  12.5 1.2 %shard_map.114 = (bf16[192,768]{1,0:T(8,128)(2,1)S(1)}, bf16[192,768]{1,0:T(8,128)(2,1)S(1)}, bf16[4,192,288]{2,1,0:T(8,128)(2,1)S(1)}, bf16[4,144,288]{2,1,0:T(...) custom-call(f32[192,192]{1,0:T(8,128)S(1)} %get-tuple-element.123.st, ...), custom_call_target="tpu_custom_call" | custom-call | tf_op jit(solution)/shard_map/pallas_call | solution.py:520
  13.7 1.9 %shard_map.115 = (f32[192,1024]{1,0:T(8,128)S(1)}, f32[48,512]{1,0:T(8,128)S(1)}, f32[48,512]{1,0:T(8,128)S(1)}, f32[48,256]{1,0:T(8,128)S(1)}, f32[48,256]{1,0:T(8,128)S(1)}) custom-call(f32[192,1024]{1,0:T(8,128)S(1)} %get-tuple-element.119.r_ref, f32[192,1024]{1,0:T(8,128)S(1)} %get-tuple-element.120.d_ref.x_ref, ...), custom_call_target="tpu_custom_call" | custom-call | tf_op jit(solution)/shard_map/pallas_call | solution.py:520
  17.2 1.1 %collective-permute-start.6 = (f32[48,256]{1,0:T(8,128)S(1)}, f32[48,256]{1,0:T(8,128)S(1)}, u32[]{:S(2)}, u32[]{:S(2)}) collective-permute-start(f32[48,256]{1,0:T(8,128)S(1)} %get-tuple-element.153), channel_id=1, source_target_pairs={{0,1},{1,0},{2,3},{3,2},{4,5},{5,4},{6,7},{7,6},{8,9},{9,8},{10,11... | collective-permute-start | bytes 147464 | tf_op jit(solution)/shard_map/ppermute | solution.py:532
  18.3 2.2 %collective-permute-start.7 = (f32[48,256]{1,0:T(8,128)S(1)}, f32[48,256]{1,0:T(8,128)S(1)}, u32[]{:S(2)}, u32[]{:S(2)}) collective-permute-start(f32[48,256]{1,0:T(8,128)S(1)} %get-tuple-element.154), channel_id=1, source_target_pairs={{0,3},{1,2},{2,1},{3,0},{4,7},{5,6},{6,5},{7,4},{8,11},{9,10},{10,... | collective-permute-start | bytes 147464 | tf_op jit(solution)/shard_map/ppermute | solution.py:537
  20.5 2.7 %shard_map.117 = (f32[192,1024]{1,0:T(8,128)S(1)}, f32[192,1024]{1,0:T(8,128)S(1)}, f32[192,1024]{1,0:T(8,128)S(1)}, f32[192,1024]{1,0:T(8,128)S(1)}, f32[48,512...) custom-call(f32[192,1024]{1,0:T(8,128)S(1)} %get-tuple-element.131.p, ...), custom_call_target="tpu_custom_call" | custom-call | tf_op jit(solution)/shard_map/pallas_call | solution.py:520
  24.2 2.4 %collective-permute-start.9 = (f32[48,512]{1,0:T(8,128)S(1)}, f32[48,512]{1,0:T(8,128)S(1)}, u32[]{:S(2)}, u32[]{:S(2)}) collective-permute-start(f32[48,512]{1,0:T(8,128)S(1)} %get-tuple-element.171), channel_id=1, source_target_pairs={{0,124},{4,8},{8,4},{12,16},{16,12},{20,24},{24,20},{28,32},{32,28... | collective-permute-start | bytes 294920 | tf_op jit(solution)/shard_map/ppermute | solution.py:537
  26.6 1.1 %collective-permute-start.10 = (f32[48,256]{1,0:T(8,128)S(1)}, f32[48,256]{1,0:T(8,128)S(1)}, u32[]{:S(2)}, u32[]{:S(2)}) collective-permute-start(f32[48,256]{1,0:T(8,128)S(1)} %get-tuple-element.172), channel_id=1, source_target_pairs={{0,1},{1,0},{2,3},{3,2},{4,5},{5,4},{6,7},{7,6},{8,9},{9,8},{10,11... | collective-permute-start | bytes 147464 | tf_op jit(solution)/shard_map/ppermute | solution.py:532
  27.7 1.1 %collective-permute-start.11 = (f32[48,256]{1,0:T(8,128)S(1)}, f32[48,256]{1,0:T(8,128)S(1)}, u32[]{:S(2)}, u32[]{:S(2)}) collective-permute-start(f32[48,256]{1,0:T(8,128)S(1)} %get-tuple-element.173), channel_id=1, source_target_pairs={{0,3},{1,2},{2,1},{3,0},{4,7},{5,6},{6,5},{7,4},{8,11},{9,10},{10,... | collective-permute-start | bytes 147464 | tf_op jit(solution)/shard_map/ppermute | solution.py:537
  28.8 3.2 %shard_map.119 = (f32[192,1024]{1,0:T(8,128)S(1)}, f32[192,1024]{1,0:T(8,128)}, f32[192,1024]{1,0:T(8,128)S(1)}, f32[192,1024]{1,0:T(8,128)S(1)}, f32[24,1024]{1,0:T(8,128)S(1)}) custom-call(f32[192,1024]{1,0:T(8,128)S(1)} %get-tuple-element.147.part_ref, f32[192,1024]{1,0:T(8,128)S(1)} %get-tuple-element.148.r_ref, ...), custom_call_target="tpu_custom_call" | custom-call | tf_op jit(solution)/shard_map/pallas_call | solution.py:520
  33.9 10.8 %all_to_all.10.rhs_ref = f32[32,8,128]{2,1,0:T(8,128)S(1)} all-to-all(f32[32,8,128]{2,1,0:T(8,128)S(1)} %get-tuple-element.174), channel_id=1, replica_groups=mesh['gx'=32,'gy'=4] {'gx'}, dimensions={0} | all-to-all | bytes 262144 | tf_op jit(solution)/shard_map/all_to_all | solution.py:628
  45.7 11.3 %all_to_all.11.sol_in = f32[32,8,128]{2,1,0:T(8,128)S(1)} all-to-all(f32[32,8,128]{2,1,0:T(8,128)S(1)} %shard_map.121), channel_id=1, replica_groups=mesh['gx'=32,'gy'=4] {'gx'}, dimensions={0} | all-to-all | bytes 262144 | tf_op jit(solution)/shard_map/all_to_all | solution.py:631
  57.8 1.9 %collective-permute-start.13 = (f32[48,512]{1,0:T(8,128)S(1)}, f32[48,512]{1,0:T(8,128)S(1)}, u32[]{:S(2)}, u32[]{:S(2)}) collective-permute-start(f32[48,512]{1,0:T(8,128)S(1)} %get-tuple-element.187), channel_id=1, source_target_pairs={{0,124},{4,8},{8,4},{12,16},{16,12},{20,24},{24,20},{28,32},{32,28... | collective-permute-start | bytes 294920 | tf_op jit(solution)/shard_map/ppermute | solution.py:537
  59.7 1.0 %collective-permute-start.14 = (f32[48,256]{1,0:T(8,128)S(1)}, f32[48,256]{1,0:T(8,128)S(1)}, u32[]{:S(2)}, u32[]{:S(2)}) collective-permute-start(f32[48,256]{1,0:T(8,128)S(1)} %get-tuple-element.188), channel_id=1, source_target_pairs={{0,1},{1,0},{2,3},{3,2},{4,5},{5,4},{6,7},{7,6},{8,9},{9,8},{10,11... | collective-permute-start | bytes 147464 | tf_op jit(solution)/shard_map/ppermute | solution.py:532
  60.7 1.1 %collective-permute-start.15 = (f32[48,256]{1,0:T(8,128)S(1)}, f32[48,256]{1,0:T(8,128)S(1)}, u32[]{:S(2)}, u32[]{:S(2)}) collective-permute-start(f32[48,256]{1,0:T(8,128)S(1)} %get-tuple-element.189), channel_id=1, source_target_pairs={{0,3},{1,2},{2,1},{3,0},{4,7},{5,6},{6,5},{7,4},{8,11},{9,10},{10,... | collective-permute-start | bytes 147464 | tf_op jit(solution)/shard_map/ppermute | solution.py:537
  61.8 2.3 %shard_map.123 = (f32[192,1024]{1,0:T(8,128)S(1)}, f32[192,1024]{1,0:T(8,128)S(1)}, f32[192,1024]{1,0:T(8,128)S(1)}, f32[48,512]{1,0:T(8,128)S(1)}, f32[48,512]{...) custom-call(f32[192,1024]{1,0:T(8,128)S(1)} %get-tuple-element.164.part_ref, ...), custom_call_target="tpu_custom_call" | custom-call | tf_op jit(solution)/shard_map/pallas_call | solution.py:520
  64.2 1.8 %collective-permute-done.15.rest_3_ = f32[48,256]{1,0:T(8,128)S(1)} collective-permute-done((f32[48,256]{1,0:T(8,128)S(1)}, f32[48,256]{1,0:T(8,128)S(1)}, u32[]{:S(2)}, u32[]{:S(2)}) %collective-permute-start.15) | collective-permute-done | bytes 49184 | tf_op jit(solution)/shard_map/ppermute | solution.py:537
  66.6 1.8 %collective-permute-start.17 = (f32[48,512]{1,0:T(8,128)S(1)}, f32[48,512]{1,0:T(8,128)S(1)}, u32[]{:S(2)}, u32[]{:S(2)}) collective-permute-start(f32[48,512]{1,0:T(8,128)S(1)} %get-tuple-element.203), channel_id=1, source_target_pairs={{0,124},{4,8},{8,4},{12,16},{16,12},{20,24},{24,20},{28,32},{32,28... | collective-permute-start | bytes 294920 | tf_op jit(solution)/shard_map/ppermute | solution.py:537
  68.7 1.3 %collective-permute-start.19 = (f32[48,256]{1,0:T(8,128)S(1)}, f32[48,256]{1,0:T(8,128)S(1)}, u32[]{:S(2)}, u32[]{:S(2)}) collective-permute-start(f32[48,256]{1,0:T(8,128)S(1)} %get-tuple-element.205), channel_id=1, source_target_pairs={{0,3},{1,2},{2,1},{3,0},{4,7},{5,6},{6,5},{7,4},{8,11},{9,10},{10,... | collective-permute-start | bytes 147464 | tf_op jit(solution)/shard_map/ppermute | solution.py:537
  70.0 2.3 %shard_map.125 = (f32[192,1024]{1,0:T(8,128)S(1)}, f32[192,1024]{1,0:T(8,128)S(1)}, f32[192,1024]{1,0:T(8,128)S(1)}, f32[192,1024]{1,0:T(8,128)S(1)}, f32[48,512...) custom-call(f32[192,1024]{1,0:T(8,128)S(1)} %get-tuple-element.183.part_ref, ...), custom_call_target="tpu_custom_call" | custom-call | tf_op jit(solution)/shard_map/pallas_call | solution.py:520
  72.5 1.5 %collective-permute-done.19.rest_3_ = f32[48,256]{1,0:T(8,128)S(1)} collective-permute-done((f32[48,256]{1,0:T(8,128)S(1)}, f32[48,256]{1,0:T(8,128)S(1)}, u32[]{:S(2)}, u32[]{:S(2)}) %collective-permute-start.19) | collective-permute-done | bytes 49184 | tf_op jit(solution)/shard_map/ppermute | solution.py:537
  74.6 2.2 %collective-permute-start.21 = (f32[48,512]{1,0:T(8,128)S(1)}, f32[48,512]{1,0:T(8,128)S(1)}, u32[]{:S(2)}, u32[]{:S(2)}) collective-permute-start(f32[48,512]{1,0:T(8,128)S(1)} %get-tuple-element.219), channel_id=1, source_target_pairs={{0,124},{4,8},{8,4},{12,16},{16,12},{20,24},{24,20},{28,32},{32,28... | collective-permute-start | bytes 294920 | tf_op jit(solution)/shard_map/ppermute | solution.py:537
  77.3 1.8 %collective-permute-start.23 = (f32[48,256]{1,0:T(8,128)S(1)}, f32[48,256]{1,0:T(8,128)S(1)}, u32[]{:S(2)}, u32[]{:S(2)}) collective-permute-start(f32[48,256]{1,0:T(8,128)S(1)} %get-tuple-element.221), channel_id=1, source_target_pairs={{0,3},{1,2},{2,1},{3,0},{4,7},{5,6},{6,5},{7,4},{8,11},{9,10},{10,... | collective-permute-start | bytes 147464 | tf_op jit(solution)/shard_map/ppermute | solution.py:537
  79.0 2.4 %shard_map.127 = (f32[192,1024]{1,0:T(8,128)S(1)}, f32[192,1024]{1,0:T(8,128)S(1)}, f32[192,1024]{1,0:T(8,128)S(1)}, f32[192,1024]{1,0:T(8,128)S(1)}, f32[48,512...) custom-call(f32[192,1024]{1,0:T(8,128)S(1)} %get-tuple-element.198.part_ref, ...), custom_call_target="tpu_custom_call" | custom-call | tf_op jit(solution)/shard_map/pallas_call | solution.py:520
  81.5 1.1 %collective-permute-done.23.rest_3_ = f32[48,256]{1,0:T(8,128)S(1)} collective-permute-done((f32[48,256]{1,0:T(8,128)S(1)}, f32[48,256]{1,0:T(8,128)S(1)}, u32[]{:S(2)}, u32[]{:S(2)}) %collective-permute-start.23) | collective-permute-done | bytes 49184 | tf_op jit(solution)/shard_map/ppermute | solution.py:537
  83.1 1.8 %collective-permute-start.25 = (f32[48,512]{1,0:T(8,128)S(1)}, f32[48,512]{1,0:T(8,128)S(1)}, u32[]{:S(2)}, u32[]{:S(2)}) collective-permute-start(f32[48,512]{1,0:T(8,128)S(1)} %get-tuple-element.233), channel_id=1, source_target_pairs={{0,124},{4,8},{8,4},{12,16},{16,12},{20,24},{24,20},{28,32},{32,28... | collective-permute-start | bytes 294920 | tf_op jit(solution)/shard_map/ppermute | solution.py:537
  85.2 1.9 %collective-permute-start.27 = (f32[48,256]{1,0:T(8,128)S(1)}, f32[48,256]{1,0:T(8,128)S(1)}, u32[]{:S(2)}, u32[]{:S(2)}) collective-permute-start(f32[48,256]{1,0:T(8,128)S(1)} %get-tuple-element.235), channel_id=1, source_target_pairs={{0,3},{1,2},{2,1},{3,0},{4,7},{5,6},{6,5},{7,4},{8,11},{9,10},{10,... | collective-permute-start | bytes 147464 | tf_op jit(solution)/shard_map/ppermute | solution.py:537
  87.1 3.2 %shard_map.129 = (f32[192,1024]{1,0:T(8,128)S(1)}, f32[192,1024]{1,0:T(8,128)}, f32[1536,128]{1,0:T(8,128)}, f32[192,1024]{1,0:T(8,128)}) custom-call(f32[192,1024]{1,0:T(8,128)S(1)} %get-tuple-element.214.part_ref, f32[192,1024]{1,0:T(8,128)S(1)} %get-tuple-element.215.r_ref, f32[192,1024]{1,0:T(8,128)S(1)} %get-tuple-element.216.d_ref, ...), custom_call_target="tpu_custom_call" | custom-call | tf_op jit(solution)/shard_map/pallas_call | solution.py:520
  90.6 1.4 %shard_map.130 = f32[1536,128]{1,0:T(8,128)} custom-call(f32[192,1024]{1,0:T(8,128)S(1)} %get-tuple-element.231.base_ref, s32[48,128]{1,0:T(8,128)S(1)} %get-tuple-element.122.ori_ref, bf16[4,192,288]{2,1,0:T(8,128)(2,1)S(1)} %get-tuple-element.132.halo_ref, f32[48,512]{1,0:T(8,128)S(1)} %collective-permute-done.24.gx_in, ...), custom_call_target="tpu_custom_call" | custom-call | tf_op jit(solution)/shard_map/pallas_call | solution.py:520
  (46 shorter events, 9.4 us)
Async XLA Ops:
  2.2 13.4 %collective-permute-start = (f32[48,512]{1,0:T(8,128)S(1)}, f32[48,512]{1,0:T(8,128)S(1)}, u32[]{:S(2)}, u32[]{:S(2)}) collective-permute-start(f32[48,512]{1,0:T(8,128)S(1)} %get-tuple-element.134), channel_id=1, source_target_pairs={{0,4},{4,0},{8,12},{12,8},{16,20},{20,16},{24,28},{28,24},{32,36},... | collective-permute-start | bytes 294920 | tf_op jit(solution)/shard_map/ppermute | solution.py:532
  2.3 13.4 %collective-permute-start.1 = (f32[48,512]{1,0:T(8,128)S(1)}, f32[48,512]{1,0:T(8,128)S(1)}, u32[]{:S(2)}, u32[]{:S(2)}) collective-permute-start(f32[48,512]{1,0:T(8,128)S(1)} %get-tuple-element.135), channel_id=1, source_target_pairs={{0,124},{4,8},{8,4},{12,16},{16,12},{20,24},{24,20},{28,32},{32,28... | collective-permute-start | bytes 294920 | tf_op jit(solution)/shard_map/ppermute | solution.py:537
  8.7 6.9 %collective-permute-start.2 = (f32[48,256]{1,0:T(8,128)S(1)}, f32[48,256]{1,0:T(8,128)S(1)}, u32[]{:S(2)}, u32[]{:S(2)}) collective-permute-start(f32[48,256]{1,0:T(8,128)S(1)} %get-tuple-element.136), channel_id=1, source_target_pairs={{0,1},{1,0},{2,3},{3,2},{4,5},{5,4},{6,7},{7,6},{8,9},{9,8},{10,11... | collective-permute-start | bytes 147464 | tf_op jit(solution)/shard_map/ppermute | solution.py:532
  10.3 5.3 %collective-permute-start.3 = (f32[48,256]{1,0:T(8,128)S(1)}, f32[48,256]{1,0:T(8,128)S(1)}, u32[]{:S(2)}, u32[]{:S(2)}) collective-permute-start(f32[48,256]{1,0:T(8,128)S(1)} %get-tuple-element.137), channel_id=1, source_target_pairs={{0,3},{1,2},{2,1},{3,0},{4,7},{5,6},{6,5},{7,4},{8,11},{9,10},{10,... | collective-permute-start | bytes 147464 | tf_op jit(solution)/shard_map/ppermute | solution.py:537
  16.1 7.5 %collective-permute-start.4 = (f32[48,512]{1,0:T(8,128)S(1)}, f32[48,512]{1,0:T(8,128)S(1)}, u32[]{:S(2)}, u32[]{:S(2)}) collective-permute-start(f32[48,512]{1,0:T(8,128)S(1)} %get-tuple-element.151), channel_id=1, source_target_pairs={{0,4},{4,0},{8,12},{12,8},{16,20},{20,16},{24,28},{28,24},{32,36},... | collective-permute-start | bytes 294920 | tf_op jit(solution)/shard_map/ppermute | solution.py:532
  16.2 7.4 %collective-permute-start.5 = (f32[48,512]{1,0:T(8,128)S(1)}, f32[48,512]{1,0:T(8,128)S(1)}, u32[]{:S(2)}, u32[]{:S(2)}) collective-permute-start(f32[48,512]{1,0:T(8,128)S(1)} %get-tuple-element.152), channel_id=1, source_target_pairs={{0,124},{4,8},{8,4},{12,16},{16,12},{20,24},{24,20},{28,32},{32,28... | collective-permute-start | bytes 294920 | tf_op jit(solution)/shard_map/ppermute | solution.py:537
  17.2 6.0 %collective-permute-start.6 = (f32[48,256]{1,0:T(8,128)S(1)}, f32[48,256]{1,0:T(8,128)S(1)}, u32[]{:S(2)}, u32[]{:S(2)}) collective-permute-start(f32[48,256]{1,0:T(8,128)S(1)} %get-tuple-element.153), channel_id=1, source_target_pairs={{0,1},{1,0},{2,3},{3,2},{4,5},{5,4},{6,7},{7,6},{8,9},{9,8},{10,11... | collective-permute-start | bytes 147464 | tf_op jit(solution)/shard_map/ppermute | solution.py:532
  18.3 5.3 %collective-permute-start.7 = (f32[48,256]{1,0:T(8,128)S(1)}, f32[48,256]{1,0:T(8,128)S(1)}, u32[]{:S(2)}, u32[]{:S(2)}) collective-permute-start(f32[48,256]{1,0:T(8,128)S(1)} %get-tuple-element.154), channel_id=1, source_target_pairs={{0,3},{1,2},{2,1},{3,0},{4,7},{5,6},{6,5},{7,4},{8,11},{9,10},{10,... | collective-permute-start | bytes 147464 | tf_op jit(solution)/shard_map/ppermute | solution.py:537
  20.5 24.2 %copy-start = (f32[1,32,32,24,24]{2,4,3,1,0:T(8,128)S(1)}, f32[1,32,32,24,24]{2,4,3,1,0:T(8,128)}, u32[]{:S(2)}) copy-start(f32[1,32,32,24,24]{2,4,3,1,0:T(8,128)} %param.18) | copy-start | bytes 7077892
  24.1 8.9 %collective-permute-start.8 = (f32[48,512]{1,0:T(8,128)S(1)}, f32[48,512]{1,0:T(8,128)S(1)}, u32[]{:S(2)}, u32[]{:S(2)}) collective-permute-start(f32[48,512]{1,0:T(8,128)S(1)} %get-tuple-element.170), channel_id=1, source_target_pairs={{0,4},{4,0},{8,12},{12,8},{16,20},{20,16},{24,28},{28,24},{32,36},... | collective-permute-start | bytes 294920 | tf_op jit(solution)/shard_map/ppermute | solution.py:532
  24.2 8.8 %collective-permute-start.9 = (f32[48,512]{1,0:T(8,128)S(1)}, f32[48,512]{1,0:T(8,128)S(1)}, u32[]{:S(2)}, u32[]{:S(2)}) collective-permute-start(f32[48,512]{1,0:T(8,128)S(1)} %get-tuple-element.171), channel_id=1, source_target_pairs={{0,124},{4,8},{8,4},{12,16},{16,12},{20,24},{24,20},{28,32},{32,28... | collective-permute-start | bytes 294920 | tf_op jit(solution)/shard_map/ppermute | solution.py:537
  26.6 5.5 %collective-permute-start.10 = (f32[48,256]{1,0:T(8,128)S(1)}, f32[48,256]{1,0:T(8,128)S(1)}, u32[]{:S(2)}, u32[]{:S(2)}) collective-permute-start(f32[48,256]{1,0:T(8,128)S(1)} %get-tuple-element.172), channel_id=1, source_target_pairs={{0,1},{1,0},{2,3},{3,2},{4,5},{5,4},{6,7},{7,6},{8,9},{9,8},{10,11... | collective-permute-start | bytes 147464 | tf_op jit(solution)/shard_map/ppermute | solution.py:532
  27.7 5.3 %collective-permute-start.11 = (f32[48,256]{1,0:T(8,128)S(1)}, f32[48,256]{1,0:T(8,128)S(1)}, u32[]{:S(2)}, u32[]{:S(2)}) collective-permute-start(f32[48,256]{1,0:T(8,128)S(1)} %get-tuple-element.173), channel_id=1, source_target_pairs={{0,3},{1,2},{2,1},{3,0},{4,7},{5,6},{6,5},{7,4},{8,11},{9,10},{10,... | collective-permute-start | bytes 147464 | tf_op jit(solution)/shard_map/ppermute | solution.py:537
  57.6 8.4 %collective-permute-start.12 = (f32[48,512]{1,0:T(8,128)S(1)}, f32[48,512]{1,0:T(8,128)S(1)}, u32[]{:S(2)}, u32[]{:S(2)}) collective-permute-start(f32[48,512]{1,0:T(8,128)S(1)} %get-tuple-element.186), channel_id=1, source_target_pairs={{0,4},{4,0},{8,12},{12,8},{16,20},{20,16},{24,28},{28,24},{32,36},... | collective-permute-start | bytes 294920 | tf_op jit(solution)/shard_map/ppermute | solution.py:532
  57.8 8.2 %collective-permute-start.13 = (f32[48,512]{1,0:T(8,128)S(1)}, f32[48,512]{1,0:T(8,128)S(1)}, u32[]{:S(2)}, u32[]{:S(2)}) collective-permute-start(f32[48,512]{1,0:T(8,128)S(1)} %get-tuple-element.187), channel_id=1, source_target_pairs={{0,124},{4,8},{8,4},{12,16},{16,12},{20,24},{24,20},{28,32},{32,28... | collective-permute-start | bytes 294920 | tf_op jit(solution)/shard_map/ppermute | solution.py:537
  59.7 4.5 %collective-permute-start.14 = (f32[48,256]{1,0:T(8,128)S(1)}, f32[48,256]{1,0:T(8,128)S(1)}, u32[]{:S(2)}, u32[]{:S(2)}) collective-permute-start(f32[48,256]{1,0:T(8,128)S(1)} %get-tuple-element.188), channel_id=1, source_target_pairs={{0,1},{1,0},{2,3},{3,2},{4,5},{5,4},{6,7},{7,6},{8,9},{9,8},{10,11... | collective-permute-start | bytes 147464 | tf_op jit(solution)/shard_map/ppermute | solution.py:532
  60.7 5.3 %collective-permute-start.15 = (f32[48,256]{1,0:T(8,128)S(1)}, f32[48,256]{1,0:T(8,128)S(1)}, u32[]{:S(2)}, u32[]{:S(2)}) collective-permute-start(f32[48,256]{1,0:T(8,128)S(1)} %get-tuple-element.189), channel_id=1, source_target_pairs={{0,3},{1,2},{2,1},{3,0},{4,7},{5,6},{6,5},{7,4},{8,11},{9,10},{10,... | collective-permute-start | bytes 147464 | tf_op jit(solution)/shard_map/ppermute | solution.py:537
  66.5 7.5 %collective-permute-start.16 = (f32[48,512]{1,0:T(8,128)S(1)}, f32[48,512]{1,0:T(8,128)S(1)}, u32[]{:S(2)}, u32[]{:S(2)}) collective-permute-start(f32[48,512]{1,0:T(8,128)S(1)} %get-tuple-element.202), channel_id=1, source_target_pairs={{0,4},{4,0},{8,12},{12,8},{16,20},{20,16},{24,28},{28,24},{32,36},... | collective-permute-start | bytes 294920 | tf_op jit(solution)/shard_map/ppermute | solution.py:532
  66.6 7.4 %collective-permute-start.17 = (f32[48,512]{1,0:T(8,128)S(1)}, f32[48,512]{1,0:T(8,128)S(1)}, u32[]{:S(2)}, u32[]{:S(2)}) collective-permute-start(f32[48,512]{1,0:T(8,128)S(1)} %get-tuple-element.203), channel_id=1, source_target_pairs={{0,124},{4,8},{8,4},{12,16},{16,12},{20,24},{24,20},{28,32},{32,28... | collective-permute-start | bytes 294920 | tf_op jit(solution)/shard_map/ppermute | solution.py:537
  68.4 4.1 %collective-permute-start.18 = (f32[48,256]{1,0:T(8,128)S(1)}, f32[48,256]{1,0:T(8,128)S(1)}, u32[]{:S(2)}, u32[]{:S(2)}) collective-permute-start(f32[48,256]{1,0:T(8,128)S(1)} %get-tuple-element.204), channel_id=1, source_target_pairs={{0,1},{1,0},{2,3},{3,2},{4,5},{5,4},{6,7},{7,6},{8,9},{9,8},{10,11... | collective-permute-start | bytes 147464 | tf_op jit(solution)/shard_map/ppermute | solution.py:532
  68.7 5.3 %collective-permute-start.19 = (f32[48,256]{1,0:T(8,128)S(1)}, f32[48,256]{1,0:T(8,128)S(1)}, u32[]{:S(2)}, u32[]{:S(2)}) collective-permute-start(f32[48,256]{1,0:T(8,128)S(1)} %get-tuple-element.205), channel_id=1, source_target_pairs={{0,3},{1,2},{2,1},{3,0},{4,7},{5,6},{6,5},{7,4},{8,11},{9,10},{10,... | collective-permute-start | bytes 147464 | tf_op jit(solution)/shard_map/ppermute | solution.py:537
  74.5 8.1 %collective-permute-start.20 = (f32[48,512]{1,0:T(8,128)S(1)}, f32[48,512]{1,0:T(8,128)S(1)}, u32[]{:S(2)}, u32[]{:S(2)}) collective-permute-start(f32[48,512]{1,0:T(8,128)S(1)} %get-tuple-element.218), channel_id=1, source_target_pairs={{0,4},{4,0},{8,12},{12,8},{16,20},{20,16},{24,28},{28,24},{32,36},... | collective-permute-start | bytes 294920 | tf_op jit(solution)/shard_map/ppermute | solution.py:532
  74.6 8.0 %collective-permute-start.21 = (f32[48,512]{1,0:T(8,128)S(1)}, f32[48,512]{1,0:T(8,128)S(1)}, u32[]{:S(2)}, u32[]{:S(2)}) collective-permute-start(f32[48,512]{1,0:T(8,128)S(1)} %get-tuple-element.219), channel_id=1, source_target_pairs={{0,124},{4,8},{8,4},{12,16},{16,12},{20,24},{24,20},{28,32},{32,28... | collective-permute-start | bytes 294920 | tf_op jit(solution)/shard_map/ppermute | solution.py:537
  76.7 4.7 %collective-permute-start.22 = (f32[48,256]{1,0:T(8,128)S(1)}, f32[48,256]{1,0:T(8,128)S(1)}, u32[]{:S(2)}, u32[]{:S(2)}) collective-permute-start(f32[48,256]{1,0:T(8,128)S(1)} %get-tuple-element.220), channel_id=1, source_target_pairs={{0,1},{1,0},{2,3},{3,2},{4,5},{5,4},{6,7},{7,6},{8,9},{9,8},{10,11... | collective-permute-start | bytes 147464 | tf_op jit(solution)/shard_map/ppermute | solution.py:532
  77.3 5.3 %collective-permute-start.23 = (f32[48,256]{1,0:T(8,128)S(1)}, f32[48,256]{1,0:T(8,128)S(1)}, u32[]{:S(2)}, u32[]{:S(2)}) collective-permute-start(f32[48,256]{1,0:T(8,128)S(1)} %get-tuple-element.221), channel_id=1, source_target_pairs={{0,3},{1,2},{2,1},{3,0},{4,7},{5,6},{6,5},{7,4},{8,11},{9,10},{10,... | collective-permute-start | bytes 147464 | tf_op jit(solution)/shard_map/ppermute | solution.py:537
  83.0 7.5 %collective-permute-start.24 = (f32[48,512]{1,0:T(8,128)S(1)}, f32[48,512]{1,0:T(8,128)S(1)}, u32[]{:S(2)}, u32[]{:S(2)}) collective-permute-start(f32[48,512]{1,0:T(8,128)S(1)} %get-tuple-element.232), channel_id=1, source_target_pairs={{0,4},{4,0},{8,12},{12,8},{16,20},{20,16},{24,28},{28,24},{32,36},... | collective-permute-start | bytes 294920 | tf_op jit(solution)/shard_map/ppermute | solution.py:532
  83.1 7.4 %collective-permute-start.25 = (f32[48,512]{1,0:T(8,128)S(1)}, f32[48,512]{1,0:T(8,128)S(1)}, u32[]{:S(2)}, u32[]{:S(2)}) collective-permute-start(f32[48,512]{1,0:T(8,128)S(1)} %get-tuple-element.233), channel_id=1, source_target_pairs={{0,124},{4,8},{8,4},{12,16},{16,12},{20,24},{24,20},{28,32},{32,28... | collective-permute-start | bytes 294920 | tf_op jit(solution)/shard_map/ppermute | solution.py:537
  84.9 5.4 %collective-permute-start.26 = (f32[48,256]{1,0:T(8,128)S(1)}, f32[48,256]{1,0:T(8,128)S(1)}, u32[]{:S(2)}, u32[]{:S(2)}) collective-permute-start(f32[48,256]{1,0:T(8,128)S(1)} %get-tuple-element.234), channel_id=1, source_target_pairs={{0,1},{1,0},{2,3},{3,2},{4,5},{5,4},{6,7},{7,6},{8,9},{9,8},{10,11... | collective-permute-start | bytes 147464 | tf_op jit(solution)/shard_map/ppermute | solution.py:532
  85.2 5.3 %collective-permute-start.27 = (f32[48,256]{1,0:T(8,128)S(1)}, f32[48,256]{1,0:T(8,128)S(1)}, u32[]{:S(2)}, u32[]{:S(2)}) collective-permute-start(f32[48,256]{1,0:T(8,128)S(1)} %get-tuple-element.235), channel_id=1, source_target_pairs={{0,3},{1,2},{2,1},{3,0},{4,7},{5,6},{6,5},{7,4},{8,11},{9,10},{10,... | collective-permute-start | bytes 147464 | tf_op jit(solution)/shard_map/ppermute | solution.py:537

commit v10 on v9

--- a/solution.py
+++ b/solution.py
@@ -370,7 +370,13 @@
         te_ref, *rest = rest
     elif then == "restrict":
         pt_ref, *rest = rest
-    r_out, d_out, x_out, part_out, *outs, xh_ref, xl_ref, t_ref, ad_ref = rest
+    if then == "close":
+        r_out, x_hbm, xh_ref, xl_ref, t_ref, ad_ref, d_out, part_out, x_out, sems = rest
+        outs = ()
+    elif then == "restrict":
+        r_out, x_out, part_out, *outs, xh_ref, xl_ref, t_ref, ad_ref, d_out = rest
+    else:
+        r_out, d_out, x_out, part_out, *outs, xh_ref, xl_ref, t_ref, ad_ref = rest
     add_halo(ad_ref, part_ref, halo_ref, [v[...] for v in (lx_ref, ux_ref, ly_ref, uy_ref)])
     keep, gain = scales
     for col in range(COLS):
@@ -386,6 +392,9 @@
             x_out[pl.ds(col, BLOCK, stride=COLS), :] = total
         else:
             x_out[:, at] = total
+    if then == "close":
+        leaving = pltpu.make_async_copy(x_out, x_hbm, sems.at[0])
+        leaving.start()
     interior(d_out, coef_ref, ori_ref, wh_ref, wl_ref, sel_ref, part_out, xh_ref, xl_ref, t_ref)
     if onward is not None:
         ahead(onward, r_out, d_out, part_out, coef_ref, sel_ref, outs[0:4])
@@ -397,6 +406,7 @@
         outs[0][...] = both[0:CW] + both[CW:] + dot(pt_ref[0:CW, :], low)
     elif then == "close":
         r_out[...] = r_out[...] - part_out[...]
+        leaving.wait()
 
 
 def routed(v, one_hot_ref):
@@ -521,7 +531,10 @@
         kernel,
         out_shape=outs,
         in_specs=specs,
-        out_specs=[pl.BlockSpec(memory_space=out_space)] * len(outs),
+        out_specs=[
+            pl.BlockSpec(memory_space=out_space[n] if isinstance(out_space, tuple) else out_space)
+            for n in range(len(outs))
+        ],
         scratch_shapes=list(scratch),
         compiler_params=pltpu.CompilerParams(vmem_limit_bytes=limit << 20),
     )(*placed)
@@ -599,13 +612,26 @@
             [coef, ori, rim, *gets, *pres],
         )
         gets = exchange(sends)
-        x_out = jax.ShapeDtypeStruct(rows, F32) if then == "close" else full
-        r, d, x, part, *outs = call(
+        scratch = [*products, full]
+        spaces = pltpu.VMEM
+        if then == "close":
+            shapes = [full, jax.ShapeDtypeStruct(rows, F32)]
+            scratch = [*scratch, full, full, field(*rows), dma((1,))]
+            spaces = (pltpu.VMEM, pltpu.HBM)
+        elif then == "restrict":
+            shapes, scratch = [full, full, full, *extra_outs], [*scratch, full]
+        else:
+            shapes = [full, full, full, full, *SENDS, *extra_outs]
+        outs = call(
             functools.partial(step_kernel, scales, onward, then),
-            [full, full, x_out, full, *([] if onward is None else SENDS), *extra_outs],
+            shapes,
             [part, r, d, x, *tables, halo, lx, ux, ly, uy, *extra],
-            [*products, full],
+            scratch,
+            out_space=spaces,
         )
+        if then in ("close", "restrict"):
+            return *outs, gets
+        r, d, x, part, *outs = outs
         return part, r, d, x, gets, outs
 
     second, third = chebyshev()
@@ -618,7 +644,7 @@
         second, third, part, r, d, d, gets, pres, "hots", [te], [hots, hots]
     )
     coarse = field(CW, ELEMS)
-    part, r, d, x, gets, (pre,) = step(
+    r, x, part, pre, gets = step(
         third, None, part, r, d, x, gets, pres, "restrict", [pt], [coarse]
     )
     packets = field(OWNERS, 8, LANES)
@@ -639,7 +665,7 @@
     )
     part, r, d, x, gets, pres = step(opening, second, part, r, r, x, gets, pres)
     part, r, d, x, gets, pres = step(second, third, part, r, d, x, gets, pres)
-    part, r, _, x, gets, _ = step(third, None, part, r, d, x, gets, pres, "close")
+    r, x, gets = step(third, None, part, r, d, x, gets, pres, "close")
     r = call(
         last_kernel,
         [jax.ShapeDtypeStruct(rows, F32)],

time: 92.3 us -> 92.2 us (level)
  Pallas kernels: 27 us -> 25.2 us
  waiting for transfers between devices: 6.32 us -> 8.04 us
    pallas_call x18, Pallas kernels: 27 us -> 25.2 us  [call(): pl.pallas_call(kernel, out_shape=outs, in_specs=specs, out_specs=[pl.Bloc...]
    ppermute x14, waiting for transfers between devices: 6.13 us -> 7.94 us  [swap_odd(): lax.ppermute(v, axis, [(i, (i + 1 if i % 2 else i - 1) % count) for i in...]
  transfers between devices with their start and end apart: 28 -> 28, of which waited for: 8 -> 8; matrix products, arithmetic and copies ran while one was open for 0% -> 0% of each run, Pallas kernels for 21% -> 19%
where the time goes in v10:
time: 92.2 us; the launch traced here: 92 us
  starting transfers between devices  35.6 us (39%)
  Pallas kernels  25.2 us (27%)
  blocking collectives  22 us (24%)
  waiting for transfers between devices  8.04 us (9%)
  between operations  1.08 us (1%)
    ppermute x14, starting transfers between devices, swap_odd(): lax.ppermute(v, axis, [(i, (i + 1 if i % 2 else i - 1) % count) for i in...  29 us
    pallas_call x18, Pallas kernels, call(): pl.pallas_call(kernel, out_shape=outs, in_specs=specs, out_specs=[pl.Bloc...  25.2 us
    all_to_all x1, blocking collectives, shards(): sol = lax.all_to_all(sol, 'gx', split_axis=0, concat_axis=0, tiled=True)  11.3 us
    all_to_all x1, blocking collectives, shards(): rhs = lax.all_to_all(rhs, 'gx', split_axis=0, concat_axis=0, tiled=True)  10.8 us
    ppermute x14, waiting for transfers between devices, swap_odd(): lax.ppermute(v, axis, [(i, (i + 1 if i % 2 else i - 1) % count) for i in...  7.94 us
    ppermute x14, starting transfers between devices, swap_even(): return lax.ppermute(v, axis, [(i, i ^ 1) for i in range(count)])  6.58 us
  transfers between devices with their start and end apart: 28, of which 8 were waited for; matrix products, arithmetic and copies ran while one was open for 0% of the time, Pallas kernels for 19%

profile of v10, /device:TPU:0, one launch (start us, length us, event | category | flops | bytes accessed | tf_op | source)
XLA Modules:
  0.0 92.0 jit_solution(6896360603369136083)
XLA Ops:
  0.6 1.6 %shard_map.113 = (f32[192,1024]{1,0:T(8,128)S(1)}, f32[192,1024]{1,0:T(8,128)S(1)}, f32[8,128]{1,0:T(8,128)S(1)}, s32[48,128]{1,0:T(8,128)S(1)}, bf16[192,192]{1...) custom-call(f32[1536,128]{1,0:T(8,128)} %bitcast.15, ...), custom_call_target="tpu_custom_call" | custom-call | tf_op jit(solution)/shard_map/pallas_call | solution.py:530
  2.3 6.4 %collective-permute-start.1 = (f32[48,512]{1,0:T(8,128)S(1)}, f32[48,512]{1,0:T(8,128)S(1)}, u32[]{:S(2)}, u32[]{:S(2)}) collective-permute-start(f32[48,512]{1,0:T(8,128)S(1)} %get-tuple-element.135), channel_id=1, source_target_pairs={{0,124},{4,8},{8,4},{12,16},{16,12},{20,24},{24,20},{28,32},{32,28... | collective-permute-start | bytes 294920 | tf_op jit(solution)/shard_map/ppermute | solution.py:550
  8.7 1.6 %collective-permute-start.2 = (f32[48,256]{1,0:T(8,128)S(1)}, f32[48,256]{1,0:T(8,128)S(1)}, u32[]{:S(2)}, u32[]{:S(2)}) collective-permute-start(f32[48,256]{1,0:T(8,128)S(1)} %get-tuple-element.136), channel_id=1, source_target_pairs={{0,1},{1,0},{2,3},{3,2},{4,5},{5,4},{6,7},{7,6},{8,9},{9,8},{10,11... | collective-permute-start | bytes 147464 | tf_op jit(solution)/shard_map/ppermute | solution.py:545
  10.3 2.2 %collective-permute-start.3 = (f32[48,256]{1,0:T(8,128)S(1)}, f32[48,256]{1,0:T(8,128)S(1)}, u32[]{:S(2)}, u32[]{:S(2)}) collective-permute-start(f32[48,256]{1,0:T(8,128)S(1)} %get-tuple-element.137), channel_id=1, source_target_pairs={{0,3},{1,2},{2,1},{3,0},{4,7},{5,6},{6,5},{7,4},{8,11},{9,10},{10,... | collective-permute-start | bytes 147464 | tf_op jit(solution)/shard_map/ppermute | solution.py:550
  12.5 1.2 %shard_map.114 = (bf16[192,768]{1,0:T(8,128)(2,1)S(1)}, bf16[192,768]{1,0:T(8,128)(2,1)S(1)}, bf16[4,192,288]{2,1,0:T(8,128)(2,1)S(1)}, bf16[4,144,288]{2,1,0:T(...) custom-call(f32[192,192]{1,0:T(8,128)S(1)} %get-tuple-element.123.st, ...), custom_call_target="tpu_custom_call" | custom-call | tf_op jit(solution)/shard_map/pallas_call | solution.py:530
  13.7 1.9 %shard_map.115 = (f32[192,1024]{1,0:T(8,128)S(1)}, f32[48,512]{1,0:T(8,128)S(1)}, f32[48,512]{1,0:T(8,128)S(1)}, f32[48,256]{1,0:T(8,128)S(1)}, f32[48,256]{1,0:T(8,128)S(1)}) custom-call(f32[192,1024]{1,0:T(8,128)S(1)} %get-tuple-element.119.r_ref, f32[192,1024]{1,0:T(8,128)S(1)} %get-tuple-element.120.d_ref.x_ref, ...), custom_call_target="tpu_custom_call" | custom-call | tf_op jit(solution)/shard_map/pallas_call | solution.py:530
  17.2 1.1 %collective-permute-start.6 = (f32[48,256]{1,0:T(8,128)S(1)}, f32[48,256]{1,0:T(8,128)S(1)}, u32[]{:S(2)}, u32[]{:S(2)}) collective-permute-start(f32[48,256]{1,0:T(8,128)S(1)} %get-tuple-element.153), channel_id=1, source_target_pairs={{0,1},{1,0},{2,3},{3,2},{4,5},{5,4},{6,7},{7,6},{8,9},{9,8},{10,11... | collective-permute-start | bytes 147464 | tf_op jit(solution)/shard_map/ppermute | solution.py:545
  18.3 2.2 %collective-permute-start.7 = (f32[48,256]{1,0:T(8,128)S(1)}, f32[48,256]{1,0:T(8,128)S(1)}, u32[]{:S(2)}, u32[]{:S(2)}) collective-permute-start(f32[48,256]{1,0:T(8,128)S(1)} %get-tuple-element.154), channel_id=1, source_target_pairs={{0,3},{1,2},{2,1},{3,0},{4,7},{5,6},{6,5},{7,4},{8,11},{9,10},{10,... | collective-permute-start | bytes 147464 | tf_op jit(solution)/shard_map/ppermute | solution.py:550
  20.5 2.7 %shard_map.117 = (f32[192,1024]{1,0:T(8,128)S(1)}, f32[192,1024]{1,0:T(8,128)S(1)}, f32[192,1024]{1,0:T(8,128)S(1)}, f32[192,1024]{1,0:T(8,128)S(1)}, f32[48,512...) custom-call(f32[192,1024]{1,0:T(8,128)S(1)} %get-tuple-element.131.p, ...), custom_call_target="tpu_custom_call" | custom-call | tf_op jit(solution)/shard_map/pallas_call | solution.py:530
  24.2 2.3 %collective-permute-start.9 = (f32[48,512]{1,0:T(8,128)S(1)}, f32[48,512]{1,0:T(8,128)S(1)}, u32[]{:S(2)}, u32[]{:S(2)}) collective-permute-start(f32[48,512]{1,0:T(8,128)S(1)} %get-tuple-element.171), channel_id=1, source_target_pairs={{0,124},{4,8},{8,4},{12,16},{16,12},{20,24},{24,20},{28,32},{32,28... | collective-permute-start | bytes 294920 | tf_op jit(solution)/shard_map/ppermute | solution.py:550
  26.6 1.1 %collective-permute-start.10 = (f32[48,256]{1,0:T(8,128)S(1)}, f32[48,256]{1,0:T(8,128)S(1)}, u32[]{:S(2)}, u32[]{:S(2)}) collective-permute-start(f32[48,256]{1,0:T(8,128)S(1)} %get-tuple-element.172), channel_id=1, source_target_pairs={{0,1},{1,0},{2,3},{3,2},{4,5},{5,4},{6,7},{7,6},{8,9},{9,8},{10,11... | collective-permute-start | bytes 147464 | tf_op jit(solution)/shard_map/ppermute | solution.py:545
  27.7 1.1 %collective-permute-start.11 = (f32[48,256]{1,0:T(8,128)S(1)}, f32[48,256]{1,0:T(8,128)S(1)}, u32[]{:S(2)}, u32[]{:S(2)}) collective-permute-start(f32[48,256]{1,0:T(8,128)S(1)} %get-tuple-element.173), channel_id=1, source_target_pairs={{0,3},{1,2},{2,1},{3,0},{4,7},{5,6},{6,5},{7,4},{8,11},{9,10},{10,... | collective-permute-start | bytes 147464 | tf_op jit(solution)/shard_map/ppermute | solution.py:550
  28.8 2.4 %shard_map.119 = (f32[192,1024]{1,0:T(8,128)S(1)}, f32[192,1024]{1,0:T(8,128)S(1)}, f32[192,1024]{1,0:T(8,128)S(1)}, f32[24,1024]{1,0:T(8,128)S(1)}) custom-call(f32[192,1024]{1,0:T(8,128)S(1)} %get-tuple-element.147.part_ref, f32[192,1024]{1,0:T(8,128)S(1)} %get-tuple-element.148.r_ref, f32[192,1024]{1,0:T(8,128)S(1)} %get-tuple-element.149.d_ref, ...), custom_call_target="tpu_custom_call" | custom-call | tf_op jit(solution)/shard_map/pallas_call | solution.py:530
  31.2 1.8 %collective-permute-done.11.gy_out = f32[48,256]{1,0:T(8,128)S(1)} collective-permute-done((f32[48,256]{1,0:T(8,128)S(1)}, f32[48,256]{1,0:T(8,128)S(1)}, u32[]{:S(2)}, u32[]{:S(2)}) %collective-permute-start.11) | collective-permute-done | bytes 49184 | tf_op jit(solution)/shard_map/ppermute | solution.py:550
  33.8 10.8 %all_to_all.10.rhs_ref = f32[32,8,128]{2,1,0:T(8,128)S(1)} all-to-all(f32[32,8,128]{2,1,0:T(8,128)S(1)} %get-tuple-element.174), channel_id=1, replica_groups=mesh['gx'=32,'gy'=4] {'gx'}, dimensions={0} | all-to-all | bytes 262144 | tf_op jit(solution)/shard_map/all_to_all | solution.py:654
  45.6 11.3 %all_to_all.11.sol_in = f32[32,8,128]{2,1,0:T(8,128)S(1)} all-to-all(f32[32,8,128]{2,1,0:T(8,128)S(1)} %shard_map.121), channel_id=1, replica_groups=mesh['gx'=32,'gy'=4] {'gx'}, dimensions={0} | all-to-all | bytes 262144 | tf_op jit(solution)/shard_map/all_to_all | solution.py:657
  57.8 1.9 %collective-permute-start.13 = (f32[48,512]{1,0:T(8,128)S(1)}, f32[48,512]{1,0:T(8,128)S(1)}, u32[]{:S(2)}, u32[]{:S(2)}) collective-permute-start(f32[48,512]{1,0:T(8,128)S(1)} %get-tuple-element.187), channel_id=1, source_target_pairs={{0,124},{4,8},{8,4},{12,16},{16,12},{20,24},{24,20},{28,32},{32,28... | collective-permute-start | bytes 294920 | tf_op jit(solution)/shard_map/ppermute | solution.py:550
  61.3 2.4 %shard_map.123 = (f32[192,1024]{1,0:T(8,128)S(1)}, f32[192,1024]{1,0:T(8,128)S(1)}, f32[192,1024]{1,0:T(8,128)S(1)}, f32[48,512]{1,0:T(8,128)S(1)}, f32[48,512]{...) custom-call(f32[192,1024]{1,0:T(8,128)S(1)} %get-tuple-element.164.part_ref, ...), custom_call_target="tpu_custom_call" | custom-call | tf_op jit(solution)/shard_map/pallas_call | solution.py:530
  63.7 1.8 %collective-permute-done.15.rest_3_ = f32[48,256]{1,0:T(8,128)S(1)} collective-permute-done((f32[48,256]{1,0:T(8,128)S(1)}, f32[48,256]{1,0:T(8,128)S(1)}, u32[]{:S(2)}, u32[]{:S(2)}) %collective-permute-start.15) | collective-permute-done | bytes 49184 | tf_op jit(solution)/shard_map/ppermute | solution.py:550
  66.0 1.8 %collective-permute-start.17 = (f32[48,512]{1,0:T(8,128)S(1)}, f32[48,512]{1,0:T(8,128)S(1)}, u32[]{:S(2)}, u32[]{:S(2)}) collective-permute-start(f32[48,512]{1,0:T(8,128)S(1)} %get-tuple-element.203), channel_id=1, source_target_pairs={{0,124},{4,8},{8,4},{12,16},{16,12},{20,24},{24,20},{28,32},{32,28... | collective-permute-start | bytes 294920 | tf_op jit(solution)/shard_map/ppermute | solution.py:550
  68.2 1.8 %collective-permute-start.19 = (f32[48,256]{1,0:T(8,128)S(1)}, f32[48,256]{1,0:T(8,128)S(1)}, u32[]{:S(2)}, u32[]{:S(2)}) collective-permute-start(f32[48,256]{1,0:T(8,128)S(1)} %get-tuple-element.205), channel_id=1, source_target_pairs={{0,3},{1,2},{2,1},{3,0},{4,7},{5,6},{6,5},{7,4},{8,11},{9,10},{10,... | collective-permute-start | bytes 147464 | tf_op jit(solution)/shard_map/ppermute | solution.py:550
  70.0 2.3 %shard_map.125 = (f32[192,1024]{1,0:T(8,128)S(1)}, f32[192,1024]{1,0:T(8,128)S(1)}, f32[192,1024]{1,0:T(8,128)S(1)}, f32[192,1024]{1,0:T(8,128)S(1)}, f32[48,512...) custom-call(f32[192,1024]{1,0:T(8,128)S(1)} %get-tuple-element.183.part_ref, ...), custom_call_target="tpu_custom_call" | custom-call | tf_op jit(solution)/shard_map/pallas_call | solution.py:530
  72.3 1.2 %collective-permute-done.19.rest_3_ = f32[48,256]{1,0:T(8,128)S(1)} collective-permute-done((f32[48,256]{1,0:T(8,128)S(1)}, f32[48,256]{1,0:T(8,128)S(1)}, u32[]{:S(2)}, u32[]{:S(2)}) %collective-permute-start.19) | collective-permute-done | bytes 49184 | tf_op jit(solution)/shard_map/ppermute | solution.py:550
  74.0 2.2 %collective-permute-start.21 = (f32[48,512]{1,0:T(8,128)S(1)}, f32[48,512]{1,0:T(8,128)S(1)}, u32[]{:S(2)}, u32[]{:S(2)}) collective-permute-start(f32[48,512]{1,0:T(8,128)S(1)} %get-tuple-element.219), channel_id=1, source_target_pairs={{0,124},{4,8},{8,4},{12,16},{16,12},{20,24},{24,20},{28,32},{32,28... | collective-permute-start | bytes 294920 | tf_op jit(solution)/shard_map/ppermute | solution.py:550
  76.7 1.8 %collective-permute-start.23 = (f32[48,256]{1,0:T(8,128)S(1)}, f32[48,256]{1,0:T(8,128)S(1)}, u32[]{:S(2)}, u32[]{:S(2)}) collective-permute-start(f32[48,256]{1,0:T(8,128)S(1)} %get-tuple-element.221), channel_id=1, source_target_pairs={{0,3},{1,2},{2,1},{3,0},{4,7},{5,6},{6,5},{7,4},{8,11},{9,10},{10,... | collective-permute-start | bytes 147464 | tf_op jit(solution)/shard_map/ppermute | solution.py:550
  78.5 2.4 %shard_map.127 = (f32[192,1024]{1,0:T(8,128)S(1)}, f32[192,1024]{1,0:T(8,128)S(1)}, f32[192,1024]{1,0:T(8,128)S(1)}, f32[192,1024]{1,0:T(8,128)S(1)}, f32[48,512...) custom-call(f32[192,1024]{1,0:T(8,128)S(1)} %get-tuple-element.198.part_ref, ...), custom_call_target="tpu_custom_call" | custom-call | tf_op jit(solution)/shard_map/pallas_call | solution.py:530
  80.9 1.1 %collective-permute-done.23.rest_3_ = f32[48,256]{1,0:T(8,128)S(1)} collective-permute-done((f32[48,256]{1,0:T(8,128)S(1)}, f32[48,256]{1,0:T(8,128)S(1)}, u32[]{:S(2)}, u32[]{:S(2)}) %collective-permute-start.23) | collective-permute-done | bytes 49184 | tf_op jit(solution)/shard_map/ppermute | solution.py:550
  82.6 1.8 %collective-permute-start.25 = (f32[48,512]{1,0:T(8,128)S(1)}, f32[48,512]{1,0:T(8,128)S(1)}, u32[]{:S(2)}, u32[]{:S(2)}) collective-permute-start(f32[48,512]{1,0:T(8,128)S(1)} %get-tuple-element.233), channel_id=1, source_target_pairs={{0,124},{4,8},{8,4},{12,16},{16,12},{20,24},{24,20},{28,32},{32,28... | collective-permute-start | bytes 294920 | tf_op jit(solution)/shard_map/ppermute | solution.py:550
  85.1 1.4 %collective-permute-start.27 = (f32[48,256]{1,0:T(8,128)S(1)}, f32[48,256]{1,0:T(8,128)S(1)}, u32[]{:S(2)}, u32[]{:S(2)}) collective-permute-start(f32[48,256]{1,0:T(8,128)S(1)} %get-tuple-element.235), channel_id=1, source_target_pairs={{0,3},{1,2},{2,1},{3,0},{4,7},{5,6},{6,5},{7,4},{8,11},{9,10},{10,... | collective-permute-start | bytes 147464 | tf_op jit(solution)/shard_map/ppermute | solution.py:550
  86.5 2.3 %shard_map.129 = (f32[192,1024]{1,0:T(8,128)S(1)}, f32[1536,128]{1,0:T(8,128)}) custom-call(f32[192,1024]{1,0:T(8,128)S(1)} %get-tuple-element.214.part_ref, f32[192,1024]{1,0:T(8,128)S(1)} %get-tuple-element.215.r_ref, f32[192,1024]{1,0:T(8,128)S(1)} %get-tuple-element.216.d_ref, f32[192,1024]{1,0:T(8,128)S(1)} %get-tuple-element.217.x_ref, ...), custom_call_target="tpu_custom_call" | custom-call | tf_op jit(solution)/shard_map/pallas_call | solution.py:530
  88.8 1.6 %collective-permute-done.27.gy_out = f32[48,256]{1,0:T(8,128)S(1)} collective-permute-done((f32[48,256]{1,0:T(8,128)S(1)}, f32[48,256]{1,0:T(8,128)S(1)}, u32[]{:S(2)}, u32[]{:S(2)}) %collective-permute-start.27) | collective-permute-done | bytes 49184 | tf_op jit(solution)/shard_map/ppermute | solution.py:550
  90.4 1.4 %shard_map.130 = f32[1536,128]{1,0:T(8,128)} custom-call(f32[192,1024]{1,0:T(8,128)S(1)} %get-tuple-element.231.base_ref, s32[48,128]{1,0:T(8,128)S(1)} %get-tuple-element.122.ori_ref, bf16[4,192,288]{2,1,0:T(8,128)(2,1)S(1)} %get-tuple-element.132.halo_ref, f32[48,512]{1,0:T(8,128)S(1)} %collective-permute-done.24.gx_in, ...), custom_call_target="tpu_custom_call" | custom-call | tf_op jit(solution)/shard_map/pallas_call | solution.py:530
  (46 shorter events, 10.2 us)
Async XLA Ops:
  2.2 13.4 %collective-permute-start = (f32[48,512]{1,0:T(8,128)S(1)}, f32[48,512]{1,0:T(8,128)S(1)}, u32[]{:S(2)}, u32[]{:S(2)}) collective-permute-start(f32[48,512]{1,0:T(8,128)S(1)} %get-tuple-element.134), channel_id=1, source_target_pairs={{0,4},{4,0},{8,12},{12,8},{16,20},{20,16},{24,28},{28,24},{32,36},... | collective-permute-start | bytes 294920 | tf_op jit(solution)/shard_map/ppermute | solution.py:545
  2.3 13.4 %collective-permute-start.1 = (f32[48,512]{1,0:T(8,128)S(1)}, f32[48,512]{1,0:T(8,128)S(1)}, u32[]{:S(2)}, u32[]{:S(2)}) collective-permute-start(f32[48,512]{1,0:T(8,128)S(1)} %get-tuple-element.135), channel_id=1, source_target_pairs={{0,124},{4,8},{8,4},{12,16},{16,12},{20,24},{24,20},{28,32},{32,28... | collective-permute-start | bytes 294920 | tf_op jit(solution)/shard_map/ppermute | solution.py:550
  8.7 6.9 %collective-permute-start.2 = (f32[48,256]{1,0:T(8,128)S(1)}, f32[48,256]{1,0:T(8,128)S(1)}, u32[]{:S(2)}, u32[]{:S(2)}) collective-permute-start(f32[48,256]{1,0:T(8,128)S(1)} %get-tuple-element.136), channel_id=1, source_target_pairs={{0,1},{1,0},{2,3},{3,2},{4,5},{5,4},{6,7},{7,6},{8,9},{9,8},{10,11... | collective-permute-start | bytes 147464 | tf_op jit(solution)/shard_map/ppermute | solution.py:545
  10.3 5.3 %collective-permute-start.3 = (f32[48,256]{1,0:T(8,128)S(1)}, f32[48,256]{1,0:T(8,128)S(1)}, u32[]{:S(2)}, u32[]{:S(2)}) collective-permute-start(f32[48,256]{1,0:T(8,128)S(1)} %get-tuple-element.137), channel_id=1, source_target_pairs={{0,3},{1,2},{2,1},{3,0},{4,7},{5,6},{6,5},{7,4},{8,11},{9,10},{10,... | collective-permute-start | bytes 147464 | tf_op jit(solution)/shard_map/ppermute | solution.py:550
  16.1 7.5 %collective-permute-start.4 = (f32[48,512]{1,0:T(8,128)S(1)}, f32[48,512]{1,0:T(8,128)S(1)}, u32[]{:S(2)}, u32[]{:S(2)}) collective-permute-start(f32[48,512]{1,0:T(8,128)S(1)} %get-tuple-element.151), channel_id=1, source_target_pairs={{0,4},{4,0},{8,12},{12,8},{16,20},{20,16},{24,28},{28,24},{32,36},... | collective-permute-start | bytes 294920 | tf_op jit(solution)/shard_map/ppermute | solution.py:545
  16.2 7.4 %collective-permute-start.5 = (f32[48,512]{1,0:T(8,128)S(1)}, f32[48,512]{1,0:T(8,128)S(1)}, u32[]{:S(2)}, u32[]{:S(2)}) collective-permute-start(f32[48,512]{1,0:T(8,128)S(1)} %get-tuple-element.152), channel_id=1, source_target_pairs={{0,124},{4,8},{8,4},{12,16},{16,12},{20,24},{24,20},{28,32},{32,28... | collective-permute-start | bytes 294920 | tf_op jit(solution)/shard_map/ppermute | solution.py:550
  17.2 6.0 %collective-permute-start.6 = (f32[48,256]{1,0:T(8,128)S(1)}, f32[48,256]{1,0:T(8,128)S(1)}, u32[]{:S(2)}, u32[]{:S(2)}) collective-permute-start(f32[48,256]{1,0:T(8,128)S(1)} %get-tuple-element.153), channel_id=1, source_target_pairs={{0,1},{1,0},{2,3},{3,2},{4,5},{5,4},{6,7},{7,6},{8,9},{9,8},{10,11... | collective-permute-start | bytes 147464 | tf_op jit(solution)/shard_map/ppermute | solution.py:545
  18.3 5.3 %collective-permute-start.7 = (f32[48,256]{1,0:T(8,128)S(1)}, f32[48,256]{1,0:T(8,128)S(1)}, u32[]{:S(2)}, u32[]{:S(2)}) collective-permute-start(f32[48,256]{1,0:T(8,128)S(1)} %get-tuple-element.154), channel_id=1, source_target_pairs={{0,3},{1,2},{2,1},{3,0},{4,7},{5,6},{6,5},{7,4},{8,11},{9,10},{10,... | collective-permute-start | bytes 147464 | tf_op jit(solution)/shard_map/ppermute | solution.py:550
  20.5 24.2 %copy-start = (f32[1,32,32,24,24]{2,4,3,1,0:T(8,128)S(1)}, f32[1,32,32,24,24]{2,4,3,1,0:T(8,128)}, u32[]{:S(2)}) copy-start(f32[1,32,32,24,24]{2,4,3,1,0:T(8,128)} %param.18) | copy-start | bytes 7077892
  24.1 8.9 %collective-permute-start.8 = (f32[48,512]{1,0:T(8,128)S(1)}, f32[48,512]{1,0:T(8,128)S(1)}, u32[]{:S(2)}, u32[]{:S(2)}) collective-permute-start(f32[48,512]{1,0:T(8,128)S(1)} %get-tuple-element.170), channel_id=1, source_target_pairs={{0,4},{4,0},{8,12},{12,8},{16,20},{20,16},{24,28},{28,24},{32,36},... | collective-permute-start | bytes 294920 | tf_op jit(solution)/shard_map/ppermute | solution.py:545
  24.2 8.8 %collective-permute-start.9 = (f32[48,512]{1,0:T(8,128)S(1)}, f32[48,512]{1,0:T(8,128)S(1)}, u32[]{:S(2)}, u32[]{:S(2)}) collective-permute-start(f32[48,512]{1,0:T(8,128)S(1)} %get-tuple-element.171), channel_id=1, source_target_pairs={{0,124},{4,8},{8,4},{12,16},{16,12},{20,24},{24,20},{28,32},{32,28... | collective-permute-start | bytes 294920 | tf_op jit(solution)/shard_map/ppermute | solution.py:550
  26.6 4.6 %collective-permute-start.10 = (f32[48,256]{1,0:T(8,128)S(1)}, f32[48,256]{1,0:T(8,128)S(1)}, u32[]{:S(2)}, u32[]{:S(2)}) collective-permute-start(f32[48,256]{1,0:T(8,128)S(1)} %get-tuple-element.172), channel_id=1, source_target_pairs={{0,1},{1,0},{2,3},{3,2},{4,5},{5,4},{6,7},{7,6},{8,9},{9,8},{10,11... | collective-permute-start | bytes 147464 | tf_op jit(solution)/shard_map/ppermute | solution.py:545
  27.7 5.3 %collective-permute-start.11 = (f32[48,256]{1,0:T(8,128)S(1)}, f32[48,256]{1,0:T(8,128)S(1)}, u32[]{:S(2)}, u32[]{:S(2)}) collective-permute-start(f32[48,256]{1,0:T(8,128)S(1)} %get-tuple-element.173), channel_id=1, source_target_pairs={{0,3},{1,2},{2,1},{3,0},{4,7},{5,6},{6,5},{7,4},{8,11},{9,10},{10,... | collective-permute-start | bytes 147464 | tf_op jit(solution)/shard_map/ppermute | solution.py:550
  57.6 7.9 %collective-permute-start.12 = (f32[48,512]{1,0:T(8,128)S(1)}, f32[48,512]{1,0:T(8,128)S(1)}, u32[]{:S(2)}, u32[]{:S(2)}) collective-permute-start(f32[48,512]{1,0:T(8,128)S(1)} %get-tuple-element.186), channel_id=1, source_target_pairs={{0,4},{4,0},{8,12},{12,8},{16,20},{20,16},{24,28},{28,24},{32,36},... | collective-permute-start | bytes 294920 | tf_op jit(solution)/shard_map/ppermute | solution.py:545
  57.8 7.7 %collective-permute-start.13 = (f32[48,512]{1,0:T(8,128)S(1)}, f32[48,512]{1,0:T(8,128)S(1)}, u32[]{:S(2)}, u32[]{:S(2)}) collective-permute-start(f32[48,512]{1,0:T(8,128)S(1)} %get-tuple-element.187), channel_id=1, source_target_pairs={{0,124},{4,8},{8,4},{12,16},{16,12},{20,24},{24,20},{28,32},{32,28... | collective-permute-start | bytes 294920 | tf_op jit(solution)/shard_map/ppermute | solution.py:550
  59.6 4.1 %collective-permute-start.14 = (f32[48,256]{1,0:T(8,128)S(1)}, f32[48,256]{1,0:T(8,128)S(1)}, u32[]{:S(2)}, u32[]{:S(2)}) collective-permute-start(f32[48,256]{1,0:T(8,128)S(1)} %get-tuple-element.188), channel_id=1, source_target_pairs={{0,1},{1,0},{2,3},{3,2},{4,5},{5,4},{6,7},{7,6},{8,9},{9,8},{10,11... | collective-permute-start | bytes 147464 | tf_op jit(solution)/shard_map/ppermute | solution.py:545
  60.2 5.3 %collective-permute-start.15 = (f32[48,256]{1,0:T(8,128)S(1)}, f32[48,256]{1,0:T(8,128)S(1)}, u32[]{:S(2)}, u32[]{:S(2)}) collective-permute-start(f32[48,256]{1,0:T(8,128)S(1)} %get-tuple-element.189), channel_id=1, source_target_pairs={{0,3},{1,2},{2,1},{3,0},{4,7},{5,6},{6,5},{7,4},{8,11},{9,10},{10,... | collective-permute-start | bytes 147464 | tf_op jit(solution)/shard_map/ppermute | solution.py:550
  65.9 7.5 %collective-permute-start.16 = (f32[48,512]{1,0:T(8,128)S(1)}, f32[48,512]{1,0:T(8,128)S(1)}, u32[]{:S(2)}, u32[]{:S(2)}) collective-permute-start(f32[48,512]{1,0:T(8,128)S(1)} %get-tuple-element.202), channel_id=1, source_target_pairs={{0,4},{4,0},{8,12},{12,8},{16,20},{20,16},{24,28},{28,24},{32,36},... | collective-permute-start | bytes 294920 | tf_op jit(solution)/shard_map/ppermute | solution.py:545
  66.0 7.4 %collective-permute-start.17 = (f32[48,512]{1,0:T(8,128)S(1)}, f32[48,512]{1,0:T(8,128)S(1)}, u32[]{:S(2)}, u32[]{:S(2)}) collective-permute-start(f32[48,512]{1,0:T(8,128)S(1)} %get-tuple-element.203), channel_id=1, source_target_pairs={{0,124},{4,8},{8,4},{12,16},{16,12},{20,24},{24,20},{28,32},{32,28... | collective-permute-start | bytes 294920 | tf_op jit(solution)/shard_map/ppermute | solution.py:550
  67.9 4.4 %collective-permute-start.18 = (f32[48,256]{1,0:T(8,128)S(1)}, f32[48,256]{1,0:T(8,128)S(1)}, u32[]{:S(2)}, u32[]{:S(2)}) collective-permute-start(f32[48,256]{1,0:T(8,128)S(1)} %get-tuple-element.204), channel_id=1, source_target_pairs={{0,1},{1,0},{2,3},{3,2},{4,5},{5,4},{6,7},{7,6},{8,9},{9,8},{10,11... | collective-permute-start | bytes 147464 | tf_op jit(solution)/shard_map/ppermute | solution.py:545
  68.2 5.3 %collective-permute-start.19 = (f32[48,256]{1,0:T(8,128)S(1)}, f32[48,256]{1,0:T(8,128)S(1)}, u32[]{:S(2)}, u32[]{:S(2)}) collective-permute-start(f32[48,256]{1,0:T(8,128)S(1)} %get-tuple-element.205), channel_id=1, source_target_pairs={{0,3},{1,2},{2,1},{3,0},{4,7},{5,6},{6,5},{7,4},{8,11},{9,10},{10,... | collective-permute-start | bytes 147464 | tf_op jit(solution)/shard_map/ppermute | solution.py:550
  73.9 8.1 %collective-permute-start.20 = (f32[48,512]{1,0:T(8,128)S(1)}, f32[48,512]{1,0:T(8,128)S(1)}, u32[]{:S(2)}, u32[]{:S(2)}) collective-permute-start(f32[48,512]{1,0:T(8,128)S(1)} %get-tuple-element.218), channel_id=1, source_target_pairs={{0,4},{4,0},{8,12},{12,8},{16,20},{20,16},{24,28},{28,24},{32,36},... | collective-permute-start | bytes 294920 | tf_op jit(solution)/shard_map/ppermute | solution.py:545
  74.0 8.0 %collective-permute-start.21 = (f32[48,512]{1,0:T(8,128)S(1)}, f32[48,512]{1,0:T(8,128)S(1)}, u32[]{:S(2)}, u32[]{:S(2)}) collective-permute-start(f32[48,512]{1,0:T(8,128)S(1)} %get-tuple-element.219), channel_id=1, source_target_pairs={{0,124},{4,8},{8,4},{12,16},{16,12},{20,24},{24,20},{28,32},{32,28... | collective-permute-start | bytes 294920 | tf_op jit(solution)/shard_map/ppermute | solution.py:550
  76.2 4.7 %collective-permute-start.22 = (f32[48,256]{1,0:T(8,128)S(1)}, f32[48,256]{1,0:T(8,128)S(1)}, u32[]{:S(2)}, u32[]{:S(2)}) collective-permute-start(f32[48,256]{1,0:T(8,128)S(1)} %get-tuple-element.220), channel_id=1, source_target_pairs={{0,1},{1,0},{2,3},{3,2},{4,5},{5,4},{6,7},{7,6},{8,9},{9,8},{10,11... | collective-permute-start | bytes 147464 | tf_op jit(solution)/shard_map/ppermute | solution.py:545
  76.7 5.3 %collective-permute-start.23 = (f32[48,256]{1,0:T(8,128)S(1)}, f32[48,256]{1,0:T(8,128)S(1)}, u32[]{:S(2)}, u32[]{:S(2)}) collective-permute-start(f32[48,256]{1,0:T(8,128)S(1)} %get-tuple-element.221), channel_id=1, source_target_pairs={{0,3},{1,2},{2,1},{3,0},{4,7},{5,6},{6,5},{7,4},{8,11},{9,10},{10,... | collective-permute-start | bytes 147464 | tf_op jit(solution)/shard_map/ppermute | solution.py:550
  82.5 7.9 %collective-permute-start.24 = (f32[48,512]{1,0:T(8,128)S(1)}, f32[48,512]{1,0:T(8,128)S(1)}, u32[]{:S(2)}, u32[]{:S(2)}) collective-permute-start(f32[48,512]{1,0:T(8,128)S(1)} %get-tuple-element.232), channel_id=1, source_target_pairs={{0,4},{4,0},{8,12},{12,8},{16,20},{20,16},{24,28},{28,24},{32,36},... | collective-permute-start | bytes 294920 | tf_op jit(solution)/shard_map/ppermute | solution.py:545
  82.6 7.8 %collective-permute-start.25 = (f32[48,512]{1,0:T(8,128)S(1)}, f32[48,512]{1,0:T(8,128)S(1)}, u32[]{:S(2)}, u32[]{:S(2)}) collective-permute-start(f32[48,512]{1,0:T(8,128)S(1)} %get-tuple-element.233), channel_id=1, source_target_pairs={{0,124},{4,8},{8,4},{12,16},{16,12},{20,24},{24,20},{28,32},{32,28... | collective-permute-start | bytes 294920 | tf_op jit(solution)/shard_map/ppermute | solution.py:550
  84.4 4.4 %collective-permute-start.26 = (f32[48,256]{1,0:T(8,128)S(1)}, f32[48,256]{1,0:T(8,128)S(1)}, u32[]{:S(2)}, u32[]{:S(2)}) collective-permute-start(f32[48,256]{1,0:T(8,128)S(1)} %get-tuple-element.234), channel_id=1, source_target_pairs={{0,1},{1,0},{2,3},{3,2},{4,5},{5,4},{6,7},{7,6},{8,9},{9,8},{10,11... | collective-permute-start | bytes 147464 | tf_op jit(solution)/shard_map/ppermute | solution.py:545
  85.1 5.3 %collective-permute-start.27 = (f32[48,256]{1,0:T(8,128)S(1)}, f32[48,256]{1,0:T(8,128)S(1)}, u32[]{:S(2)}, u32[]{:S(2)}) collective-permute-start(f32[48,256]{1,0:T(8,128)S(1)} %get-tuple-element.235), channel_id=1, source_target_pairs={{0,3},{1,2},{2,1},{3,0},{4,7},{5,6},{6,5},{7,4},{8,11},{9,10},{10,... | collective-permute-start | bytes 147464 | tf_op jit(solution)/shard_map/ppermute | solution.py:550
